TPU v7x, 512 devices: a whole 4x8x8 slice. The times are simulated.
512 devices in a mesh: group: 2 (over core), dp: 64 (over y, x, z_hi), mp: 4 (over z_lo).
Axes of the slice: x: 4, y: 8, z: 8 (z_hi: 2, z_lo: 4; z = z_hi * 4 + z_lo), core: 2. Of those that a mesh axis runs over, the one named last changes fastest.
Arguments:
- x_arrive: bfloat16 [256, 256, 1152], P(('group', 'dp')), may hold values from -6 to 6
- cond_first: int32 [128], P(('group', 'dp')), may hold values 0 or 1
- labels: int32 [128], P(('group', 'dp')), may hold values from 0 to 999
- step_ids: int32 [128], P(('group', 'dp')), may hold values from 0 to 999
- guidance: float32 [1], replicated, may hold values from 2 to 6
- time_table: bfloat16 [1000, 1152], P(None, 'mp'), may hold values from -6 to 6
- class_table: bfloat16 [1001, 1152], P(None, 'mp'), may hold values from -6 to 6
- ada_weight: bfloat16 [1152, 6912], P('mp', 'dp'), may hold values from -0.1875 to 0.1875
- final_ada: bfloat16 [1152, 2304], P('mp'), may hold values from -0.1875 to 0.1875
- qkv_weight: bfloat16 [3, 1152, 1152], P(None, 'dp', 'mp'), may hold values from -2 to 2
- proj_weight: bfloat16 [1152, 1152], P('mp', 'dp'), may hold values from -0.1875 to 0.1875
- fc1_weight: bfloat16 [1152, 4608], P('dp', 'mp'), may hold values from -0.1875 to 0.1875
- fc2_weight: bfloat16 [4608, 1152], P('mp', 'dp'), may hold values from -0.09375 to 0.09375
- out_weight: bfloat16 [1152, 16], replicated, may hold values from -0.1875 to 0.1875
Outputs:
- guided: float32 [128, 4096], P(('group', 'dp'), 'mp')
All inputs are finite; a program needn't handle non-finite values. No bound on the sum of `cond_first` on one device may be relied on, other than what follows from the above.
Results may differ from a plain program's by a relative error of at most 0.025.
Values may be sent and summed in bfloat16 or wider, within the bound.
No kernel may reach another device: no remote copies, remote signals or barrier semaphores. Data moves between devices by JAX's collectives and lax.ppermute only.
A program may use at most 64 MiB of HBM per device.

v0:
```python
import jax
import jax.numpy as jnp
from jax import lax
from jax.sharding import Mesh
from jax.sharding import PartitionSpec as P

HEADS = 16
CLASSES = 1000
DP = ("dp_0", "dp_1", "dp_2")
GROUP_DP = ("group", "dp_0", "dp_1", "dp_2")


def from_everyone(x, axis):
    size = lax.axis_size(axis)
    return lax.all_to_all(jnp.broadcast_to(x[None], (size, *x.shape)), axis, 0, 0, tiled=True)


def laid_out(pieces, dim):
    pieces = jnp.moveaxis(pieces, 0, dim)
    shape = pieces.shape
    return pieces.reshape(*shape[:dim], shape[dim] * shape[dim + 1], *shape[dim + 2 :])


def collect(x, axis, dim):
    pieces = from_everyone(x, axis)
    return laid_out(pieces, dim)


def of_everyone(x, axis):
    everything = from_everyone(x, axis)
    return jnp.sum(everything.astype(jnp.float32), axis=0)


def gathered_by_axis(x, axes, dim):
    for axis in reversed(axes):
        x = lax.all_gather(x, axis, axis=dim, tiled=True)
    return x


def cut_along(x, dim, size):
    shape = x.shape
    pieces = x.reshape(*shape[:dim], size, shape[dim] // size, *shape[dim + 1 :])
    return jnp.moveaxis(pieces, dim, 0)


def sum_at_owner(x, axis, dim):
    size = lax.axis_size(axis)
    pieces = lax.all_to_all(cut_along(x, dim, size), axis, 0, 0, tiled=True)
    return jnp.sum(pieces.astype(jnp.float32), axis=0)


def layer_norm(values):
    mean = jnp.mean(values, axis=-1, keepdims=True)
    centred = values - mean
    spread = jnp.mean(centred * centred, axis=-1, keepdims=True)
    return centred * lax.rsqrt(spread + 1e-06)


def on_device(
    x_arrive,
    cond_first,
    labels,
    step_ids,
    guidance,
    time_table,
    class_table,
    ada_weight,
    final_ada,
    qkv_weight,
    proj_weight,
    fc1_weight,
    fc2_weight,
    out_weight,
):
    pair_count = labels.shape[0]
    tokens = x_arrive.shape[1]
    width = x_arrive.shape[2]
    image_count = 2 * pair_count
    row_count = image_count * tokens
    split_rows = x_arrive.reshape(pair_count, 2, tokens, width)
    first = (cond_first == 1)[:, None, None]
    cond_rows = jnp.where(first, split_rows[:, 0], split_rows[:, 1])
    uncond_rows = jnp.where(first, split_rows[:, 1], split_rows[:, 0])
    x_sides = jnp.stack([cond_rows, uncond_rows])
    time_part = jnp.take(time_table, step_ids, axis=0).astype(jnp.float32)
    class_part = jnp.take(class_table, labels, axis=0).astype(jnp.float32)
    null_part = class_table[CLASSES].astype(jnp.float32)[None, :]
    emb_sides = time_part[None] + jnp.stack([class_part, null_part])
    act_sides = jax.nn.silu(emb_sides).astype(jnp.bfloat16)
    images, acts = (x_sides, act_sides)
    images = images.reshape(image_count, tokens, width)
    acts = acts.reshape(image_count, act_sides.shape[2])
    partial_final = jnp.dot(acts, final_ada, preferred_element_type=jnp.float32)
    every_act = collect(acts, DP, 0)
    column_part = jnp.dot(every_act, ada_weight, preferred_element_type=jnp.float32)
    summed, fmods = (
        of_everyone(column_part.astype(jnp.bfloat16), "mp").astype(jnp.float32),
        of_everyone(partial_final.astype(jnp.bfloat16), "mp").astype(jnp.float32),
    )
    mods = lax.all_to_all(
        summed.astype(jnp.bfloat16), DP, split_axis=0, concat_axis=1, tiled=True
    ).astype(summed.dtype)
    shift_a, scale_a, gate_a, shift_m, scale_m, gate_m = jnp.split(mods, 6, axis=1)
    shift_f, scale_f = jnp.split(fmods, 2, axis=1)
    images_f = images.astype(jnp.float32)
    hidden = (layer_norm(images_f) * (1.0 + scale_a[:, None]) + shift_a[:, None]).astype(
        jnp.bfloat16
    )
    hidden = hidden.reshape(row_count, width)
    quarter = qkv_weight.shape[2]
    head_dim = width // HEADS
    local_heads = quarter // head_dim
    columns = hidden
    qkv = jnp.einsum(
        "rd,kdc->krc",
        columns,
        lax.all_gather(qkv_weight, DP, axis=1, tiled=True),
        preferred_element_type=jnp.float32,
    ).astype(jnp.bfloat16)
    query = qkv[0].reshape(image_count, tokens, local_heads, head_dim)
    keys = qkv[1].reshape(image_count, tokens, local_heads, head_dim)
    values = qkv[2].reshape(image_count, tokens, local_heads, head_dim)
    scores = jnp.einsum(
        "bqhe,bkhe->bhqk", query, keys, preferred_element_type=jnp.float32
    ) * head_dim ** (-0.5)
    probs = jax.nn.softmax(scores, axis=-1).astype(jnp.bfloat16)
    mixed = jnp.einsum("bhqk,bkhe->bqhe", probs, values, preferred_element_type=jnp.float32).astype(
        jnp.bfloat16
    )
    mixed = mixed.reshape(row_count, quarter)
    attn_part = jnp.dot(mixed, collect(proj_weight, DP, 1), preferred_element_type=jnp.float32)
    attn = (
        lax.psum(attn_part.astype(jnp.bfloat16), "mp")
        .astype(jnp.float32)
        .reshape(image_count, tokens, width)
    )
    first_sum = images_f + gate_a[:, None] * attn
    hidden_two = (layer_norm(first_sum) * (1.0 + scale_m[:, None]) + shift_m[:, None]).astype(
        jnp.bfloat16
    )
    hidden_two = hidden_two.reshape(row_count, width)
    ff_quarter = fc1_weight.shape[1]
    columns = hidden_two
    up = jnp.dot(columns, gathered_by_axis(fc1_weight, DP, 0), preferred_element_type=jnp.float32)
    gelu_h = (
        jax.nn.gelu(up, approximate=True)
        .astype(jnp.bfloat16)
        .reshape(image_count, tokens, ff_quarter)
    )
    down_full = gathered_by_axis(fc2_weight, DP, 1)
    token_share = tokens // lax.axis_size("mp")
    mlp = sum_at_owner(
        jnp.einsum("btf,fd->tbd", gelu_h, down_full, preferred_element_type=jnp.float32).astype(
            jnp.bfloat16
        ),
        "mp",
        0,
    )
    token_start = lax.axis_index("mp") * token_share
    own_first = lax.dynamic_slice_in_dim(first_sum, token_start, token_share, 1).transpose(1, 0, 2)
    second_sum = own_first + gate_m[None] * mlp
    fin = (layer_norm(second_sum) * (1.0 + scale_f[None]) + shift_f[None]).astype(jnp.bfloat16)
    noise = jnp.einsum("tbd,do->bto", fin, out_weight, preferred_element_type=jnp.float32)
    noise = noise.reshape(2, pair_count, token_share * out_weight.shape[1])
    return noise[1] + guidance[0] * (noise[0] - noise[1])


def solution(mesh):
    torus = Mesh(
        mesh.devices.reshape(mesh.shape["group"], 8, 4, 2, mesh.shape["mp"]),
        ("group", "dp_0", "dp_1", "dp_2", "mp"),
    )
    placed = (
        P(GROUP_DP, None, None),
        P(GROUP_DP),
        P(GROUP_DP),
        P(GROUP_DP),
        P(),
        P(None, "mp"),
        P(None, "mp"),
        P("mp", DP),
        P("mp", None),
        P(None, DP, "mp"),
        P("mp", DP),
        P(DP, "mp"),
        P("mp", DP),
        P(),
    )
    return jax.shard_map(
        on_device, mesh=torus, in_specs=placed, out_specs=P(GROUP_DP, "mp"), check_vma=False
    )
```

profile of v0, /device:TPU:6, one launch (start us, length us, event | category | flops | bytes accessed | tf_op | source)
XLA Modules:
  0.0 341.8 jit_solution(6708045404015547400)
XLA Ops:
  7.4 1.6 copy.106
  13.9 19.2 %all-to-all-start = ((bf16[64,2,288]{2,1,0:T(2,128)(2,1)}), bf16[64,2,288]{2,1,0:T(2,128)(2,1)S(1)}, u32[]{:S(2)}, u32[]{:S(2)}) async-start(bf16[64,2,288]{2,1,0:T(2,128)(2,1)} %broadcast_in_dim.50), calls=%async_computation | async-start | bytes 196608 | tf_op jit(solution)/shard_map/all_to_all | solution.py:15
  33.8 12.2 %all-to-all-done = bf16[64,2,288]{2,1,0:T(2,128)(2,1)S(1)} async-done(((bf16[64,2,288]{2,1,0:T(2,128)(2,1)}), bf16[64,2,288]{2,1,0:T(2,128)(2,1)S(1)}, u32[]{:S(2)}, u32[]{:S(2)}) %all-to-all-start) | async-done | bytes 73760 | tf_op jit(solution)/shard_map/all_to_all | solution.py:15
  47.8 4.5 %all-to-all-start.1 = ((bf16[4,128,108]{1,2,0:T(8,128)(2,1)}), bf16[4,128,108]{1,2,0:T(8,128)(2,1)S(1)}, u32[]{:S(2)}, u32[]{:S(2)}) async-start(bf16[4,128,108]{1,2,0:T(8,128)(2,1)} %broadcast_in_dim.84), calls=%async_computation.1 | async-start | bytes 229376 | tf_op jit(solution)/shard_map/all_to_all | solution.py:15
  53.7 4.5 %all-to-all-done.1 = bf16[4,128,108]{1,2,0:T(8,128)(2,1)S(1)} async-done(((bf16[4,128,108]{1,2,0:T(8,128)(2,1)}), bf16[4,128,108]{1,2,0:T(8,128)(2,1)S(1)}, u32[]{:S(2)}, u32[]{:S(2)}) %all-to-all-start.1) | async-done | bytes 110624 | tf_op jit(solution)/shard_map/all_to_all | solution.py:15
  58.9 6.4 %all-to-all-start.2 = ((bf16[64,2,108]{2,1,0:T(2,128)(2,1)}), bf16[64,2,108]{2,1,0:T(2,128)(2,1)S(1)}, u32[]{:S(2)}, u32[]{:S(2)}) async-start(bf16[64,2,108]{2,1,0:T(2,128)(2,1)} %bitcast.7), calls=%async_computation.2 | async-start | bytes 65536 | tf_op jit(solution)/shard_map/all_to_all | solution.py:100
  65.5 12.5 %all-to-all-done.2 = bf16[64,2,108]{2,1,0:T(2,128)(2,1)S(1)} async-done(((bf16[64,2,108]{2,1,0:T(2,128)(2,1)}), bf16[64,2,108]{2,1,0:T(2,128)(2,1)S(1)}, u32[]{:S(2)}, u32[]{:S(2)}) %all-to-all-start.2) | async-done | bytes 27680 | tf_op jit(solution)/shard_map/all_to_all | solution.py:100
  79.1 7.1 %all-to-all-start.3 = ((bf16[64,288,18]{1,2,0:T(8,128)(2,1)}), bf16[64,288,18]{1,2,0:T(8,128)(2,1)}, u32[]{:S(2)}, u32[]{:S(2)}) async-start(bf16[64,288,18]{1,2,0:T(8,128)(2,1)} %broadcast_in_dim.85), calls=%async_computation.3 | async-start | bytes 2359296 | tf_op jit(solution)/shard_map/all_to_all | solution.py:15
  87.0 1.7 fusion.16
  88.7 31.2 %all-to-all-done.3 = bf16[64,288,18]{1,2,0:T(8,128)(2,1)} async-done(((bf16[64,288,18]{1,2,0:T(8,128)(2,1)}), bf16[64,288,18]{1,2,0:T(8,128)(2,1)}, u32[]{:S(2)}, u32[]{:S(2)}) %all-to-all-start.3) | async-done | bytes 663584 | tf_op jit(solution)/shard_map/all_to_all | solution.py:15
  119.9 1.6 reshape.262
  121.5 51.2 %all-gather.8.cloned.1.call-done = bf16[3,1152,288]{2,0,1:T(4,128)(2,1)} async-done(((bf16[3,18,288]{2,0,1:T(4,128)(2,1)}), bf16[3,1152,288]{2,0,1:T(4,128)(2,1)}) %all-gather.8.cloned.1.call-update) | async-done | bytes 1990672 | tf_op jit(solution)/shard_map/all_gather | solution.py:117
  172.8 3.7 %fusion.26 = bf16[3,512,288]{1,2,0:T(8,128)(2,1)S(1)} fusion(bf16[3,1152,288]{2,0,1:T(4,128)(2,1)} %all-gather.8.cloned.1.call-done, bf16[512,1152]{1,0:T(8,128)(2,1)} %fusion.16), kind=kOutput, calls=%fused_computation.41 | convolution fusion | flops 1019658240 | bytes 4055040 | tf_op jit(solution)/shard_map/rd,kdc->krc/dot_general | solution.py:114
  177.5 1.7 reshape_squeeze.10
  179.2 1.7 reshape_squeeze.11
  180.9 1.8 reshape_squeeze.9
  182.7 3.2 fusion.65
  185.9 2.0 fusion.30
  188.3 2.0 convolution_convert_fusion.2
  190.4 9.3 %all-gather = bf16[2,18,1152]{2,1,0:T(8,128)(2,1)S(1)} all-gather(bf16[1,18,1152]{2,1,0:T(8,128)(2,1)S(1)} %bitcast.125), channel_id=1, replica_groups=mesh['group'=2,'dp_0'=8,'dp_1'=4,'dp_2'=2,'mp'=4] {'dp_2'}, dimensions={0}, use_global_device_ids=true | all-gather | bytes 124416 | tf_op jit(solution)/shard_map/all_gather | solution.py:36
  199.7 12.7 %all-gather.1 = bf16[4,36,1152]{2,1,0:T(8,128)(2,1)S(1)} all-gather(bf16[1,36,1152]{2,1,0:T(8,128)(2,1)S(1)} %reshape.323), channel_id=1, replica_groups=mesh['group'=2,'dp_0'=8,'dp_1'=4,'dp_2'=2,'mp'=4] {'dp_1'}, dimensions={0}, use_global_device_ids=true | all-gather | bytes 414720 | tf_op jit(solution)/shard_map/all_gather | solution.py:36
  213.3 10.3 %all-gather.2 = bf16[2,18,1152]{2,1,0:T(8,128)(2,1)S(1)} all-gather(bf16[1,18,1152]{2,1,0:T(8,128)(2,1)S(1)} %bitcast.126), channel_id=1, replica_groups=mesh['group'=2,'dp_0'=8,'dp_1'=4,'dp_2'=2,'mp'=4] {'dp_2'}, dimensions={0}, use_global_device_ids=true | all-gather | bytes 124416 | tf_op jit(solution)/shard_map/all_gather | solution.py:36
  223.6 12.5 %all-gather.3 = bf16[4,36,1152]{2,1,0:T(8,128)(2,1)S(1)} all-gather(bf16[1,36,1152]{2,1,0:T(8,128)(2,1)S(1)} %reshape.327), channel_id=1, replica_groups=mesh['group'=2,'dp_0'=8,'dp_1'=4,'dp_2'=2,'mp'=4] {'dp_1'}, dimensions={0}, use_global_device_ids=true | all-gather | bytes 414720 | tf_op jit(solution)/shard_map/all_gather | solution.py:36
  237.9 3.4 %all-to-all-start.5 = ((bf16[4,2,2304]{2,1,0:T(2,128)(2,1)}), bf16[4,2,2304]{2,1,0:T(2,128)(2,1)S(1)}, u32[]{:S(2)}, u32[]{:S(2)}) async-start(bf16[4,2,2304]{2,1,0:T(2,128)(2,1)} %broadcast_in_dim.86), calls=%async_computation.5 | async-start | bytes 73728 | tf_op jit(solution)/shard_map/all_to_all | solution.py:15
  241.4 19.6 %all-reduce.2.cloned.1.call-done = bf16[512,1152]{1,0:T(8,128)(2,1)} async-done(((bf16[512,1152]{1,0:T(8,128)(2,1)}), bf16[512,1152]{1,0:T(8,128)(2,1)}) %all-reduce.2.cloned.1.call-update) | async-done | bytes 1179664 | tf_op jit(solution)/shard_map/psum | solution.py:133
  261.0 1.7 fusion.60
  264.9 2.0 fusion.12
  266.9 4.0 %fusion.11 = bf16[512,1152]{1,0:T(8,128)(2,1)S(1)} fusion(bf16[512,1152]{1,0:T(8,128)(2,1)} %fusion.12, bf16[1152,1152]{1,0:T(8,128)(2,1)} %all-gather.10.cloned.1.call-done), kind=kOutput, calls=%fused_computation.15 | convolution fusion | flops 1364262912 | bytes 5013504 | tf_op jit(solution)/shard_map/dot_general | solution.py:144
  270.9 25.6 %all-gather.12.cloned.1.call-done = bf16[1152,1152]{0,1:T(8,128)(2,1)} async-done(((bf16[1152,144]{0,1:T(8,128)(2,1)}), bf16[1152,1152]{0,1:T(8,128)(2,1)}) %all-gather.12.cloned.1.call-update) | async-done | bytes 2654224 | tf_op jit(solution)/shard_map/all_gather | solution.py:36
  296.5 3.6 %convolution_convert_fusion.1 = bf16[2,256,1152]{2,1,0:T(8,128)(2,1)S(1)} fusion(bf16[2,256,1152]{2,1,0:T(8,128)(2,1)S(1)} %bitcast.131, bf16[1152,1152]{0,1:T(8,128)(2,1)} %all-gather.12.cloned.1.call-done), kind=kOutput, calls=%fused_computation.3 | convolution fusion | flops 1359544320 | bytes 5013504 | tf_op jit(solution)/shard_map/btf,fd->tbd/dot_general | solution.py:153
  301.2 5.1 %all-to-all-start.4 = ((bf16[4,64,2,1152]{3,1,2,0:T(8,128)(2,1)}), bf16[4,64,2,1152]{3,1,2,0:T(8,128)(2,1)S(1)}, u32[]{:S(2)}, u32[]{:S(2)}) async-start(bf16[4,64,2,1152]{3,1,2,0:T(8,128)(2,1)} %copy.113), calls=%async_computation.4 | async-start | bytes 2359296 | tf_op jit(solution)/shard_map/all_to_all | solution.py:48
  307.0 24.5 %all-to-all-done.4 = bf16[4,64,2,1152]{3,1,2,0:T(8,128)(2,1)S(1)} async-done(((bf16[4,64,2,1152]{3,1,2,0:T(8,128)(2,1)}), bf16[4,64,2,1152]{3,1,2,0:T(8,128)(2,1)S(1)}, u32[]{:S(2)}, u32[]{:S(2)}) %all-to-all-start.4) | async-done | bytes 1179680 | tf_op jit(solution)/shard_map/all_to_all | solution.py:48
  (83 shorter events, 19.9 us)
Async XLA Ops:
  7.4 229.6 %copy-start = (bf16[288,2304]{1,0:T(8,128)(2,1)S(1)}, bf16[288,2304]{1,0:T(8,128)(2,1)}, u32[]{:S(2)}) copy-start(bf16[288,2304]{1,0:T(8,128)(2,1)} %param.22) | copy-start | bytes 3981316
  7.4 165.4 %all-gather.8.cloned.1.call-start = ((), (), s32[]{:S(2)}) async-start(), calls=%async_computation.6 | async-start | bytes 3594240 | tf_op jit(solution)/shard_map/all_gather | solution.py:117
  12.7 0.6 copy-start.6
  13.9 64.1 %copy-start.5 = (bf16[288,18]{0,1:T(8,128)(2,1)S(1)}, bf16[288,18]{0,1:T(8,128)(2,1)}, u32[]{:S(2)}) copy-start(bf16[288,18]{0,1:T(8,128)(2,1)} %param.24) | copy-start | bytes 31108
  13.9 32.0 %all-to-all-start = ((bf16[64,2,288]{2,1,0:T(2,128)(2,1)}), bf16[64,2,288]{2,1,0:T(2,128)(2,1)S(1)}, u32[]{:S(2)}, u32[]{:S(2)}) async-start(bf16[64,2,288]{2,1,0:T(2,128)(2,1)} %broadcast_in_dim.50), calls=%async_computation | async-start | bytes 196608 | tf_op jit(solution)/shard_map/all_to_all | solution.py:15
  47.8 10.4 %all-to-all-start.1 = ((bf16[4,128,108]{1,2,0:T(8,128)(2,1)}), bf16[4,128,108]{1,2,0:T(8,128)(2,1)S(1)}, u32[]{:S(2)}, u32[]{:S(2)}) async-start(bf16[4,128,108]{1,2,0:T(8,128)(2,1)} %broadcast_in_dim.84), calls=%async_computation.1 | async-start | bytes 229376 | tf_op jit(solution)/shard_map/all_to_all | solution.py:15
  58.9 19.1 %all-to-all-start.2 = ((bf16[64,2,108]{2,1,0:T(2,128)(2,1)}), bf16[64,2,108]{2,1,0:T(2,128)(2,1)S(1)}, u32[]{:S(2)}, u32[]{:S(2)}) async-start(bf16[64,2,108]{2,1,0:T(2,128)(2,1)} %bitcast.7), calls=%async_computation.2 | async-start | bytes 65536 | tf_op jit(solution)/shard_map/all_to_all | solution.py:100
  79.1 40.7 %all-to-all-start.3 = ((bf16[64,288,18]{1,2,0:T(8,128)(2,1)}), bf16[64,288,18]{1,2,0:T(8,128)(2,1)}, u32[]{:S(2)}, u32[]{:S(2)}) async-start(bf16[64,288,18]{1,2,0:T(8,128)(2,1)} %broadcast_in_dim.85), calls=%async_computation.3 | async-start | bytes 2359296 | tf_op jit(solution)/shard_map/all_to_all | solution.py:15
  86.3 174.7 %all-reduce.2.cloned.1.call-start = ((), (), s32[]{:S(2)}) async-start(), calls=%async_computation.7 | async-start | bytes 2359296 | tf_op jit(solution)/shard_map/psum | solution.py:133
  187.9 2.4 copy-start.3
  188.3 25.0 %copy-start.4 = (bf16[1152,18]{0,1:T(8,128)(2,1)S(1)}, bf16[1152,18]{0,1:T(8,128)(2,1)}, u32[]{:S(2)}) copy-start(bf16[1152,18]{0,1:T(8,128)(2,1)} %param.26) | copy-start | bytes 124420
  190.3 46.7 %copy-start.7 = (bf16[2,288]{1,0:T(2,128)(2,1)S(1)}, bf16[2,288]{1,0:T(2,128)(2,1)}, u32[]{:S(2)}) copy-start(bf16[2,288]{1,0:T(2,128)(2,1)} %copy-done.6) | copy-start | bytes 3460
  190.3 76.6 %all-gather.10.cloned.1.call-start = ((), (), s32[]{:S(2)}) async-start(), calls=%async_computation.8 | async-start | bytes 2985984 | tf_op jit(solution)/shard_map/all_gather | solution.py:36
  213.2 83.2 %all-gather.12.cloned.1.call-start = ((), (), s32[]{:S(2)}) async-start(), calls=%async_computation.9 | async-start | bytes 2985984 | tf_op jit(solution)/shard_map/all_gather | solution.py:36
  237.9 63.3 %all-to-all-start.5 = ((bf16[4,2,2304]{2,1,0:T(2,128)(2,1)}), bf16[4,2,2304]{2,1,0:T(2,128)(2,1)S(1)}, u32[]{:S(2)}, u32[]{:S(2)}) async-start(bf16[4,2,2304]{2,1,0:T(2,128)(2,1)} %broadcast_in_dim.86), calls=%async_computation.5 | async-start | bytes 73728 | tf_op jit(solution)/shard_map/all_to_all | solution.py:15
  262.7 1.4 copy-start.1
  262.7 2.1 copy-start.2
  301.2 30.3 %all-to-all-start.4 = ((bf16[4,64,2,1152]{3,1,2,0:T(8,128)(2,1)}), bf16[4,64,2,1152]{3,1,2,0:T(8,128)(2,1)S(1)}, u32[]{:S(2)}, u32[]{:S(2)}) async-start(bf16[4,64,2,1152]{3,1,2,0:T(8,128)(2,1)} %copy.113), calls=%async_computation.4 | async-start | bytes 2359296 | tf_op jit(solution)/shard_map/all_to_all | solution.py:48
  306.3 26.8 %copy-start.8 = (bf16[1152,16]{0,1:T(8,128)(2,1)S(1)}, bf16[1152,16]{0,1:T(8,128)(2,1)}, u32[]{:S(2)}) copy-start(bf16[1152,16]{0,1:T(8,128)(2,1)} %param.27) | copy-start | bytes 110596
Sparse Core Ops, SparseCore 0:
  12.5 160.1 all-gather.7
  190.4 70.5 all-reduce.1
Sparse Core Ops, SparseCore 1:
  213.3 37.4 all-gather.9
  252.7 43.7 all-gather.11
where the time goes:
time: 343 us; the launch traced here: 342 us
  waiting for transfers between devices  181 us (53%)
  starting transfers between devices  45.8 us (13%)
  blocking collectives  44.8 us (13%)
  local copies, waits for them, and re-layouts  21.6 us (6%)
  matrix products  20.2 us (6%)
  between operations  17.8 us (5%)
  other arithmetic  10.3 us (3%)
    all_gather x1, waiting for transfers between devices, on_device(): lax.all_gather(qkv_weight, DP, axis=1, tiled=True)  51.2 us
    all_to_all x4, waiting for transfers between devices, from_everyone(): lax.all_to_all(jnp.broadcast_to(x[None], (size, *x.shape)), axis, 0, 0, t...  47.9 us
    all_gather x4, blocking collectives, gathered_by_axis(): x = lax.all_gather(x, axis, axis=dim, tiled=True)  44.8 us
    all_to_all x4, starting transfers between devices, from_everyone(): lax.all_to_all(jnp.broadcast_to(x[None], (size, *x.shape)), axis, 0, 0, t...  34.3 us
    all_gather x2, waiting for transfers between devices, gathered_by_axis(): x = lax.all_gather(x, axis, axis=dim, tiled=True)  25.6 us
    all_to_all x1, waiting for transfers between devices, sum_at_owner(): pieces = lax.all_to_all(cut_along(x, dim, size), axis, 0, 0, tiled=True)  24.5 us
    psum x1, waiting for transfers between devices, on_device(): lax.psum(attn_part.astype(jnp.bfloat16), 'mp').astype(jnp.float32)  19.6 us
    all_to_all x1, waiting for transfers between devices, on_device(): lax.all_to_all(summed.astype(jnp.bfloat16), DP, split_axis=0, concat_axis...  12.5 us
  transfers between devices with their start and end apart: 10, of which 8 were waited for; matrix products, arithmetic and copies ran while one was open for 8% of the time, Pallas kernels for 0%

commit v1 on v0

v1 whole, which is shorter than its diff:
```python
import jax
import jax.numpy as jnp
from jax import lax
from jax.experimental import pallas as pl
from jax.experimental.pallas import tpu as pltpu
from jax.sharding import Mesh
from jax.sharding import PartitionSpec as P

HEADS = 16
CLASSES = 1000
DP = ("dp_0", "dp_1", "dp_2")
GROUP_DP = ("group", "dp_0", "dp_1", "dp_2")
BF16 = jnp.bfloat16
F32 = jnp.float32


def to_everyone(x, axis):
    size = lax.axis_size(axis)
    return lax.all_to_all(jnp.broadcast_to(x[None], (size, *x.shape)), axis, 0, 0, tiled=True)


def shift(x, axis, step):
    size = lax.axis_size(axis)
    return lax.ppermute(x, axis, [(i, (i + step) % size) for i in range(size)])


def swap(x, axis, bit):
    size = lax.axis_size(axis)
    return lax.ppermute(x, axis, [(i, i ^ bit) for i in range(size)])


def gather_y(block):
    pieces = to_everyone(block, "dp_0")
    return pieces.reshape(pieces.shape[0] * pieces.shape[1], pieces.shape[2])


def gather_x(block):
    half = block.shape[0] // 2
    left = shift(block, "dp_1", 1)
    right = shift(block, "dp_1", -1)
    far_top = shift(left[:half], "dp_1", 1)
    far_bottom = shift(right[half:], "dp_1", -1)
    return jnp.concatenate([block, left, right, far_top, far_bottom], axis=0)


def layer_norm(values):
    mean = jnp.mean(values, axis=-1, keepdims=True)
    centred = values - mean
    spread = jnp.mean(centred * centred, axis=-1, keepdims=True)
    return centred * lax.rsqrt(spread + 1e-06)


def dot(a, b):
    return jnp.dot(a, b, preferred_element_type=F32)


def dot_t(a, b):
    return lax.dot_general(a, b, (((1,), (1,)), ((), ())), preferred_element_type=F32)


def attention_body(first_ref, second_ref, out_ref):
    head_dim = first_ref.shape[1] // 6
    scale = head_dim ** (-0.5)
    for side, ref in enumerate((first_ref, second_ref)):
        for head in range(2):
            at = head * head_dim
            query = ref[:, at : at + head_dim]
            keys = ref[:, 2 * head_dim + at : 3 * head_dim + at]
            values = ref[:, 4 * head_dim + at : 5 * head_dim + at]
            scores = dot_t(query, keys) * scale
            top = jnp.max(scores, axis=-1, keepdims=True)
            weights = jnp.exp(scores - top)
            total = jnp.sum(weights, axis=-1, keepdims=True)
            probs = (weights / total).astype(BF16)
            mixed = dot(probs, values).astype(BF16)
            column = (2 * side + head) * head_dim
            out_ref[:, column : column + head_dim] = mixed


def attention(first, second, images, tokens):
    width = first.shape[1]
    return pl.pallas_call(
        attention_body,
        grid=(images,),
        in_specs=[
            pl.BlockSpec((tokens, width), lambda i: (i, 0)),
            pl.BlockSpec((tokens, width), lambda i: (i, 0)),
        ],
        out_specs=pl.BlockSpec((tokens, 2 * width // 3), lambda i: (i, 0)),
        out_shape=jax.ShapeDtypeStruct((images * tokens, 2 * width // 3), BF16),
        name="attention",
    )(first, second)


def on_device(
    x_arrive,
    cond_first,
    labels,
    step_ids,
    guidance,
    time_table,
    class_table,
    ada_weight,
    final_ada,
    qkv_weight,
    proj_weight,
    fc1_weight,
    fc2_weight,
    out_weight,
):
    tokens = x_arrive.shape[1]
    width = x_arrive.shape[2]
    rows = qkv_weight.shape[1]
    quarter = qkv_weight.shape[2]
    core = lax.axis_index("group")
    column = lax.axis_index("dp_1")
    high = lax.axis_index("dp_2")
    place = lax.axis_index("mp")
    n_y, n_x, n_z = (lax.axis_size(axis) for axis in DP)
    n_mp = lax.axis_size("mp")
    half = quarter // 2

    time_part = jnp.take(time_table, step_ids, axis=0).astype(F32)
    class_part = jnp.take(class_table, labels, axis=0).astype(F32)
    null_part = class_table[CLASSES].astype(F32)[None, :]
    acts = jax.nn.silu(jnp.concatenate([time_part + class_part, time_part + null_part])).astype(BF16)
    every_act = to_everyone(acts, DP).reshape(-1, acts.shape[1])

    qkv_first = jnp.where(core == 0, qkv_weight[:, :, :half], qkv_weight[:, :, half:])
    qkv_first = qkv_first.transpose(1, 0, 2).reshape(rows, 3 * half)
    proj_rows = proj_weight.T
    around = to_everyone(jnp.concatenate([qkv_first, proj_rows], axis=1), ("dp_2", "mp"))
    around = around.reshape(n_z, n_mp, rows, 3 * half + quarter)
    own_qkv = lax.dynamic_index_in_dim(around, place, 1, keepdims=False)[:, :, : 3 * half]
    own_proj = lax.dynamic_slice_in_dim(around, core * (n_mp // 2), n_mp // 2, 1)[..., 3 * half :]
    own_proj = own_proj.transpose(0, 2, 1, 3).reshape(n_z, rows, n_mp // 2 * quarter)
    block_a = jnp.concatenate([own_qkv, own_proj], axis=2).reshape(n_z * rows, -1)
    pad = -block_a.shape[1] % 128
    block_a = jnp.pad(block_a, ((0, 0), (0, pad)))

    feed = jnp.stack([fc1_weight, fc2_weight.T])
    near = []
    spots = [(c, z, m) for c in range(2) for z in range(n_z) for m in range(n_mp)]
    number = {spot: i for i, spot in enumerate(spots)}
    for flip in range(n_z):
        pairs = [(number[c, z, m], number[c, z ^ flip, m ^ (2 * c)]) for c, z, m in spots]
        near.append(lax.ppermute(feed, ("group", "dp_2", "mp"), pairs))
    low = jnp.where(high == 0, near[0], near[1])
    up_part = jnp.where(high == 0, near[1], near[0])
    feed = jnp.concatenate([low, up_part], axis=1)

    part_a = gather_x(gather_y(block_a))
    both_a = to_everyone(part_a, "group")
    part_b = gather_x(gather_y(feed[0]))
    other_b = swap(part_b, "group", 1)
    part_c = gather_x(gather_y(feed[1]))
    other_c = swap(part_c, "group", 1)

    mod_part = dot(every_act, ada_weight).astype(BF16)
    mod_part = lax.all_to_all(mod_part, DP, split_axis=0, concat_axis=1, tiled=True)
    final_part = dot(acts, final_ada).astype(BF16)
    mod_parts = to_everyone(jnp.concatenate([mod_part, final_part], axis=1), "mp")

    spot = lax.broadcasted_iota(jnp.int32, (1, width), 1)
    per_x = n_y * n_z * rows
    per_y = n_z * rows
    block = spot // per_x
    offset = jnp.where(block == 1, n_x - 1, jnp.where(block == 2, 1, jnp.where(block == 3, 2, 0)))
    from_x = (column + offset) % n_x
    inside = spot % per_x
    natural = (inside // per_y * n_x + from_x) * per_y + inside % per_y
    order = (lax.broadcasted_iota(jnp.int32, (width, width), 0) == natural).astype(BF16)

    first = cond_first[0] == 1
    cond_rows = jnp.where(first, x_arrive[0], x_arrive[1])
    uncond_rows = jnp.where(first, x_arrive[1], x_arrive[0])
    images = dot(jnp.concatenate([cond_rows, uncond_rows]), order)
    images = images.reshape(2, tokens, width)
    out_local = lax.dot_general(
        order, out_weight, (((0,), (0,)), ((), ())), preferred_element_type=F32
    ).astype(BF16)
    mods = dot(mod_parts.reshape(-1, width), order).reshape(n_mp, 2, -1, 1, width)
    mods = jnp.sum(mods, axis=0)
    shift_a, scale_a, gate_a, shift_m, scale_m, gate_m, shift_f, scale_f = (
        mods[:, i] for i in range(8)
    )

    hidden = (layer_norm(images) * (1.0 + scale_a) + shift_a).astype(BF16)
    hidden = hidden.reshape(2 * tokens, width)
    cut = 3 * half
    qkv_a = dot(hidden, both_a[0, :, :cut]).astype(BF16)
    qkv_b = dot(hidden, both_a[1, :, :cut]).astype(BF16)
    mixed = attention(qkv_a, qkv_b, 2, tokens)
    share = tokens // n_mp
    mixed = mixed.reshape(2, n_mp, share, quarter).transpose(1, 0, 2, 3)
    mixed = lax.all_to_all(mixed.reshape(n_mp, 2 * share, quarter), "mp", 0, 0, tiled=True)
    mixed = mixed.transpose(1, 0, 2).reshape(2 * share, width)
    middle = n_mp // 2 * quarter
    attn = dot_t(mixed[:, :middle], both_a[0, :, cut : cut + middle])
    attn = attn + dot_t(mixed[:, middle:], both_a[1, :, cut : cut + middle])

    own = lax.dynamic_slice_in_dim(images, place * share, share, 1)
    first_sum = own + gate_a * attn.reshape(2, share, width)
    hidden_two = (layer_norm(first_sum) * (1.0 + scale_m) + shift_m).astype(BF16)
    hidden_two = hidden_two.reshape(2 * share, width)
    feed_rows = jnp.concatenate([hidden_two, swap(hidden_two, "mp", 1)])
    gelu_b = jax.nn.gelu(dot(feed_rows, part_b), approximate=True).astype(BF16)
    gelu_c = jax.nn.gelu(dot(feed_rows, other_b), approximate=True).astype(BF16)
    down = dot_t(gelu_b, part_c) + dot_t(gelu_c, other_c)
    from_pair = swap(down[2 * share :].astype(BF16), "mp", 1).astype(F32)
    mlp = (down[: 2 * share] + from_pair).reshape(2, share, width)
    second_sum = first_sum + gate_m * mlp
    fin = (layer_norm(second_sum) * (1.0 + scale_f) + shift_f).astype(BF16)
    noise = dot(fin.reshape(2 * share, width), out_local)
    noise = noise.reshape(2, 1, share * out_weight.shape[1])
    return noise[1] + guidance[0] * (noise[0] - noise[1])


def solution(mesh):
    torus = Mesh(
        mesh.devices.reshape(mesh.shape["group"], 8, 4, 2, mesh.shape["mp"]),
        ("group", "dp_0", "dp_1", "dp_2", "mp"),
    )
    placed = (
        P(GROUP_DP, None, None),
        P(GROUP_DP),
        P(GROUP_DP),
        P(GROUP_DP),
        P(),
        P(None, "mp"),
        P(None, "mp"),
        P("mp", DP),
        P("mp", None),
        P(None, DP, "mp"),
        P("mp", DP),
        P(DP, "mp"),
        P("mp", DP),
        P(),
    )
    return jax.shard_map(
        on_device, mesh=torus, in_specs=placed, out_specs=P(GROUP_DP, "mp"), check_vma=False
    )
```

time: 343 us -> 285 us (0.83)
  waiting for transfers between devices: 181 us -> 93 us
  starting transfers between devices: 45.8 us -> 104 us
  blocking collectives: 44.8 us -> 7.66 us
  between operations: 17.8 us -> 3.39 us
  local copies, waits for them, and re-layouts: 21.6 us -> 35.2 us
  Pallas kernels: 0 us -> 5.56 us
    all_gather x3 -> x0, waiting for transfers between devices: 76.8 us -> none  [the longest x1 51.2 us: on_device(): lax.all_gather(qkv_weight, DP, axis=1, tiled=True)]
    ppermute x0 -> x18, starting transfers between devices: none -> 60.2 us  [the longest x12 40.3 us: shift(): return lax.ppermute(x, axis, [(i, (i + step) % size) for i in range(size)])]
    all_gather x4 -> x0, blocking collectives: 44.8 us -> none  [gathered_by_axis(): x = lax.all_gather(x, axis, axis=dim, tiled=True)]
    psum x1 -> x0, waiting for transfers between devices: 19.6 us -> none  [on_device(): lax.psum(attn_part.astype(jnp.bfloat16), 'mp').astype(jnp.float32)]
    ppermute x0 -> x18, waiting for transfers between devices: none -> 15.1 us  [the longest x4 12.4 us: swap(): return lax.ppermute(x, axis, [(i, i ^ bit) for i in range(size)])]
    unnamed x31 -> x49, local copies, waits for them, and re-layouts: 5.89 us -> 14.6 us
    all_to_all x0 -> x1, blocking collectives: none -> 7.66 us  [to_everyone(): lax.all_to_all(jnp.broadcast_to(x[None], (size, *x.shape)), axis, 0, 0, t...]
    all_to_all x6 -> x8, waiting for transfers between devices: 84.8 us -> 77.9 us  [the longest x6 55.3 us: to_everyone(): lax.all_to_all(jnp.broadcast_to(x[None], (size, *x.shape)), axis, 0, 0, t...]
  transfers between devices with their start and end apart: 10 -> 26, of which waited for: 8 -> 13; matrix products, arithmetic and copies ran while one was open for 8% -> 17% of each run, Pallas kernels for 0% -> 2%
where the time goes in v1:
time: 285 us; the launch traced here: 283 us
  starting transfers between devices  104 us (36%)
  waiting for transfers between devices  93 us (33%)
  local copies, waits for them, and re-layouts  35.2 us (12%)
  matrix products  22.5 us (8%)
  other arithmetic  11.7 us (4%)
  blocking collectives  7.66 us (3%)
  Pallas kernels  5.56 us (2%)
  between operations  3.39 us (1%)
    all_to_all x6, waiting for transfers between devices, to_everyone(): lax.all_to_all(jnp.broadcast_to(x[None], (size, *x.shape)), axis, 0, 0, t...  55.3 us
    ppermute x12, starting transfers between devices, shift(): return lax.ppermute(x, axis, [(i, (i + step) % size) for i in range(size)])  40.3 us
    all_to_all x6, starting transfers between devices, to_everyone(): lax.all_to_all(jnp.broadcast_to(x[None], (size, *x.shape)), axis, 0, 0, t...  30.5 us
    dot_general x4, matrix products, dot_t(): lax.dot_general(a, b, (((1,), (1,)), ((), ())), preferred_element_type=F32)  14.8 us
    unnamed x49, local copies, waits for them, and re-layouts  14.6 us
    all_to_all x1, waiting for transfers between devices, on_device(): lax.all_to_all(mod_part, DP, split_axis=0, concat_axis=1, tiled=True)  12.7 us
    ppermute x4, waiting for transfers between devices, swap(): return lax.ppermute(x, axis, [(i, i ^ bit) for i in range(size)])  12.4 us
    ppermute x2, starting transfers between devices, on_device(): near.append(lax.ppermute(feed, ('group', 'dp_2', 'mp'), pairs))  11.6 us
  transfers between devices with their start and end apart: 26, of which 13 were waited for; matrix products, arithmetic and copies ran while one was open for 17% of the time, Pallas kernels for 2%

profile of v1, /device:TPU:6, one launch (start us, length us, event | category | flops | bytes accessed | tf_op | source)
XLA Modules:
  0.0 282.8 jit_solution(11088146298078623643)
XLA Ops:
  1.7 10.9 %collective-permute-start.6 = (bf16[2,18,1152]{2,1,0:T(8,128)(2,1)S(1)}, bf16[2,18,1152]{2,1,0:T(8,128)(2,1)S(1)}, u32[]{:S(2)}, u32[]{:S(2)}) collective-permute-start(bf16[2,18,1152]{2,1,0:T(8,128)(2,1)S(1)} %pad_maximum_fusion.11), channel_id=1, source_target_pairs={{0,4},{1,5},{2,6},{3,7},{4,0},{5,1},{6,2},{7,3},{256,262},{257,263... | collective-permute-start | bytes 248840 | tf_op jit(solution)/shard_map/ppermute | solution.py:147
  17.0 10.6 %all-to-all-start = ((bf16[64,2,288]{2,1,0:T(2,128)(2,1)}), bf16[64,2,288]{2,1,0:T(2,128)(2,1)S(1)}, u32[]{:S(2)}, u32[]{:S(2)}) async-start(bf16[64,2,288]{2,1,0:T(2,128)(2,1)} %broadcast_in_dim.88), calls=%async_computation | async-start | bytes 196608 | tf_op jit(solution)/shard_map/all_to_all | solution.py:19
  28.2 12.2 %all-to-all-done = bf16[64,2,288]{2,1,0:T(2,128)(2,1)S(1)} async-done(((bf16[64,2,288]{2,1,0:T(2,128)(2,1)}), bf16[64,2,288]{2,1,0:T(2,128)(2,1)S(1)}, u32[]{:S(2)}, u32[]{:S(2)}) %all-to-all-start) | async-done | bytes 73760 | tf_op jit(solution)/shard_map/all_to_all | solution.py:19
  41.4 6.6 %all-to-all-start.1 = ((bf16[64,2,108]{2,1,0:T(2,128)(2,1)}), bf16[64,2,108]{2,1,0:T(2,128)(2,1)S(1)}, u32[]{:S(2)}, u32[]{:S(2)}) async-start(bf16[64,2,108]{2,1,0:T(2,128)(2,1)} %bitcast.8), calls=%async_computation.1 | async-start | bytes 65536 | tf_op jit(solution)/shard_map/all_to_all | solution.py:160
  48.1 12.7 %all-to-all-done.1 = bf16[64,2,108]{2,1,0:T(2,128)(2,1)S(1)} async-done(((bf16[64,2,108]{2,1,0:T(2,128)(2,1)}), bf16[64,2,108]{2,1,0:T(2,128)(2,1)S(1)}, u32[]{:S(2)}, u32[]{:S(2)}) %all-to-all-start.1) | async-done | bytes 27680 | tf_op jit(solution)/shard_map/all_to_all | solution.py:160
  61.5 5.1 %all-to-all-start.3 = ((bf16[8,18,720]{2,1,0:T(8,128)(2,1)}), bf16[8,18,720]{2,1,0:T(8,128)(2,1)S(1)}, u32[]{:S(2)}, u32[]{:S(2)}) async-start(bf16[8,18,720]{2,1,0:T(8,128)(2,1)} %broadcast_in_dim.90), calls=%async_computation.3 | async-start | bytes 589824 | tf_op jit(solution)/shard_map/all_to_all | solution.py:19
  66.8 11.2 %all-to-all-done.3 = bf16[8,18,720]{2,1,0:T(8,128)(2,1)S(1)} async-done(((bf16[8,18,720]{2,1,0:T(8,128)(2,1)}), bf16[8,18,720]{2,1,0:T(8,128)(2,1)S(1)}, u32[]{:S(2)}, u32[]{:S(2)}) %all-to-all-start.3) | async-done | bytes 207392 | tf_op jit(solution)/shard_map/all_to_all | solution.py:19
  78.7 3.3 %all-to-all-start.2 = ((bf16[4,2,9216]{2,1,0:T(2,128)(2,1)}), bf16[4,2,9216]{2,1,0:T(2,128)(2,1)S(1)}, u32[]{:S(2)}, u32[]{:S(2)}) async-start(bf16[4,2,9216]{2,1,0:T(2,128)(2,1)} %broadcast_in_dim.89), calls=%async_computation.2 | async-start | bytes 294912 | tf_op jit(solution)/shard_map/all_to_all | solution.py:19
  82.7 5.3 %all-to-all-done.2 = bf16[4,2,9216]{2,1,0:T(2,128)(2,1)S(1)} async-done(((bf16[4,2,9216]{2,1,0:T(2,128)(2,1)}), bf16[4,2,9216]{2,1,0:T(2,128)(2,1)S(1)}, u32[]{:S(2)}, u32[]{:S(2)}) %all-to-all-start.2) | async-done | bytes 147488 | tf_op jit(solution)/shard_map/all_to_all | solution.py:19
  88.9 3.5 %all-to-all-start.8 = ((bf16[8,36,1152]{2,1,0:T(8,128)(2,1)}), bf16[8,36,1152]{2,1,0:T(8,128)(2,1)S(1)}, u32[]{:S(2)}, u32[]{:S(2)}) async-start(bf16[8,36,1152]{2,1,0:T(8,128)(2,1)} %broadcast_in_dim.96), calls=%async_computation.8 | async-start | bytes 1474560 | tf_op jit(solution)/shard_map/all_to_all | solution.py:19
  93.3 3.3 %fusion.90 = (f32[512]{0:T(512)S(1)}, f32[512,1152]{1,0:T(8,128)}) fusion(s32[1152]{0:T(1024)S(1)} %fusion.58, bf16[256,1152]{1,0:T(8,128)(2,1)S(1)} %get-tuple-element.32, bf16[256,1152]{1,0:T(8,128)(2,1)S(1)} %get-tuple-element.31), kind=kOutput, calls=%fused_computation.175 | convolution fusion | flops 1363230208 | bytes 3545600 | tf_op jit(solution)/shard_map/dot_general | solution.py:54
  96.6 13.7 %all-to-all-done.8 = bf16[8,36,1152]{2,1,0:T(8,128)(2,1)S(1)} async-done(((bf16[8,36,1152]{2,1,0:T(8,128)(2,1)}), bf16[8,36,1152]{2,1,0:T(8,128)(2,1)S(1)}, u32[]{:S(2)}, u32[]{:S(2)}) %all-to-all-start.8) | async-done | bytes 663584 | tf_op jit(solution)/shard_map/all_to_all | solution.py:19
  111.3 3.7 %all-to-all-start.7 = ((bf16[8,36,1152]{2,1,0:T(8,128)(2,1)}), bf16[8,36,1152]{2,1,0:T(8,128)(2,1)S(1)}, u32[]{:S(2)}, u32[]{:S(2)}) async-start(bf16[8,36,1152]{2,1,0:T(8,128)(2,1)} %broadcast_in_dim.94), calls=%async_computation.7 | async-start | bytes 1474560 | tf_op jit(solution)/shard_map/all_to_all | solution.py:19
  119.4 13.0 %all-to-all-done.7 = bf16[8,36,1152]{2,1,0:T(8,128)(2,1)S(1)} async-done(((bf16[8,36,1152]{2,1,0:T(8,128)(2,1)}), bf16[8,36,1152]{2,1,0:T(8,128)(2,1)S(1)}, u32[]{:S(2)}, u32[]{:S(2)}) %all-to-all-start.7) | async-done | bytes 663584 | tf_op jit(solution)/shard_map/all_to_all | solution.py:19
  133.3 4.2 %all-to-all-start.4 = ((bf16[8,36,1024]{2,1,0:T(8,128)(2,1)}), bf16[8,36,1024]{2,1,0:T(8,128)(2,1)}, u32[]{:S(2)}, u32[]{:S(2)}) async-start(bf16[8,36,1024]{2,1,0:T(8,128)(2,1)} %broadcast_in_dim.91), calls=%async_computation.4 | async-start | bytes 1310720 | tf_op jit(solution)/shard_map/all_to_all | solution.py:19
  138.3 4.2 %collective-permute-start.11 = (bf16[288,1152]{1,0:T(8,128)(2,1)S(1)}, bf16[288,1152]{1,0:T(8,128)(2,1)}, u32[]{:S(2)}, u32[]{:S(2)}) collective-permute-start(bf16[288,1152]{1,0:T(8,128)(2,1)S(1)} %reshape.368), channel_id=1, source_target_pairs={{0,8},{8,16},{16,24},{24,0},{1,9},{9,17},{17,25},{25,1},{2,10},{10... | collective-permute-start | bytes 1990664 | tf_op jit(solution)/shard_map/ppermute | solution.py:24
  143.3 3.3 %fusion.8 = bf16[512,1152]{1,0:T(8,128)(2,1)} fusion(f32[512,1152]{1,0:T(8,128)} %get-tuple-element.52, f32[2,1152]{1,0:T(2,128)S(1)} %get-tuple-element.57, f32[2,1152]{1,0:T(2,128)S(1)} %get-tuple-element.58, f32[512]{0:T(512)} %add_rsqrt_fusion, f32[512]{0:T(512)S(1)} %broadcast_multiply_fusion), kind=kLoop, calls=%fused_computation.12 | loop fusion | flops 2949120 | bytes 3561472 | tf_op jit(solution)/shard_map/convert_element_type | solution.py:188
  149.6 5.1 %collective-permute-start.7 = (bf16[288,1152]{1,0:T(8,128)(2,1)S(1)}, bf16[288,1152]{1,0:T(8,128)(2,1)}, u32[]{:S(2)}, u32[]{:S(2)}) collective-permute-start(bf16[288,1152]{1,0:T(8,128)(2,1)S(1)} %reshape.367), channel_id=1, source_target_pairs={{0,8},{8,16},{16,24},{24,0},{1,9},{9,17},{17,25},{25,1},{2,10},{10... | collective-permute-start | bytes 1990664 | tf_op jit(solution)/shard_map/ppermute | solution.py:24
  158.7 5.1 %collective-permute-start = (bf16[288,1024]{1,0:T(8,128)(2,1)S(1)}, bf16[288,1024]{1,0:T(8,128)(2,1)S(1)}, u32[]{:S(2)}, u32[]{:S(2)}) collective-permute-start(bf16[288,1024]{1,0:T(8,128)(2,1)S(1)} %reshape.361), channel_id=1, source_target_pairs={{0,8},{8,16},{16,24},{24,0},{1,9},{9,17},{17,25},{25,1},{2,10},{10... | collective-permute-start | bytes 1769480 | tf_op jit(solution)/shard_map/ppermute | solution.py:24
  168.9 5.1 %collective-permute-start.13 = (bf16[144,1152]{1,0:T(8,128)(2,1)S(1)}, bf16[144,1152]{1,0:T(8,128)(2,1)S(1)}, u32[]{:S(2)}, u32[]{:S(2)}) collective-permute-start(bf16[144,1152]{1,0:T(8,128)(2,1)S(1)} %slice.171), channel_id=1, source_target_pairs={{0,8},{8,16},{16,24},{24,0},{1,9},{9,17},{17,25},{25,1},{2,10},{10... | collective-permute-start | bytes 995336 | tf_op jit(solution)/shard_map/ppermute | solution.py:24
  181.9 5.1 %collective-permute-start.9 = (bf16[144,1152]{1,0:T(8,128)(2,1)S(1)}, bf16[144,1152]{1,0:T(8,128)(2,1)S(1)}, u32[]{:S(2)}, u32[]{:S(2)}) collective-permute-start(bf16[144,1152]{1,0:T(8,128)(2,1)S(1)} %slice.169), channel_id=1, source_target_pairs={{0,8},{8,16},{16,24},{24,0},{1,9},{9,17},{17,25},{25,1},{2,10},{10... | collective-permute-start | bytes 995336 | tf_op jit(solution)/shard_map/ppermute | solution.py:24
  193.1 4.0 %collective-permute-start.2 = (bf16[144,1024]{1,0:T(8,128)(2,1)S(1)}, bf16[144,1024]{1,0:T(8,128)(2,1)S(1)}, u32[]{:S(2)}, u32[]{:S(2)}) collective-permute-start(bf16[144,1024]{1,0:T(8,128)(2,1)S(1)} %slice.156), channel_id=1, source_target_pairs={{0,8},{8,16},{16,24},{24,0},{1,9},{9,17},{17,25},{25,1},{2,10},{10... | collective-permute-start | bytes 884744 | tf_op jit(solution)/shard_map/ppermute | solution.py:24
  208.6 7.7 %all_to_all.59 = bf16[2,1152,1024]{2,1,0:T(8,128)(2,1)S(1)} all-to-all(bf16[2,1152,1024]{2,1,0:T(8,128)(2,1)S(1)} %broadcast_in_dim.92), channel_id=1, replica_groups=mesh['group'=2,'dp_0'=8,'dp_1'=4,'dp_2'=2,'mp'=4] {'group'}, dimensions={0} | all-to-all | bytes 9437184 | tf_op jit(solution)/shard_map/all_to_all | solution.py:19
  221.2 5.6 %attention.1 = bf16[512,288]{1,0:T(8,128)(2,1)} custom-call(bf16[512,432]{1,0:T(8,128)(2,1)} %copy.64.first_ref, bf16[512,432]{1,0:T(8,128)(2,1)} %copy.65.second_ref), custom_call_target="tpu_custom_call" | custom-call | tf_op jit(solution)/shard_map/attention/pallas_call | solution.py:82
  228.7 6.6 %all-to-all-start.6 = ((bf16[4,128,288]{1,2,0:T(8,128)(2,1)}), bf16[4,128,288]{1,2,0:T(8,128)(2,1)S(1)}, u32[]{:S(2)}, u32[]{:S(2)}) async-start(bf16[4,128,288]{1,2,0:T(8,128)(2,1)} %copy.67), calls=%async_computation.6 | async-start | bytes 589824 | tf_op jit(solution)/shard_map/all_to_all | solution.py:196
  235.3 9.9 %all-to-all-done.6 = bf16[4,128,288]{1,2,0:T(8,128)(2,1)S(1)} async-done(((bf16[4,128,288]{1,2,0:T(8,128)(2,1)}), bf16[4,128,288]{1,2,0:T(8,128)(2,1)S(1)}, u32[]{:S(2)}, u32[]{:S(2)}) %all-to-all-start.6) | async-done | bytes 294944 | tf_op jit(solution)/shard_map/all_to_all | solution.py:196
  247.4 2.2 convolution_add_fusion.1
  253.9 6.2 %collective-permute-done.4 = bf16[128,1152]{1,0:T(8,128)(2,1)S(1)} collective-permute-done((bf16[128,1152]{1,0:T(8,128)(2,1)S(1)}, bf16[128,1152]{1,0:T(8,128)(2,1)S(1)}, u32[]{:S(2)}, u32[]{:S(2)}) %collective-permute-start.4) | collective-permute-done | bytes 294944 | tf_op jit(solution)/shard_map/ppermute | solution.py:29
  260.9 5.5 %fusion.34 = f32[256,1152]{1,0:T(8,128)} fusion(bf16[1152,1152]{1,0:T(8,128)(2,1)} %collective-permute-done.16, bf16[1152,1152]{1,0:T(8,128)(2,1)} %collective-permute-done.15, bf16[128,1152]{1,0:T(8,128)(2,1)S(1)} %collective-permute-done.4, bf16[128,1152]{1,0:T(8,128)(2,1)S(1)} %bitcast.114), kind=kOutput, calls=%fused_computation.47 | convolution fusion | flops 1362788352 | bytes 7077888 | tf_op jit(solution)/shard_map/dot_general | solution.py:58
  266.4 4.8 %convolution_add_fusion = f32[256,1152]{1,0:T(8,128)S(1)} fusion(f32[256,1152]{1,0:T(8,128)} %fusion.34, bf16[1152,1152]{1,0:T(8,128)(2,1)} %constant_dynamic-update-slice_fusion.10, bf16[1152,1152]{1,0:T(8,128)(2,1)} %constant_dynamic-update-slice_fusion.5, bf16[128,1152]{1,0:T(8,128)(2,1)} %copy-done.12, bf16[128,1152]{1,0:T(8,128)(2,1)S(1)} %bitcast.115), kind=kOutput, calls=%fused_computation.6 | convolution fusion | flops 1363083264 | bytes 8257536 | tf_op jit(solution)/shard_map/dot_general | solution.py:58
  271.2 2.4 collective-permute-start.17
  273.7 6.1 %collective-permute-done.17 = bf16[128,1152]{1,0:T(8,128)(2,1)S(1)} collective-permute-done((bf16[128,1152]{1,0:T(8,128)(2,1)S(1)}, bf16[128,1152]{1,0:T(8,128)(2,1)S(1)}, u32[]{:S(2)}, u32[]{:S(2)}) %collective-permute-start.17) | collective-permute-done | bytes 294944 | tf_op jit(solution)/shard_map/ppermute | solution.py:29
  (155 shorter events, 70.9 us)
Async XLA Ops:
  0.0 27.6 %copy-start = (bf16[288,2304]{1,0:T(8,128)(2,1)S(1)}, bf16[288,2304]{1,0:T(8,128)(2,1)}, u32[]{:S(2)}) copy-start(bf16[288,2304]{1,0:T(8,128)(2,1)} %param.22) | copy-start | bytes 3981316
  0.0 27.9 %copy-start.7 = (bf16[3,18,288]{2,1,0:T(8,128)(2,1)S(1)}, bf16[3,18,288]{2,1,0:T(8,128)(2,1)}, u32[]{:S(2)}) copy-start(bf16[3,18,288]{2,1,0:T(8,128)(2,1)} %param.23) | copy-start | bytes 93316
  0.0 28.1 %copy-start.9 = (bf16[288,18]{0,1:T(8,128)(2,1)S(1)}, bf16[288,18]{0,1:T(8,128)(2,1)}, u32[]{:S(2)}) copy-start(bf16[288,18]{0,1:T(8,128)(2,1)} %param.24) | copy-start | bytes 31108
  0.0 40.5 %copy-start.8 = (bf16[288,108]{1,0:T(8,128)(2,1)S(1)}, bf16[288,108]{1,0:T(8,128)(2,1)}, u32[]{:S(2)}) copy-start(bf16[288,108]{1,0:T(8,128)(2,1)} %param.21) | copy-start | bytes 186628
  1.0 47.1 %collective-permute-start.5 = (bf16[2,18,1152]{2,1,0:T(8,128)(2,1)S(1)}, bf16[2,18,1152]{2,1,0:T(8,128)(2,1)S(1)}, u32[]{:S(2)}, u32[]{:S(2)}) collective-permute-start(bf16[2,18,1152]{2,1,0:T(8,128)(2,1)S(1)} %pad_maximum_fusion.11), channel_id=1, source_target_pairs={{0,0},{1,1},{2,2},{3,3},{4,4},{5,5},{6,6},{7,7},{256,258},{257,259... | collective-permute-start | bytes 248840 | tf_op jit(solution)/shard_map/ppermute | solution.py:147
  1.7 46.4 %collective-permute-start.6 = (bf16[2,18,1152]{2,1,0:T(8,128)(2,1)S(1)}, bf16[2,18,1152]{2,1,0:T(8,128)(2,1)S(1)}, u32[]{:S(2)}, u32[]{:S(2)}) collective-permute-start(bf16[2,18,1152]{2,1,0:T(8,128)(2,1)S(1)} %pad_maximum_fusion.11), channel_id=1, source_target_pairs={{0,4},{1,5},{2,6},{3,7},{4,0},{5,1},{6,2},{7,3},{256,262},{257,263... | collective-permute-start | bytes 248840 | tf_op jit(solution)/shard_map/ppermute | solution.py:147
  17.0 23.4 %all-to-all-start = ((bf16[64,2,288]{2,1,0:T(2,128)(2,1)}), bf16[64,2,288]{2,1,0:T(2,128)(2,1)S(1)}, u32[]{:S(2)}, u32[]{:S(2)}) async-start(bf16[64,2,288]{2,1,0:T(2,128)(2,1)} %broadcast_in_dim.88), calls=%async_computation | async-start | bytes 196608 | tf_op jit(solution)/shard_map/all_to_all | solution.py:19
  41.4 19.3 %all-to-all-start.1 = ((bf16[64,2,108]{2,1,0:T(2,128)(2,1)}), bf16[64,2,108]{2,1,0:T(2,128)(2,1)S(1)}, u32[]{:S(2)}, u32[]{:S(2)}) async-start(bf16[64,2,108]{2,1,0:T(2,128)(2,1)} %bitcast.8), calls=%async_computation.1 | async-start | bytes 65536 | tf_op jit(solution)/shard_map/all_to_all | solution.py:160
  48.0 45.1 %copy-start.2 = (bf16[2,256,1152]{2,1,0:T(8,128)(2,1)S(1)}, bf16[2,256,1152]{2,1,0:T(8,128)(2,1)}, u32[]{:S(2)}) copy-start(bf16[2,256,1152]{2,1,0:T(8,128)(2,1)} %param.14) | copy-start | bytes 3538948
  61.5 16.5 %all-to-all-start.3 = ((bf16[8,18,720]{2,1,0:T(8,128)(2,1)}), bf16[8,18,720]{2,1,0:T(8,128)(2,1)S(1)}, u32[]{:S(2)}, u32[]{:S(2)}) async-start(bf16[8,18,720]{2,1,0:T(8,128)(2,1)} %broadcast_in_dim.90), calls=%async_computation.3 | async-start | bytes 589824 | tf_op jit(solution)/shard_map/all_to_all | solution.py:19
  78.7 9.3 %all-to-all-start.2 = ((bf16[4,2,9216]{2,1,0:T(2,128)(2,1)}), bf16[4,2,9216]{2,1,0:T(2,128)(2,1)S(1)}, u32[]{:S(2)}, u32[]{:S(2)}) async-start(bf16[4,2,9216]{2,1,0:T(2,128)(2,1)} %broadcast_in_dim.89), calls=%async_computation.2 | async-start | bytes 294912 | tf_op jit(solution)/shard_map/all_to_all | solution.py:19
  88.9 21.5 %all-to-all-start.8 = ((bf16[8,36,1152]{2,1,0:T(8,128)(2,1)}), bf16[8,36,1152]{2,1,0:T(8,128)(2,1)S(1)}, u32[]{:S(2)}, u32[]{:S(2)}) async-start(bf16[8,36,1152]{2,1,0:T(8,128)(2,1)} %broadcast_in_dim.96), calls=%async_computation.8 | async-start | bytes 1474560 | tf_op jit(solution)/shard_map/all_to_all | solution.py:19
  93.1 25.1 %copy-start.10 = (s32[1152]{0:T(1024)}, s32[1152]{0:T(1024)S(1)}, u32[]{:S(2)}) copy-start(s32[1152]{0:T(1024)S(1)} %fusion.58) | copy-start | bytes 13828
  111.3 21.1 %all-to-all-start.7 = ((bf16[8,36,1152]{2,1,0:T(8,128)(2,1)}), bf16[8,36,1152]{2,1,0:T(8,128)(2,1)S(1)}, u32[]{:S(2)}, u32[]{:S(2)}) async-start(bf16[8,36,1152]{2,1,0:T(8,128)(2,1)} %broadcast_in_dim.94), calls=%async_computation.7 | async-start | bytes 1474560 | tf_op jit(solution)/shard_map/all_to_all | solution.py:19
  133.3 24.2 %all-to-all-start.4 = ((bf16[8,36,1024]{2,1,0:T(8,128)(2,1)}), bf16[8,36,1024]{2,1,0:T(8,128)(2,1)}, u32[]{:S(2)}, u32[]{:S(2)}) async-start(bf16[8,36,1024]{2,1,0:T(8,128)(2,1)} %broadcast_in_dim.91), calls=%async_computation.4 | async-start | bytes 1310720 | tf_op jit(solution)/shard_map/all_to_all | solution.py:19
  138.3 25.6 %collective-permute-start.11 = (bf16[288,1152]{1,0:T(8,128)(2,1)S(1)}, bf16[288,1152]{1,0:T(8,128)(2,1)}, u32[]{:S(2)}, u32[]{:S(2)}) collective-permute-start(bf16[288,1152]{1,0:T(8,128)(2,1)S(1)} %reshape.368), channel_id=1, source_target_pairs={{0,8},{8,16},{16,24},{24,0},{1,9},{9,17},{17,25},{25,1},{2,10},{10... | collective-permute-start | bytes 1990664 | tf_op jit(solution)/shard_map/ppermute | solution.py:24
  146.6 22.3 %collective-permute-start.12 = (bf16[288,1152]{1,0:T(8,128)(2,1)S(1)}, bf16[288,1152]{1,0:T(8,128)(2,1)}, u32[]{:S(2)}, u32[]{:S(2)}) collective-permute-start(bf16[288,1152]{1,0:T(8,128)(2,1)S(1)} %reshape.368), channel_id=1, source_target_pairs={{0,24},{8,0},{16,8},{24,16},{1,25},{9,1},{17,9},{25,17},{2,26},{10... | collective-permute-start | bytes 1990664 | tf_op jit(solution)/shard_map/ppermute | solution.py:24
  149.6 27.4 %collective-permute-start.7 = (bf16[288,1152]{1,0:T(8,128)(2,1)S(1)}, bf16[288,1152]{1,0:T(8,128)(2,1)}, u32[]{:S(2)}, u32[]{:S(2)}) collective-permute-start(bf16[288,1152]{1,0:T(8,128)(2,1)S(1)} %reshape.367), channel_id=1, source_target_pairs={{0,8},{8,16},{16,24},{24,0},{1,9},{9,17},{17,25},{25,1},{2,10},{10... | collective-permute-start | bytes 1990664 | tf_op jit(solution)/shard_map/ppermute | solution.py:24
  155.6 26.3 %collective-permute-start.8 = (bf16[288,1152]{1,0:T(8,128)(2,1)S(1)}, bf16[288,1152]{1,0:T(8,128)(2,1)}, u32[]{:S(2)}, u32[]{:S(2)}) collective-permute-start(bf16[288,1152]{1,0:T(8,128)(2,1)S(1)} %reshape.367), channel_id=1, source_target_pairs={{0,24},{8,0},{16,8},{24,16},{1,25},{9,1},{17,9},{25,17},{2,26},{10... | collective-permute-start | bytes 1990664 | tf_op jit(solution)/shard_map/ppermute | solution.py:24
  158.7 31.3 %collective-permute-start = (bf16[288,1024]{1,0:T(8,128)(2,1)S(1)}, bf16[288,1024]{1,0:T(8,128)(2,1)S(1)}, u32[]{:S(2)}, u32[]{:S(2)}) collective-permute-start(bf16[288,1024]{1,0:T(8,128)(2,1)S(1)} %reshape.361), channel_id=1, source_target_pairs={{0,8},{8,16},{16,24},{24,0},{1,9},{9,17},{17,25},{25,1},{2,10},{10... | collective-permute-start | bytes 1769480 | tf_op jit(solution)/shard_map/ppermute | solution.py:24
  163.9 29.2 %collective-permute-start.1 = (bf16[288,1024]{1,0:T(8,128)(2,1)S(1)}, bf16[288,1024]{1,0:T(8,128)(2,1)S(1)}, u32[]{:S(2)}, u32[]{:S(2)}) collective-permute-start(bf16[288,1024]{1,0:T(8,128)(2,1)S(1)} %reshape.361), channel_id=1, source_target_pairs={{0,24},{8,0},{16,8},{24,16},{1,25},{9,1},{17,9},{25,17},{2,26},{10... | collective-permute-start | bytes 1769480 | tf_op jit(solution)/shard_map/ppermute | solution.py:24
  168.9 28.4 %collective-permute-start.13 = (bf16[144,1152]{1,0:T(8,128)(2,1)S(1)}, bf16[144,1152]{1,0:T(8,128)(2,1)S(1)}, u32[]{:S(2)}, u32[]{:S(2)}) collective-permute-start(bf16[144,1152]{1,0:T(8,128)(2,1)S(1)} %slice.171), channel_id=1, source_target_pairs={{0,8},{8,16},{16,24},{24,0},{1,9},{9,17},{17,25},{25,1},{2,10},{10... | collective-permute-start | bytes 995336 | tf_op jit(solution)/shard_map/ppermute | solution.py:24
  177.0 23.2 %collective-permute-start.14 = (bf16[144,1152]{1,0:T(8,128)(2,1)S(1)}, bf16[144,1152]{1,0:T(8,128)(2,1)S(1)}, u32[]{:S(2)}, u32[]{:S(2)}) collective-permute-start(bf16[144,1152]{1,0:T(8,128)(2,1)S(1)} %slice.172), channel_id=1, source_target_pairs={{0,24},{8,0},{16,8},{24,16},{1,25},{9,1},{17,9},{25,17},{2,26},{10... | collective-permute-start | bytes 995336 | tf_op jit(solution)/shard_map/ppermute | solution.py:24
  181.9 21.0 %collective-permute-start.9 = (bf16[144,1152]{1,0:T(8,128)(2,1)S(1)}, bf16[144,1152]{1,0:T(8,128)(2,1)S(1)}, u32[]{:S(2)}, u32[]{:S(2)}) collective-permute-start(bf16[144,1152]{1,0:T(8,128)(2,1)S(1)} %slice.169), channel_id=1, source_target_pairs={{0,8},{8,16},{16,24},{24,0},{1,9},{9,17},{17,25},{25,1},{2,10},{10... | collective-permute-start | bytes 995336 | tf_op jit(solution)/shard_map/ppermute | solution.py:24
  190.0 14.7 %collective-permute-start.10 = (bf16[144,1152]{1,0:T(8,128)(2,1)S(1)}, bf16[144,1152]{1,0:T(8,128)(2,1)S(1)}, u32[]{:S(2)}, u32[]{:S(2)}) collective-permute-start(bf16[144,1152]{1,0:T(8,128)(2,1)S(1)} %slice.170), channel_id=1, source_target_pairs={{0,24},{8,0},{16,8},{24,16},{1,25},{9,1},{17,9},{25,17},{2,26},{10... | collective-permute-start | bytes 995336 | tf_op jit(solution)/shard_map/ppermute | solution.py:24
  193.1 14.5 %collective-permute-start.2 = (bf16[144,1024]{1,0:T(8,128)(2,1)S(1)}, bf16[144,1024]{1,0:T(8,128)(2,1)S(1)}, u32[]{:S(2)}, u32[]{:S(2)}) collective-permute-start(bf16[144,1024]{1,0:T(8,128)(2,1)S(1)} %slice.156), channel_id=1, source_target_pairs={{0,8},{8,16},{16,24},{24,0},{1,9},{9,17},{17,25},{25,1},{2,10},{10... | collective-permute-start | bytes 884744 | tf_op jit(solution)/shard_map/ppermute | solution.py:24
  197.3 10.6 %collective-permute-start.3 = (bf16[144,1024]{1,0:T(8,128)(2,1)S(1)}, bf16[144,1024]{1,0:T(8,128)(2,1)S(1)}, u32[]{:S(2)}, u32[]{:S(2)}) collective-permute-start(bf16[144,1024]{1,0:T(8,128)(2,1)S(1)} %slice.157), channel_id=1, source_target_pairs={{0,24},{8,0},{16,8},{24,16},{1,25},{9,1},{17,9},{25,17},{2,26},{10... | collective-permute-start | bytes 884744 | tf_op jit(solution)/shard_map/ppermute | solution.py:24
  201.0 59.2 %collective-permute-start.16 = (bf16[1152,1152]{1,0:T(8,128)(2,1)}, bf16[1152,1152]{1,0:T(8,128)(2,1)}, u32[]{:S(2)}, u32[]{:S(2)}) collective-permute-start(bf16[1152,1152]{1,0:T(8,128)(2,1)} %constant_dynamic-update-slice_fusion.10), channel_id=1, source_target_pairs={{0,256},{256,0},{1,257},{257,1},{2,258},{258,2},{3,259},{259,3},{4... | collective-permute-start | bytes 7962632 | tf_op jit(solution)/shard_map/ppermute | solution.py:29
  205.5 54.7 %collective-permute-start.15 = (bf16[1152,1152]{1,0:T(8,128)(2,1)}, bf16[1152,1152]{1,0:T(8,128)(2,1)}, u32[]{:S(2)}, u32[]{:S(2)}) collective-permute-start(bf16[1152,1152]{1,0:T(8,128)(2,1)} %constant_dynamic-update-slice_fusion.5), channel_id=1, source_target_pairs={{0,256},{256,0},{1,257},{257,1},{2,258},{258,2},{3,259},{259,3},{4... | collective-permute-start | bytes 7962632 | tf_op jit(solution)/shard_map/ppermute | solution.py:29
  228.7 16.5 %all-to-all-start.6 = ((bf16[4,128,288]{1,2,0:T(8,128)(2,1)}), bf16[4,128,288]{1,2,0:T(8,128)(2,1)S(1)}, u32[]{:S(2)}, u32[]{:S(2)}) async-start(bf16[4,128,288]{1,2,0:T(8,128)(2,1)} %copy.67), calls=%async_computation.6 | async-start | bytes 589824 | tf_op jit(solution)/shard_map/all_to_all | solution.py:196
  251.3 8.8 %collective-permute-start.4 = (bf16[128,1152]{1,0:T(8,128)(2,1)S(1)}, bf16[128,1152]{1,0:T(8,128)(2,1)S(1)}, u32[]{:S(2)}, u32[]{:S(2)}) collective-permute-start(bf16[128,1152]{1,0:T(8,128)(2,1)S(1)} %bitcast.113), channel_id=1, source_target_pairs={{0,1},{1,0},{2,3},{3,2},{4,5},{5,4},{6,7},{7,6},{8,9},{9,8},{10,11... | collective-permute-start | bytes 884744 | tf_op jit(solution)/shard_map/ppermute | solution.py:29
  271.2 8.6 %collective-permute-start.17 = (bf16[128,1152]{1,0:T(8,128)(2,1)S(1)}, bf16[128,1152]{1,0:T(8,128)(2,1)S(1)}, u32[]{:S(2)}, u32[]{:S(2)}) collective-permute-start(bf16[128,1152]{1,0:T(8,128)(2,1)S(1)} %slice.210), channel_id=1, source_target_pairs={{0,1},{1,0},{2,3},{3,2},{4,5},{5,4},{6,7},{7,6},{8,9},{9,8},{10,11... | collective-permute-start | bytes 884744 | tf_op jit(solution)/shard_map/ppermute | solution.py:29
  (8 other events, 49.0 us)

commit v2 on v1

v2 whole, which is shorter than its diff:
```python
import jax
import jax.numpy as jnp
from jax import lax
from jax.experimental import pallas as pl
from jax.experimental.pallas import tpu as pltpu
from jax.sharding import Mesh
from jax.sharding import PartitionSpec as P

CLASSES = 1000
DP = ("dp_0", "dp_1", "dp_2")
GROUP_DP = ("group", "dp_0", "dp_1", "dp_2")
BF16 = jnp.bfloat16
F32 = jnp.float32


def to_everyone(x, axis):
    size = lax.axis_size(axis)
    return lax.all_to_all(jnp.broadcast_to(x[None], (size, *x.shape)), axis, 0, 0, tiled=True)


def shift(x, axis, step):
    size = lax.axis_size(axis)
    return lax.ppermute(x, axis, [(i, (i + step) % size) for i in range(size)])


def swap(x, axis, bit):
    size = lax.axis_size(axis)
    return lax.ppermute(x, axis, [(i, i ^ bit) for i in range(size)])


def gather_y(block):
    pieces = to_everyone(block, "dp_0")
    return pieces.reshape(pieces.shape[0] * pieces.shape[1], pieces.shape[2])


def gather_x(block):
    half = block.shape[0] // 2
    left = shift(block, "dp_1", 1)
    right = shift(block, "dp_1", -1)
    far_top = shift(left[:half], "dp_1", 1)
    far_bottom = shift(right[half:], "dp_1", -1)
    return jnp.concatenate([block, left, right, far_top, far_bottom], axis=0)


def by_height(own, other, high):
    own_low = high == 0
    return jnp.concatenate([jnp.where(own_low, own, other), jnp.where(own_low, other, own)])


def lanes_full(x):
    return jnp.pad(x, ((0, 0), (0, -x.shape[1] % 128)))


def layer_norm(values):
    mean = jnp.mean(values, axis=-1, keepdims=True)
    centred = values - mean
    spread = jnp.mean(centred * centred, axis=-1, keepdims=True)
    return centred * lax.rsqrt(spread + 1e-06)


def dot(a, b):
    return jnp.dot(a, b, preferred_element_type=F32)


def dot_t(a, b):
    return lax.dot_general(a, b, (((1,), (1,)), ((), ())), preferred_element_type=F32)


def whole(shape):
    return pl.BlockSpec(shape, lambda *_: (0,) * len(shape))


def attention_body(core_ref, x_ref, shift_ref, scale_ref, mine_ref, other_ref, out_ref):
    images, tokens, _ = x_ref.shape
    pieces, quarter, _ = out_ref.shape
    head_dim = quarter // 4
    share = tokens // pieces
    scale = head_dim ** (-0.5)
    low = core_ref[0] == 0
    for image in range(images):
        x = x_ref[image].astype(F32)
        hidden = (layer_norm(x) * (1.0 + scale_ref[image]) + shift_ref[image]).astype(BF16)
        sides = []
        for ref in (mine_ref, other_ref):
            qkv = dot(hidden, ref[...]).astype(BF16)
            heads = []
            for head in range(2):
                at = head * head_dim
                query = qkv[:, at : at + head_dim]
                keys = qkv[:, 2 * head_dim + at : 3 * head_dim + at]
                values = qkv[:, 4 * head_dim + at : 5 * head_dim + at]
                scores = dot_t(query, keys) * scale
                top = jnp.max(scores, axis=-1, keepdims=True)
                weights = jnp.exp(scores - top)
                total = jnp.sum(weights, axis=-1, keepdims=True)
                probs = (weights / total).astype(BF16)
                mixed = lax.dot_general(
                    values, probs, (((0,), (1,)), ((), ())), preferred_element_type=F32
                )
                heads.append(mixed.astype(BF16))
            sides.append(jnp.concatenate(heads, axis=0))
        first = jnp.where(low, sides[0], sides[1])
        second = jnp.where(low, sides[1], sides[0])
        mixed = jnp.concatenate([first, second], axis=0)
        for piece in range(pieces):
            part = mixed[:, piece * share : (piece + 1) * share]
            out_ref[piece, :, image * share : (image + 1) * share] = part


def attention(core, x, shift_a, scale_a, mine, other, n_mp, quarter):
    images, tokens, width = x.shape
    vector = whole((images, 1, width))
    out_shape = (n_mp, quarter, images * tokens // n_mp)
    return pl.pallas_call(
        attention_body,
        grid_spec=pltpu.PrefetchScalarGridSpec(
            num_scalar_prefetch=1,
            grid=(1,),
            in_specs=[whole(x.shape), vector, vector, whole(mine.shape), whole(other.shape)],
            out_specs=whole(out_shape),
        ),
        out_shape=jax.ShapeDtypeStruct(out_shape, BF16),
        name="attention",
    )(core, x, shift_a, scale_a, mine, other)


def project_body(base_ref, mixed_ref, mine_ref, other_ref, own_ref, gate_ref, shift_ref, scale_ref,
                 sum_ref, hidden_ref, rows_ref):
    quarter = mixed_ref.shape[1]
    base = base_ref[0]
    for i in range(4):
        rows_ref[i * quarter : (i + 1) * quarter] = mixed_ref[base ^ i]
    middle = 2 * quarter
    both = (((0,), (1,)), ((), ()))
    attn = lax.dot_general(
        rows_ref[:middle], mine_ref[:, :middle], both, preferred_element_type=F32
    ) + lax.dot_general(
        rows_ref[middle:], other_ref[:, :middle], both, preferred_element_type=F32
    )
    share = own_ref.shape[1]
    for i in range(2):
        total = own_ref[i].astype(F32) + gate_ref[i] * attn[i * share : (i + 1) * share]
        sum_ref[i] = total
        hidden_ref[i] = (layer_norm(total) * (1.0 + scale_ref[i]) + shift_ref[i]).astype(BF16)


def project(base, mixed, mine, other, own, gate_a, shift_m, scale_m):
    _, share, width = own.shape
    vector = whole((2, 1, width))
    aside = pl.BlockSpec(
        (pl.Element(width), pl.Element(mine.shape[1] - width)), lambda *_: (0, width)
    )
    return pl.pallas_call(
        project_body,
        grid_spec=pltpu.PrefetchScalarGridSpec(
            num_scalar_prefetch=1,
            grid=(1,),
            in_specs=[
                whole(mixed.shape),
                aside,
                aside,
                whole(own.shape),
                vector,
                vector,
                vector,
            ],
            out_specs=[whole(own.shape), whole(own.shape)],
            scratch_shapes=[pltpu.VMEM((4 * mixed.shape[1], 2 * share), BF16)],
        ),
        out_shape=[
            jax.ShapeDtypeStruct(own.shape, F32),
            jax.ShapeDtypeStruct(own.shape, BF16),
        ],
        name="project",
    )(base, mixed, mine, other, own, gate_a, shift_m, scale_m)


def feed_body(own_ref, pair_ref, up_ref, up_other_ref, down_ref, down_other_ref,
              keep_ref, send_ref, rows_ref, sum_ref):
    step = pl.program_id(0)
    half = pl.num_programs(0) // 2
    count = own_ref.shape[0]

    @pl.when(step == 0)
    def _():
        rows_ref[:count] = own_ref[...]
        rows_ref[count:] = pair_ref[...]

    def part(up, down):
        hidden = jax.nn.gelu(dot(rows_ref[...], up[...]), approximate=True).astype(BF16)
        return dot_t(hidden, down[...])

    @pl.when(step == 0)
    def _():
        sum_ref[...] = part(up_ref, down_ref)

    @pl.when((step > 0) & (step < half))
    def _():
        sum_ref[...] += part(up_ref, down_ref)

    @pl.when(step >= half)
    def _():
        sum_ref[...] += part(up_other_ref, down_other_ref)

    @pl.when(step == pl.num_programs(0) - 1)
    def _():
        keep_ref[...] = sum_ref[:count]
        send_ref[...] = sum_ref[count:].astype(BF16)


def feed_forward(own, pair, up, up_other, down, down_other):
    count, width = own.shape
    steps = 3
    piece = width // steps
    first = pl.BlockSpec((width, piece), lambda i: (0, jnp.minimum(i, steps - 1)))
    second = pl.BlockSpec((width, piece), lambda i: (0, jnp.maximum(i - steps, 0)))
    return pl.pallas_call(
        feed_body,
        grid=(2 * steps,),
        in_specs=[whole(own.shape), whole(own.shape), first, second, first, second],
        out_specs=[whole(own.shape), whole(own.shape)],
        out_shape=[
            jax.ShapeDtypeStruct(own.shape, F32),
            jax.ShapeDtypeStruct(own.shape, BF16),
        ],
        scratch_shapes=[pltpu.VMEM((2 * count, width), BF16), pltpu.VMEM((2 * count, width), F32)],
        name="feed_forward",
    )(own, pair, up, up_other, down, down_other)


def finish_body(scale_by_ref, keep_ref, recv_ref, first_ref, gate_ref, shift_ref, scale_ref, out_w_ref, out_ref):
    share = first_ref.shape[1]
    noise = []
    for i in range(2):
        part = slice(i * share, (i + 1) * share)
        mlp = keep_ref[part] + recv_ref[part].astype(F32)
        total = first_ref[i] + gate_ref[i] * mlp
        fin = (layer_norm(total) * (1.0 + scale_ref[i]) + shift_ref[i]).astype(BF16)
        noise.append(dot(fin, out_w_ref[...]))
    out_ref[...] = noise[1] + scale_by_ref[0] * (noise[0] - noise[1])


def finish(guidance, keep, recv, first_sum, gate_m, shift_f, scale_f, out_local):
    _, share, width = first_sum.shape
    vector = whole((2, 1, width))
    return pl.pallas_call(
        finish_body,
        grid_spec=pltpu.PrefetchScalarGridSpec(
            num_scalar_prefetch=1,
            grid=(1,),
            in_specs=[
                whole(keep.shape),
                whole(recv.shape),
                whole(first_sum.shape),
                vector,
                vector,
                vector,
                whole(out_local.shape),
            ],
            out_specs=whole((share, out_local.shape[1])),
        ),
        out_shape=jax.ShapeDtypeStruct((share, out_local.shape[1]), F32),
        name="finish",
    )(guidance, keep, recv, first_sum, gate_m, shift_f, scale_f, out_local)


def on_device(
    x_arrive,
    cond_first,
    labels,
    step_ids,
    guidance,
    time_table,
    class_table,
    ada_weight,
    final_ada,
    qkv_weight,
    proj_weight,
    fc1_weight,
    fc2_weight,
    out_weight,
):
    tokens = x_arrive.shape[1]
    width = x_arrive.shape[2]
    rows = qkv_weight.shape[1]
    quarter = qkv_weight.shape[2]
    core = lax.axis_index("group")
    column = lax.axis_index("dp_1")
    high = lax.axis_index("dp_2")
    place = lax.axis_index("mp")
    n_y, n_x, n_z = (lax.axis_size(axis) for axis in DP)
    n_mp = lax.axis_size("mp")
    half = quarter // 2

    time_part = jnp.take(time_table, step_ids, axis=0).astype(F32)
    class_part = jnp.take(class_table, labels, axis=0).astype(F32)
    null_part = class_table[CLASSES].astype(F32)[None, :]
    acts = jax.nn.silu(jnp.concatenate([time_part + class_part, time_part + null_part])).astype(BF16)
    every_act = to_everyone(acts, DP).reshape(-1, acts.shape[1])

    qkv_own = jnp.where(core == 0, qkv_weight[:, :, :half], qkv_weight[:, :, half:])
    qkv_own = qkv_own.transpose(1, 0, 2).reshape(rows, 3 * half)
    qkv_other = swap(qkv_own, "dp_2", 1)
    qkv_block = lanes_full(by_height(qkv_own, qkv_other, high))

    proj_rows = proj_weight.T
    feed = jnp.concatenate([fc2_weight.T, fc1_weight, proj_rows], axis=1)
    spots = [(c, z, m) for c in range(2) for z in range(n_z) for m in range(n_mp)]
    number = {spot: i for i, spot in enumerate(spots)}

    def fetch(x, flip, along):
        pairs = [(number[c, z, m], number[c, z ^ flip, m ^ (2 * c) ^ along]) for c, z, m in spots]
        return lax.ppermute(x, ("group", "dp_2", "mp"), pairs)

    feed = by_height(fetch(feed, 0, 0), fetch(feed, 1, 0), high)
    proj_beside = by_height(fetch(proj_rows, 0, 1), fetch(proj_rows, 1, 1), high)
    feed = lanes_full(jnp.concatenate([feed, proj_beside], axis=1))
    feed = lax.all_gather(feed, "dp_0", axis=0, tiled=True)

    qkv_block, every_act = lax.optimization_barrier((qkv_block, every_act))
    qkv_block = gather_y(qkv_block)
    qkv_block, every_act = lax.optimization_barrier((qkv_block, every_act))
    part_a = gather_x(qkv_block)
    other_a = swap(part_a, "group", 1)

    mod_part = dot(every_act, ada_weight).astype(BF16)
    mod_part = lax.all_to_all(mod_part, DP, split_axis=0, concat_axis=1, tiled=True)
    feed, mod_part = lax.optimization_barrier((feed, mod_part))
    early = lax.all_gather(feed[:, width:], "dp_1", axis=0, tiled=True)
    other_early = swap(early, "group", 1)
    part_c = lax.all_gather(feed[:, :width], "dp_1", axis=0, tiled=True)
    other_c = swap(part_c, "group", 1)
    final_part = dot(acts, final_ada).astype(BF16)
    mod_parts = to_everyone(jnp.concatenate([mod_part, final_part], axis=1), "mp")

    spot = lax.broadcasted_iota(jnp.int32, (1, width), 1)
    per_x = n_y * n_z * rows
    per_y = n_z * rows
    block = spot // per_x
    inside = spot % per_x
    offset = jnp.where(block == 1, n_x - 1, jnp.where(block == 2, 1, jnp.where(block == 3, 2, 0)))

    def order_of(from_x):
        natural = (inside // per_y * n_x + from_x) * per_y + inside % per_y
        return (lax.broadcasted_iota(jnp.int32, (width, width), 0) == natural).astype(BF16)

    near_order = order_of((column + offset) % n_x)
    order = order_of(block)

    first = cond_first[0] == 1
    cond_rows = jnp.where(first, x_arrive[0], x_arrive[1])
    uncond_rows = jnp.where(first, x_arrive[1], x_arrive[0])
    arrived = jnp.stack([cond_rows, uncond_rows])
    share = tokens // n_mp
    own = lax.dynamic_slice_in_dim(arrived, place * share, share, 1)
    own = dot(own.reshape(-1, width), order).astype(BF16).reshape(2, share, width)
    images = dot(arrived.reshape(-1, width), near_order).astype(BF16)
    images = images.reshape(2, tokens, width)
    out_local = lax.dot_general(
        order, out_weight, (((0,), (0,)), ((), ())), preferred_element_type=F32
    ).astype(BF16)
    mod_parts = mod_parts.reshape(n_mp * 2, -1, width)

    def mods_in(pieces, by):
        count = pieces.shape[1]
        values = dot(pieces.reshape(-1, width), by).reshape(n_mp, 2, count, 1, width)
        values = jnp.sum(values, axis=0)
        return [values[:, i] for i in range(count)]

    shift_a, scale_a = mods_in(mod_parts[:, :2], near_order)
    gate_a, shift_m, scale_m, gate_m, shift_f, scale_f = mods_in(mod_parts[:, 2:], order)

    cores = core.reshape(1).astype(jnp.int32)
    mixed = attention(cores, images, shift_a, scale_a, part_a, other_a, n_mp, quarter)
    mixed = lax.all_to_all(mixed, "mp", 0, 0, tiled=True)
    base = (place ^ (2 * core)).reshape(1).astype(jnp.int32)
    first_sum, hidden_two = project(base, mixed, early, other_early, own, gate_a, shift_m, scale_m)
    hidden_two = hidden_two.reshape(2 * share, width)
    pair = swap(hidden_two, "mp", 1)
    keep, send = feed_forward(hidden_two, pair, early, other_early, part_c, other_c)
    recv = swap(send, "mp", 1)
    guided = finish(guidance, keep, recv, first_sum, gate_m, shift_f, scale_f, out_local)
    return guided.reshape(1, share * out_weight.shape[1])


def solution(mesh):
    torus = Mesh(
        mesh.devices.reshape(mesh.shape["group"], 8, 4, 2, mesh.shape["mp"]),
        ("group", "dp_0", "dp_1", "dp_2", "mp"),
    )
    placed = (
        P(GROUP_DP, None, None),
        P(GROUP_DP),
        P(GROUP_DP),
        P(GROUP_DP),
        P(),
        P(None, "mp"),
        P(None, "mp"),
        P("mp", DP),
        P("mp", None),
        P(None, DP, "mp"),
        P("mp", DP),
        P(DP, "mp"),
        P("mp", DP),
        P(),
    )
    return jax.shard_map(
        on_device, mesh=torus, in_specs=placed, out_specs=P(GROUP_DP, "mp"), check_vma=False
    )
```

time: 285 us -> 287 us (level)
  starting transfers between devices: 104 us -> 66.9 us
  blocking collectives: 7.66 us -> 37.2 us
  local copies, waits for them, and re-layouts: 35.2 us -> 14 us
  Pallas kernels: 5.56 us -> 25.9 us
  waiting for transfers between devices: 93 us -> 110 us
  matrix products: 22.5 us -> 9.56 us
  between operations: 3.39 us -> 16.2 us
  other arithmetic: 11.7 us -> 4.17 us
    all_gather x0 -> x3, waiting for transfers between devices: none -> 50.7 us  [the longest x1 40.7 us: on_device(): early = lax.all_gather(feed[:, width:], 'dp_1', axis=0, tiled=True)]
    all_to_all x6 -> x2, waiting for transfers between devices: 55.3 us -> 17.9 us  [to_everyone(): lax.all_to_all(jnp.broadcast_to(x[None], (size, *x.shape)), axis, 0, 0, t...]
    ppermute x12 -> x4, starting transfers between devices: 40.3 us -> 13.5 us  [shift(): return lax.ppermute(x, axis, [(i, (i + step) % size) for i in range(size)])]
    all_to_all x0 -> x1, blocking collectives: none -> 21.3 us  [on_device(): lax.all_to_all(mod_part, DP, split_axis=0, concat_axis=1, tiled=True)]
    pallas_call x1 -> x4, Pallas kernels: 5.56 us -> 25.9 us  [the longest x1 10.2 us: feed_forward(): pl.pallas_call(feed_body, grid=(2 * steps,), in_specs=[whole(own.shape),...]
    all_to_all x2 -> x1, waiting for transfers between devices: 22.6 us -> 7 us  [on_device(): mixed = lax.all_to_all(mixed, 'mp', 0, 0, tiled=True)]
    dot_general x4 -> x1, matrix products: 14.8 us -> 0.91 us  [on_device(): lax.dot_general(order, out_weight, (((0,), (0,)), ((), ())), preferred_el...]
    ppermute x12 -> x4, waiting for transfers between devices: 2.7 us -> 14.9 us  [shift(): return lax.ppermute(x, axis, [(i, (i + step) % size) for i in range(size)])]
  transfers between devices with their start and end apart: 26 -> 20, of which waited for: 13 -> 12; matrix products, arithmetic and copies ran while one was open for 17% -> 7% of each run, Pallas kernels for 2% -> 5%
where the time goes in v2:
time: 287 us; the launch traced here: 284 us
  waiting for transfers between devices  110 us (38%)
  starting transfers between devices  66.9 us (23%)
  blocking collectives  37.2 us (13%)
  Pallas kernels  25.9 us (9%)
  between operations  16.2 us (6%)
  local copies, waits for them, and re-layouts  14 us (5%)
  matrix products  9.56 us (3%)
  other arithmetic  4.17 us (1%)
    all_gather x1, waiting for transfers between devices, on_device(): early = lax.all_gather(feed[:, width:], 'dp_1', axis=0, tiled=True)  40.7 us
    all_to_all x1, blocking collectives, on_device(): lax.all_to_all(mod_part, DP, split_axis=0, concat_axis=1, tiled=True)  21.3 us
    all_to_all x2, starting transfers between devices, to_everyone(): lax.all_to_all(jnp.broadcast_to(x[None], (size, *x.shape)), axis, 0, 0, t...  20.1 us
    all_to_all x2, waiting for transfers between devices, to_everyone(): lax.all_to_all(jnp.broadcast_to(x[None], (size, *x.shape)), axis, 0, 0, t...  17.9 us
    ppermute x4, starting transfers between devices, fetch(): return lax.ppermute(x, ('group', 'dp_2', 'mp'), pairs)  17 us
    all_to_all x1, blocking collectives, to_everyone(): lax.all_to_all(jnp.broadcast_to(x[None], (size, *x.shape)), axis, 0, 0, t...  15.9 us
    ppermute x4, waiting for transfers between devices, shift(): return lax.ppermute(x, axis, [(i, (i + step) % size) for i in range(size)])  14.9 us
    ppermute x4, starting transfers between devices, shift(): return lax.ppermute(x, axis, [(i, (i + step) % size) for i in range(size)])  13.5 us
  transfers between devices with their start and end apart: 20, of which 12 were waited for; matrix products, arithmetic and copies ran while one was open for 7% of the time, Pallas kernels for 5%

profile of v2, /device:TPU:6, one launch (start us, length us, event | category | flops | bytes accessed | tf_op | source)
XLA Modules:
  0.0 284.1 jit_solution(16399387364186615282)
XLA Ops:
  6.5 4.4 %collective-permute-start.2 = (bf16[18,288]{1,0:T(8,128)(2,1)}, bf16[18,288]{1,0:T(8,128)(2,1)S(1)}, u32[]{:S(2)}, u32[]{:S(2)}) collective-permute-start(bf16[18,288]{1,0:T(8,128)(2,1)} %bitcast.74), channel_id=1, source_target_pairs={{0,1},{1,0},{2,3},{3,2},{4,5},{5,4},{6,7},{7,6},{256,259},{257,258... | collective-permute-start | bytes 31112 | tf_op jit(solution)/shard_map/ppermute | solution.py:313
  10.9 9.1 %collective-permute-start.3 = (bf16[18,288]{1,0:T(8,128)(2,1)}, bf16[18,288]{1,0:T(8,128)(2,1)S(1)}, u32[]{:S(2)}, u32[]{:S(2)}) collective-permute-start(bf16[18,288]{1,0:T(8,128)(2,1)} %bitcast.75), channel_id=1, source_target_pairs={{0,5},{1,4},{2,7},{3,6},{4,1},{5,0},{6,3},{7,2},{256,263},{257,262... | collective-permute-start | bytes 31112 | tf_op jit(solution)/shard_map/ppermute | solution.py:313
  21.6 2.8 collective-permute-start.1
  24.5 8.5 %collective-permute-done.1 = bf16[18,2592]{1,0:T(8,128)(2,1)S(1)} collective-permute-done((bf16[18,2592]{1,0:T(8,128)(2,1)S(1)}, bf16[18,2592]{1,0:T(8,128)(2,1)S(1)}, u32[]{:S(2)}, u32[]{:S(2)}) %collective-permute-start.1) | collective-permute-done | bytes 93344 | tf_op jit(solution)/shard_map/ppermute | solution.py:313
  34.1 2.8 collective-permute-start.4
  41.4 15.0 %all-to-all-start = ((bf16[64,2,288]{2,1,0:T(2,128)(2,1)}), bf16[64,2,288]{2,1,0:T(2,128)(2,1)S(1)}, u32[]{:S(2)}, u32[]{:S(2)}) async-start(bf16[64,2,288]{2,1,0:T(2,128)(2,1)} %broadcast_in_dim.56), calls=%async_computation | async-start | bytes 196608 | tf_op jit(solution)/shard_map/all_to_all | solution.py:18
  56.5 14.1 %all-to-all-done = bf16[64,2,288]{2,1,0:T(2,128)(2,1)S(1)} async-done(((bf16[64,2,288]{2,1,0:T(2,128)(2,1)}), bf16[64,2,288]{2,1,0:T(2,128)(2,1)S(1)}, u32[]{:S(2)}, u32[]{:S(2)}) %all-to-all-start) | async-done | bytes 73760 | tf_op jit(solution)/shard_map/all_to_all | solution.py:18
  70.8 15.9 %all_to_all.39 = bf16[8,36,512]{2,1,0:T(8,128)(2,1)S(1)} all-to-all(bf16[8,36,512]{2,1,0:T(8,128)(2,1)S(1)} %broadcast_in_dim.57), channel_id=1, replica_groups=mesh['group'=2,'dp_0'=8,'dp_1'=4,'dp_2'=2,'mp'=4] {'dp_0'}, dimensions={0} | all-to-all | bytes 589824 | tf_op jit(solution)/shard_map/all_to_all | solution.py:18
  87.1 21.3 %all_to_all.40 = bf16[64,2,108]{2,1,0:T(2,128)(2,1)S(1)} all-to-all(bf16[64,2,108]{2,1,0:T(2,128)(2,1)S(1)} %bitcast.69), channel_id=1, replica_groups=mesh['group'=2,'dp_0'=8,'dp_1'=4,'dp_2'=2,'mp'=4] {'dp_0','dp_1','dp_2'}, dimensions={0} | all-to-all | bytes 55296 | tf_op jit(solution)/shard_map/all_to_all | solution.py:327
  114.4 40.7 %all-gather.5.cloned.1.call-done.mine_ref.up_ref = bf16[1152,1792]{1,0:T(8,128)(2,1)} async-done(((bf16[288,1792]{1,0:T(8,128)(2,1)}), bf16[1152,1792]{1,0:T(8,128)(2,1)}) %all-gather.5.cloned.1.call-update) | async-done | bytes 4128784 | tf_op jit(solution)/shard_map/all_gather | solution.py:329
  157.4 2.9 %fusion.9 = bf16[512,1152]{1,0:T(8,128)(2,1)} fusion(bf16[512,1152]{1,0:T(8,128)(2,1)S(1)} %bitcast.63, s32[1152]{0:T(1024)S(1)} %fusion.41), kind=kOutput, calls=%fused_computation.10 | convolution fusion | flops 1360871424 | bytes 2363904 | tf_op jit(solution)/shard_map/dot_general | solution.py:62
  160.4 4.2 %collective-permute-start.5 = (bf16[288,512]{1,0:T(8,128)(2,1)S(1)}, bf16[288,512]{1,0:T(8,128)(2,1)S(1)}, u32[]{:S(2)}, u32[]{:S(2)}) collective-permute-start(bf16[288,512]{1,0:T(8,128)(2,1)S(1)} %reshape.238), channel_id=1, source_target_pairs={{0,8},{8,16},{16,24},{24,0},{1,9},{9,17},{17,25},{25,1},{2,10},{10... | collective-permute-start | bytes 884744 | tf_op jit(solution)/shard_map/ppermute | solution.py:23
  164.6 1.9 collective-permute-start.6
  167.3 4.4 %collective-permute-done.5 = bf16[288,512]{1,0:T(8,128)(2,1)S(1)} collective-permute-done((bf16[288,512]{1,0:T(8,128)(2,1)S(1)}, bf16[288,512]{1,0:T(8,128)(2,1)S(1)}, u32[]{:S(2)}, u32[]{:S(2)}) %collective-permute-start.5) | collective-permute-done | bytes 294944 | tf_op jit(solution)/shard_map/ppermute | solution.py:23
  171.7 5.4 %collective-permute-start.7 = (bf16[144,512]{1,0:T(8,128)(2,1)S(1)}, bf16[144,512]{1,0:T(8,128)(2,1)S(1)}, u32[]{:S(2)}, u32[]{:S(2)}) collective-permute-start(bf16[144,512]{1,0:T(8,128)(2,1)S(1)} %slice.95), channel_id=1, source_target_pairs={{0,8},{8,16},{16,24},{24,0},{1,9},{9,17},{17,25},{25,1},{2,10},{10... | collective-permute-start | bytes 442376 | tf_op jit(solution)/shard_map/ppermute | solution.py:23
  179.2 4.9 %collective-permute-done.7 = bf16[144,512]{1,0:T(8,128)(2,1)S(1)} collective-permute-done((bf16[144,512]{1,0:T(8,128)(2,1)S(1)}, bf16[144,512]{1,0:T(8,128)(2,1)S(1)}, u32[]{:S(2)}, u32[]{:S(2)}) %collective-permute-start.7) | collective-permute-done | bytes 147488 | tf_op jit(solution)/shard_map/ppermute | solution.py:23
  184.1 5.6 %collective-permute-done.8 = bf16[144,512]{1,0:T(8,128)(2,1)S(1)} collective-permute-done((bf16[144,512]{1,0:T(8,128)(2,1)S(1)}, bf16[144,512]{1,0:T(8,128)(2,1)S(1)}, u32[]{:S(2)}, u32[]{:S(2)}) %collective-permute-start.8) | collective-permute-done | bytes 147488 | tf_op jit(solution)/shard_map/ppermute | solution.py:23
  189.7 1.9 collective-permute-start.9
  191.6 10.0 %all-gather.7.cloned.1.call-done.down_ref = bf16[1152,1152]{1,0:T(8,128)(2,1)} async-done(((bf16[288,1152]{1,0:T(8,128)(2,1)}), bf16[1152,1152]{1,0:T(8,128)(2,1)}) %all-gather.7.cloned.1.call-update) | async-done | bytes 2654224 | tf_op jit(solution)/shard_map/all_gather | solution.py:331
  204.4 5.1 %all-to-all-start.3 = ((bf16[4,2,9216]{2,1,0:T(2,128)(2,1)}), bf16[4,2,9216]{2,1,0:T(2,128)(2,1)S(1)}, u32[]{:S(2)}, u32[]{:S(2)}) async-start(bf16[4,2,9216]{2,1,0:T(2,128)(2,1)} %broadcast_in_dim.58), calls=%async_computation.3 | async-start | bytes 294912 | tf_op jit(solution)/shard_map/all_to_all | solution.py:18
  209.4 2.9 %fusion.15 = bf16[128,1152]{1,0:T(8,128)(2,1)} fusion(bf16[128,1152]{1,0:T(8,128)(2,1)} %bitcast.67, s32[1152]{0:T(1024)S(1)} %multiply_add_fusion), kind=kOutput, calls=%fused_computation.16 | convolution fusion | flops 341213184 | bytes 594432 | tf_op jit(solution)/shard_map/dot_general | solution.py:62
  212.4 3.8 %all-to-all-done.3 = bf16[4,2,9216]{2,1,0:T(2,128)(2,1)S(1)} async-done(((bf16[4,2,9216]{2,1,0:T(2,128)(2,1)}), bf16[4,2,9216]{2,1,0:T(2,128)(2,1)S(1)}, u32[]{:S(2)}, u32[]{:S(2)}) %all-to-all-start.3) | async-done | bytes 147488 | tf_op jit(solution)/shard_map/all_to_all | solution.py:18
  218.0 9.1 %attention.1 = bf16[4,288,128]{2,1,0:T(8,128)(2,1)} custom-call(s32[1]{0:T(128)} %bitcast.1.core_ref, bf16[2,256,1152]{2,1,0:T(8,128)(2,1)} %bitcast.62, f32[2,1,1152]{2,1,0:T(1,128)} %get-tuple-element.64.shift_ref, f32[2,1,1152]{2,1,0:T(1,128)} %get-tuple-element.63.scale_ref, bf16[1152,512]{1,0:T(8,128)(2,1)} %copy-done.1, ...), custom_call_target="tpu_custom_call" | custom-call | tf_op jit(solution)/shard_map/attention/pallas_call | solution.py:114
  227.1 3.5 %all-to-all-start.4 = ((bf16[4,288,128]{2,1,0:T(8,128)(2,1)}), bf16[4,288,128]{2,1,0:T(8,128)(2,1)S(1)}, u32[]{:S(2)}, u32[]{:S(2)}) async-start(bf16[4,288,128]{2,1,0:T(8,128)(2,1)} %attention.1), calls=%async_computation.4 | async-start | bytes 589824 | tf_op jit(solution)/shard_map/all_to_all | solution.py:375
  232.4 7.0 %all-to-all-done.4.mixed_ref = bf16[4,288,128]{2,1,0:T(8,128)(2,1)S(1)} async-done(((bf16[4,288,128]{2,1,0:T(8,128)(2,1)}), bf16[4,288,128]{2,1,0:T(8,128)(2,1)S(1)}, u32[]{:S(2)}, u32[]{:S(2)}) %all-to-all-start.4) | async-done | bytes 294944 | tf_op jit(solution)/shard_map/all_to_all | solution.py:375
  240.2 4.0 %project.1 = (f32[2,64,1152]{2,1,0:T(8,128)}, bf16[2,64,1152]{2,1,0:T(8,128)(2,1)}) custom-call(s32[1]{0:T(128)} %bitcast.base_ref, bf16[4,288,128]{2,1,0:T(8,128)(2,1)} %copy-done.2, bf16[1152,1792]{1,0:T(8,128)(2,1)} %all-gather.5.cloned.1.call-done.mine_ref.up_ref, bf16[1152,1792]{1,0:T(8,128)(2,1)} %collective-permute-done.10.other_ref.up_other_ref, ...), custom_call_target="tpu_custom_call" | custom-call | tf_op jit(solution)/shard_map/project/pallas_call | solution.py:153
  244.2 2.1 collective-permute-start.11
  246.2 7.0 %collective-permute-done.11.pair_ref = bf16[128,1152]{1,0:T(8,128)(2,1)S(1)} collective-permute-done((bf16[128,1152]{1,0:T(8,128)(2,1)}, bf16[128,1152]{1,0:T(8,128)(2,1)S(1)}, u32[]{:S(2)}, u32[]{:S(2)}) %collective-permute-start.11) | collective-permute-done | bytes 294944 | tf_op jit(solution)/shard_map/ppermute | solution.py:28
  253.9 10.2 %feed_forward.1 = (f32[128,1152]{1,0:T(8,128)}, bf16[128,1152]{1,0:T(8,128)(2,1)}) custom-call(bf16[128,1152]{1,0:T(8,128)(2,1)} %bitcast.65, bf16[128,1152]{1,0:T(8,128)(2,1)} %copy-done.3, bf16[1152,1792]{1,0:T(8,128)(2,1)} %all-gather.5.cloned.1.call-done.mine_ref.up_ref, bf16[1152,1792]{1,0:T(8,128)(2,1)} %collective-permute-done.10.other_ref.up_other_ref, ...), custom_call_target="tpu_custom_call" | custom-call | tf_op jit(solution)/shard_map/feed_forward/pallas_call | solution.py:217
  264.1 2.2 collective-permute-start.13
  268.8 4.1 %collective-permute-done.13.recv_ref = bf16[128,1152]{1,0:T(8,128)(2,1)S(1)} collective-permute-done((bf16[128,1152]{1,0:T(8,128)(2,1)}, bf16[128,1152]{1,0:T(8,128)(2,1)S(1)}, u32[]{:S(2)}, u32[]{:S(2)}) %collective-permute-start.13) | collective-permute-done | bytes 294944 | tf_op jit(solution)/shard_map/ppermute | solution.py:28
  273.6 2.6 finish.1
  (87 shorter events, 28.6 us)
Async XLA Ops:
  6.5 150.5 %copy-start = (bf16[288,2304]{1,0:T(8,128)(2,1)S(1)}, bf16[288,2304]{1,0:T(8,128)(2,1)}, u32[]{:S(2)}) copy-start(bf16[288,2304]{1,0:T(8,128)(2,1)} %param.22) | copy-start | bytes 3981316
  6.5 27.3 %copy-start.5 = (bf16[3,18,288]{2,1,0:T(8,128)(2,1)S(1)}, bf16[3,18,288]{2,1,0:T(8,128)(2,1)}, u32[]{:S(2)}) copy-start(bf16[3,18,288]{2,1,0:T(8,128)(2,1)} %param.23) | copy-start | bytes 93316
  6.5 102.0 %all-gather.9.cloned.1.call-start = ((), (), s32[]{:S(2)}) async-start(), calls=%async_computation.7 | async-start | bytes 2119680 | tf_op jit(solution)/shard_map/all_gather | solution.py:318
  6.5 17.9 %collective-permute-start.2 = (bf16[18,288]{1,0:T(8,128)(2,1)}, bf16[18,288]{1,0:T(8,128)(2,1)S(1)}, u32[]{:S(2)}, u32[]{:S(2)}) collective-permute-start(bf16[18,288]{1,0:T(8,128)(2,1)} %bitcast.74), channel_id=1, source_target_pairs={{0,1},{1,0},{2,3},{3,2},{4,5},{5,4},{6,7},{7,6},{256,259},{257,258... | collective-permute-start | bytes 31112 | tf_op jit(solution)/shard_map/ppermute | solution.py:313
  10.9 13.5 %collective-permute-start.3 = (bf16[18,288]{1,0:T(8,128)(2,1)}, bf16[18,288]{1,0:T(8,128)(2,1)S(1)}, u32[]{:S(2)}, u32[]{:S(2)}) collective-permute-start(bf16[18,288]{1,0:T(8,128)(2,1)} %bitcast.75), channel_id=1, source_target_pairs={{0,5},{1,4},{2,7},{3,6},{4,1},{5,0},{6,3},{7,2},{256,263},{257,262... | collective-permute-start | bytes 31112 | tf_op jit(solution)/shard_map/ppermute | solution.py:313
  20.9 3.6 %collective-permute-start = (bf16[18,2592]{1,0:T(8,128)(2,1)S(1)}, bf16[18,2592]{1,0:T(8,128)(2,1)S(1)}, u32[]{:S(2)}, u32[]{:S(2)}) collective-permute-start(bf16[18,2592]{1,0:T(8,128)(2,1)S(1)} %pad_maximum_fusion.1), channel_id=1, source_target_pairs={{0,0},{1,1},{2,2},{3,3},{4,4},{5,5},{6,6},{7,7},{256,258},{257,259... | collective-permute-start | bytes 279944 | tf_op jit(solution)/shard_map/ppermute | solution.py:313
  21.6 11.4 %collective-permute-start.1 = (bf16[18,2592]{1,0:T(8,128)(2,1)S(1)}, bf16[18,2592]{1,0:T(8,128)(2,1)S(1)}, u32[]{:S(2)}, u32[]{:S(2)}) collective-permute-start(bf16[18,2592]{1,0:T(8,128)(2,1)S(1)} %pad_maximum_fusion.1), channel_id=1, source_target_pairs={{0,4},{1,5},{2,6},{3,7},{4,0},{5,1},{6,2},{7,3},{256,262},{257,263... | collective-permute-start | bytes 279944 | tf_op jit(solution)/shard_map/ppermute | solution.py:313
  34.1 22.4 %collective-permute-start.4 = (bf16[18,432]{1,0:T(8,128)(2,1)S(1)}, bf16[18,432]{1,0:T(8,128)(2,1)S(1)}, u32[]{:S(2)}, u32[]{:S(2)}) collective-permute-start(bf16[18,432]{1,0:T(8,128)(2,1)S(1)} %reshape.236), channel_id=1, source_target_pairs={{0,4},{4,0},{1,5},{5,1},{2,6},{6,2},{3,7},{7,3},{8,12},{12,8},{9,1... | collective-permute-start | bytes 46664 | tf_op jit(solution)/shard_map/ppermute | solution.py:28
  39.4 47.3 %copy-start.6 = (bf16[288,108]{1,0:T(8,128)(2,1)S(1)}, bf16[288,108]{1,0:T(8,128)(2,1)}, u32[]{:S(2)}) copy-start(bf16[288,108]{1,0:T(8,128)(2,1)} %param.21) | copy-start | bytes 186628
  41.4 29.3 %all-to-all-start = ((bf16[64,2,288]{2,1,0:T(2,128)(2,1)}), bf16[64,2,288]{2,1,0:T(2,128)(2,1)S(1)}, u32[]{:S(2)}, u32[]{:S(2)}) async-start(bf16[64,2,288]{2,1,0:T(2,128)(2,1)} %broadcast_in_dim.56), calls=%async_computation | async-start | bytes 196608 | tf_op jit(solution)/shard_map/all_to_all | solution.py:18
  56.4 98.7 %all-gather.5.cloned.1.call-start = ((), (), s32[]{:S(2)}) async-start(), calls=%async_computation.5 | async-start | bytes 5160960 | tf_op jit(solution)/shard_map/all_gather | solution.py:329
  111.4 90.3 %all-gather.7.cloned.1.call-start = ((), (), s32[]{:S(2)}) async-start(), calls=%async_computation.6 | async-start | bytes 3317760 | tf_op jit(solution)/shard_map/all_gather | solution.py:331
  155.1 84.4 %collective-permute-start.10 = (bf16[1152,1792]{1,0:T(8,128)(2,1)}, bf16[1152,1792]{1,0:T(8,128)(2,1)}, u32[]{:S(2)}, u32[]{:S(2)}) collective-permute-start(bf16[1152,1792]{1,0:T(8,128)(2,1)} %all-gather.5.cloned.1.call-done.mine_ref.up_ref), channel_id=1, source_target_pairs={{0,256},{256,0},{1,257},{257,1},{2,258},{258,2},{3,259},{259,3},{4... | collective-permute-start | bytes 12386312 | tf_op jit(solution)/shard_map/ppermute | solution.py:28
  160.4 11.3 %collective-permute-start.5 = (bf16[288,512]{1,0:T(8,128)(2,1)S(1)}, bf16[288,512]{1,0:T(8,128)(2,1)S(1)}, u32[]{:S(2)}, u32[]{:S(2)}) collective-permute-start(bf16[288,512]{1,0:T(8,128)(2,1)S(1)} %reshape.238), channel_id=1, source_target_pairs={{0,8},{8,16},{16,24},{24,0},{1,9},{9,17},{17,25},{25,1},{2,10},{10... | collective-permute-start | bytes 884744 | tf_op jit(solution)/shard_map/ppermute | solution.py:23
  164.6 12.6 %collective-permute-start.6 = (bf16[288,512]{1,0:T(8,128)(2,1)S(1)}, bf16[288,512]{1,0:T(8,128)(2,1)S(1)}, u32[]{:S(2)}, u32[]{:S(2)}) collective-permute-start(bf16[288,512]{1,0:T(8,128)(2,1)S(1)} %reshape.238), channel_id=1, source_target_pairs={{0,24},{8,0},{16,8},{24,16},{1,25},{9,1},{17,9},{25,17},{2,26},{10... | collective-permute-start | bytes 884744 | tf_op jit(solution)/shard_map/ppermute | solution.py:23
  171.7 12.4 %collective-permute-start.7 = (bf16[144,512]{1,0:T(8,128)(2,1)S(1)}, bf16[144,512]{1,0:T(8,128)(2,1)S(1)}, u32[]{:S(2)}, u32[]{:S(2)}) collective-permute-start(bf16[144,512]{1,0:T(8,128)(2,1)S(1)} %slice.95), channel_id=1, source_target_pairs={{0,8},{8,16},{16,24},{24,0},{1,9},{9,17},{17,25},{25,1},{2,10},{10... | collective-permute-start | bytes 442376 | tf_op jit(solution)/shard_map/ppermute | solution.py:23
  177.2 12.5 %collective-permute-start.8 = (bf16[144,512]{1,0:T(8,128)(2,1)S(1)}, bf16[144,512]{1,0:T(8,128)(2,1)S(1)}, u32[]{:S(2)}, u32[]{:S(2)}) collective-permute-start(bf16[144,512]{1,0:T(8,128)(2,1)S(1)} %slice.96), channel_id=1, source_target_pairs={{0,24},{8,0},{16,8},{24,16},{1,25},{9,1},{17,9},{25,17},{2,26},{10... | collective-permute-start | bytes 442376 | tf_op jit(solution)/shard_map/ppermute | solution.py:23
  189.7 22.7 %copy-start.1 = (bf16[1152,512]{1,0:T(8,128)(2,1)}, bf16[1152,512]{1,0:T(8,128)(2,1)S(1)}, u32[]{:S(2)}) copy-start(bf16[1152,512]{1,0:T(8,128)(2,1)S(1)} %constant_dynamic-update-slice_fusion.mine_ref) | copy-start | bytes 3538948
  189.7 28.3 %collective-permute-start.9 = (bf16[1152,512]{1,0:T(8,128)(2,1)S(1)}, bf16[1152,512]{1,0:T(8,128)(2,1)}, u32[]{:S(2)}, u32[]{:S(2)}) collective-permute-start(bf16[1152,512]{1,0:T(8,128)(2,1)S(1)} %constant_dynamic-update-slice_fusion.mine_ref), channel_id=1, source_target_pairs={{0,256},{256,0},{1,257},{257,1},{2,258},{258,2},{3,259},{259,3},{4... | collective-permute-start | bytes 3538952 | tf_op jit(solution)/shard_map/ppermute | solution.py:28
  201.7 44.6 %collective-permute-start.12 = (bf16[1152,1152]{1,0:T(8,128)(2,1)}, bf16[1152,1152]{1,0:T(8,128)(2,1)}, u32[]{:S(2)}, u32[]{:S(2)}) collective-permute-start(bf16[1152,1152]{1,0:T(8,128)(2,1)} %all-gather.7.cloned.1.call-done.down_ref), channel_id=1, source_target_pairs={{0,256},{256,0},{1,257},{257,1},{2,258},{258,2},{3,259},{259,3},{4... | collective-permute-start | bytes 7962632 | tf_op jit(solution)/shard_map/ppermute | solution.py:28
  204.4 11.8 %all-to-all-start.3 = ((bf16[4,2,9216]{2,1,0:T(2,128)(2,1)}), bf16[4,2,9216]{2,1,0:T(2,128)(2,1)S(1)}, u32[]{:S(2)}, u32[]{:S(2)}) async-start(bf16[4,2,9216]{2,1,0:T(2,128)(2,1)} %broadcast_in_dim.58), calls=%async_computation.3 | async-start | bytes 294912 | tf_op jit(solution)/shard_map/all_to_all | solution.py:18
  227.1 12.3 %all-to-all-start.4 = ((bf16[4,288,128]{2,1,0:T(8,128)(2,1)}), bf16[4,288,128]{2,1,0:T(8,128)(2,1)S(1)}, u32[]{:S(2)}, u32[]{:S(2)}) async-start(bf16[4,288,128]{2,1,0:T(8,128)(2,1)} %attention.1), calls=%async_computation.4 | async-start | bytes 589824 | tf_op jit(solution)/shard_map/all_to_all | solution.py:375
  239.4 0.7 copy-start.2
  244.2 22.1 %copy-start.7 = (bf16[1152,16]{0,1:T(8,128)(2,1)S(1)}, bf16[1152,16]{0,1:T(8,128)(2,1)}, u32[]{:S(2)}) copy-start(bf16[1152,16]{0,1:T(8,128)(2,1)} %param.27) | copy-start | bytes 110596
  244.2 9.0 %collective-permute-start.11 = (bf16[128,1152]{1,0:T(8,128)(2,1)}, bf16[128,1152]{1,0:T(8,128)(2,1)S(1)}, u32[]{:S(2)}, u32[]{:S(2)}) collective-permute-start(bf16[128,1152]{1,0:T(8,128)(2,1)} %bitcast.64), channel_id=1, source_target_pairs={{0,1},{1,0},{2,3},{3,2},{4,5},{5,4},{6,7},{7,6},{8,9},{9,8},{10,11... | collective-permute-start | bytes 884744 | tf_op jit(solution)/shard_map/ppermute | solution.py:28
  253.2 0.7 copy-start.3
  264.1 8.8 %collective-permute-start.13 = (bf16[128,1152]{1,0:T(8,128)(2,1)}, bf16[128,1152]{1,0:T(8,128)(2,1)S(1)}, u32[]{:S(2)}, u32[]{:S(2)}) collective-permute-start(bf16[128,1152]{1,0:T(8,128)(2,1)} %get-tuple-element.23), channel_id=1, source_target_pairs={{0,1},{1,0},{2,3},{3,2},{4,5},{5,4},{6,7},{7,6},{8,9},{9,8},{10,11... | collective-permute-start | bytes 884744 | tf_op jit(solution)/shard_map/ppermute | solution.py:28
  272.9 0.7 copy-start.4
Sparse Core Ops, SparseCore 0:
  34.0 45.4 all-gather.8
  111.5 43.5 all-gather.4
  157.2 44.4 all-gather.6

commit v3 on v2

--- a/solution.py
+++ b/solution.py
@@ -82,7 +82,7 @@
         hidden = (layer_norm(x) * (1.0 + scale_ref[image]) + shift_ref[image]).astype(BF16)
         sides = []
         for ref in (mine_ref, other_ref):
-            qkv = dot(hidden, ref[...]).astype(BF16)
+            qkv = dot(hidden, ref[:, : 6 * head_dim]).astype(BF16)
             heads = []
             for head in range(2):
                 at = head * head_dim
@@ -124,32 +124,35 @@
     )(core, x, shift_a, scale_a, mine, other)
 
 
-def project_body(base_ref, mixed_ref, mine_ref, other_ref, own_ref, gate_ref, shift_ref, scale_ref,
+def project_body(base_ref, mixed_ref, mine_ref, other_ref, change_ref, own_ref, gate_ref, shift_ref, scale_ref,
                  sum_ref, hidden_ref, rows_ref):
     quarter = mixed_ref.shape[1]
+    start = 3 * quarter // 2
+    lead = start % 128
     base = base_ref[0]
+    rows_ref[...] = jnp.zeros(rows_ref.shape, BF16)
     for i in range(4):
-        rows_ref[i * quarter : (i + 1) * quarter] = mixed_ref[base ^ i]
-    middle = 2 * quarter
+        at = lead + i % 2 * quarter
+        rows_ref[i // 2, at : at + quarter] = mixed_ref[base ^ i]
     both = (((0,), (1,)), ((), ()))
     attn = lax.dot_general(
-        rows_ref[:middle], mine_ref[:, :middle], both, preferred_element_type=F32
+        rows_ref[0], mine_ref[:, start - lead :], both, preferred_element_type=F32
     ) + lax.dot_general(
-        rows_ref[middle:], other_ref[:, :middle], both, preferred_element_type=F32
+        rows_ref[1], other_ref[:, start - lead :], both, preferred_element_type=F32
     )
     share = own_ref.shape[1]
     for i in range(2):
         total = own_ref[i].astype(F32) + gate_ref[i] * attn[i * share : (i + 1) * share]
         sum_ref[i] = total
-        hidden_ref[i] = (layer_norm(total) * (1.0 + scale_ref[i]) + shift_ref[i]).astype(BF16)
-
-
-def project(base, mixed, mine, other, own, gate_a, shift_m, scale_m):
+        hidden = (layer_norm(total) * (1.0 + scale_ref[i]) + shift_ref[i]).astype(BF16)
+        hidden_ref[i] = dot_t(hidden, change_ref[...]).astype(BF16)
+
+
+def project(base, mixed, mine, other, change, own, gate_a, shift_m, scale_m):
     _, share, width = own.shape
     vector = whole((2, 1, width))
-    aside = pl.BlockSpec(
-        (pl.Element(width), pl.Element(mine.shape[1] - width)), lambda *_: (0, width)
-    )
+    start = 3 * mixed.shape[1] // 2
+    depth = mine.shape[1] - start // 128 * 128
     return pl.pallas_call(
         project_body,
         grid_spec=pltpu.PrefetchScalarGridSpec(
@@ -157,22 +160,23 @@
             grid=(1,),
             in_specs=[
                 whole(mixed.shape),
-                aside,
-                aside,
+                whole(mine.shape),
+                whole(other.shape),
+                whole(change.shape),
                 whole(own.shape),
                 vector,
                 vector,
                 vector,
             ],
             out_specs=[whole(own.shape), whole(own.shape)],
-            scratch_shapes=[pltpu.VMEM((4 * mixed.shape[1], 2 * share), BF16)],
+            scratch_shapes=[pltpu.VMEM((2, depth, 2 * share), BF16)],
         ),
         out_shape=[
             jax.ShapeDtypeStruct(own.shape, F32),
             jax.ShapeDtypeStruct(own.shape, BF16),
         ],
         name="project",
-    )(base, mixed, mine, other, own, gate_a, shift_m, scale_m)
+    )(base, mixed, mine, other, change, own, gate_a, shift_m, scale_m)
 
 
 def feed_body(own_ref, pair_ref, up_ref, up_other_ref, down_ref, down_other_ref,
@@ -301,7 +305,7 @@
     qkv_own = jnp.where(core == 0, qkv_weight[:, :, :half], qkv_weight[:, :, half:])
     qkv_own = qkv_own.transpose(1, 0, 2).reshape(rows, 3 * half)
     qkv_other = swap(qkv_own, "dp_2", 1)
-    qkv_block = lanes_full(by_height(qkv_own, qkv_other, high))
+    qkv_block = by_height(qkv_own, qkv_other, high)
 
     proj_rows = proj_weight.T
     feed = jnp.concatenate([fc2_weight.T, fc1_weight, proj_rows], axis=1)
@@ -314,22 +318,21 @@
 
     feed = by_height(fetch(feed, 0, 0), fetch(feed, 1, 0), high)
     proj_beside = by_height(fetch(proj_rows, 0, 1), fetch(proj_rows, 1, 1), high)
-    feed = lanes_full(jnp.concatenate([feed, proj_beside], axis=1))
-    feed = lax.all_gather(feed, "dp_0", axis=0, tiled=True)
-
-    qkv_block, every_act = lax.optimization_barrier((qkv_block, every_act))
-    qkv_block = gather_y(qkv_block)
-    qkv_block, every_act = lax.optimization_barrier((qkv_block, every_act))
-    part_a = gather_x(qkv_block)
+    part_a = lanes_full(jnp.concatenate([qkv_block, feed[:, 2 * width :], proj_beside], axis=1))
+    part_a, every_act = lax.optimization_barrier((part_a, every_act))
+    part_a = gather_y(part_a)
+    part_a, every_act = lax.optimization_barrier((part_a, every_act))
+    part_a = gather_x(part_a)
     other_a = swap(part_a, "group", 1)
+
+    feed = lax.all_gather(feed[:, : 2 * width], "dp_0", axis=0, tiled=True)
+    part_b = lax.all_gather(feed[:, width:], "dp_1", axis=0, tiled=True)
+    other_b = swap(part_b, "group", 1)
+    part_c = gather_x(feed[:, :width])
+    other_c = swap(part_c, "group", 1)
 
     mod_part = dot(every_act, ada_weight).astype(BF16)
     mod_part = lax.all_to_all(mod_part, DP, split_axis=0, concat_axis=1, tiled=True)
-    feed, mod_part = lax.optimization_barrier((feed, mod_part))
-    early = lax.all_gather(feed[:, width:], "dp_1", axis=0, tiled=True)
-    other_early = swap(early, "group", 1)
-    part_c = lax.all_gather(feed[:, :width], "dp_1", axis=0, tiled=True)
-    other_c = swap(part_c, "group", 1)
     final_part = dot(acts, final_ada).astype(BF16)
     mod_parts = to_everyone(jnp.concatenate([mod_part, final_part], axis=1), "mp")
 
@@ -340,12 +343,11 @@
     inside = spot % per_x
     offset = jnp.where(block == 1, n_x - 1, jnp.where(block == 2, 1, jnp.where(block == 3, 2, 0)))
 
-    def order_of(from_x):
-        natural = (inside // per_y * n_x + from_x) * per_y + inside % per_y
-        return (lax.broadcasted_iota(jnp.int32, (width, width), 0) == natural).astype(BF16)
-
-    near_order = order_of((column + offset) % n_x)
-    order = order_of(block)
+    from_x = (column + offset) % n_x
+    final = (inside // per_y * n_x + from_x) * per_y + inside % per_y
+    order = (lax.broadcasted_iota(jnp.int32, (width, width), 0) == final).astype(BF16)
+    up_natural = (inside // per_y * n_x + block) * per_y + inside % per_y
+    change = (up_natural.reshape(width, 1) == final).astype(BF16)
 
     first = cond_first[0] == 1
     cond_rows = jnp.where(first, x_arrive[0], x_arrive[1])
@@ -354,7 +356,7 @@
     share = tokens // n_mp
     own = lax.dynamic_slice_in_dim(arrived, place * share, share, 1)
     own = dot(own.reshape(-1, width), order).astype(BF16).reshape(2, share, width)
-    images = dot(arrived.reshape(-1, width), near_order).astype(BF16)
+    images = dot(arrived.reshape(-1, width), order).astype(BF16)
     images = images.reshape(2, tokens, width)
     out_local = lax.dot_general(
         order, out_weight, (((0,), (0,)), ((), ())), preferred_element_type=F32
@@ -367,17 +369,17 @@
         values = jnp.sum(values, axis=0)
         return [values[:, i] for i in range(count)]
 
-    shift_a, scale_a = mods_in(mod_parts[:, :2], near_order)
+    shift_a, scale_a = mods_in(mod_parts[:, :2], order)
     gate_a, shift_m, scale_m, gate_m, shift_f, scale_f = mods_in(mod_parts[:, 2:], order)
 
     cores = core.reshape(1).astype(jnp.int32)
     mixed = attention(cores, images, shift_a, scale_a, part_a, other_a, n_mp, quarter)
     mixed = lax.all_to_all(mixed, "mp", 0, 0, tiled=True)
     base = (place ^ (2 * core)).reshape(1).astype(jnp.int32)
-    first_sum, hidden_two = project(base, mixed, early, other_early, own, gate_a, shift_m, scale_m)
+    first_sum, hidden_two = project(base, mixed, part_a, other_a, change, own, gate_a, shift_m, scale_m)
     hidden_two = hidden_two.reshape(2 * share, width)
     pair = swap(hidden_two, "mp", 1)
-    keep, send = feed_forward(hidden_two, pair, early, other_early, part_c, other_c)
+    keep, send = feed_forward(hidden_two, pair, part_b, other_b, part_c, other_c)
     recv = swap(send, "mp", 1)
     guided = finish(guidance, keep, recv, first_sum, gate_m, shift_f, scale_f, out_local)
     return guided.reshape(1, share * out_weight.shape[1])

time: 287 us -> 264 us (0.920)
  waiting for transfers between devices: 110 us -> 69.3 us
  blocking collectives: 37.2 us -> 0 us
  starting transfers between devices: 66.9 us -> 101 us
  local copies, waits for them, and re-layouts: 14 us -> 30.9 us
  Pallas kernels: 25.9 us -> 29.5 us
    all_gather x3 -> x2, waiting for transfers between devices: 50.7 us -> 6.69 us  [the longest x1 6.67 us: on_device(): feed = lax.all_gather(feed[:, :2 * width], 'dp_0', axis=0, tiled=True)]
    all_to_all x2 -> x0, blocking collectives: 37.2 us -> none  [the longest x1 21.3 us: on_device(): lax.all_to_all(mod_part, DP, split_axis=0, concat_axis=1, tiled=True)]
    unnamed x23 -> x35, local copies, waits for them, and re-layouts: 2.53 us -> 13.9 us
    ppermute x4 -> x8, starting transfers between devices: 13.5 us -> 24.5 us  [shift(): return lax.ppermute(x, axis, [(i, (i + step) % size) for i in range(size)])]
    all_to_all x0 -> x1, starting transfers between devices: none -> 10.7 us  [on_device(): lax.all_to_all(mod_part, DP, split_axis=0, concat_axis=1, tiled=True)]
    all_to_all x0 -> x1, waiting for transfers between devices: none -> 8.2 us  [on_device(): lax.all_to_all(mod_part, DP, split_axis=0, concat_axis=1, tiled=True)]
    ppermute x4, starting transfers between devices: 17 us -> 22.9 us  [fetch(): return lax.ppermute(x, ('group', 'dp_2', 'mp'), pairs)]
    ppermute x6, starting transfers between devices: 12.8 us -> 17.9 us  [swap(): return lax.ppermute(x, axis, [(i, i ^ bit) for i in range(size)])]
  transfers between devices with their start and end apart: 20 -> 25, of which waited for: 12 -> 12; matrix products, arithmetic and copies ran while one was open for 7% -> 15% of each run, Pallas kernels for 5% -> 6%
where the time goes in v3:
time: 264 us; the launch traced here: 262 us
  starting transfers between devices  101 us (38%)
  waiting for transfers between devices  69.3 us (26%)
  local copies, waits for them, and re-layouts  30.9 us (12%)
  Pallas kernels  29.5 us (11%)
  between operations  16.5 us (6%)
  matrix products  8.59 us (3%)
  other arithmetic  6.57 us (2%)
    ppermute x8, starting transfers between devices, shift(): return lax.ppermute(x, axis, [(i, (i + step) % size) for i in range(size)])  24.5 us
    ppermute x4, starting transfers between devices, fetch(): return lax.ppermute(x, ('group', 'dp_2', 'mp'), pairs)  22.9 us
    all_to_all x3, starting transfers between devices, to_everyone(): lax.all_to_all(jnp.broadcast_to(x[None], (size, *x.shape)), axis, 0, 0, t...  21.6 us
    all_to_all x3, waiting for transfers between devices, to_everyone(): lax.all_to_all(jnp.broadcast_to(x[None], (size, *x.shape)), axis, 0, 0, t...  18 us
    ppermute x6, starting transfers between devices, swap(): return lax.ppermute(x, axis, [(i, i ^ bit) for i in range(size)])  17.9 us
    unnamed x35, local copies, waits for them, and re-layouts  13.9 us
    ppermute x8, waiting for transfers between devices, shift(): return lax.ppermute(x, axis, [(i, (i + step) % size) for i in range(size)])  13.6 us
    ppermute x6, waiting for transfers between devices, swap(): return lax.ppermute(x, axis, [(i, i ^ bit) for i in range(size)])  10.9 us
  transfers between devices with their start and end apart: 25, of which 12 were waited for; matrix products, arithmetic and copies ran while one was open for 15% of the time, Pallas kernels for 6%

profile of v3, /device:TPU:6, one launch (start us, length us, event | category | flops | bytes accessed | tf_op | source)
XLA Modules:
  0.0 262.4 jit_solution(3477439956542348874)
XLA Ops:
  8.2 10.9 %collective-permute-start.2 = (bf16[18,2592]{1,0:T(8,128)(2,1)S(1)}, bf16[18,2592]{1,0:T(8,128)(2,1)S(1)}, u32[]{:S(2)}, u32[]{:S(2)}) collective-permute-start(bf16[18,2592]{1,0:T(8,128)(2,1)S(1)} %pad_maximum_fusion.2), channel_id=1, source_target_pairs={{0,4},{1,5},{2,6},{3,7},{4,0},{5,1},{6,2},{7,3},{256,262},{257,263... | collective-permute-start | bytes 279944 | tf_op jit(solution)/shard_map/ppermute | solution.py:317
  19.2 3.8 %collective-permute-done.2 = bf16[18,2592]{1,0:T(8,128)(2,1)S(1)} collective-permute-done((bf16[18,2592]{1,0:T(8,128)(2,1)S(1)}, bf16[18,2592]{1,0:T(8,128)(2,1)S(1)}, u32[]{:S(2)}, u32[]{:S(2)}) %collective-permute-start.2) | collective-permute-done | bytes 93344 | tf_op jit(solution)/shard_map/ppermute | solution.py:317
  23.8 4.2 %collective-permute-start.3 = (bf16[18,288]{1,0:T(8,128)(2,1)}, bf16[18,288]{1,0:T(8,128)(2,1)}, u32[]{:S(2)}, u32[]{:S(2)}) collective-permute-start(bf16[18,288]{1,0:T(8,128)(2,1)} %bitcast.70), channel_id=1, source_target_pairs={{0,1},{1,0},{2,3},{3,2},{4,5},{5,4},{6,7},{7,6},{256,259},{257,258... | collective-permute-start | bytes 31112 | tf_op jit(solution)/shard_map/ppermute | solution.py:317
  28.0 7.1 %collective-permute-start.4 = (bf16[18,288]{1,0:T(8,128)(2,1)}, bf16[18,288]{1,0:T(8,128)(2,1)}, u32[]{:S(2)}, u32[]{:S(2)}) collective-permute-start(bf16[18,288]{1,0:T(8,128)(2,1)} %bitcast.71), channel_id=1, source_target_pairs={{0,5},{1,4},{2,7},{3,6},{4,1},{5,0},{6,3},{7,2},{256,263},{257,262... | collective-permute-start | bytes 31112 | tf_op jit(solution)/shard_map/ppermute | solution.py:317
  39.5 11.6 %all-to-all-start = ((bf16[64,2,288]{2,1,0:T(2,128)(2,1)}), bf16[64,2,288]{2,1,0:T(2,128)(2,1)}, u32[]{:S(2)}, u32[]{:S(2)}) async-start(bf16[64,2,288]{2,1,0:T(2,128)(2,1)} %broadcast_in_dim.56), calls=%async_computation | async-start | bytes 196608 | tf_op jit(solution)/shard_map/all_to_all | solution.py:18
  51.5 7.3 %collective-permute-start = (bf16[18,432]{1,0:T(8,128)(2,1)S(1)}, bf16[18,432]{1,0:T(8,128)(2,1)}, u32[]{:S(2)}, u32[]{:S(2)}) collective-permute-start(bf16[18,432]{1,0:T(8,128)(2,1)S(1)} %reshape.266), channel_id=1, source_target_pairs={{0,4},{4,0},{1,5},{5,1},{2,6},{6,2},{3,7},{7,3},{8,12},{12,8},{9,1... | collective-permute-start | bytes 46664 | tf_op jit(solution)/shard_map/ppermute | solution.py:28
  60.5 3.0 %fusion.8 = bf16[512,1152]{1,0:T(8,128)(2,1)} fusion(bf16[512,1152]{1,0:T(8,128)(2,1)S(1)} %bitcast.58, s32[1152]{0:T(1024)S(1)} %fusion.36), kind=kOutput, calls=%fused_computation.9 | convolution fusion | flops 1360871424 | bytes 2363904 | tf_op jit(solution)/shard_map/dot_general | solution.py:62
  63.5 6.7 %all-gather.6.cloned.1.call-done = bf16[8,36,2304]{2,1,0:T(8,128)(2,1)} async-done(((bf16[1,36,2304]{2,1,0:T(8,128)(2,1)}), bf16[8,36,2304]{2,1,0:T(8,128)(2,1)}) %all-gather.6.cloned.1.call-update) | async-done | bytes 1327120 | tf_op jit(solution)/shard_map/all_gather | solution.py:328
  76.7 5.5 %all-to-all-start.1 = ((bf16[8,36,1024]{2,1,0:T(8,128)(2,1)}), bf16[8,36,1024]{2,1,0:T(8,128)(2,1)S(1)}, u32[]{:S(2)}, u32[]{:S(2)}) async-start(bf16[8,36,1024]{2,1,0:T(8,128)(2,1)} %broadcast_in_dim.57), calls=%async_computation.1 | async-start | bytes 1310720 | tf_op jit(solution)/shard_map/all_to_all | solution.py:18
  84.2 13.7 %all-to-all-done.1 = bf16[8,36,1024]{2,1,0:T(8,128)(2,1)S(1)} async-done(((bf16[8,36,1024]{2,1,0:T(8,128)(2,1)}), bf16[8,36,1024]{2,1,0:T(8,128)(2,1)S(1)}, u32[]{:S(2)}, u32[]{:S(2)}) %all-to-all-start.1) | async-done | bytes 589856 | tf_op jit(solution)/shard_map/all_to_all | solution.py:18
  98.7 2.6 collective-permute-start.5
  101.6 3.4 %collective-permute-start.6 = (bf16[288,1024]{1,0:T(8,128)(2,1)}, bf16[288,1024]{1,0:T(8,128)(2,1)}, u32[]{:S(2)}, u32[]{:S(2)}) collective-permute-start(bf16[288,1024]{1,0:T(8,128)(2,1)} %reshape.268), channel_id=1, source_target_pairs={{0,24},{8,0},{16,8},{24,16},{1,25},{9,1},{17,9},{25,17},{2,26},{10... | collective-permute-start | bytes 1769480 | tf_op jit(solution)/shard_map/ppermute | solution.py:23
  105.8 3.7 %collective-permute-start.12 = (bf16[288,1152]{1,0:T(8,128)(2,1)}, bf16[288,1152]{1,0:T(8,128)(2,1)S(1)}, u32[]{:S(2)}, u32[]{:S(2)}) collective-permute-start(bf16[288,1152]{1,0:T(8,128)(2,1)} %get-tuple-element.43), channel_id=1, source_target_pairs={{0,8},{8,16},{16,24},{24,0},{1,9},{9,17},{17,25},{25,1},{2,10},{10... | collective-permute-start | bytes 1990664 | tf_op jit(solution)/shard_map/ppermute | solution.py:23
  112.6 10.7 %all-to-all-start.2 = ((bf16[64,2,108]{2,1,0:T(2,128)(2,1)}), bf16[64,2,108]{2,1,0:T(2,128)(2,1)S(1)}, u32[]{:S(2)}, u32[]{:S(2)}) async-start(bf16[64,2,108]{2,1,0:T(2,128)(2,1)} %bitcast.12), calls=%async_computation.2 | async-start | bytes 65536 | tf_op jit(solution)/shard_map/all_to_all | solution.py:335
  123.3 4.1 %collective-permute-done.5 = bf16[288,1024]{1,0:T(8,128)(2,1)} collective-permute-done((bf16[288,1024]{1,0:T(8,128)(2,1)}, bf16[288,1024]{1,0:T(8,128)(2,1)}, u32[]{:S(2)}, u32[]{:S(2)}) %collective-permute-start.5) | collective-permute-done | bytes 589856 | tf_op jit(solution)/shard_map/ppermute | solution.py:23
  128.3 4.3 %collective-permute-start.7 = (bf16[144,1024]{1,0:T(8,128)(2,1)S(1)}, bf16[144,1024]{1,0:T(8,128)(2,1)S(1)}, u32[]{:S(2)}, u32[]{:S(2)}) collective-permute-start(bf16[144,1024]{1,0:T(8,128)(2,1)S(1)} %slice.111), channel_id=1, source_target_pairs={{0,8},{8,16},{16,24},{24,0},{1,9},{9,17},{17,25},{25,1},{2,10},{10... | collective-permute-start | bytes 884744 | tf_op jit(solution)/shard_map/ppermute | solution.py:23
  133.5 8.2 %all-to-all-done.2 = bf16[64,2,108]{2,1,0:T(2,128)(2,1)S(1)} async-done(((bf16[64,2,108]{2,1,0:T(2,128)(2,1)}), bf16[64,2,108]{2,1,0:T(2,128)(2,1)S(1)}, u32[]{:S(2)}, u32[]{:S(2)}) %all-to-all-start.2) | async-done | bytes 27680 | tf_op jit(solution)/shard_map/all_to_all | solution.py:335
  142.9 2.5 collective-permute-start.8
  150.0 2.8 %collective-permute-done.8 = bf16[144,1024]{1,0:T(8,128)(2,1)S(1)} collective-permute-done((bf16[144,1024]{1,0:T(8,128)(2,1)S(1)}, bf16[144,1024]{1,0:T(8,128)(2,1)S(1)}, u32[]{:S(2)}, u32[]{:S(2)}) %collective-permute-start.8) | collective-permute-done | bytes 294944 | tf_op jit(solution)/shard_map/ppermute | solution.py:23
  155.4 3.3 %collective-permute-start.14 = (bf16[144,1152]{1,0:T(8,128)(2,1)S(1)}, bf16[144,1152]{1,0:T(8,128)(2,1)S(1)}, u32[]{:S(2)}, u32[]{:S(2)}) collective-permute-start(bf16[144,1152]{1,0:T(8,128)(2,1)S(1)} %slice.119), channel_id=1, source_target_pairs={{0,8},{8,16},{16,24},{24,0},{1,9},{9,17},{17,25},{25,1},{2,10},{10... | collective-permute-start | bytes 995336 | tf_op jit(solution)/shard_map/ppermute | solution.py:23
  159.7 2.7 %collective-permute-start.15 = (bf16[144,1152]{1,0:T(8,128)(2,1)S(1)}, bf16[144,1152]{1,0:T(8,128)(2,1)S(1)}, u32[]{:S(2)}, u32[]{:S(2)}) collective-permute-start(bf16[144,1152]{1,0:T(8,128)(2,1)S(1)} %slice.120), channel_id=1, source_target_pairs={{0,24},{8,0},{16,8},{24,16},{1,25},{9,1},{17,9},{25,17},{2,26},{10... | collective-permute-start | bytes 995336 | tf_op jit(solution)/shard_map/ppermute | solution.py:23
  168.3 4.6 %collective-permute-done.15 = bf16[144,1152]{1,0:T(8,128)(2,1)S(1)} collective-permute-done((bf16[144,1152]{1,0:T(8,128)(2,1)S(1)}, bf16[144,1152]{1,0:T(8,128)(2,1)S(1)}, u32[]{:S(2)}, u32[]{:S(2)}) %collective-permute-start.15) | collective-permute-done | bytes 331808 | tf_op jit(solution)/shard_map/ppermute | solution.py:23
  178.8 4.5 %all-to-all-start.3 = ((bf16[4,2,9216]{2,1,0:T(2,128)(2,1)}), bf16[4,2,9216]{2,1,0:T(2,128)(2,1)S(1)}, u32[]{:S(2)}, u32[]{:S(2)}) async-start(bf16[4,2,9216]{2,1,0:T(2,128)(2,1)} %broadcast_in_dim.58), calls=%async_computation.3 | async-start | bytes 294912 | tf_op jit(solution)/shard_map/all_to_all | solution.py:18
  185.2 4.4 %all-to-all-done.3 = bf16[4,2,9216]{2,1,0:T(2,128)(2,1)S(1)} async-done(((bf16[4,2,9216]{2,1,0:T(2,128)(2,1)}), bf16[4,2,9216]{2,1,0:T(2,128)(2,1)S(1)}, u32[]{:S(2)}, u32[]{:S(2)}) %all-to-all-start.3) | async-done | bytes 147488 | tf_op jit(solution)/shard_map/all_to_all | solution.py:18
  192.6 9.9 %attention.1 = bf16[4,288,128]{2,1,0:T(8,128)(2,1)} custom-call(s32[1]{0:T(128)} %bitcast.1.core_ref, bf16[2,256,1152]{2,1,0:T(8,128)(2,1)} %bitcast.59, f32[2,1,1152]{2,1,0:T(1,128)} %get-tuple-element.63.shift_ref, f32[2,1,1152]{2,1,0:T(1,128)} %get-tuple-element.62.scale_ref, bf16[1152,1024]{1,0:T(8,128)(2,1)} %constant_dynamic-update-slice_fusion.mine_ref, ...), custom_call_target="tpu_custom_call" | custom-call | tf_op jit(solution)/shard_map/attention/pallas_call | solution.py:114
  202.5 3.5 %all-to-all-start.4 = ((bf16[4,288,128]{2,1,0:T(8,128)(2,1)}), bf16[4,288,128]{2,1,0:T(8,128)(2,1)S(1)}, u32[]{:S(2)}, u32[]{:S(2)}) async-start(bf16[4,288,128]{2,1,0:T(8,128)(2,1)} %attention.1), calls=%async_computation.4 | async-start | bytes 589824 | tf_op jit(solution)/shard_map/all_to_all | solution.py:377
  206.6 8.0 %all-to-all-done.4.mixed_ref = bf16[4,288,128]{2,1,0:T(8,128)(2,1)S(1)} async-done(((bf16[4,288,128]{2,1,0:T(8,128)(2,1)}), bf16[4,288,128]{2,1,0:T(8,128)(2,1)S(1)}, u32[]{:S(2)}, u32[]{:S(2)}) %all-to-all-start.4) | async-done | bytes 294944 | tf_op jit(solution)/shard_map/all_to_all | solution.py:377
  215.3 7.0 %project.1 = (f32[2,64,1152]{2,1,0:T(8,128)}, bf16[2,64,1152]{2,1,0:T(8,128)(2,1)}) custom-call(s32[1]{0:T(128)} %bitcast.base_ref, bf16[4,288,128]{2,1,0:T(8,128)(2,1)} %copy-done.4, bf16[1152,1024]{1,0:T(8,128)(2,1)} %constant_dynamic-update-slice_fusion.mine_ref, bf16[1152,1024]{1,0:T(8,128)(2,1)} %collective-permute-done.9.other_ref, ...), custom_call_target="tpu_custom_call" | custom-call | tf_op jit(solution)/shard_map/project/pallas_call | solution.py:156
  224.6 6.7 %collective-permute-done.10.pair_ref = bf16[128,1152]{1,0:T(8,128)(2,1)S(1)} collective-permute-done((bf16[128,1152]{1,0:T(8,128)(2,1)}, bf16[128,1152]{1,0:T(8,128)(2,1)S(1)}, u32[]{:S(2)}, u32[]{:S(2)}) %collective-permute-start.10) | collective-permute-done | bytes 294944 | tf_op jit(solution)/shard_map/ppermute | solution.py:28
  231.9 10.2 %feed_forward.1 = (f32[128,1152]{1,0:T(8,128)}, bf16[128,1152]{1,0:T(8,128)(2,1)}) custom-call(bf16[128,1152]{1,0:T(8,128)(2,1)} %bitcast.62, bf16[128,1152]{1,0:T(8,128)(2,1)} %copy-done.6, bf16[1152,1152]{1,0:T(8,128)(2,1)} %all-gather.4.cloned.1.call-done.up_ref, bf16[1152,1152]{1,0:T(8,128)(2,1)} %collective-permute-done.11.up_other_ref, ...), custom_call_target="tpu_custom_call" | custom-call | tf_op jit(solution)/shard_map/feed_forward/pallas_call | solution.py:221
  246.7 4.2 %collective-permute-done.17.recv_ref = bf16[128,1152]{1,0:T(8,128)(2,1)S(1)} collective-permute-done((bf16[128,1152]{1,0:T(8,128)(2,1)}, bf16[128,1152]{1,0:T(8,128)(2,1)S(1)}, u32[]{:S(2)}, u32[]{:S(2)}) %collective-permute-start.17) | collective-permute-done | bytes 294944 | tf_op jit(solution)/shard_map/ppermute | solution.py:28
  251.6 2.5 finish.1
  (109 shorter events, 58.9 us)
Async XLA Ops:
  6.5 94.8 %copy-start = (bf16[288,2304]{1,0:T(8,128)(2,1)S(1)}, bf16[288,2304]{1,0:T(8,128)(2,1)}, u32[]{:S(2)}) copy-start(bf16[288,2304]{1,0:T(8,128)(2,1)} %param.22) | copy-start | bytes 3981316
  6.5 44.7 %copy-start.9 = (bf16[3,18,288]{2,1,0:T(8,128)(2,1)S(1)}, bf16[3,18,288]{2,1,0:T(8,128)(2,1)}, u32[]{:S(2)}) copy-start(bf16[3,18,288]{2,1,0:T(8,128)(2,1)} %param.23) | copy-start | bytes 93316
  6.5 52.9 %copy-start.5 = (bf16[2,256,1152]{2,1,0:T(8,128)(2,1)S(1)}, bf16[2,256,1152]{2,1,0:T(8,128)(2,1)}, u32[]{:S(2)}) copy-start(bf16[2,256,1152]{2,1,0:T(8,128)(2,1)} %param.14) | copy-start | bytes 3538948
  6.5 63.6 %all-gather.6.cloned.1.call-start = ((), (), s32[]{:S(2)}) async-start(), calls=%async_computation.6 | async-start | bytes 1658880 | tf_op jit(solution)/shard_map/all_gather | solution.py:328
  7.6 11.6 %collective-permute-start.1 = (bf16[18,2592]{1,0:T(8,128)(2,1)S(1)}, bf16[18,2592]{1,0:T(8,128)(2,1)S(1)}, u32[]{:S(2)}, u32[]{:S(2)}) collective-permute-start(bf16[18,2592]{1,0:T(8,128)(2,1)S(1)} %pad_maximum_fusion.2), channel_id=1, source_target_pairs={{0,0},{1,1},{2,2},{3,3},{4,4},{5,5},{6,6},{7,7},{256,258},{257,259... | collective-permute-start | bytes 279944 | tf_op jit(solution)/shard_map/ppermute | solution.py:317
  8.2 14.8 %collective-permute-start.2 = (bf16[18,2592]{1,0:T(8,128)(2,1)S(1)}, bf16[18,2592]{1,0:T(8,128)(2,1)S(1)}, u32[]{:S(2)}, u32[]{:S(2)}) collective-permute-start(bf16[18,2592]{1,0:T(8,128)(2,1)S(1)} %pad_maximum_fusion.2), channel_id=1, source_target_pairs={{0,4},{1,5},{2,6},{3,7},{4,0},{5,1},{6,2},{7,3},{256,262},{257,263... | collective-permute-start | bytes 279944 | tf_op jit(solution)/shard_map/ppermute | solution.py:317
  23.8 49.3 %collective-permute-start.3 = (bf16[18,288]{1,0:T(8,128)(2,1)}, bf16[18,288]{1,0:T(8,128)(2,1)}, u32[]{:S(2)}, u32[]{:S(2)}) collective-permute-start(bf16[18,288]{1,0:T(8,128)(2,1)} %bitcast.70), channel_id=1, source_target_pairs={{0,1},{1,0},{2,3},{3,2},{4,5},{5,4},{6,7},{7,6},{256,259},{257,258... | collective-permute-start | bytes 31112 | tf_op jit(solution)/shard_map/ppermute | solution.py:317
  28.0 45.1 %collective-permute-start.4 = (bf16[18,288]{1,0:T(8,128)(2,1)}, bf16[18,288]{1,0:T(8,128)(2,1)}, u32[]{:S(2)}, u32[]{:S(2)}) collective-permute-start(bf16[18,288]{1,0:T(8,128)(2,1)} %bitcast.71), channel_id=1, source_target_pairs={{0,5},{1,4},{2,7},{3,6},{4,1},{5,0},{6,3},{7,2},{256,263},{257,262... | collective-permute-start | bytes 31112 | tf_op jit(solution)/shard_map/ppermute | solution.py:317
  39.5 35.2 %all-to-all-start = ((bf16[64,2,288]{2,1,0:T(2,128)(2,1)}), bf16[64,2,288]{2,1,0:T(2,128)(2,1)}, u32[]{:S(2)}, u32[]{:S(2)}) async-start(bf16[64,2,288]{2,1,0:T(2,128)(2,1)} %broadcast_in_dim.56), calls=%async_computation | async-start | bytes 196608 | tf_op jit(solution)/shard_map/all_to_all | solution.py:18
  51.2 124.4 %all-gather.4.cloned.1.call-start = ((), (), s32[]{:S(2)}) async-start(), calls=%async_computation.5 | async-start | bytes 3317760 | tf_op jit(solution)/shard_map/all_gather | solution.py:329
  51.5 22.4 %collective-permute-start = (bf16[18,432]{1,0:T(8,128)(2,1)S(1)}, bf16[18,432]{1,0:T(8,128)(2,1)}, u32[]{:S(2)}, u32[]{:S(2)}) collective-permute-start(bf16[18,432]{1,0:T(8,128)(2,1)S(1)} %reshape.266), channel_id=1, source_target_pairs={{0,4},{4,0},{1,5},{5,1},{2,6},{6,2},{3,7},{7,3},{8,12},{12,8},{9,1... | collective-permute-start | bytes 46664 | tf_op jit(solution)/shard_map/ppermute | solution.py:28
  76.7 21.2 %all-to-all-start.1 = ((bf16[8,36,1024]{2,1,0:T(8,128)(2,1)}), bf16[8,36,1024]{2,1,0:T(8,128)(2,1)S(1)}, u32[]{:S(2)}, u32[]{:S(2)}) async-start(bf16[8,36,1024]{2,1,0:T(8,128)(2,1)} %broadcast_in_dim.57), calls=%async_computation.1 | async-start | bytes 1310720 | tf_op jit(solution)/shard_map/all_to_all | solution.py:18
  82.1 22.9 %copy-start.2 = (bf16[1,256,1152]{2,1,0:T(8,128)(2,1)S(1)}, bf16[1,256,1152]{2,1,0:T(8,128)(2,1)}, u32[]{:S(2)}) copy-start(bf16[1,256,1152]{2,1,0:T(8,128)(2,1)} %copy-done.1) | copy-start | bytes 1769476
  84.2 27.5 %copy-start.10 = (bf16[288,108]{1,0:T(8,128)(2,1)S(1)}, bf16[288,108]{1,0:T(8,128)(2,1)}, u32[]{:S(2)}) copy-start(bf16[288,108]{1,0:T(8,128)(2,1)} %param.21) | copy-start | bytes 186628
  98.7 33.9 %copy-start.3 = (bf16[288,1024]{1,0:T(8,128)(2,1)S(1)}, bf16[288,1024]{1,0:T(8,128)(2,1)}, u32[]{:S(2)}) copy-start(bf16[288,1024]{1,0:T(8,128)(2,1)} %reshape.268) | copy-start | bytes 1769476
  98.7 28.6 %collective-permute-start.5 = (bf16[288,1024]{1,0:T(8,128)(2,1)}, bf16[288,1024]{1,0:T(8,128)(2,1)}, u32[]{:S(2)}, u32[]{:S(2)}) collective-permute-start(bf16[288,1024]{1,0:T(8,128)(2,1)} %reshape.268), channel_id=1, source_target_pairs={{0,8},{8,16},{16,24},{24,0},{1,9},{9,17},{17,25},{25,1},{2,10},{10... | collective-permute-start | bytes 1769480 | tf_op jit(solution)/shard_map/ppermute | solution.py:23
  101.6 40.3 %collective-permute-start.6 = (bf16[288,1024]{1,0:T(8,128)(2,1)}, bf16[288,1024]{1,0:T(8,128)(2,1)}, u32[]{:S(2)}, u32[]{:S(2)}) collective-permute-start(bf16[288,1024]{1,0:T(8,128)(2,1)} %reshape.268), channel_id=1, source_target_pairs={{0,24},{8,0},{16,8},{24,16},{1,25},{9,1},{17,9},{25,17},{2,26},{10... | collective-permute-start | bytes 1769480 | tf_op jit(solution)/shard_map/ppermute | solution.py:23
  105.8 49.6 %collective-permute-start.12 = (bf16[288,1152]{1,0:T(8,128)(2,1)}, bf16[288,1152]{1,0:T(8,128)(2,1)S(1)}, u32[]{:S(2)}, u32[]{:S(2)}) collective-permute-start(bf16[288,1152]{1,0:T(8,128)(2,1)} %get-tuple-element.43), channel_id=1, source_target_pairs={{0,8},{8,16},{16,24},{24,0},{1,9},{9,17},{17,25},{25,1},{2,10},{10... | collective-permute-start | bytes 1990664 | tf_op jit(solution)/shard_map/ppermute | solution.py:23
  109.4 49.3 %collective-permute-start.13 = (bf16[288,1152]{1,0:T(8,128)(2,1)}, bf16[288,1152]{1,0:T(8,128)(2,1)}, u32[]{:S(2)}, u32[]{:S(2)}) collective-permute-start(bf16[288,1152]{1,0:T(8,128)(2,1)} %get-tuple-element.43), channel_id=1, source_target_pairs={{0,24},{8,0},{16,8},{24,16},{1,25},{9,1},{17,9},{25,17},{2,26},{10... | collective-permute-start | bytes 1990664 | tf_op jit(solution)/shard_map/ppermute | solution.py:23
  112.6 29.1 %all-to-all-start.2 = ((bf16[64,2,108]{2,1,0:T(2,128)(2,1)}), bf16[64,2,108]{2,1,0:T(2,128)(2,1)S(1)}, u32[]{:S(2)}, u32[]{:S(2)}) async-start(bf16[64,2,108]{2,1,0:T(2,128)(2,1)} %bitcast.12), calls=%async_computation.2 | async-start | bytes 65536 | tf_op jit(solution)/shard_map/all_to_all | solution.py:335
  128.3 20.9 %collective-permute-start.7 = (bf16[144,1024]{1,0:T(8,128)(2,1)S(1)}, bf16[144,1024]{1,0:T(8,128)(2,1)S(1)}, u32[]{:S(2)}, u32[]{:S(2)}) collective-permute-start(bf16[144,1024]{1,0:T(8,128)(2,1)S(1)} %slice.111), channel_id=1, source_target_pairs={{0,8},{8,16},{16,24},{24,0},{1,9},{9,17},{17,25},{25,1},{2,10},{10... | collective-permute-start | bytes 884744 | tf_op jit(solution)/shard_map/ppermute | solution.py:23
  142.9 9.8 %collective-permute-start.8 = (bf16[144,1024]{1,0:T(8,128)(2,1)S(1)}, bf16[144,1024]{1,0:T(8,128)(2,1)S(1)}, u32[]{:S(2)}, u32[]{:S(2)}) collective-permute-start(bf16[144,1024]{1,0:T(8,128)(2,1)S(1)} %slice.112), channel_id=1, source_target_pairs={{0,24},{8,0},{16,8},{24,16},{1,25},{9,1},{17,9},{25,17},{2,26},{10... | collective-permute-start | bytes 884744 | tf_op jit(solution)/shard_map/ppermute | solution.py:23
  153.4 39.2 %collective-permute-start.9 = (bf16[1152,1024]{1,0:T(8,128)(2,1)}, bf16[1152,1024]{1,0:T(8,128)(2,1)}, u32[]{:S(2)}, u32[]{:S(2)}) collective-permute-start(bf16[1152,1024]{1,0:T(8,128)(2,1)} %constant_dynamic-update-slice_fusion.mine_ref), channel_id=1, source_target_pairs={{0,256},{256,0},{1,257},{257,1},{2,258},{258,2},{3,259},{259,3},{4... | collective-permute-start | bytes 7077896 | tf_op jit(solution)/shard_map/ppermute | solution.py:28
  155.4 12.1 %collective-permute-start.14 = (bf16[144,1152]{1,0:T(8,128)(2,1)S(1)}, bf16[144,1152]{1,0:T(8,128)(2,1)S(1)}, u32[]{:S(2)}, u32[]{:S(2)}) collective-permute-start(bf16[144,1152]{1,0:T(8,128)(2,1)S(1)} %slice.119), channel_id=1, source_target_pairs={{0,8},{8,16},{16,24},{24,0},{1,9},{9,17},{17,25},{25,1},{2,10},{10... | collective-permute-start | bytes 995336 | tf_op jit(solution)/shard_map/ppermute | solution.py:23
  159.7 23.5 %copy-start.7 = (bf16[2,64,1152]{2,1,0:T(8,128)(2,1)S(1)}, bf16[2,64,1152]{2,1,0:T(8,128)(2,1)}, u32[]{:S(2)}) copy-start(bf16[2,64,1152]{2,1,0:T(8,128)(2,1)} %fusion.22) | copy-start | bytes 884740
  159.7 13.2 %collective-permute-start.15 = (bf16[144,1152]{1,0:T(8,128)(2,1)S(1)}, bf16[144,1152]{1,0:T(8,128)(2,1)S(1)}, u32[]{:S(2)}, u32[]{:S(2)}) collective-permute-start(bf16[144,1152]{1,0:T(8,128)(2,1)S(1)} %slice.120), channel_id=1, source_target_pairs={{0,24},{8,0},{16,8},{24,16},{1,25},{9,1},{17,9},{25,17},{2,26},{10... | collective-permute-start | bytes 995336 | tf_op jit(solution)/shard_map/ppermute | solution.py:23
  173.6 57.6 %collective-permute-start.16 = (bf16[1152,1152]{1,0:T(8,128)(2,1)}, bf16[1152,1152]{1,0:T(8,128)(2,1)}, u32[]{:S(2)}, u32[]{:S(2)}) collective-permute-start(bf16[1152,1152]{1,0:T(8,128)(2,1)} %constant_dynamic-update-slice_fusion.5.down_ref), channel_id=1, source_target_pairs={{0,256},{256,0},{1,257},{257,1},{2,258},{258,2},{3,259},{259,3},{4... | collective-permute-start | bytes 7962632 | tf_op jit(solution)/shard_map/ppermute | solution.py:28
  175.6 55.7 %collective-permute-start.11 = (bf16[1152,1152]{1,0:T(8,128)(2,1)}, bf16[1152,1152]{1,0:T(8,128)(2,1)}, u32[]{:S(2)}, u32[]{:S(2)}) collective-permute-start(bf16[1152,1152]{1,0:T(8,128)(2,1)} %all-gather.4.cloned.1.call-done.up_ref), channel_id=1, source_target_pairs={{0,256},{256,0},{1,257},{257,1},{2,258},{258,2},{3,259},{259,3},{4... | collective-permute-start | bytes 7962632 | tf_op jit(solution)/shard_map/ppermute | solution.py:28
  178.8 10.8 %all-to-all-start.3 = ((bf16[4,2,9216]{2,1,0:T(2,128)(2,1)}), bf16[4,2,9216]{2,1,0:T(2,128)(2,1)S(1)}, u32[]{:S(2)}, u32[]{:S(2)}) async-start(bf16[4,2,9216]{2,1,0:T(2,128)(2,1)} %broadcast_in_dim.58), calls=%async_computation.3 | async-start | bytes 294912 | tf_op jit(solution)/shard_map/all_to_all | solution.py:18
  202.5 12.1 %all-to-all-start.4 = ((bf16[4,288,128]{2,1,0:T(8,128)(2,1)}), bf16[4,288,128]{2,1,0:T(8,128)(2,1)S(1)}, u32[]{:S(2)}, u32[]{:S(2)}) async-start(bf16[4,288,128]{2,1,0:T(8,128)(2,1)} %attention.1), calls=%async_computation.4 | async-start | bytes 589824 | tf_op jit(solution)/shard_map/all_to_all | solution.py:377
  222.3 8.9 %collective-permute-start.10 = (bf16[128,1152]{1,0:T(8,128)(2,1)}, bf16[128,1152]{1,0:T(8,128)(2,1)S(1)}, u32[]{:S(2)}, u32[]{:S(2)}) collective-permute-start(bf16[128,1152]{1,0:T(8,128)(2,1)} %bitcast.61), channel_id=1, source_target_pairs={{0,1},{1,0},{2,3},{3,2},{4,5},{5,4},{6,7},{7,6},{8,9},{9,8},{10,11... | collective-permute-start | bytes 884744 | tf_op jit(solution)/shard_map/ppermute | solution.py:28
  242.1 8.8 %collective-permute-start.17 = (bf16[128,1152]{1,0:T(8,128)(2,1)}, bf16[128,1152]{1,0:T(8,128)(2,1)S(1)}, u32[]{:S(2)}, u32[]{:S(2)}) collective-permute-start(bf16[128,1152]{1,0:T(8,128)(2,1)} %get-tuple-element.19), channel_id=1, source_target_pairs={{0,1},{1,0},{2,3},{3,2},{4,5},{5,4},{6,7},{7,6},{8,9},{9,8},{10,11... | collective-permute-start | bytes 884744 | tf_op jit(solution)/shard_map/ppermute | solution.py:28
  (5 other events, 24.9 us)
Sparse Core Ops, SparseCore 0:
  23.9 46.2 all-gather.5
  73.2 51.8 all-gather.3

commit v4 on v3

--- a/solution.py
+++ b/solution.py
@@ -93,7 +93,7 @@
                 top = jnp.max(scores, axis=-1, keepdims=True)
                 weights = jnp.exp(scores - top)
                 total = jnp.sum(weights, axis=-1, keepdims=True)
-                probs = (weights / total).astype(BF16)
+                probs = (weights * (1.0 / total)).astype(BF16)
                 mixed = lax.dot_general(
                     values, probs, (((0,), (1,)), ((), ())), preferred_element_type=F32
                 )
@@ -140,12 +140,12 @@
     ) + lax.dot_general(
         rows_ref[1], other_ref[:, start - lead :], both, preferred_element_type=F32
     )
+    attn = dot(attn.astype(BF16), change_ref[...])
     share = own_ref.shape[1]
     for i in range(2):
         total = own_ref[i].astype(F32) + gate_ref[i] * attn[i * share : (i + 1) * share]
         sum_ref[i] = total
-        hidden = (layer_norm(total) * (1.0 + scale_ref[i]) + shift_ref[i]).astype(BF16)
-        hidden_ref[i] = dot_t(hidden, change_ref[...]).astype(BF16)
+        hidden_ref[i] = (layer_norm(total) * (1.0 + scale_ref[i]) + shift_ref[i]).astype(BF16)
 
 
 def project(base, mixed, mine, other, change, own, gate_a, shift_m, scale_m):
@@ -179,57 +179,74 @@
     )(base, mixed, mine, other, change, own, gate_a, shift_m, scale_m)
 
 
-def feed_body(own_ref, pair_ref, up_ref, up_other_ref, down_ref, down_other_ref,
-              keep_ref, send_ref, rows_ref, sum_ref):
-    step = pl.program_id(0)
-    half = pl.num_programs(0) // 2
+def feed_part(rows_ref, own_ref, pair_ref, up_ref, down_ref, so_far):
     count = own_ref.shape[0]
 
-    @pl.when(step == 0)
+    @pl.when(pl.program_id(0) == 0)
     def _():
         rows_ref[:count] = own_ref[...]
         rows_ref[count:] = pair_ref[...]
 
-    def part(up, down):
-        hidden = jax.nn.gelu(dot(rows_ref[...], up[...]), approximate=True).astype(BF16)
-        return dot_t(hidden, down[...])
-
-    @pl.when(step == 0)
+    hidden = jax.nn.gelu(dot(rows_ref[...], up_ref[...]), approximate=True).astype(BF16)
+    return so_far() + dot_t(hidden, down_ref[...])
+
+
+def feed_first_body(own_ref, pair_ref, up_ref, down_ref, sum_ref, rows_ref):
+    @pl.when(pl.program_id(0) == 0)
     def _():
-        sum_ref[...] = part(up_ref, down_ref)
-
-    @pl.when((step > 0) & (step < half))
+        sum_ref[...] = jnp.zeros(sum_ref.shape, F32)
+
+    sum_ref[...] = feed_part(rows_ref, own_ref, pair_ref, up_ref, down_ref, lambda: sum_ref[...])
+
+
+def feed_second_body(own_ref, pair_ref, up_ref, down_ref, before_ref, keep_ref, send_ref, rows_ref, sum_ref):
+    count = own_ref.shape[0]
+
+    @pl.when(pl.program_id(0) == 0)
     def _():
-        sum_ref[...] += part(up_ref, down_ref)
-
-    @pl.when(step >= half)
-    def _():
-        sum_ref[...] += part(up_other_ref, down_other_ref)
-
-    @pl.when(step == pl.num_programs(0) - 1)
+        sum_ref[...] = before_ref[...]
+
+    sum_ref[...] = feed_part(rows_ref, own_ref, pair_ref, up_ref, down_ref, lambda: sum_ref[...])
+
+    @pl.when(pl.program_id(0) == pl.num_programs(0) - 1)
     def _():
         keep_ref[...] = sum_ref[:count]
         send_ref[...] = sum_ref[count:].astype(BF16)
 
 
-def feed_forward(own, pair, up, up_other, down, down_other):
+def feed_first(own, pair, weights):
     count, width = own.shape
     steps = 3
-    piece = width // steps
-    first = pl.BlockSpec((width, piece), lambda i: (0, jnp.minimum(i, steps - 1)))
-    second = pl.BlockSpec((width, piece), lambda i: (0, jnp.maximum(i - steps, 0)))
+    up = pl.BlockSpec((width, width // steps), lambda i: (0, steps + i))
+    down = pl.BlockSpec((width, width // steps), lambda i: (0, i))
     return pl.pallas_call(
-        feed_body,
-        grid=(2 * steps,),
-        in_specs=[whole(own.shape), whole(own.shape), first, second, first, second],
+        feed_first_body,
+        grid=(steps,),
+        in_specs=[whole(own.shape), whole(own.shape), up, down],
+        out_specs=whole((2 * count, width)),
+        out_shape=jax.ShapeDtypeStruct((2 * count, width), F32),
+        scratch_shapes=[pltpu.VMEM((2 * count, width), BF16)],
+        name="feed_first",
+    )(own, pair, weights, weights)
+
+
+def feed_second(own, pair, weights, before):
+    count, width = own.shape
+    steps = 3
+    up = pl.BlockSpec((width, width // steps), lambda i: (0, steps + i))
+    down = pl.BlockSpec((width, width // steps), lambda i: (0, i))
+    return pl.pallas_call(
+        feed_second_body,
+        grid=(steps,),
+        in_specs=[whole(own.shape), whole(own.shape), up, down, whole(before.shape)],
         out_specs=[whole(own.shape), whole(own.shape)],
         out_shape=[
             jax.ShapeDtypeStruct(own.shape, F32),
             jax.ShapeDtypeStruct(own.shape, BF16),
         ],
         scratch_shapes=[pltpu.VMEM((2 * count, width), BF16), pltpu.VMEM((2 * count, width), F32)],
-        name="feed_forward",
-    )(own, pair, up, up_other, down, down_other)
+        name="feed_second",
+    )(own, pair, weights, weights, before)
 
 
 def finish_body(scale_by_ref, keep_ref, recv_ref, first_ref, gate_ref, shift_ref, scale_ref, out_w_ref, out_ref):
@@ -304,20 +321,17 @@
 
     qkv_own = jnp.where(core == 0, qkv_weight[:, :, :half], qkv_weight[:, :, half:])
     qkv_own = qkv_own.transpose(1, 0, 2).reshape(rows, 3 * half)
-    qkv_other = swap(qkv_own, "dp_2", 1)
-    qkv_block = by_height(qkv_own, qkv_other, high)
-
-    proj_rows = proj_weight.T
-    feed = jnp.concatenate([fc2_weight.T, fc1_weight, proj_rows], axis=1)
-    spots = [(c, z, m) for c in range(2) for z in range(n_z) for m in range(n_mp)]
-    number = {spot: i for i, spot in enumerate(spots)}
-
-    def fetch(x, flip, along):
-        pairs = [(number[c, z, m], number[c, z ^ flip, m ^ (2 * c) ^ along]) for c, z, m in spots]
-        return lax.ppermute(x, ("group", "dp_2", "mp"), pairs)
-
-    feed = by_height(fetch(feed, 0, 0), fetch(feed, 1, 0), high)
-    proj_beside = by_height(fetch(proj_rows, 0, 1), fetch(proj_rows, 1, 1), high)
+
+    shards = jnp.concatenate([fc2_weight.T, fc1_weight, proj_weight.T, qkv_own], axis=1)
+    shards = by_height(shards, swap(shards, "dp_2", 1), high)
+    qkv_block = shards[:, 2 * width + quarter :]
+
+    def fetch(x, along):
+        pairs = [(c * n_mp + m, c * n_mp + (m ^ (2 * c) ^ along)) for c in range(2) for m in range(n_mp)]
+        return lax.ppermute(x, ("group", "mp"), pairs)
+
+    feed = fetch(shards[:, : 2 * width + quarter], 0)
+    proj_beside = fetch(shards[:, 2 * width : 2 * width + quarter], 1)
     part_a = lanes_full(jnp.concatenate([qkv_block, feed[:, 2 * width :], proj_beside], axis=1))
     part_a, every_act = lax.optimization_barrier((part_a, every_act))
     part_a = gather_y(part_a)
@@ -326,10 +340,8 @@
     other_a = swap(part_a, "group", 1)
 
     feed = lax.all_gather(feed[:, : 2 * width], "dp_0", axis=0, tiled=True)
-    part_b = lax.all_gather(feed[:, width:], "dp_1", axis=0, tiled=True)
-    other_b = swap(part_b, "group", 1)
-    part_c = gather_x(feed[:, :width])
-    other_c = swap(part_c, "group", 1)
+    feed = lax.all_gather(feed, "dp_1", axis=0, tiled=True)
+    other_feed = swap(feed, "group", 1)
 
     mod_part = dot(every_act, ada_weight).astype(BF16)
     mod_part = lax.all_to_all(mod_part, DP, split_axis=0, concat_axis=1, tiled=True)
@@ -345,9 +357,10 @@
 
     from_x = (column + offset) % n_x
     final = (inside // per_y * n_x + from_x) * per_y + inside % per_y
-    order = (lax.broadcasted_iota(jnp.int32, (width, width), 0) == final).astype(BF16)
-    up_natural = (inside // per_y * n_x + block) * per_y + inside % per_y
-    change = (up_natural.reshape(width, 1) == final).astype(BF16)
+    near_order = (lax.broadcasted_iota(jnp.int32, (width, width), 0) == final).astype(BF16)
+    natural = (inside // per_y * n_x + block) * per_y + inside % per_y
+    order = (lax.broadcasted_iota(jnp.int32, (width, width), 0) == natural).astype(BF16)
+    change = (final.reshape(width, 1) == natural).astype(BF16)
 
     first = cond_first[0] == 1
     cond_rows = jnp.where(first, x_arrive[0], x_arrive[1])
@@ -356,7 +369,7 @@
     share = tokens // n_mp
     own = lax.dynamic_slice_in_dim(arrived, place * share, share, 1)
     own = dot(own.reshape(-1, width), order).astype(BF16).reshape(2, share, width)
-    images = dot(arrived.reshape(-1, width), order).astype(BF16)
+    images = dot(arrived.reshape(-1, width), near_order).astype(BF16)
     images = images.reshape(2, tokens, width)
     out_local = lax.dot_general(
         order, out_weight, (((0,), (0,)), ((), ())), preferred_element_type=F32
@@ -369,7 +382,7 @@
         values = jnp.sum(values, axis=0)
         return [values[:, i] for i in range(count)]
 
-    shift_a, scale_a = mods_in(mod_parts[:, :2], order)
+    shift_a, scale_a = mods_in(mod_parts[:, :2], near_order)
     gate_a, shift_m, scale_m, gate_m, shift_f, scale_f = mods_in(mod_parts[:, 2:], order)
 
     cores = core.reshape(1).astype(jnp.int32)
@@ -379,7 +392,8 @@
     first_sum, hidden_two = project(base, mixed, part_a, other_a, change, own, gate_a, shift_m, scale_m)
     hidden_two = hidden_two.reshape(2 * share, width)
     pair = swap(hidden_two, "mp", 1)
-    keep, send = feed_forward(hidden_two, pair, part_b, other_b, part_c, other_c)
+    before = feed_first(hidden_two, pair, feed)
+    keep, send = feed_second(hidden_two, pair, other_feed, before)
     recv = swap(send, "mp", 1)
     guided = finish(guidance, keep, recv, first_sum, gate_m, shift_f, scale_f, out_local)
     return guided.reshape(1, share * out_weight.shape[1])
@@ -406,6 +420,4 @@
         P("mp", DP),
         P(),
     )
-    return jax.shard_map(
-        on_device, mesh=torus, in_specs=placed, out_specs=P(GROUP_DP, "mp"), check_vma=False
-    )
+    return jax.shard_map(on_device, mesh=torus, in_specs=placed, out_specs=P(GROUP_DP, "mp"), check_vma=False)

time: 264 us -> 302 us (1.14)
  waiting for transfers between devices: 69.3 us -> 135 us
  starting transfers between devices: 101 us -> 77 us
  local copies, waits for them, and re-layouts: 30.9 us -> 22.9 us
    all_gather x1, waiting for transfers between devices: 6.67 us -> 54.4 us  [on_device(): feed = lax.all_gather(feed[:, :2 * width], 'dp_0', axis=0, tiled=True)]
    all_gather x1, waiting for transfers between devices: 0.02 us -> 25.7 us  [on_device(): feed = lax.all_gather(feed, 'dp_1', axis=0, tiled=True)]
    ppermute x4 -> x2, starting transfers between devices: 22.9 us -> 3.33 us  [fetch(): return lax.ppermute(x, ('group', 'mp'), pairs)]
    ppermute x8 -> x4, starting transfers between devices: 24.5 us -> 13.2 us  [shift(): return lax.ppermute(x, axis, [(i, (i + step) % size) for i in range(size)])]
    all_to_all x3, waiting for transfers between devices: 18 us -> 9.56 us  [to_everyone(): lax.all_to_all(jnp.broadcast_to(x[None], (size, *x.shape)), axis, 0, 0, t...]
    all_to_all x1, starting transfers between devices: 10.7 us -> 15.1 us  [on_device(): lax.all_to_all(mod_part, DP, split_axis=0, concat_axis=1, tiled=True)]
    all_to_all x1, waiting for transfers between devices: 8.2 us -> 12.6 us  [on_device(): lax.all_to_all(mod_part, DP, split_axis=0, concat_axis=1, tiled=True)]
    unnamed x35 -> x33, local copies, waits for them, and re-layouts: 13.9 us -> 9.95 us
  transfers between devices with their start and end apart: 25 -> 18, of which waited for: 12 -> 11; matrix products, arithmetic and copies ran while one was open for 15% -> 11% of each run, Pallas kernels for 6% -> 7%
where the time goes in v4:
time: 302 us; the launch traced here: 300 us
  waiting for transfers between devices  135 us (45%)
  starting transfers between devices  77 us (25%)
  Pallas kernels  30.9 us (10%)
  local copies, waits for them, and re-layouts  22.9 us (8%)
  between operations  16.4 us (5%)
  matrix products  9.95 us (3%)
  other arithmetic  7.83 us (3%)
    all_gather x1, waiting for transfers between devices, on_device(): feed = lax.all_gather(feed[:, :2 * width], 'dp_0', axis=0, tiled=True)  54.4 us
    all_gather x1, waiting for transfers between devices, on_device(): feed = lax.all_gather(feed, 'dp_1', axis=0, tiled=True)  25.7 us
    ppermute x5, starting transfers between devices, swap(): return lax.ppermute(x, axis, [(i, i ^ bit) for i in range(size)])  21.2 us
    all_to_all x3, starting transfers between devices, to_everyone(): lax.all_to_all(jnp.broadcast_to(x[None], (size, *x.shape)), axis, 0, 0, t...  20.7 us
    all_to_all x1, starting transfers between devices, on_device(): lax.all_to_all(mod_part, DP, split_axis=0, concat_axis=1, tiled=True)  15.1 us
    ppermute x4, starting transfers between devices, shift(): return lax.ppermute(x, axis, [(i, (i + step) % size) for i in range(size)])  13.2 us
    ppermute x4, waiting for transfers between devices, shift(): return lax.ppermute(x, axis, [(i, (i + step) % size) for i in range(size)])  13.1 us
    all_to_all x1, waiting for transfers between devices, on_device(): lax.all_to_all(mod_part, DP, split_axis=0, concat_axis=1, tiled=True)  12.6 us
  transfers between devices with their start and end apart: 18, of which 11 were waited for; matrix products, arithmetic and copies ran while one was open for 11% of the time, Pallas kernels for 7%

profile of v4, /device:TPU:6, one launch (start us, length us, event | category | flops | bytes accessed | tf_op | source)
XLA Modules:
  0.0 299.5 jit_solution(16719846518404719288)
XLA Ops:
  8.6 10.9 %collective-permute-start = (bf16[18,3024]{1,0:T(8,128)(2,1)S(1)}, bf16[18,3024]{1,0:T(8,128)(2,1)S(1)}, u32[]{:S(2)}, u32[]{:S(2)}) collective-permute-start(bf16[18,3024]{1,0:T(8,128)(2,1)S(1)} %concatenate.25), channel_id=1, source_target_pairs={{0,4},{4,0},{1,5},{5,1},{2,6},{6,2},{3,7},{7,3},{8,12},{12,8},{9,1... | collective-permute-start | bytes 326600 | tf_op jit(solution)/shard_map/ppermute | solution.py:28
  19.5 3.9 %collective-permute-done = bf16[18,3024]{1,0:T(8,128)(2,1)S(1)} collective-permute-done((bf16[18,3024]{1,0:T(8,128)(2,1)S(1)}, bf16[18,3024]{1,0:T(8,128)(2,1)S(1)}, u32[]{:S(2)}, u32[]{:S(2)}) %collective-permute-start) | collective-permute-done | bytes 108896 | tf_op jit(solution)/shard_map/ppermute | solution.py:28
  25.0 54.4 %all-gather.6.cloned.1.call-done = bf16[8,36,2304]{2,1,0:T(8,128)(2,1)} async-done(((bf16[1,36,2304]{2,1,0:T(8,128)(2,1)}), bf16[8,36,2304]{2,1,0:T(8,128)(2,1)}) %all-gather.6.cloned.1.call-update) | async-done | bytes 1327120 | tf_op jit(solution)/shard_map/all_gather | solution.py:342
  79.4 2.3 reshape.349
  86.2 13.5 %all-to-all-start = ((bf16[64,2,288]{2,1,0:T(2,128)(2,1)}), bf16[64,2,288]{2,1,0:T(2,128)(2,1)S(1)}, u32[]{:S(2)}, u32[]{:S(2)}) async-start(bf16[64,2,288]{2,1,0:T(2,128)(2,1)} %broadcast_in_dim.56), calls=%async_computation | async-start | bytes 196608 | tf_op jit(solution)/shard_map/all_to_all | solution.py:18
  103.4 2.7 collective-permute-start.2
  106.7 5.7 %all-to-all-done = bf16[64,2,288]{2,1,0:T(2,128)(2,1)S(1)} async-done(((bf16[64,2,288]{2,1,0:T(2,128)(2,1)}), bf16[64,2,288]{2,1,0:T(2,128)(2,1)S(1)}, u32[]{:S(2)}, u32[]{:S(2)}) %all-to-all-start) | async-done | bytes 73760 | tf_op jit(solution)/shard_map/all_to_all | solution.py:18
  113.6 3.7 %all-to-all-start.1 = ((bf16[8,36,1024]{2,1,0:T(8,128)(2,1)}), bf16[8,36,1024]{2,1,0:T(8,128)(2,1)S(1)}, u32[]{:S(2)}, u32[]{:S(2)}) async-start(bf16[8,36,1024]{2,1,0:T(8,128)(2,1)} %broadcast_in_dim.57), calls=%async_computation.1 | async-start | bytes 1310720 | tf_op jit(solution)/shard_map/all_to_all | solution.py:18
  117.3 25.7 %all-gather.4.cloned.1.call-done.up_ref.down_ref = bf16[1152,2304]{1,0:T(8,128)(2,1)} async-done(((bf16[288,2304]{1,0:T(8,128)(2,1)}), bf16[1152,2304]{1,0:T(8,128)(2,1)}) %all-gather.4.cloned.1.call-update) | async-done | bytes 5308432 | tf_op jit(solution)/shard_map/all_gather | solution.py:343
  144.9 2.8 compare_convert_fusion.change_ref
  148.7 4.0 %collective-permute-start.3 = (bf16[288,1024]{1,0:T(8,128)(2,1)}, bf16[288,1024]{1,0:T(8,128)(2,1)S(1)}, u32[]{:S(2)}, u32[]{:S(2)}) collective-permute-start(bf16[288,1024]{1,0:T(8,128)(2,1)} %reshape.290), channel_id=1, source_target_pairs={{0,8},{8,16},{16,24},{24,0},{1,9},{9,17},{17,25},{25,1},{2,10},{10... | collective-permute-start | bytes 1769480 | tf_op jit(solution)/shard_map/ppermute | solution.py:23
  155.0 4.3 %fusion.9 = bf16[512,1152]{1,0:T(8,128)(2,1)} fusion(bf16[512,1152]{1,0:T(8,128)(2,1)} %bitcast.65, s32[1152]{0:T(1024)S(1)} %copy-done.7), kind=kOutput, calls=%fused_computation.11 | convolution fusion | flops 1360871424 | bytes 2363904 | tf_op jit(solution)/shard_map/dot_general | solution.py:62
  159.3 7.2 %collective-permute-done.3 = bf16[288,1024]{1,0:T(8,128)(2,1)S(1)} collective-permute-done((bf16[288,1024]{1,0:T(8,128)(2,1)}, bf16[288,1024]{1,0:T(8,128)(2,1)S(1)}, u32[]{:S(2)}, u32[]{:S(2)}) %collective-permute-start.3) | collective-permute-done | bytes 589856 | tf_op jit(solution)/shard_map/ppermute | solution.py:23
  166.6 5.3 %collective-permute-start.5 = (bf16[144,1024]{1,0:T(8,128)(2,1)S(1)}, bf16[144,1024]{1,0:T(8,128)(2,1)S(1)}, u32[]{:S(2)}, u32[]{:S(2)}) collective-permute-start(bf16[144,1024]{1,0:T(8,128)(2,1)S(1)} %slice.110), channel_id=1, source_target_pairs={{0,8},{8,16},{16,24},{24,0},{1,9},{9,17},{17,25},{25,1},{2,10},{10... | collective-permute-start | bytes 884744 | tf_op jit(solution)/shard_map/ppermute | solution.py:23
  176.5 2.0 constant_dynamic-update-slice_fusion.2
  179.3 5.9 %collective-permute-done.6 = bf16[144,1024]{1,0:T(8,128)(2,1)S(1)} collective-permute-done((bf16[144,1024]{1,0:T(8,128)(2,1)S(1)}, bf16[144,1024]{1,0:T(8,128)(2,1)S(1)}, u32[]{:S(2)}, u32[]{:S(2)}) %collective-permute-start.6) | collective-permute-done | bytes 294944 | tf_op jit(solution)/shard_map/ppermute | solution.py:23
  188.7 15.1 %all-to-all-start.2 = ((bf16[64,2,108]{2,1,0:T(2,128)(2,1)}), bf16[64,2,108]{2,1,0:T(2,128)(2,1)S(1)}, u32[]{:S(2)}, u32[]{:S(2)}) async-start(bf16[64,2,108]{2,1,0:T(2,128)(2,1)} %bitcast.12), calls=%async_computation.2 | async-start | bytes 65536 | tf_op jit(solution)/shard_map/all_to_all | solution.py:347
  203.9 12.6 %all-to-all-done.2 = bf16[64,2,108]{2,1,0:T(2,128)(2,1)S(1)} async-done(((bf16[64,2,108]{2,1,0:T(2,128)(2,1)}), bf16[64,2,108]{2,1,0:T(2,128)(2,1)S(1)}, u32[]{:S(2)}, u32[]{:S(2)}) %all-to-all-start.2) | async-done | bytes 27680 | tf_op jit(solution)/shard_map/all_to_all | solution.py:347
  217.5 3.5 %all-to-all-start.3 = ((bf16[4,2,9216]{2,1,0:T(2,128)(2,1)}), bf16[4,2,9216]{2,1,0:T(2,128)(2,1)S(1)}, u32[]{:S(2)}, u32[]{:S(2)}) async-start(bf16[4,2,9216]{2,1,0:T(2,128)(2,1)} %broadcast_in_dim.58), calls=%async_computation.3 | async-start | bytes 294912 | tf_op jit(solution)/shard_map/all_to_all | solution.py:18
  221.0 2.0 fusion.15
  223.0 3.8 %all-to-all-done.3 = bf16[4,2,9216]{2,1,0:T(2,128)(2,1)S(1)} async-done(((bf16[4,2,9216]{2,1,0:T(2,128)(2,1)}), bf16[4,2,9216]{2,1,0:T(2,128)(2,1)S(1)}, u32[]{:S(2)}, u32[]{:S(2)}) %all-to-all-start.3) | async-done | bytes 147488 | tf_op jit(solution)/shard_map/all_to_all | solution.py:18
  229.9 9.9 %attention.1 = bf16[4,288,128]{2,1,0:T(8,128)(2,1)} custom-call(s32[1]{0:T(128)} %bitcast.1.core_ref, bf16[2,256,1152]{2,1,0:T(8,128)(2,1)} %bitcast.66, f32[2,1,1152]{2,1,0:T(1,128)} %get-tuple-element.56.shift_ref, f32[2,1,1152]{2,1,0:T(1,128)} %get-tuple-element.55.scale_ref, bf16[1152,1024]{1,0:T(8,128)(2,1)} %constant_dynamic-update-slice_fusion.mine_ref, ...), custom_call_target="tpu_custom_call" | custom-call | tf_op jit(solution)/shard_map/attention/pallas_call | solution.py:114
  239.8 3.5 %all-to-all-start.4 = ((bf16[4,288,128]{2,1,0:T(8,128)(2,1)}), bf16[4,288,128]{2,1,0:T(8,128)(2,1)S(1)}, u32[]{:S(2)}, u32[]{:S(2)}) async-start(bf16[4,288,128]{2,1,0:T(8,128)(2,1)} %attention.1), calls=%async_computation.4 | async-start | bytes 589824 | tf_op jit(solution)/shard_map/all_to_all | solution.py:390
  243.9 6.5 %all-to-all-done.4.mixed_ref = bf16[4,288,128]{2,1,0:T(8,128)(2,1)S(1)} async-done(((bf16[4,288,128]{2,1,0:T(8,128)(2,1)}), bf16[4,288,128]{2,1,0:T(8,128)(2,1)S(1)}, u32[]{:S(2)}, u32[]{:S(2)}) %all-to-all-start.4) | async-done | bytes 294944 | tf_op jit(solution)/shard_map/all_to_all | solution.py:390
  251.1 5.8 %project.1 = (f32[2,64,1152]{2,1,0:T(8,128)}, bf16[2,64,1152]{2,1,0:T(8,128)(2,1)}) custom-call(s32[1]{0:T(128)} %bitcast.base_ref, bf16[4,288,128]{2,1,0:T(8,128)(2,1)} %copy-done.3, bf16[1152,1024]{1,0:T(8,128)(2,1)} %constant_dynamic-update-slice_fusion.mine_ref, bf16[1152,1024]{1,0:T(8,128)(2,1)} %collective-permute-done.7.other_ref, ...), custom_call_target="tpu_custom_call" | custom-call | tf_op jit(solution)/shard_map/project/pallas_call | solution.py:156
  256.9 3.2 %collective-permute-start.8 = (bf16[128,1152]{1,0:T(8,128)(2,1)}, bf16[128,1152]{1,0:T(8,128)(2,1)S(1)}, u32[]{:S(2)}, u32[]{:S(2)}) collective-permute-start(bf16[128,1152]{1,0:T(8,128)(2,1)} %bitcast.62), channel_id=1, source_target_pairs={{0,1},{1,0},{2,3},{3,2},{4,5},{5,4},{6,7},{7,6},{8,9},{9,8},{10,11... | collective-permute-start | bytes 884744 | tf_op jit(solution)/shard_map/ppermute | solution.py:28
  260.2 5.6 %collective-permute-done.8.pair_ref = bf16[128,1152]{1,0:T(8,128)(2,1)S(1)} collective-permute-done((bf16[128,1152]{1,0:T(8,128)(2,1)}, bf16[128,1152]{1,0:T(8,128)(2,1)S(1)}, u32[]{:S(2)}, u32[]{:S(2)}) %collective-permute-start.8) | collective-permute-done | bytes 294944 | tf_op jit(solution)/shard_map/ppermute | solution.py:28
  266.4 6.1 %feed_first.1.before_ref = f32[256,1152]{1,0:T(8,128)} custom-call(bf16[128,1152]{1,0:T(8,128)(2,1)} %bitcast.63, bf16[128,1152]{1,0:T(8,128)(2,1)} %copy-done.2, bf16[1152,2304]{1,0:T(8,128)(2,1)} %all-gather.4.cloned.1.call-done.up_ref.down_ref, bf16[1152,2304]{1,0:T(8,128)(2,1)} %all-gather.4.cloned.1.call-done.up_ref.down_ref), custom_call_target="tpu_custom_call" | custom-call | tf_op jit(solution)/shard_map/feed_first/pallas_call | solution.py:222
  272.6 6.5 %feed_second.1 = (f32[128,1152]{1,0:T(8,128)}, bf16[128,1152]{1,0:T(8,128)(2,1)}) custom-call(bf16[128,1152]{1,0:T(8,128)(2,1)} %bitcast.64, bf16[128,1152]{1,0:T(8,128)(2,1)} %copy-done.2, bf16[1152,2304]{1,0:T(8,128)(2,1)} %collective-permute-done.9.up_ref.down_ref, bf16[1152,2304]{1,0:T(8,128)(2,1)} %collective-permute-done.9.up_ref.down_ref, ...), custom_call_target="tpu_custom_call" | custom-call | tf_op jit(solution)/shard_map/feed_second/pallas_call | solution.py:238
  279.2 3.2 %collective-permute-start.10 = (bf16[128,1152]{1,0:T(8,128)(2,1)}, bf16[128,1152]{1,0:T(8,128)(2,1)S(1)}, u32[]{:S(2)}, u32[]{:S(2)}) collective-permute-start(bf16[128,1152]{1,0:T(8,128)(2,1)} %get-tuple-element.19), channel_id=1, source_target_pairs={{0,1},{1,0},{2,3},{3,2},{4,5},{5,4},{6,7},{7,6},{8,9},{9,8},{10,11... | collective-permute-start | bytes 884744 | tf_op jit(solution)/shard_map/ppermute | solution.py:28
  284.9 3.1 %collective-permute-done.10.recv_ref = bf16[128,1152]{1,0:T(8,128)(2,1)S(1)} collective-permute-done((bf16[128,1152]{1,0:T(8,128)(2,1)}, bf16[128,1152]{1,0:T(8,128)(2,1)S(1)}, u32[]{:S(2)}, u32[]{:S(2)}) %collective-permute-start.10) | collective-permute-done | bytes 294944 | tf_op jit(solution)/shard_map/ppermute | solution.py:28
  288.7 2.5 finish.1
  (89 shorter events, 35.7 us)
Async XLA Ops:
  6.5 148.2 %copy-start = (bf16[288,2304]{1,0:T(8,128)(2,1)S(1)}, bf16[288,2304]{1,0:T(8,128)(2,1)}, u32[]{:S(2)}) copy-start(bf16[288,2304]{1,0:T(8,128)(2,1)} %param.22) | copy-start | bytes 3981316
  6.5 72.8 %all-gather.6.cloned.1.call-start = ((), (), s32[]{:S(2)}) async-start(), calls=%async_computation.6 | async-start | bytes 1658880 | tf_op jit(solution)/shard_map/all_gather | solution.py:342
  8.6 14.9 %collective-permute-start = (bf16[18,3024]{1,0:T(8,128)(2,1)S(1)}, bf16[18,3024]{1,0:T(8,128)(2,1)S(1)}, u32[]{:S(2)}, u32[]{:S(2)}) collective-permute-start(bf16[18,3024]{1,0:T(8,128)(2,1)S(1)} %concatenate.25), channel_id=1, source_target_pairs={{0,4},{4,0},{1,5},{5,1},{2,6},{6,2},{3,7},{7,3},{8,12},{12,8},{9,1... | collective-permute-start | bytes 326600 | tf_op jit(solution)/shard_map/ppermute | solution.py:28
  23.5 0.7 collective-permute-start.1
  24.9 118.1 %all-gather.4.cloned.1.call-start = ((), (), s32[]{:S(2)}) async-start(), calls=%async_computation.5 | async-start | bytes 6635520 | tf_op jit(solution)/shard_map/all_gather | solution.py:343
  85.4 15.5 %copy-start.9 = (bf16[2,288]{1,0:T(2,128)(2,1)}, bf16[2,288]{1,0:T(2,128)(2,1)S(1)}, u32[]{:S(2)}) copy-start(bf16[2,288]{1,0:T(2,128)(2,1)S(1)} %fusion.48) | copy-start | bytes 3460
  86.2 26.3 %all-to-all-start = ((bf16[64,2,288]{2,1,0:T(2,128)(2,1)}), bf16[64,2,288]{2,1,0:T(2,128)(2,1)S(1)}, u32[]{:S(2)}, u32[]{:S(2)}) async-start(bf16[64,2,288]{2,1,0:T(2,128)(2,1)} %broadcast_in_dim.56), calls=%async_computation | async-start | bytes 196608 | tf_op jit(solution)/shard_map/all_to_all | solution.py:18
  103.4 9.1 %collective-permute-start.2 = (bf16[36,288]{1,0:T(8,128)(2,1)S(1)}, bf16[36,288]{1,0:T(8,128)(2,1)S(1)}, u32[]{:S(2)}, u32[]{:S(2)}) collective-permute-start(bf16[36,288]{1,0:T(8,128)(2,1)S(1)} %pad_maximum_fusion.2), channel_id=1, source_target_pairs={{0,1},{1,0},{2,3},{3,2},{256,259},{257,258},{258,257},{259,256},{4... | collective-permute-start | bytes 62216 | tf_op jit(solution)/shard_map/ppermute | solution.py:331
  113.6 41.1 %copy-start.10 = (bf16[2,288]{1,0:T(2,128)(2,1)S(1)}, bf16[2,288]{1,0:T(2,128)(2,1)}, u32[]{:S(2)}) copy-start(bf16[2,288]{1,0:T(2,128)(2,1)} %copy-done.9) | copy-start | bytes 3460
  113.6 34.1 %all-to-all-start.1 = ((bf16[8,36,1024]{2,1,0:T(8,128)(2,1)}), bf16[8,36,1024]{2,1,0:T(8,128)(2,1)S(1)}, u32[]{:S(2)}, u32[]{:S(2)}) async-start(bf16[8,36,1024]{2,1,0:T(8,128)(2,1)} %broadcast_in_dim.57), calls=%async_computation.1 | async-start | bytes 1310720 | tf_op jit(solution)/shard_map/all_to_all | solution.py:18
  117.3 37.7 %copy-start.7 = (s32[1152]{0:T(1024)S(1)}, s32[1152]{0:T(1024)}, u32[]{:S(2)}) copy-start(s32[1152]{0:T(1024)} %fusion.38) | copy-start | bytes 13828
  143.0 129.6 %collective-permute-start.9 = (bf16[1152,2304]{1,0:T(8,128)(2,1)}, bf16[1152,2304]{1,0:T(8,128)(2,1)}, u32[]{:S(2)}, u32[]{:S(2)}) collective-permute-start(bf16[1152,2304]{1,0:T(8,128)(2,1)} %all-gather.4.cloned.1.call-done.up_ref.down_ref), channel_id=1, source_target_pairs={{0,256},{256,0},{1,257},{257,1},{2,258},{258,2},{3,259},{259,3},{4... | collective-permute-start | bytes 15925256 | tf_op jit(solution)/shard_map/ppermute | solution.py:28
  148.7 17.8 %collective-permute-start.3 = (bf16[288,1024]{1,0:T(8,128)(2,1)}, bf16[288,1024]{1,0:T(8,128)(2,1)S(1)}, u32[]{:S(2)}, u32[]{:S(2)}) collective-permute-start(bf16[288,1024]{1,0:T(8,128)(2,1)} %reshape.290), channel_id=1, source_target_pairs={{0,8},{8,16},{16,24},{24,0},{1,9},{9,17},{17,25},{25,1},{2,10},{10... | collective-permute-start | bytes 1769480 | tf_op jit(solution)/shard_map/ppermute | solution.py:23
  152.8 19.9 %collective-permute-start.4 = (bf16[288,1024]{1,0:T(8,128)(2,1)}, bf16[288,1024]{1,0:T(8,128)(2,1)}, u32[]{:S(2)}, u32[]{:S(2)}) collective-permute-start(bf16[288,1024]{1,0:T(8,128)(2,1)} %reshape.290), channel_id=1, source_target_pairs={{0,24},{8,0},{16,8},{24,16},{1,25},{9,1},{17,9},{25,17},{2,26},{10... | collective-permute-start | bytes 1769480 | tf_op jit(solution)/shard_map/ppermute | solution.py:23
  155.0 16.8 %copy-start.1 = (bf16[288,1024]{1,0:T(8,128)(2,1)S(1)}, bf16[288,1024]{1,0:T(8,128)(2,1)}, u32[]{:S(2)}) copy-start(bf16[288,1024]{1,0:T(8,128)(2,1)} %reshape.290) | copy-start | bytes 1769476
  166.6 11.9 %collective-permute-start.5 = (bf16[144,1024]{1,0:T(8,128)(2,1)S(1)}, bf16[144,1024]{1,0:T(8,128)(2,1)S(1)}, u32[]{:S(2)}, u32[]{:S(2)}) collective-permute-start(bf16[144,1024]{1,0:T(8,128)(2,1)S(1)} %slice.110), channel_id=1, source_target_pairs={{0,8},{8,16},{16,24},{24,0},{1,9},{9,17},{17,25},{25,1},{2,10},{10... | collective-permute-start | bytes 884744 | tf_op jit(solution)/shard_map/ppermute | solution.py:23
  172.7 15.1 %copy-start.5 = (bf16[288,108]{1,0:T(8,128)(2,1)S(1)}, bf16[288,108]{1,0:T(8,128)(2,1)}, u32[]{:S(2)}) copy-start(bf16[288,108]{1,0:T(8,128)(2,1)} %param.21) | copy-start | bytes 186628
  173.7 11.4 %collective-permute-start.6 = (bf16[144,1024]{1,0:T(8,128)(2,1)S(1)}, bf16[144,1024]{1,0:T(8,128)(2,1)S(1)}, u32[]{:S(2)}, u32[]{:S(2)}) collective-permute-start(bf16[144,1024]{1,0:T(8,128)(2,1)S(1)} %slice.111), channel_id=1, source_target_pairs={{0,24},{8,0},{16,8},{24,16},{1,25},{9,1},{17,9},{25,17},{2,26},{10... | collective-permute-start | bytes 884744 | tf_op jit(solution)/shard_map/ppermute | solution.py:23
  176.5 44.5 %copy-start.6 = (s32[1152]{0:T(1024)S(1)}, s32[1152]{0:T(1024)}, u32[]{:S(2)}) copy-start(s32[1152]{0:T(1024)} %multiply_add_fusion) | copy-start | bytes 13828
  185.9 44.0 %collective-permute-start.7 = (bf16[1152,1024]{1,0:T(8,128)(2,1)}, bf16[1152,1024]{1,0:T(8,128)(2,1)}, u32[]{:S(2)}, u32[]{:S(2)}) collective-permute-start(bf16[1152,1024]{1,0:T(8,128)(2,1)} %constant_dynamic-update-slice_fusion.mine_ref), channel_id=1, source_target_pairs={{0,256},{256,0},{1,257},{257,1},{2,258},{258,2},{3,259},{259,3},{4... | collective-permute-start | bytes 7077896 | tf_op jit(solution)/shard_map/ppermute | solution.py:28
  188.7 27.8 %all-to-all-start.2 = ((bf16[64,2,108]{2,1,0:T(2,128)(2,1)}), bf16[64,2,108]{2,1,0:T(2,128)(2,1)S(1)}, u32[]{:S(2)}, u32[]{:S(2)}) async-start(bf16[64,2,108]{2,1,0:T(2,128)(2,1)} %bitcast.12), calls=%async_computation.2 | async-start | bytes 65536 | tf_op jit(solution)/shard_map/all_to_all | solution.py:347
  203.9 23.1 %copy-start.8 = (s32[1152]{0:T(1024)S(1)}, s32[1152]{0:T(1024)}, u32[]{:S(2)}) copy-start(s32[1152]{0:T(1024)} %fusion.38) | copy-start | bytes 13828
  217.5 9.3 %all-to-all-start.3 = ((bf16[4,2,9216]{2,1,0:T(2,128)(2,1)}), bf16[4,2,9216]{2,1,0:T(2,128)(2,1)S(1)}, u32[]{:S(2)}, u32[]{:S(2)}) async-start(bf16[4,2,9216]{2,1,0:T(2,128)(2,1)} %broadcast_in_dim.58), calls=%async_computation.3 | async-start | bytes 294912 | tf_op jit(solution)/shard_map/all_to_all | solution.py:18
  239.8 10.7 %all-to-all-start.4 = ((bf16[4,288,128]{2,1,0:T(8,128)(2,1)}), bf16[4,288,128]{2,1,0:T(8,128)(2,1)S(1)}, u32[]{:S(2)}, u32[]{:S(2)}) async-start(bf16[4,288,128]{2,1,0:T(8,128)(2,1)} %attention.1), calls=%async_computation.4 | async-start | bytes 589824 | tf_op jit(solution)/shard_map/all_to_all | solution.py:390
  250.4 0.7 copy-start.3
  256.9 8.8 %collective-permute-start.8 = (bf16[128,1152]{1,0:T(8,128)(2,1)}, bf16[128,1152]{1,0:T(8,128)(2,1)S(1)}, u32[]{:S(2)}, u32[]{:S(2)}) collective-permute-start(bf16[128,1152]{1,0:T(8,128)(2,1)} %bitcast.62), channel_id=1, source_target_pairs={{0,1},{1,0},{2,3},{3,2},{4,5},{5,4},{6,7},{7,6},{8,9},{9,8},{10,11... | collective-permute-start | bytes 884744 | tf_op jit(solution)/shard_map/ppermute | solution.py:28
  265.7 0.7 copy-start.2
  272.6 10.5 %copy-start.11 = (bf16[1152,16]{0,1:T(8,128)(2,1)S(1)}, bf16[1152,16]{0,1:T(8,128)(2,1)}, u32[]{:S(2)}) copy-start(bf16[1152,16]{0,1:T(8,128)(2,1)} %param.27) | copy-start | bytes 110596
  279.2 8.8 %collective-permute-start.10 = (bf16[128,1152]{1,0:T(8,128)(2,1)}, bf16[128,1152]{1,0:T(8,128)(2,1)S(1)}, u32[]{:S(2)}, u32[]{:S(2)}) collective-permute-start(bf16[128,1152]{1,0:T(8,128)(2,1)} %get-tuple-element.19), channel_id=1, source_target_pairs={{0,1},{1,0},{2,3},{3,2},{4,5},{5,4},{6,7},{7,6},{8,9},{9,8},{10,11... | collective-permute-start | bytes 884744 | tf_op jit(solution)/shard_map/ppermute | solution.py:28
  288.0 0.7 copy-start.4
Sparse Core Ops, SparseCore 0:
  25.0 54.3 all-gather.5
  81.8 61.1 all-gather.3

commit v5 on v4

--- a/solution.py
+++ b/solution.py
@@ -26,11 +26,6 @@
 def swap(x, axis, bit):
     size = lax.axis_size(axis)
     return lax.ppermute(x, axis, [(i, i ^ bit) for i in range(size)])
-
-
-def gather_y(block):
-    pieces = to_everyone(block, "dp_0")
-    return pieces.reshape(pieces.shape[0] * pieces.shape[1], pieces.shape[2])
 
 
 def gather_x(block):
@@ -258,7 +253,13 @@
         total = first_ref[i] + gate_ref[i] * mlp
         fin = (layer_norm(total) * (1.0 + scale_ref[i]) + shift_ref[i]).astype(BF16)
         noise.append(dot(fin, out_w_ref[...]))
-    out_ref[...] = noise[1] + scale_by_ref[0] * (noise[0] - noise[1])
+    guided = noise[1] + scale_by_ref[0] * (noise[0] - noise[1])
+    outs = guided.shape[1]
+    wide = jnp.concatenate([guided] * (128 // outs), axis=1)
+    wide = jnp.concatenate([wide] * (share * outs // 128), axis=1)
+    token = lax.broadcasted_iota(jnp.int32, wide.shape, 0)
+    mine = lax.broadcasted_iota(jnp.int32, wide.shape, 1) // outs == token
+    out_ref[...] = jnp.sum(jnp.where(mine, wide, 0.0), axis=0, keepdims=True)
 
 
 def finish(guidance, keep, recv, first_sum, gate_m, shift_f, scale_f, out_local):
@@ -278,9 +279,9 @@
                 vector,
                 whole(out_local.shape),
             ],
-            out_specs=whole((share, out_local.shape[1])),
+            out_specs=whole((1, share * out_local.shape[1])),
         ),
-        out_shape=jax.ShapeDtypeStruct((share, out_local.shape[1]), F32),
+        out_shape=jax.ShapeDtypeStruct((1, share * out_local.shape[1]), F32),
         name="finish",
     )(guidance, keep, recv, first_sum, gate_m, shift_f, scale_f, out_local)
 
@@ -333,9 +334,21 @@
     feed = fetch(shards[:, : 2 * width + quarter], 0)
     proj_beside = fetch(shards[:, 2 * width : 2 * width + quarter], 1)
     part_a = lanes_full(jnp.concatenate([qkv_block, feed[:, 2 * width :], proj_beside], axis=1))
-    part_a, every_act = lax.optimization_barrier((part_a, every_act))
-    part_a = gather_y(part_a)
-    part_a, every_act = lax.optimization_barrier((part_a, every_act))
+
+    mod_part = dot(every_act, ada_weight).astype(BF16)
+    pad = -mod_part.shape[1] % 128
+    columns = mod_part.shape[1]
+    mod_part = jnp.pad(mod_part, ((0, 0), (0, pad))).reshape(n_y, n_x * n_z, 2, columns + pad)
+    mod_part = mod_part.transpose(1, 0, 2, 3)
+    mod_part = lax.all_to_all(mod_part, DP[1:], 0, 0, tiled=True)
+    mod_part = mod_part.transpose(1, 2, 0, 3).reshape(n_y, -1, part_a.shape[1])
+    block_rows = part_a.shape[0]
+    part_a = jnp.broadcast_to(part_a[None], (n_y, *part_a.shape))
+    part_a = jnp.concatenate([part_a, mod_part], axis=1)
+    part_a = lax.all_to_all(part_a, "dp_0", 0, 0, tiled=True)
+    mod_part = part_a[:, block_rows:].reshape(n_y, 2, n_x * n_z, columns + pad)
+    mod_part = mod_part[..., :columns].transpose(1, 0, 2, 3).reshape(2, -1)
+    part_a = part_a[:, :block_rows].reshape(n_y * block_rows, -1)
     part_a = gather_x(part_a)
     other_a = swap(part_a, "group", 1)
 
@@ -343,8 +356,6 @@
     feed = lax.all_gather(feed, "dp_1", axis=0, tiled=True)
     other_feed = swap(feed, "group", 1)
 
-    mod_part = dot(every_act, ada_weight).astype(BF16)
-    mod_part = lax.all_to_all(mod_part, DP, split_axis=0, concat_axis=1, tiled=True)
     final_part = dot(acts, final_ada).astype(BF16)
     mod_parts = to_everyone(jnp.concatenate([mod_part, final_part], axis=1), "mp")
 
@@ -395,8 +406,7 @@
     before = feed_first(hidden_two, pair, feed)
     keep, send = feed_second(hidden_two, pair, other_feed, before)
     recv = swap(send, "mp", 1)
-    guided = finish(guidance, keep, recv, first_sum, gate_m, shift_f, scale_f, out_local)
-    return guided.reshape(1, share * out_weight.shape[1])
+    return finish(guidance, keep, recv, first_sum, gate_m, shift_f, scale_f, out_local)
 
 
 def solution(mesh):
@@ -420,4 +430,6 @@
         P("mp", DP),
         P(),
     )
-    return jax.shard_map(on_device, mesh=torus, in_specs=placed, out_specs=P(GROUP_DP, "mp"), check_vma=False)
+    return jax.shard_map(
+        on_device, mesh=torus, in_specs=placed, out_specs=P(GROUP_DP, "mp"), check_vma=False
+    )

time: 302 us -> 276 us (0.914)
  waiting for transfers between devices: 135 us -> 120 us
  starting transfers between devices: 77 us -> 66.4 us
    all_gather x1, waiting for transfers between devices: 25.7 us -> 11.2 us  [on_device(): feed = lax.all_gather(feed, 'dp_1', axis=0, tiled=True)]
    all_to_all x1 -> x2, waiting for transfers between devices: 12.6 us -> 5.52 us  [the longest x1 5.52 us: on_device(): mod_part = lax.all_to_all(mod_part, DP[1:], 0, 0, tiled=True)]
    all_to_all x1 -> x2, starting transfers between devices: 15.1 us -> 9.15 us  [the longest x1 5.61 us: on_device(): mod_part = lax.all_to_all(mod_part, DP[1:], 0, 0, tiled=True)]
    all_to_all x3 -> x2, waiting for transfers between devices: 9.56 us -> 13.4 us  [to_everyone(): lax.all_to_all(jnp.broadcast_to(x[None], (size, *x.shape)), axis, 0, 0, t...]
    all_to_all x3 -> x2, starting transfers between devices: 20.7 us -> 18.4 us  [to_everyone(): lax.all_to_all(jnp.broadcast_to(x[None], (size, *x.shape)), axis, 0, 0, t...]
    unnamed x33 -> x24, local copies, waits for them, and re-layouts: 9.95 us -> 11.1 us
  transfers between devices with their start and end apart: 18 -> 18, of which waited for: 11 -> 11; matrix products, arithmetic and copies ran while one was open for 11% -> 12% of each run, Pallas kernels for 7% -> 8%
where the time goes in v5:
time: 276 us; the launch traced here: 275 us
  waiting for transfers between devices  120 us (43%)
  starting transfers between devices  66.4 us (24%)
  Pallas kernels  30.9 us (11%)
  local copies, waits for them, and re-layouts  22.7 us (8%)
  between operations  16.4 us (6%)
  matrix products  10.9 us (4%)
  other arithmetic  7.62 us (3%)
    all_gather x1, waiting for transfers between devices, on_device(): feed = lax.all_gather(feed[:, :2 * width], 'dp_0', axis=0, tiled=True)  54.4 us
    ppermute x5, starting transfers between devices, swap(): return lax.ppermute(x, axis, [(i, i ^ bit) for i in range(size)])  18.8 us
    all_to_all x2, starting transfers between devices, to_everyone(): lax.all_to_all(jnp.broadcast_to(x[None], (size, *x.shape)), axis, 0, 0, t...  18.4 us
    ppermute x5, waiting for transfers between devices, swap(): return lax.ppermute(x, axis, [(i, i ^ bit) for i in range(size)])  15 us
    all_to_all x2, waiting for transfers between devices, to_everyone(): lax.all_to_all(jnp.broadcast_to(x[None], (size, *x.shape)), axis, 0, 0, t...  13.4 us
    ppermute x4, starting transfers between devices, shift(): return lax.ppermute(x, axis, [(i, (i + step) % size) for i in range(size)])  13.2 us
    ppermute x4, waiting for transfers between devices, shift(): return lax.ppermute(x, axis, [(i, (i + step) % size) for i in range(size)])  12.2 us
    all_gather x1, waiting for transfers between devices, on_device(): feed = lax.all_gather(feed, 'dp_1', axis=0, tiled=True)  11.2 us
  transfers between devices with their start and end apart: 18, of which 11 were waited for; matrix products, arithmetic and copies ran while one was open for 12% of the time, Pallas kernels for 8%

profile of v5, /device:TPU:6, one launch (start us, length us, event | category | flops | bytes accessed | tf_op | source)
XLA Modules:
  0.0 274.9 jit_solution(16998199089318185046)
XLA Ops:
  8.6 10.9 %collective-permute-start = (bf16[18,3024]{1,0:T(8,128)(2,1)S(1)}, bf16[18,3024]{1,0:T(8,128)(2,1)S(1)}, u32[]{:S(2)}, u32[]{:S(2)}) collective-permute-start(bf16[18,3024]{1,0:T(8,128)(2,1)S(1)} %concatenate.28), channel_id=1, source_target_pairs={{0,4},{4,0},{1,5},{5,1},{2,6},{6,2},{3,7},{7,3},{8,12},{12,8},{9,1... | collective-permute-start | bytes 326600 | tf_op jit(solution)/shard_map/ppermute | solution.py:28
  19.5 3.9 %collective-permute-done = bf16[18,3024]{1,0:T(8,128)(2,1)S(1)} collective-permute-done((bf16[18,3024]{1,0:T(8,128)(2,1)S(1)}, bf16[18,3024]{1,0:T(8,128)(2,1)S(1)}, u32[]{:S(2)}, u32[]{:S(2)}) %collective-permute-start) | collective-permute-done | bytes 108896 | tf_op jit(solution)/shard_map/ppermute | solution.py:28
  25.0 54.4 %all-gather.6.cloned.1.call-done = bf16[8,36,2304]{2,1,0:T(8,128)(2,1)} async-done(((bf16[1,36,2304]{2,1,0:T(8,128)(2,1)}), bf16[8,36,2304]{2,1,0:T(8,128)(2,1)}) %all-gather.6.cloned.1.call-update) | async-done | bytes 1327120 | tf_op jit(solution)/shard_map/all_gather | solution.py:355
  79.4 2.3 reshape.358
  86.2 13.5 %all-to-all-start = ((bf16[64,2,288]{2,1,0:T(2,128)(2,1)}), bf16[64,2,288]{2,1,0:T(2,128)(2,1)S(1)}, u32[]{:S(2)}, u32[]{:S(2)}) async-start(bf16[64,2,288]{2,1,0:T(2,128)(2,1)} %broadcast_in_dim.57), calls=%async_computation | async-start | bytes 196608 | tf_op jit(solution)/shard_map/all_to_all | solution.py:18
  102.9 9.7 %all-to-all-done = bf16[64,2,288]{2,1,0:T(2,128)(2,1)S(1)} async-done(((bf16[64,2,288]{2,1,0:T(2,128)(2,1)}), bf16[64,2,288]{2,1,0:T(2,128)(2,1)S(1)}, u32[]{:S(2)}, u32[]{:S(2)}) %all-to-all-start) | async-done | bytes 73760 | tf_op jit(solution)/shard_map/all_to_all | solution.py:18
  113.7 5.6 %all-to-all-start.1 = ((bf16[8,8,2,128]{3,2,1,0:T(2,128)(2,1)}), bf16[8,8,2,128]{3,2,1,0:T(2,128)(2,1)S(1)}, u32[]{:S(2)}, u32[]{:S(2)}) async-start(bf16[8,8,2,128]{3,2,1,0:T(2,128)(2,1)} %copy.50), calls=%async_computation.1 | async-start | bytes 65536 | tf_op jit(solution)/shard_map/all_to_all | solution.py:343
  119.3 2.7 collective-permute-start.2
  122.0 5.5 %all-to-all-done.1 = bf16[8,8,2,128]{3,2,1,0:T(2,128)(2,1)S(1)} async-done(((bf16[8,8,2,128]{3,2,1,0:T(2,128)(2,1)}), bf16[8,8,2,128]{3,2,1,0:T(2,128)(2,1)S(1)}, u32[]{:S(2)}, u32[]{:S(2)}) %all-to-all-start.1) | async-done | bytes 32800 | tf_op jit(solution)/shard_map/all_to_all | solution.py:343
  128.7 3.5 %all-to-all-start.2 = ((bf16[8,38,1024]{2,1,0:T(8,128)(2,1)}), bf16[8,38,1024]{2,1,0:T(8,128)(2,1)S(1)}, u32[]{:S(2)}, u32[]{:S(2)}) async-start(bf16[8,38,1024]{2,1,0:T(8,128)(2,1)} %pad_maximum_fusion.1), calls=%async_computation.2 | async-start | bytes 1310720 | tf_op jit(solution)/shard_map/all_to_all | solution.py:348
  132.2 11.2 %all-gather.4.cloned.1.call-done.up_ref.down_ref = bf16[1152,2304]{1,0:T(8,128)(2,1)} async-done(((bf16[288,2304]{1,0:T(8,128)(2,1)}), bf16[1152,2304]{1,0:T(8,128)(2,1)}) %all-gather.4.cloned.1.call-update) | async-done | bytes 5308432 | tf_op jit(solution)/shard_map/all_gather | solution.py:356
  145.3 2.1 compare_convert_fusion.change_ref
  148.4 4.0 %collective-permute-start.3 = (bf16[288,1024]{1,0:T(8,128)(2,1)}, bf16[288,1024]{1,0:T(8,128)(2,1)}, u32[]{:S(2)}, u32[]{:S(2)}) collective-permute-start(bf16[288,1024]{1,0:T(8,128)(2,1)} %reshape.301), channel_id=1, source_target_pairs={{0,8},{8,16},{16,24},{24,0},{1,9},{9,17},{17,25},{25,1},{2,10},{10... | collective-permute-start | bytes 1769480 | tf_op jit(solution)/shard_map/ppermute | solution.py:23
  152.5 1.9 collective-permute-start.4
  154.7 4.3 %fusion.9 = bf16[512,1152]{1,0:T(8,128)(2,1)} fusion(bf16[512,1152]{1,0:T(8,128)(2,1)} %bitcast.78, s32[1152]{0:T(1024)S(1)} %fusion.38), kind=kOutput, calls=%fused_computation.11 | convolution fusion | flops 1360871424 | bytes 2363904 | tf_op jit(solution)/shard_map/dot_general | solution.py:57
  159.0 7.4 %collective-permute-done.3 = bf16[288,1024]{1,0:T(8,128)(2,1)} collective-permute-done((bf16[288,1024]{1,0:T(8,128)(2,1)}, bf16[288,1024]{1,0:T(8,128)(2,1)}, u32[]{:S(2)}, u32[]{:S(2)}) %collective-permute-start.3) | collective-permute-done | bytes 589856 | tf_op jit(solution)/shard_map/ppermute | solution.py:23
  167.3 5.3 %collective-permute-start.5 = (bf16[144,1024]{1,0:T(8,128)(2,1)S(1)}, bf16[144,1024]{1,0:T(8,128)(2,1)S(1)}, u32[]{:S(2)}, u32[]{:S(2)}) collective-permute-start(bf16[144,1024]{1,0:T(8,128)(2,1)S(1)} %slice.125), channel_id=1, source_target_pairs={{0,8},{8,16},{16,24},{24,0},{1,9},{9,17},{17,25},{25,1},{2,10},{10... | collective-permute-start | bytes 884744 | tf_op jit(solution)/shard_map/ppermute | solution.py:23
  181.0 4.9 %collective-permute-done.6 = bf16[144,1024]{1,0:T(8,128)(2,1)S(1)} collective-permute-done((bf16[144,1024]{1,0:T(8,128)(2,1)S(1)}, bf16[144,1024]{1,0:T(8,128)(2,1)S(1)}, u32[]{:S(2)}, u32[]{:S(2)}) %collective-permute-start.6) | collective-permute-done | bytes 294944 | tf_op jit(solution)/shard_map/ppermute | solution.py:23
  190.3 4.9 %all-to-all-start.3 = ((bf16[4,2,9216]{2,1,0:T(2,128)(2,1)}), bf16[4,2,9216]{2,1,0:T(2,128)(2,1)S(1)}, u32[]{:S(2)}, u32[]{:S(2)}) async-start(bf16[4,2,9216]{2,1,0:T(2,128)(2,1)} %broadcast_in_dim.58), calls=%async_computation.3 | async-start | bytes 294912 | tf_op jit(solution)/shard_map/all_to_all | solution.py:18
  195.2 2.9 %fusion.15 = bf16[128,1152]{1,0:T(8,128)(2,1)} fusion(bf16[128,1152]{1,0:T(8,128)(2,1)} %bitcast.81, s32[1152]{0:T(1024)S(1)} %multiply_add_fusion), kind=kOutput, calls=%fused_computation.17 | convolution fusion | flops 341213184 | bytes 594432 | tf_op jit(solution)/shard_map/dot_general | solution.py:57
  198.1 3.8 %all-to-all-done.3 = bf16[4,2,9216]{2,1,0:T(2,128)(2,1)S(1)} async-done(((bf16[4,2,9216]{2,1,0:T(2,128)(2,1)}), bf16[4,2,9216]{2,1,0:T(2,128)(2,1)S(1)}, u32[]{:S(2)}, u32[]{:S(2)}) %all-to-all-start.3) | async-done | bytes 147488 | tf_op jit(solution)/shard_map/all_to_all | solution.py:18
  205.0 9.8 %attention.1 = bf16[4,288,128]{2,1,0:T(8,128)(2,1)} custom-call(s32[1]{0:T(128)} %bitcast.1.core_ref, bf16[2,256,1152]{2,1,0:T(8,128)(2,1)} %bitcast.79, f32[2,1,1152]{2,1,0:T(1,128)} %get-tuple-element.48.shift_ref, f32[2,1,1152]{2,1,0:T(1,128)} %get-tuple-element.47.scale_ref, bf16[1152,1024]{1,0:T(8,128)(2,1)} %constant_dynamic-update-slice_fusion.mine_ref, ...), custom_call_target="tpu_custom_call" | custom-call | tf_op jit(solution)/shard_map/attention/pallas_call | solution.py:109
  214.8 3.5 %all-to-all-start.4 = ((bf16[4,288,128]{2,1,0:T(8,128)(2,1)}), bf16[4,288,128]{2,1,0:T(8,128)(2,1)S(1)}, u32[]{:S(2)}, u32[]{:S(2)}) async-start(bf16[4,288,128]{2,1,0:T(8,128)(2,1)} %attention.1), calls=%async_computation.4 | async-start | bytes 589824 | tf_op jit(solution)/shard_map/all_to_all | solution.py:401
  218.9 8.2 %all-to-all-done.4.mixed_ref = bf16[4,288,128]{2,1,0:T(8,128)(2,1)S(1)} async-done(((bf16[4,288,128]{2,1,0:T(8,128)(2,1)}), bf16[4,288,128]{2,1,0:T(8,128)(2,1)S(1)}, u32[]{:S(2)}, u32[]{:S(2)}) %all-to-all-start.4) | async-done | bytes 294944 | tf_op jit(solution)/shard_map/all_to_all | solution.py:401
  227.8 5.8 %project.1 = (f32[2,64,1152]{2,1,0:T(8,128)}, bf16[2,64,1152]{2,1,0:T(8,128)(2,1)}) custom-call(s32[1]{0:T(128)} %bitcast.base_ref, bf16[4,288,128]{2,1,0:T(8,128)(2,1)} %copy-done.3, bf16[1152,1024]{1,0:T(8,128)(2,1)} %constant_dynamic-update-slice_fusion.mine_ref, bf16[1152,1024]{1,0:T(8,128)(2,1)} %collective-permute-done.7.other_ref, ...), custom_call_target="tpu_custom_call" | custom-call | tf_op jit(solution)/shard_map/project/pallas_call | solution.py:151
  233.6 1.9 collective-permute-start.8
  235.5 7.0 %collective-permute-done.8.pair_ref = bf16[128,1152]{1,0:T(8,128)(2,1)S(1)} collective-permute-done((bf16[128,1152]{1,0:T(8,128)(2,1)}, bf16[128,1152]{1,0:T(8,128)(2,1)S(1)}, u32[]{:S(2)}, u32[]{:S(2)}) %collective-permute-start.8) | collective-permute-done | bytes 294944 | tf_op jit(solution)/shard_map/ppermute | solution.py:28
  243.2 6.1 %feed_first.1.before_ref = f32[256,1152]{1,0:T(8,128)} custom-call(bf16[128,1152]{1,0:T(8,128)(2,1)} %bitcast.76, bf16[128,1152]{1,0:T(8,128)(2,1)} %copy-done.2, bf16[1152,2304]{1,0:T(8,128)(2,1)} %all-gather.4.cloned.1.call-done.up_ref.down_ref, bf16[1152,2304]{1,0:T(8,128)(2,1)} %all-gather.4.cloned.1.call-done.up_ref.down_ref), custom_call_target="tpu_custom_call" | custom-call | tf_op jit(solution)/shard_map/feed_first/pallas_call | solution.py:217
  249.3 6.5 %feed_second.1 = (f32[128,1152]{1,0:T(8,128)}, bf16[128,1152]{1,0:T(8,128)(2,1)}) custom-call(bf16[128,1152]{1,0:T(8,128)(2,1)} %bitcast.77, bf16[128,1152]{1,0:T(8,128)(2,1)} %copy-done.2, bf16[1152,2304]{1,0:T(8,128)(2,1)} %collective-permute-done.9.up_ref.down_ref, bf16[1152,2304]{1,0:T(8,128)(2,1)} %collective-permute-done.9.up_ref.down_ref, ...), custom_call_target="tpu_custom_call" | custom-call | tf_op jit(solution)/shard_map/feed_second/pallas_call | solution.py:233
  255.8 2.2 collective-permute-start.10
  260.5 4.1 %collective-permute-done.10.recv_ref = bf16[128,1152]{1,0:T(8,128)(2,1)S(1)} collective-permute-done((bf16[128,1152]{1,0:T(8,128)(2,1)}, bf16[128,1152]{1,0:T(8,128)(2,1)S(1)}, u32[]{:S(2)}, u32[]{:S(2)}) %collective-permute-start.10) | collective-permute-done | bytes 294944 | tf_op jit(solution)/shard_map/ppermute | solution.py:28
  265.4 2.7 finish.1
  (84 shorter events, 36.0 us)
Async XLA Ops:
  6.5 147.9 %copy-start = (bf16[288,2304]{1,0:T(8,128)(2,1)S(1)}, bf16[288,2304]{1,0:T(8,128)(2,1)}, u32[]{:S(2)}) copy-start(bf16[288,2304]{1,0:T(8,128)(2,1)} %param.22) | copy-start | bytes 3981316
  6.5 72.9 %all-gather.6.cloned.1.call-start = ((), (), s32[]{:S(2)}) async-start(), calls=%async_computation.6 | async-start | bytes 1658880 | tf_op jit(solution)/shard_map/all_gather | solution.py:355
  8.6 14.9 %collective-permute-start = (bf16[18,3024]{1,0:T(8,128)(2,1)S(1)}, bf16[18,3024]{1,0:T(8,128)(2,1)S(1)}, u32[]{:S(2)}, u32[]{:S(2)}) collective-permute-start(bf16[18,3024]{1,0:T(8,128)(2,1)S(1)} %concatenate.28), channel_id=1, source_target_pairs={{0,4},{4,0},{1,5},{5,1},{2,6},{6,2},{3,7},{7,3},{8,12},{12,8},{9,1... | collective-permute-start | bytes 326600 | tf_op jit(solution)/shard_map/ppermute | solution.py:28
  23.5 0.7 collective-permute-start.1
  24.9 118.5 %all-gather.4.cloned.1.call-start = ((), (), s32[]{:S(2)}) async-start(), calls=%async_computation.5 | async-start | bytes 6635520 | tf_op jit(solution)/shard_map/all_gather | solution.py:356
  86.2 26.4 %all-to-all-start = ((bf16[64,2,288]{2,1,0:T(2,128)(2,1)}), bf16[64,2,288]{2,1,0:T(2,128)(2,1)S(1)}, u32[]{:S(2)}, u32[]{:S(2)}) async-start(bf16[64,2,288]{2,1,0:T(2,128)(2,1)} %broadcast_in_dim.57), calls=%async_computation | async-start | bytes 196608 | tf_op jit(solution)/shard_map/all_to_all | solution.py:18
  101.7 11.0 %copy-start.5 = (bf16[288,108]{1,0:T(8,128)(2,1)S(1)}, bf16[288,108]{1,0:T(8,128)(2,1)}, u32[]{:S(2)}) copy-start(bf16[288,108]{1,0:T(8,128)(2,1)} %param.21) | copy-start | bytes 186628
  113.7 13.8 %all-to-all-start.1 = ((bf16[8,8,2,128]{3,2,1,0:T(2,128)(2,1)}), bf16[8,8,2,128]{3,2,1,0:T(2,128)(2,1)S(1)}, u32[]{:S(2)}, u32[]{:S(2)}) async-start(bf16[8,8,2,128]{3,2,1,0:T(2,128)(2,1)} %copy.50), calls=%async_computation.1 | async-start | bytes 65536 | tf_op jit(solution)/shard_map/all_to_all | solution.py:343
  119.3 8.2 %collective-permute-start.2 = (bf16[36,288]{1,0:T(8,128)(2,1)S(1)}, bf16[36,288]{1,0:T(8,128)(2,1)S(1)}, u32[]{:S(2)}, u32[]{:S(2)}) collective-permute-start(bf16[36,288]{1,0:T(8,128)(2,1)S(1)} %pad_maximum_fusion.3), channel_id=1, source_target_pairs={{0,1},{1,0},{2,3},{3,2},{256,259},{257,258},{258,257},{259,256},{4... | collective-permute-start | bytes 62216 | tf_op jit(solution)/shard_map/ppermute | solution.py:332
  128.7 18.8 %all-to-all-start.2 = ((bf16[8,38,1024]{2,1,0:T(8,128)(2,1)}), bf16[8,38,1024]{2,1,0:T(8,128)(2,1)S(1)}, u32[]{:S(2)}, u32[]{:S(2)}) async-start(bf16[8,38,1024]{2,1,0:T(8,128)(2,1)} %pad_maximum_fusion.1), calls=%async_computation.2 | async-start | bytes 1310720 | tf_op jit(solution)/shard_map/all_to_all | solution.py:348
  143.4 105.9 %collective-permute-start.9 = (bf16[1152,2304]{1,0:T(8,128)(2,1)}, bf16[1152,2304]{1,0:T(8,128)(2,1)}, u32[]{:S(2)}, u32[]{:S(2)}) collective-permute-start(bf16[1152,2304]{1,0:T(8,128)(2,1)} %all-gather.4.cloned.1.call-done.up_ref.down_ref), channel_id=1, source_target_pairs={{0,256},{256,0},{1,257},{257,1},{2,258},{258,2},{3,259},{259,3},{4... | collective-permute-start | bytes 15925256 | tf_op jit(solution)/shard_map/ppermute | solution.py:28
  148.4 17.9 %collective-permute-start.3 = (bf16[288,1024]{1,0:T(8,128)(2,1)}, bf16[288,1024]{1,0:T(8,128)(2,1)}, u32[]{:S(2)}, u32[]{:S(2)}) collective-permute-start(bf16[288,1024]{1,0:T(8,128)(2,1)} %reshape.301), channel_id=1, source_target_pairs={{0,8},{8,16},{16,24},{24,0},{1,9},{9,17},{17,25},{25,1},{2,10},{10... | collective-permute-start | bytes 1769480 | tf_op jit(solution)/shard_map/ppermute | solution.py:23
  152.5 21.0 %collective-permute-start.4 = (bf16[288,1024]{1,0:T(8,128)(2,1)}, bf16[288,1024]{1,0:T(8,128)(2,1)}, u32[]{:S(2)}, u32[]{:S(2)}) collective-permute-start(bf16[288,1024]{1,0:T(8,128)(2,1)} %reshape.301), channel_id=1, source_target_pairs={{0,24},{8,0},{16,8},{24,16},{1,25},{9,1},{17,9},{25,17},{2,26},{10... | collective-permute-start | bytes 1769480 | tf_op jit(solution)/shard_map/ppermute | solution.py:23
  154.7 17.9 %copy-start.1 = (bf16[288,1024]{1,0:T(8,128)(2,1)S(1)}, bf16[288,1024]{1,0:T(8,128)(2,1)}, u32[]{:S(2)}) copy-start(bf16[288,1024]{1,0:T(8,128)(2,1)} %reshape.301) | copy-start | bytes 1769476
  167.3 12.9 %collective-permute-start.5 = (bf16[144,1024]{1,0:T(8,128)(2,1)S(1)}, bf16[144,1024]{1,0:T(8,128)(2,1)S(1)}, u32[]{:S(2)}, u32[]{:S(2)}) collective-permute-start(bf16[144,1024]{1,0:T(8,128)(2,1)S(1)} %slice.125), channel_id=1, source_target_pairs={{0,8},{8,16},{16,24},{24,0},{1,9},{9,17},{17,25},{25,1},{2,10},{10... | collective-permute-start | bytes 884744 | tf_op jit(solution)/shard_map/ppermute | solution.py:23
  174.5 11.4 %collective-permute-start.6 = (bf16[144,1024]{1,0:T(8,128)(2,1)S(1)}, bf16[144,1024]{1,0:T(8,128)(2,1)S(1)}, u32[]{:S(2)}, u32[]{:S(2)}) collective-permute-start(bf16[144,1024]{1,0:T(8,128)(2,1)S(1)} %slice.126), channel_id=1, source_target_pairs={{0,24},{8,0},{16,8},{24,16},{1,25},{9,1},{17,9},{25,17},{2,26},{10... | collective-permute-start | bytes 884744 | tf_op jit(solution)/shard_map/ppermute | solution.py:23
  186.6 18.4 %collective-permute-start.7 = (bf16[1152,1024]{1,0:T(8,128)(2,1)}, bf16[1152,1024]{1,0:T(8,128)(2,1)}, u32[]{:S(2)}, u32[]{:S(2)}) collective-permute-start(bf16[1152,1024]{1,0:T(8,128)(2,1)} %constant_dynamic-update-slice_fusion.mine_ref), channel_id=1, source_target_pairs={{0,256},{256,0},{1,257},{257,1},{2,258},{258,2},{3,259},{259,3},{4... | collective-permute-start | bytes 7077896 | tf_op jit(solution)/shard_map/ppermute | solution.py:28
  190.3 11.6 %all-to-all-start.3 = ((bf16[4,2,9216]{2,1,0:T(2,128)(2,1)}), bf16[4,2,9216]{2,1,0:T(2,128)(2,1)S(1)}, u32[]{:S(2)}, u32[]{:S(2)}) async-start(bf16[4,2,9216]{2,1,0:T(2,128)(2,1)} %broadcast_in_dim.58), calls=%async_computation.3 | async-start | bytes 294912 | tf_op jit(solution)/shard_map/all_to_all | solution.py:18
  214.8 12.3 %all-to-all-start.4 = ((bf16[4,288,128]{2,1,0:T(8,128)(2,1)}), bf16[4,288,128]{2,1,0:T(8,128)(2,1)S(1)}, u32[]{:S(2)}, u32[]{:S(2)}) async-start(bf16[4,288,128]{2,1,0:T(8,128)(2,1)} %attention.1), calls=%async_computation.4 | async-start | bytes 589824 | tf_op jit(solution)/shard_map/all_to_all | solution.py:401
  227.1 0.7 copy-start.3
  233.6 8.9 %collective-permute-start.8 = (bf16[128,1152]{1,0:T(8,128)(2,1)}, bf16[128,1152]{1,0:T(8,128)(2,1)S(1)}, u32[]{:S(2)}, u32[]{:S(2)}) collective-permute-start(bf16[128,1152]{1,0:T(8,128)(2,1)} %bitcast.75), channel_id=1, source_target_pairs={{0,1},{1,0},{2,3},{3,2},{4,5},{5,4},{6,7},{7,6},{8,9},{9,8},{10,11... | collective-permute-start | bytes 884744 | tf_op jit(solution)/shard_map/ppermute | solution.py:28
  242.5 0.7 copy-start.2
  249.3 9.4 %copy-start.6 = (bf16[1152,16]{0,1:T(8,128)(2,1)S(1)}, bf16[1152,16]{0,1:T(8,128)(2,1)}, u32[]{:S(2)}) copy-start(bf16[1152,16]{0,1:T(8,128)(2,1)} %param.27) | copy-start | bytes 110596
  255.8 8.8 %collective-permute-start.10 = (bf16[128,1152]{1,0:T(8,128)(2,1)}, bf16[128,1152]{1,0:T(8,128)(2,1)S(1)}, u32[]{:S(2)}, u32[]{:S(2)}) collective-permute-start(bf16[128,1152]{1,0:T(8,128)(2,1)} %get-tuple-element.11), channel_id=1, source_target_pairs={{0,1},{1,0},{2,3},{3,2},{4,5},{5,4},{6,7},{7,6},{8,9},{9,8},{10,11... | collective-permute-start | bytes 884744 | tf_op jit(solution)/shard_map/ppermute | solution.py:28
  264.6 0.7 copy-start.4
Sparse Core Ops, SparseCore 0:
  25.0 54.3 all-gather.5
  81.9 61.4 all-gather.3

commit v6 on v4

--- a/solution.py
+++ b/solution.py
@@ -7,6 +7,7 @@
 from jax.sharding import PartitionSpec as P
 
 CLASSES = 1000
+GATHER_FLOOR = 1 << 20
 DP = ("dp_0", "dp_1", "dp_2")
 GROUP_DP = ("group", "dp_0", "dp_1", "dp_2")
 BF16 = jnp.bfloat16
@@ -258,7 +259,13 @@
         total = first_ref[i] + gate_ref[i] * mlp
         fin = (layer_norm(total) * (1.0 + scale_ref[i]) + shift_ref[i]).astype(BF16)
         noise.append(dot(fin, out_w_ref[...]))
-    out_ref[...] = noise[1] + scale_by_ref[0] * (noise[0] - noise[1])
+    guided = noise[1] + scale_by_ref[0] * (noise[0] - noise[1])
+    outs = guided.shape[1]
+    wide = jnp.concatenate([guided] * (128 // outs), axis=1)
+    wide = jnp.concatenate([wide] * (share * outs // 128), axis=1)
+    token = lax.broadcasted_iota(jnp.int32, wide.shape, 0)
+    mine = lax.broadcasted_iota(jnp.int32, wide.shape, 1) // outs == token
+    out_ref[...] = jnp.sum(jnp.where(mine, wide, 0.0), axis=0, keepdims=True)
 
 
 def finish(guidance, keep, recv, first_sum, gate_m, shift_f, scale_f, out_local):
@@ -278,9 +285,9 @@
                 vector,
                 whole(out_local.shape),
             ],
-            out_specs=whole((share, out_local.shape[1])),
+            out_specs=whole((1, share * out_local.shape[1])),
         ),
-        out_shape=jax.ShapeDtypeStruct((share, out_local.shape[1]), F32),
+        out_shape=jax.ShapeDtypeStruct((1, share * out_local.shape[1]), F32),
         name="finish",
     )(guidance, keep, recv, first_sum, gate_m, shift_f, scale_f, out_local)
 
@@ -339,8 +346,10 @@
     part_a = gather_x(part_a)
     other_a = swap(part_a, "group", 1)
 
-    feed = lax.all_gather(feed[:, : 2 * width], "dp_0", axis=0, tiled=True)
-    feed = lax.all_gather(feed, "dp_1", axis=0, tiled=True)
+    wide = max(2 * width, -(-GATHER_FLOOR // (2 * n_x * feed.shape[0] * 128)) * 128)
+    feed = jnp.pad(feed[:, : 2 * width], ((0, 0), (0, wide - 2 * width)))
+    feed = lax.all_gather(feed, "dp_1", axis=0, tiled=True)[:, : 2 * width]
+    feed = lax.all_gather(feed, "dp_0", axis=0, tiled=True)
     other_feed = swap(feed, "group", 1)
 
     mod_part = dot(every_act, ada_weight).astype(BF16)
@@ -358,9 +367,7 @@
     from_x = (column + offset) % n_x
     final = (inside // per_y * n_x + from_x) * per_y + inside % per_y
     near_order = (lax.broadcasted_iota(jnp.int32, (width, width), 0) == final).astype(BF16)
-    natural = (inside // per_y * n_x + block) * per_y + inside % per_y
-    order = (lax.broadcasted_iota(jnp.int32, (width, width), 0) == natural).astype(BF16)
-    change = (final.reshape(width, 1) == natural).astype(BF16)
+    change = (final.reshape(width, 1) == spot).astype(BF16)
 
     first = cond_first[0] == 1
     cond_rows = jnp.where(first, x_arrive[0], x_arrive[1])
@@ -368,22 +375,16 @@
     arrived = jnp.stack([cond_rows, uncond_rows])
     share = tokens // n_mp
     own = lax.dynamic_slice_in_dim(arrived, place * share, share, 1)
-    own = dot(own.reshape(-1, width), order).astype(BF16).reshape(2, share, width)
     images = dot(arrived.reshape(-1, width), near_order).astype(BF16)
     images = images.reshape(2, tokens, width)
-    out_local = lax.dot_general(
-        order, out_weight, (((0,), (0,)), ((), ())), preferred_element_type=F32
-    ).astype(BF16)
     mod_parts = mod_parts.reshape(n_mp * 2, -1, width)
 
-    def mods_in(pieces, by):
-        count = pieces.shape[1]
-        values = dot(pieces.reshape(-1, width), by).reshape(n_mp, 2, count, 1, width)
-        values = jnp.sum(values, axis=0)
-        return [values[:, i] for i in range(count)]
-
-    shift_a, scale_a = mods_in(mod_parts[:, :2], near_order)
-    gate_a, shift_m, scale_m, gate_m, shift_f, scale_f = mods_in(mod_parts[:, 2:], order)
+    turned = dot(mod_parts[:, :2].reshape(-1, width), near_order).reshape(n_mp, 2, 2, 1, width)
+    turned = jnp.sum(turned, axis=0)
+    shift_a, scale_a = turned[:, 0], turned[:, 1]
+    mods = mod_parts[:, 2:].astype(F32).reshape(n_mp, 2, -1, 1, width)
+    mods = jnp.sum(mods, axis=0)
+    gate_a, shift_m, scale_m, gate_m, shift_f, scale_f = (mods[:, i] for i in range(6))
 
     cores = core.reshape(1).astype(jnp.int32)
     mixed = attention(cores, images, shift_a, scale_a, part_a, other_a, n_mp, quarter)
@@ -395,8 +396,7 @@
     before = feed_first(hidden_two, pair, feed)
     keep, send = feed_second(hidden_two, pair, other_feed, before)
     recv = swap(send, "mp", 1)
-    guided = finish(guidance, keep, recv, first_sum, gate_m, shift_f, scale_f, out_local)
-    return guided.reshape(1, share * out_weight.shape[1])
+    return finish(guidance, keep, recv, first_sum, gate_m, shift_f, scale_f, out_weight)
 
 
 def solution(mesh):

time: 302 us -> 306 us (1.013)
  waiting for transfers between devices: 135 us -> 149 us
  matrix products: 9.95 us -> 4.55 us
  local copies, waits for them, and re-layouts: 22.9 us -> 19.3 us
    all_gather x2, waiting for transfers between devices: 80.1 us -> 88 us  [the longest x1 46.5 us: on_device(): feed = lax.all_gather(feed, 'dp_0', axis=0, tiled=True)]
    dot_general x6 -> x4, matrix products: 9.03 us -> 4.55 us  [dot(): return jnp.dot(a, b, preferred_element_type=F32)]
    all_to_all x3, waiting for transfers between devices: 9.56 us -> 13.5 us  [to_everyone(): lax.all_to_all(jnp.broadcast_to(x[None], (size, *x.shape)), axis, 0, 0, t...]
    unnamed x33 -> x32, local copies, waits for them, and re-layouts: 9.95 us -> 8.87 us
  transfers between devices with their start and end apart: 18 -> 18, of which waited for: 11 -> 12; matrix products, arithmetic and copies ran while one was open for 11% -> 8% of each run, Pallas kernels for 7% -> 7%
where the time goes in v6:
time: 306 us; the launch traced here: 304 us
  waiting for transfers between devices  149 us (49%)
  starting transfers between devices  76.3 us (25%)
  Pallas kernels  30.9 us (10%)
  local copies, waits for them, and re-layouts  19.3 us (6%)
  between operations  16.4 us (5%)
  other arithmetic  6.99 us (2%)
  matrix products  4.55 us (1%)
    all_gather x1, waiting for transfers between devices, on_device(): feed = lax.all_gather(feed, 'dp_0', axis=0, tiled=True)  46.5 us
    all_gather x1, waiting for transfers between devices, on_device(): feed = lax.all_gather(feed, 'dp_1', axis=0, tiled=True)[:, :2 * width]  41.5 us
    all_to_all x3, starting transfers between devices, to_everyone(): lax.all_to_all(jnp.broadcast_to(x[None], (size, *x.shape)), axis, 0, 0, t...  23.1 us
    ppermute x5, starting transfers between devices, swap(): return lax.ppermute(x, axis, [(i, i ^ bit) for i in range(size)])  21.3 us
    ppermute x4, waiting for transfers between devices, shift(): return lax.ppermute(x, axis, [(i, (i + step) % size) for i in range(size)])  15.6 us
    ppermute x5, waiting for transfers between devices, swap(): return lax.ppermute(x, axis, [(i, i ^ bit) for i in range(size)])  13.5 us
    all_to_all x3, waiting for transfers between devices, to_everyone(): lax.all_to_all(jnp.broadcast_to(x[None], (size, *x.shape)), axis, 0, 0, t...  13.5 us
    all_to_all x1, starting transfers between devices, on_device(): lax.all_to_all(mod_part, DP, split_axis=0, concat_axis=1, tiled=True)  13.2 us
  transfers between devices with their start and end apart: 18, of which 12 were waited for; matrix products, arithmetic and copies ran while one was open for 8% of the time, Pallas kernels for 7%

profile of v6, /device:TPU:6, one launch (start us, length us, event | category | flops | bytes accessed | tf_op | source)
XLA Modules:
  0.0 303.9 jit_solution(16859019039896502984)
XLA Ops:
  8.6 10.9 %collective-permute-start = (bf16[18,3024]{1,0:T(8,128)(2,1)S(1)}, bf16[18,3024]{1,0:T(8,128)(2,1)S(1)}, u32[]{:S(2)}, u32[]{:S(2)}) collective-permute-start(bf16[18,3024]{1,0:T(8,128)(2,1)S(1)} %concatenate.25), channel_id=1, source_target_pairs={{0,4},{4,0},{1,5},{5,1},{2,6},{6,2},{3,7},{7,3},{8,12},{12,8},{9,1... | collective-permute-start | bytes 326600 | tf_op jit(solution)/shard_map/ppermute | solution.py:29
  19.5 3.9 %collective-permute-done = bf16[18,3024]{1,0:T(8,128)(2,1)S(1)} collective-permute-done((bf16[18,3024]{1,0:T(8,128)(2,1)S(1)}, bf16[18,3024]{1,0:T(8,128)(2,1)S(1)}, u32[]{:S(2)}, u32[]{:S(2)}) %collective-permute-start) | collective-permute-done | bytes 108896 | tf_op jit(solution)/shard_map/ppermute | solution.py:29
  25.0 41.5 %all-gather.6.cloned.1.call-done = bf16[4,36,3712]{2,1,0:T(8,128)(2,1)} async-done(((bf16[1,36,3712]{2,1,0:T(8,128)(2,1)}), bf16[4,36,3712]{2,1,0:T(8,128)(2,1)}) %all-gather.6.cloned.1.call-update) | async-done | bytes 1069072 | tf_op jit(solution)/shard_map/all_gather | solution.py:351
  73.3 16.0 %all-to-all-start = ((bf16[64,2,288]{2,1,0:T(2,128)(2,1)}), bf16[64,2,288]{2,1,0:T(2,128)(2,1)S(1)}, u32[]{:S(2)}, u32[]{:S(2)}) async-start(bf16[64,2,288]{2,1,0:T(2,128)(2,1)} %broadcast_in_dim.56), calls=%async_computation | async-start | bytes 196608 | tf_op jit(solution)/shard_map/all_to_all | solution.py:19
  91.3 2.6 collective-permute-start.2
  94.6 8.4 %all-to-all-done = bf16[64,2,288]{2,1,0:T(2,128)(2,1)S(1)} async-done(((bf16[64,2,288]{2,1,0:T(2,128)(2,1)}), bf16[64,2,288]{2,1,0:T(2,128)(2,1)S(1)}, u32[]{:S(2)}, u32[]{:S(2)}) %all-to-all-start) | async-done | bytes 73760 | tf_op jit(solution)/shard_map/all_to_all | solution.py:19
  104.2 3.5 %all-to-all-start.1 = ((bf16[8,36,1024]{2,1,0:T(8,128)(2,1)}), bf16[8,36,1024]{2,1,0:T(8,128)(2,1)S(1)}, u32[]{:S(2)}, u32[]{:S(2)}) async-start(bf16[8,36,1024]{2,1,0:T(8,128)(2,1)} %broadcast_in_dim.57), calls=%async_computation.1 | async-start | bytes 1310720 | tf_op jit(solution)/shard_map/all_to_all | solution.py:19
  107.7 46.5 %all-gather.4.cloned.1.call-done.up_ref.down_ref = bf16[1152,2304]{1,0:T(8,128)(2,1)} async-done(((bf16[144,2304]{1,0:T(8,128)(2,1)}), bf16[1152,2304]{1,0:T(8,128)(2,1)}) %all-gather.4.cloned.1.call-update) | async-done | bytes 5308432 | tf_op jit(solution)/shard_map/all_gather | solution.py:352
  156.1 2.8 fusion.2.change_ref
  159.9 2.4 collective-permute-start.3
  162.4 3.4 %collective-permute-start.4 = (bf16[288,1024]{1,0:T(8,128)(2,1)}, bf16[288,1024]{1,0:T(8,128)(2,1)S(1)}, u32[]{:S(2)}, u32[]{:S(2)}) collective-permute-start(bf16[288,1024]{1,0:T(8,128)(2,1)} %reshape.272), channel_id=1, source_target_pairs={{0,24},{8,0},{16,8},{24,16},{1,25},{9,1},{17,9},{25,17},{2,26},{10... | collective-permute-start | bytes 1769480 | tf_op jit(solution)/shard_map/ppermute | solution.py:24
  165.9 2.9 fusion.5
  168.8 8.9 %collective-permute-done.3 = bf16[288,1024]{1,0:T(8,128)(2,1)S(1)} collective-permute-done((bf16[288,1024]{1,0:T(8,128)(2,1)}, bf16[288,1024]{1,0:T(8,128)(2,1)S(1)}, u32[]{:S(2)}, u32[]{:S(2)}) %collective-permute-start.3) | collective-permute-done | bytes 589856 | tf_op jit(solution)/shard_map/ppermute | solution.py:24
  177.8 3.7 %collective-permute-start.5 = (bf16[144,1024]{1,0:T(8,128)(2,1)S(1)}, bf16[144,1024]{1,0:T(8,128)(2,1)S(1)}, u32[]{:S(2)}, u32[]{:S(2)}) collective-permute-start(bf16[144,1024]{1,0:T(8,128)(2,1)S(1)} %slice.114), channel_id=1, source_target_pairs={{0,8},{8,16},{16,24},{24,0},{1,9},{9,17},{17,25},{25,1},{2,10},{10... | collective-permute-start | bytes 884744 | tf_op jit(solution)/shard_map/ppermute | solution.py:24
  182.4 2.3 collective-permute-start.6
  189.0 4.9 %collective-permute-done.6 = bf16[144,1024]{1,0:T(8,128)(2,1)S(1)} collective-permute-done((bf16[144,1024]{1,0:T(8,128)(2,1)S(1)}, bf16[144,1024]{1,0:T(8,128)(2,1)S(1)}, u32[]{:S(2)}, u32[]{:S(2)}) %collective-permute-start.6) | collective-permute-done | bytes 294944 | tf_op jit(solution)/shard_map/ppermute | solution.py:24
  194.6 2.0 collective-permute-start.7
  197.6 13.2 %all-to-all-start.2 = ((bf16[64,2,108]{2,1,0:T(2,128)(2,1)}), bf16[64,2,108]{2,1,0:T(2,128)(2,1)S(1)}, u32[]{:S(2)}, u32[]{:S(2)}) async-start(bf16[64,2,108]{2,1,0:T(2,128)(2,1)} %bitcast.12), calls=%async_computation.2 | async-start | bytes 65536 | tf_op jit(solution)/shard_map/all_to_all | solution.py:356
  211.2 12.3 %all-to-all-done.2 = bf16[64,2,108]{2,1,0:T(2,128)(2,1)S(1)} async-done(((bf16[64,2,108]{2,1,0:T(2,128)(2,1)}), bf16[64,2,108]{2,1,0:T(2,128)(2,1)S(1)}, u32[]{:S(2)}, u32[]{:S(2)}) %all-to-all-start.2) | async-done | bytes 27680 | tf_op jit(solution)/shard_map/all_to_all | solution.py:356
  224.4 3.5 %all-to-all-start.3 = ((bf16[4,2,9216]{2,1,0:T(2,128)(2,1)}), bf16[4,2,9216]{2,1,0:T(2,128)(2,1)S(1)}, u32[]{:S(2)}, u32[]{:S(2)}) async-start(bf16[4,2,9216]{2,1,0:T(2,128)(2,1)} %broadcast_in_dim.58), calls=%async_computation.3 | async-start | bytes 294912 | tf_op jit(solution)/shard_map/all_to_all | solution.py:19
  228.7 5.1 %all-to-all-done.3 = bf16[4,2,9216]{2,1,0:T(2,128)(2,1)S(1)} async-done(((bf16[4,2,9216]{2,1,0:T(2,128)(2,1)}), bf16[4,2,9216]{2,1,0:T(2,128)(2,1)S(1)}, u32[]{:S(2)}, u32[]{:S(2)}) %all-to-all-start.3) | async-done | bytes 147488 | tf_op jit(solution)/shard_map/all_to_all | solution.py:19
  235.7 9.8 %attention.1 = bf16[4,288,128]{2,1,0:T(8,128)(2,1)} custom-call(s32[1]{0:T(128)} %bitcast.1.core_ref, bf16[2,256,1152]{2,1,0:T(8,128)(2,1)} %bitcast.55, f32[2,1,1152]{2,1,0:T(1,128)} %get-tuple-element.56.shift_ref, f32[2,1,1152]{2,1,0:T(1,128)} %get-tuple-element.55.scale_ref, bf16[1152,1024]{1,0:T(8,128)(2,1)} %constant_dynamic-update-slice_fusion.mine_ref, ...), custom_call_target="tpu_custom_call" | custom-call | tf_op jit(solution)/shard_map/attention/pallas_call | solution.py:115
  245.6 3.5 %all-to-all-start.4 = ((bf16[4,288,128]{2,1,0:T(8,128)(2,1)}), bf16[4,288,128]{2,1,0:T(8,128)(2,1)S(1)}, u32[]{:S(2)}, u32[]{:S(2)}) async-start(bf16[4,288,128]{2,1,0:T(8,128)(2,1)} %attention.1), calls=%async_computation.4 | async-start | bytes 589824 | tf_op jit(solution)/shard_map/all_to_all | solution.py:391
  249.7 6.6 %all-to-all-done.4.mixed_ref = bf16[4,288,128]{2,1,0:T(8,128)(2,1)S(1)} async-done(((bf16[4,288,128]{2,1,0:T(8,128)(2,1)}), bf16[4,288,128]{2,1,0:T(8,128)(2,1)S(1)}, u32[]{:S(2)}, u32[]{:S(2)}) %all-to-all-start.4) | async-done | bytes 294944 | tf_op jit(solution)/shard_map/all_to_all | solution.py:391
  257.0 5.8 %project.1 = (f32[2,64,1152]{2,1,0:T(8,128)}, bf16[2,64,1152]{2,1,0:T(8,128)(2,1)}) custom-call(s32[1]{0:T(128)} %bitcast.base_ref, bf16[4,288,128]{2,1,0:T(8,128)(2,1)} %copy-done.3, bf16[1152,1024]{1,0:T(8,128)(2,1)} %constant_dynamic-update-slice_fusion.mine_ref, bf16[1152,1024]{1,0:T(8,128)(2,1)} %collective-permute-done.7.other_ref, ...), custom_call_target="tpu_custom_call" | custom-call | tf_op jit(solution)/shard_map/project/pallas_call | solution.py:157
  262.7 3.2 %collective-permute-start.8 = (bf16[128,1152]{1,0:T(8,128)(2,1)}, bf16[128,1152]{1,0:T(8,128)(2,1)S(1)}, u32[]{:S(2)}, u32[]{:S(2)}) collective-permute-start(bf16[128,1152]{1,0:T(8,128)(2,1)} %bitcast.51), channel_id=1, source_target_pairs={{0,1},{1,0},{2,3},{3,2},{4,5},{5,4},{6,7},{7,6},{8,9},{9,8},{10,11... | collective-permute-start | bytes 884744 | tf_op jit(solution)/shard_map/ppermute | solution.py:29
  266.0 5.6 %collective-permute-done.8.pair_ref = bf16[128,1152]{1,0:T(8,128)(2,1)S(1)} collective-permute-done((bf16[128,1152]{1,0:T(8,128)(2,1)}, bf16[128,1152]{1,0:T(8,128)(2,1)S(1)}, u32[]{:S(2)}, u32[]{:S(2)}) %collective-permute-start.8) | collective-permute-done | bytes 294944 | tf_op jit(solution)/shard_map/ppermute | solution.py:29
  272.3 6.1 %feed_first.1.before_ref = f32[256,1152]{1,0:T(8,128)} custom-call(bf16[128,1152]{1,0:T(8,128)(2,1)} %bitcast.52, bf16[128,1152]{1,0:T(8,128)(2,1)} %copy-done.2, bf16[1152,2304]{1,0:T(8,128)(2,1)} %all-gather.4.cloned.1.call-done.up_ref.down_ref, bf16[1152,2304]{1,0:T(8,128)(2,1)} %all-gather.4.cloned.1.call-done.up_ref.down_ref), custom_call_target="tpu_custom_call" | custom-call | tf_op jit(solution)/shard_map/feed_first/pallas_call | solution.py:223
  278.4 6.5 %feed_second.1 = (f32[128,1152]{1,0:T(8,128)}, bf16[128,1152]{1,0:T(8,128)(2,1)}) custom-call(bf16[128,1152]{1,0:T(8,128)(2,1)} %bitcast.53, bf16[128,1152]{1,0:T(8,128)(2,1)} %copy-done.2, bf16[1152,2304]{1,0:T(8,128)(2,1)} %collective-permute-done.9.up_ref.down_ref, bf16[1152,2304]{1,0:T(8,128)(2,1)} %collective-permute-done.9.up_ref.down_ref, ...), custom_call_target="tpu_custom_call" | custom-call | tf_op jit(solution)/shard_map/feed_second/pallas_call | solution.py:239
  284.9 3.2 %collective-permute-start.10 = (bf16[128,1152]{1,0:T(8,128)(2,1)}, bf16[128,1152]{1,0:T(8,128)(2,1)S(1)}, u32[]{:S(2)}, u32[]{:S(2)}) collective-permute-start(bf16[128,1152]{1,0:T(8,128)(2,1)} %get-tuple-element.19), channel_id=1, source_target_pairs={{0,1},{1,0},{2,3},{3,2},{4,5},{5,4},{6,7},{7,6},{8,9},{9,8},{10,11... | collective-permute-start | bytes 884744 | tf_op jit(solution)/shard_map/ppermute | solution.py:29
  289.7 4.0 %collective-permute-done.10.recv_ref = bf16[128,1152]{1,0:T(8,128)(2,1)S(1)} collective-permute-done((bf16[128,1152]{1,0:T(8,128)(2,1)}, bf16[128,1152]{1,0:T(8,128)(2,1)S(1)}, u32[]{:S(2)}, u32[]{:S(2)}) %collective-permute-start.10) | collective-permute-done | bytes 294944 | tf_op jit(solution)/shard_map/ppermute | solution.py:29
  294.4 2.7 finish.1
  (85 shorter events, 29.5 us)
Async XLA Ops:
  6.5 204.3 %copy-start = (bf16[288,2304]{1,0:T(8,128)(2,1)S(1)}, bf16[288,2304]{1,0:T(8,128)(2,1)}, u32[]{:S(2)}) copy-start(bf16[288,2304]{1,0:T(8,128)(2,1)} %param.22) | copy-start | bytes 3981316
  6.5 60.0 %all-gather.6.cloned.1.call-start = ((), (), s32[]{:S(2)}) async-start(), calls=%async_computation.6 | async-start | bytes 1484800 | tf_op jit(solution)/shard_map/all_gather | solution.py:351
  8.6 14.9 %collective-permute-start = (bf16[18,3024]{1,0:T(8,128)(2,1)S(1)}, bf16[18,3024]{1,0:T(8,128)(2,1)S(1)}, u32[]{:S(2)}, u32[]{:S(2)}) collective-permute-start(bf16[18,3024]{1,0:T(8,128)(2,1)S(1)} %concatenate.25), channel_id=1, source_target_pairs={{0,4},{4,0},{1,5},{5,1},{2,6},{6,2},{3,7},{7,3},{8,12},{12,8},{9,1... | collective-permute-start | bytes 326600 | tf_op jit(solution)/shard_map/ppermute | solution.py:29
  23.5 0.7 collective-permute-start.1
  25.0 129.2 %all-gather.4.cloned.1.call-start = ((), (), s32[]{:S(2)}) async-start(), calls=%async_computation.5 | async-start | bytes 5971968 | tf_op jit(solution)/shard_map/all_gather | solution.py:352
  72.6 17.4 %copy-start.9 = (bf16[2,288]{1,0:T(2,128)(2,1)}, bf16[2,288]{1,0:T(2,128)(2,1)S(1)}, u32[]{:S(2)}) copy-start(bf16[2,288]{1,0:T(2,128)(2,1)S(1)} %fusion.36) | copy-start | bytes 3460
  73.3 29.8 %all-to-all-start = ((bf16[64,2,288]{2,1,0:T(2,128)(2,1)}), bf16[64,2,288]{2,1,0:T(2,128)(2,1)S(1)}, u32[]{:S(2)}, u32[]{:S(2)}) async-start(bf16[64,2,288]{2,1,0:T(2,128)(2,1)} %broadcast_in_dim.56), calls=%async_computation | async-start | bytes 196608 | tf_op jit(solution)/shard_map/all_to_all | solution.py:19
  91.3 11.8 %collective-permute-start.2 = (bf16[36,288]{1,0:T(8,128)(2,1)S(1)}, bf16[36,288]{1,0:T(8,128)(2,1)S(1)}, u32[]{:S(2)}, u32[]{:S(2)}) collective-permute-start(bf16[36,288]{1,0:T(8,128)(2,1)S(1)} %pad_maximum_fusion.2), channel_id=1, source_target_pairs={{0,1},{1,0},{2,3},{3,2},{256,259},{257,258},{258,257},{259,256},{4... | collective-permute-start | bytes 62216 | tf_op jit(solution)/shard_map/ppermute | solution.py:338
  104.2 54.8 %all-to-all-start.1 = ((bf16[8,36,1024]{2,1,0:T(8,128)(2,1)}), bf16[8,36,1024]{2,1,0:T(8,128)(2,1)S(1)}, u32[]{:S(2)}, u32[]{:S(2)}) async-start(bf16[8,36,1024]{2,1,0:T(8,128)(2,1)} %broadcast_in_dim.57), calls=%async_computation.1 | async-start | bytes 1310720 | tf_op jit(solution)/shard_map/all_to_all | solution.py:19
  154.2 124.2 %collective-permute-start.9 = (bf16[1152,2304]{1,0:T(8,128)(2,1)}, bf16[1152,2304]{1,0:T(8,128)(2,1)}, u32[]{:S(2)}, u32[]{:S(2)}) collective-permute-start(bf16[1152,2304]{1,0:T(8,128)(2,1)} %all-gather.4.cloned.1.call-done.up_ref.down_ref), channel_id=1, source_target_pairs={{0,256},{256,0},{1,257},{257,1},{2,258},{258,2},{3,259},{259,3},{4... | collective-permute-start | bytes 15925256 | tf_op jit(solution)/shard_map/ppermute | solution.py:29
  159.0 6.9 %copy-start.7 = (s32[1152]{0:T(1024)S(1)}, s32[1152]{0:T(1024)}, u32[]{:S(2)}) copy-start(s32[1152]{0:T(1024)} %fusion.24) | copy-start | bytes 13828
  159.9 17.8 %collective-permute-start.3 = (bf16[288,1024]{1,0:T(8,128)(2,1)}, bf16[288,1024]{1,0:T(8,128)(2,1)S(1)}, u32[]{:S(2)}, u32[]{:S(2)}) collective-permute-start(bf16[288,1024]{1,0:T(8,128)(2,1)} %reshape.272), channel_id=1, source_target_pairs={{0,8},{8,16},{16,24},{24,0},{1,9},{9,17},{17,25},{25,1},{2,10},{10... | collective-permute-start | bytes 1769480 | tf_op jit(solution)/shard_map/ppermute | solution.py:24
  162.4 20.0 %collective-permute-start.4 = (bf16[288,1024]{1,0:T(8,128)(2,1)}, bf16[288,1024]{1,0:T(8,128)(2,1)S(1)}, u32[]{:S(2)}, u32[]{:S(2)}) collective-permute-start(bf16[288,1024]{1,0:T(8,128)(2,1)} %reshape.272), channel_id=1, source_target_pairs={{0,24},{8,0},{16,8},{24,16},{1,25},{9,1},{17,9},{25,17},{2,26},{10... | collective-permute-start | bytes 1769480 | tf_op jit(solution)/shard_map/ppermute | solution.py:24
  165.9 15.5 %copy-start.1 = (bf16[288,1024]{1,0:T(8,128)(2,1)S(1)}, bf16[288,1024]{1,0:T(8,128)(2,1)}, u32[]{:S(2)}) copy-start(bf16[288,1024]{1,0:T(8,128)(2,1)} %reshape.272) | copy-start | bytes 1769476
  177.8 10.4 %collective-permute-start.5 = (bf16[144,1024]{1,0:T(8,128)(2,1)S(1)}, bf16[144,1024]{1,0:T(8,128)(2,1)S(1)}, u32[]{:S(2)}, u32[]{:S(2)}) collective-permute-start(bf16[144,1024]{1,0:T(8,128)(2,1)S(1)} %slice.114), channel_id=1, source_target_pairs={{0,8},{8,16},{16,24},{24,0},{1,9},{9,17},{17,25},{25,1},{2,10},{10... | collective-permute-start | bytes 884744 | tf_op jit(solution)/shard_map/ppermute | solution.py:24
  182.3 14.3 %copy-start.5 = (bf16[288,108]{1,0:T(8,128)(2,1)S(1)}, bf16[288,108]{1,0:T(8,128)(2,1)}, u32[]{:S(2)}) copy-start(bf16[288,108]{1,0:T(8,128)(2,1)} %param.21) | copy-start | bytes 186628
  182.3 28.5 %copy-start.10 = (bf16[2,288]{1,0:T(2,128)(2,1)S(1)}, bf16[2,288]{1,0:T(2,128)(2,1)}, u32[]{:S(2)}) copy-start(bf16[2,288]{1,0:T(2,128)(2,1)} %copy-done.9) | copy-start | bytes 3460
  182.4 11.5 %collective-permute-start.6 = (bf16[144,1024]{1,0:T(8,128)(2,1)S(1)}, bf16[144,1024]{1,0:T(8,128)(2,1)S(1)}, u32[]{:S(2)}, u32[]{:S(2)}) collective-permute-start(bf16[144,1024]{1,0:T(8,128)(2,1)S(1)} %slice.115), channel_id=1, source_target_pairs={{0,24},{8,0},{16,8},{24,16},{1,25},{9,1},{17,9},{25,17},{2,26},{10... | collective-permute-start | bytes 884744 | tf_op jit(solution)/shard_map/ppermute | solution.py:24
  194.6 39.4 %copy-start.8 = (s32[1152]{0:T(1024)S(1)}, s32[1152]{0:T(1024)}, u32[]{:S(2)}) copy-start(s32[1152]{0:T(1024)} %fusion.24) | copy-start | bytes 13828
  194.6 41.1 %collective-permute-start.7 = (bf16[1152,1024]{1,0:T(8,128)(2,1)}, bf16[1152,1024]{1,0:T(8,128)(2,1)}, u32[]{:S(2)}, u32[]{:S(2)}) collective-permute-start(bf16[1152,1024]{1,0:T(8,128)(2,1)} %constant_dynamic-update-slice_fusion.mine_ref), channel_id=1, source_target_pairs={{0,256},{256,0},{1,257},{257,1},{2,258},{258,2},{3,259},{259,3},{4... | collective-permute-start | bytes 7077896 | tf_op jit(solution)/shard_map/ppermute | solution.py:29
  197.6 25.9 %all-to-all-start.2 = ((bf16[64,2,108]{2,1,0:T(2,128)(2,1)}), bf16[64,2,108]{2,1,0:T(2,128)(2,1)S(1)}, u32[]{:S(2)}, u32[]{:S(2)}) async-start(bf16[64,2,108]{2,1,0:T(2,128)(2,1)} %bitcast.12), calls=%async_computation.2 | async-start | bytes 65536 | tf_op jit(solution)/shard_map/all_to_all | solution.py:356
  224.4 9.3 %all-to-all-start.3 = ((bf16[4,2,9216]{2,1,0:T(2,128)(2,1)}), bf16[4,2,9216]{2,1,0:T(2,128)(2,1)S(1)}, u32[]{:S(2)}, u32[]{:S(2)}) async-start(bf16[4,2,9216]{2,1,0:T(2,128)(2,1)} %broadcast_in_dim.58), calls=%async_computation.3 | async-start | bytes 294912 | tf_op jit(solution)/shard_map/all_to_all | solution.py:19
  245.6 10.7 %all-to-all-start.4 = ((bf16[4,288,128]{2,1,0:T(8,128)(2,1)}), bf16[4,288,128]{2,1,0:T(8,128)(2,1)S(1)}, u32[]{:S(2)}, u32[]{:S(2)}) async-start(bf16[4,288,128]{2,1,0:T(8,128)(2,1)} %attention.1), calls=%async_computation.4 | async-start | bytes 589824 | tf_op jit(solution)/shard_map/all_to_all | solution.py:391
  256.2 0.7 copy-start.3
  262.7 8.8 %collective-permute-start.8 = (bf16[128,1152]{1,0:T(8,128)(2,1)}, bf16[128,1152]{1,0:T(8,128)(2,1)S(1)}, u32[]{:S(2)}, u32[]{:S(2)}) collective-permute-start(bf16[128,1152]{1,0:T(8,128)(2,1)} %bitcast.51), channel_id=1, source_target_pairs={{0,1},{1,0},{2,3},{3,2},{4,5},{5,4},{6,7},{7,6},{8,9},{9,8},{10,11... | collective-permute-start | bytes 884744 | tf_op jit(solution)/shard_map/ppermute | solution.py:29
  271.5 0.7 copy-start.2
  278.4 10.4 %copy-start.6 = (bf16[1152,16]{0,1:T(8,128)(2,1)S(1)}, bf16[1152,16]{0,1:T(8,128)(2,1)}, u32[]{:S(2)}) copy-start(bf16[1152,16]{0,1:T(8,128)(2,1)} %param.27) | copy-start | bytes 110596
  284.9 8.8 %collective-permute-start.10 = (bf16[128,1152]{1,0:T(8,128)(2,1)}, bf16[128,1152]{1,0:T(8,128)(2,1)S(1)}, u32[]{:S(2)}, u32[]{:S(2)}) collective-permute-start(bf16[128,1152]{1,0:T(8,128)(2,1)} %get-tuple-element.19), channel_id=1, source_target_pairs={{0,1},{1,0},{2,3},{3,2},{4,5},{5,4},{6,7},{7,6},{8,9},{9,8},{10,11... | collective-permute-start | bytes 884744 | tf_op jit(solution)/shard_map/ppermute | solution.py:29
  293.7 0.7 copy-start.4
Sparse Core Ops, SparseCore 0:
  25.1 41.4 all-gather.5
  69.0 85.2 all-gather.3

commit v7 on v6

--- a/solution.py
+++ b/solution.py
@@ -135,13 +135,11 @@
     for i in range(4):
         at = lead + i % 2 * quarter
         rows_ref[i // 2, at : at + quarter] = mixed_ref[base ^ i]
-    both = (((0,), (1,)), ((), ()))
+    attn = dot(mine_ref[:, start - lead :], rows_ref[0])
+    attn = (attn + dot(other_ref[:, start - lead :], rows_ref[1])).astype(BF16)
     attn = lax.dot_general(
-        rows_ref[0], mine_ref[:, start - lead :], both, preferred_element_type=F32
-    ) + lax.dot_general(
-        rows_ref[1], other_ref[:, start - lead :], both, preferred_element_type=F32
+        attn, change_ref[...], (((0,), (0,)), ((), ())), preferred_element_type=F32
     )
-    attn = dot(attn.astype(BF16), change_ref[...])
     share = own_ref.shape[1]
     for i in range(2):
         total = own_ref[i].astype(F32) + gate_ref[i] * attn[i * share : (i + 1) * share]
@@ -189,7 +187,7 @@
         rows_ref[count:] = pair_ref[...]
 
     hidden = jax.nn.gelu(dot(rows_ref[...], up_ref[...]), approximate=True).astype(BF16)
-    return so_far() + dot_t(hidden, down_ref[...])
+    return so_far() + dot_t(down_ref[...], hidden)
 
 
 def feed_first_body(own_ref, pair_ref, up_ref, down_ref, sum_ref, rows_ref):
@@ -211,8 +209,9 @@
 
     @pl.when(pl.program_id(0) == pl.num_programs(0) - 1)
     def _():
-        keep_ref[...] = sum_ref[:count]
-        send_ref[...] = sum_ref[count:].astype(BF16)
+        total = sum_ref[...].T
+        keep_ref[...] = total[:count]
+        send_ref[...] = total[count:].astype(BF16)
 
 
 def feed_first(own, pair, weights):
@@ -224,8 +223,8 @@
         feed_first_body,
         grid=(steps,),
         in_specs=[whole(own.shape), whole(own.shape), up, down],
-        out_specs=whole((2 * count, width)),
-        out_shape=jax.ShapeDtypeStruct((2 * count, width), F32),
+        out_specs=whole((width, 2 * count)),
+        out_shape=jax.ShapeDtypeStruct((width, 2 * count), F32),
         scratch_shapes=[pltpu.VMEM((2 * count, width), BF16)],
         name="feed_first",
     )(own, pair, weights, weights)
@@ -245,7 +244,7 @@
             jax.ShapeDtypeStruct(own.shape, F32),
             jax.ShapeDtypeStruct(own.shape, BF16),
         ],
-        scratch_shapes=[pltpu.VMEM((2 * count, width), BF16), pltpu.VMEM((2 * count, width), F32)],
+        scratch_shapes=[pltpu.VMEM((2 * count, width), BF16), pltpu.VMEM((width, 2 * count), F32)],
         name="feed_second",
     )(own, pair, weights, weights, before)
 

time: 306 us -> 306 us (level)
  no operation moved by 1% of the time
where the time goes in v7:
time: 306 us; the launch traced here: 304 us
  waiting for transfers between devices  149 us (49%)
  starting transfers between devices  76.2 us (25%)
  Pallas kernels  31.3 us (10%)
  local copies, waits for them, and re-layouts  19.3 us (6%)
  between operations  16.4 us (5%)
  other arithmetic  6.99 us (2%)
  matrix products  4.55 us (1%)
    all_gather x1, waiting for transfers between devices, on_device(): feed = lax.all_gather(feed, 'dp_0', axis=0, tiled=True)  46.5 us
    all_gather x1, waiting for transfers between devices, on_device(): feed = lax.all_gather(feed, 'dp_1', axis=0, tiled=True)[:, :2 * width]  41.5 us
    all_to_all x3, starting transfers between devices, to_everyone(): lax.all_to_all(jnp.broadcast_to(x[None], (size, *x.shape)), axis, 0, 0, t...  23.1 us
    ppermute x5, starting transfers between devices, swap(): return lax.ppermute(x, axis, [(i, i ^ bit) for i in range(size)])  21.3 us
    ppermute x4, waiting for transfers between devices, shift(): return lax.ppermute(x, axis, [(i, (i + step) % size) for i in range(size)])  15.6 us
    ppermute x5, waiting for transfers between devices, swap(): return lax.ppermute(x, axis, [(i, i ^ bit) for i in range(size)])  13.5 us
    all_to_all x3, waiting for transfers between devices, to_everyone(): lax.all_to_all(jnp.broadcast_to(x[None], (size, *x.shape)), axis, 0, 0, t...  13.5 us
    all_to_all x1, starting transfers between devices, on_device(): lax.all_to_all(mod_part, DP, split_axis=0, concat_axis=1, tiled=True)  13.2 us
  transfers between devices with their start and end apart: 18, of which 12 were waited for; matrix products, arithmetic and copies ran while one was open for 8% of the time, Pallas kernels for 7%

profile of v7, /device:TPU:6, one launch (start us, length us, event | category | flops | bytes accessed | tf_op | source)
XLA Modules:
  0.0 304.3 jit_solution(9950387927929704424)
XLA Ops:
  8.6 10.9 %collective-permute-start = (bf16[18,3024]{1,0:T(8,128)(2,1)S(1)}, bf16[18,3024]{1,0:T(8,128)(2,1)S(1)}, u32[]{:S(2)}, u32[]{:S(2)}) collective-permute-start(bf16[18,3024]{1,0:T(8,128)(2,1)S(1)} %concatenate.25), channel_id=1, source_target_pairs={{0,4},{4,0},{1,5},{5,1},{2,6},{6,2},{3,7},{7,3},{8,12},{12,8},{9,1... | collective-permute-start | bytes 326600 | tf_op jit(solution)/shard_map/ppermute | solution.py:29
  19.5 3.9 %collective-permute-done = bf16[18,3024]{1,0:T(8,128)(2,1)S(1)} collective-permute-done((bf16[18,3024]{1,0:T(8,128)(2,1)S(1)}, bf16[18,3024]{1,0:T(8,128)(2,1)S(1)}, u32[]{:S(2)}, u32[]{:S(2)}) %collective-permute-start) | collective-permute-done | bytes 108896 | tf_op jit(solution)/shard_map/ppermute | solution.py:29
  25.0 41.5 %all-gather.6.cloned.1.call-done = bf16[4,36,3712]{2,1,0:T(8,128)(2,1)} async-done(((bf16[1,36,3712]{2,1,0:T(8,128)(2,1)}), bf16[4,36,3712]{2,1,0:T(8,128)(2,1)}) %all-gather.6.cloned.1.call-update) | async-done | bytes 1069072 | tf_op jit(solution)/shard_map/all_gather | solution.py:350
  73.3 16.0 %all-to-all-start = ((bf16[64,2,288]{2,1,0:T(2,128)(2,1)}), bf16[64,2,288]{2,1,0:T(2,128)(2,1)S(1)}, u32[]{:S(2)}, u32[]{:S(2)}) async-start(bf16[64,2,288]{2,1,0:T(2,128)(2,1)} %broadcast_in_dim.56), calls=%async_computation | async-start | bytes 196608 | tf_op jit(solution)/shard_map/all_to_all | solution.py:19
  91.3 2.6 collective-permute-start.2
  94.6 8.4 %all-to-all-done = bf16[64,2,288]{2,1,0:T(2,128)(2,1)S(1)} async-done(((bf16[64,2,288]{2,1,0:T(2,128)(2,1)}), bf16[64,2,288]{2,1,0:T(2,128)(2,1)S(1)}, u32[]{:S(2)}, u32[]{:S(2)}) %all-to-all-start) | async-done | bytes 73760 | tf_op jit(solution)/shard_map/all_to_all | solution.py:19
  104.2 3.5 %all-to-all-start.1 = ((bf16[8,36,1024]{2,1,0:T(8,128)(2,1)}), bf16[8,36,1024]{2,1,0:T(8,128)(2,1)S(1)}, u32[]{:S(2)}, u32[]{:S(2)}) async-start(bf16[8,36,1024]{2,1,0:T(8,128)(2,1)} %broadcast_in_dim.57), calls=%async_computation.1 | async-start | bytes 1310720 | tf_op jit(solution)/shard_map/all_to_all | solution.py:19
  107.7 46.5 %all-gather.4.cloned.1.call-done.up_ref.down_ref = bf16[1152,2304]{1,0:T(8,128)(2,1)} async-done(((bf16[144,2304]{1,0:T(8,128)(2,1)}), bf16[1152,2304]{1,0:T(8,128)(2,1)}) %all-gather.4.cloned.1.call-update) | async-done | bytes 5308432 | tf_op jit(solution)/shard_map/all_gather | solution.py:351
  156.1 2.8 fusion.2.change_ref
  159.9 2.4 collective-permute-start.3
  162.4 3.4 %collective-permute-start.4 = (bf16[288,1024]{1,0:T(8,128)(2,1)}, bf16[288,1024]{1,0:T(8,128)(2,1)S(1)}, u32[]{:S(2)}, u32[]{:S(2)}) collective-permute-start(bf16[288,1024]{1,0:T(8,128)(2,1)} %reshape.272), channel_id=1, source_target_pairs={{0,24},{8,0},{16,8},{24,16},{1,25},{9,1},{17,9},{25,17},{2,26},{10... | collective-permute-start | bytes 1769480 | tf_op jit(solution)/shard_map/ppermute | solution.py:24
  165.9 2.9 fusion.5
  168.8 8.9 %collective-permute-done.3 = bf16[288,1024]{1,0:T(8,128)(2,1)S(1)} collective-permute-done((bf16[288,1024]{1,0:T(8,128)(2,1)}, bf16[288,1024]{1,0:T(8,128)(2,1)S(1)}, u32[]{:S(2)}, u32[]{:S(2)}) %collective-permute-start.3) | collective-permute-done | bytes 589856 | tf_op jit(solution)/shard_map/ppermute | solution.py:24
  177.8 3.7 %collective-permute-start.5 = (bf16[144,1024]{1,0:T(8,128)(2,1)S(1)}, bf16[144,1024]{1,0:T(8,128)(2,1)S(1)}, u32[]{:S(2)}, u32[]{:S(2)}) collective-permute-start(bf16[144,1024]{1,0:T(8,128)(2,1)S(1)} %slice.114), channel_id=1, source_target_pairs={{0,8},{8,16},{16,24},{24,0},{1,9},{9,17},{17,25},{25,1},{2,10},{10... | collective-permute-start | bytes 884744 | tf_op jit(solution)/shard_map/ppermute | solution.py:24
  182.4 2.3 collective-permute-start.6
  189.0 4.9 %collective-permute-done.6 = bf16[144,1024]{1,0:T(8,128)(2,1)S(1)} collective-permute-done((bf16[144,1024]{1,0:T(8,128)(2,1)S(1)}, bf16[144,1024]{1,0:T(8,128)(2,1)S(1)}, u32[]{:S(2)}, u32[]{:S(2)}) %collective-permute-start.6) | collective-permute-done | bytes 294944 | tf_op jit(solution)/shard_map/ppermute | solution.py:24
  194.6 2.0 collective-permute-start.7
  197.6 13.2 %all-to-all-start.2 = ((bf16[64,2,108]{2,1,0:T(2,128)(2,1)}), bf16[64,2,108]{2,1,0:T(2,128)(2,1)S(1)}, u32[]{:S(2)}, u32[]{:S(2)}) async-start(bf16[64,2,108]{2,1,0:T(2,128)(2,1)} %bitcast.12), calls=%async_computation.2 | async-start | bytes 65536 | tf_op jit(solution)/shard_map/all_to_all | solution.py:355
  211.2 12.3 %all-to-all-done.2 = bf16[64,2,108]{2,1,0:T(2,128)(2,1)S(1)} async-done(((bf16[64,2,108]{2,1,0:T(2,128)(2,1)}), bf16[64,2,108]{2,1,0:T(2,128)(2,1)S(1)}, u32[]{:S(2)}, u32[]{:S(2)}) %all-to-all-start.2) | async-done | bytes 27680 | tf_op jit(solution)/shard_map/all_to_all | solution.py:355
  224.4 3.5 %all-to-all-start.3 = ((bf16[4,2,9216]{2,1,0:T(2,128)(2,1)}), bf16[4,2,9216]{2,1,0:T(2,128)(2,1)S(1)}, u32[]{:S(2)}, u32[]{:S(2)}) async-start(bf16[4,2,9216]{2,1,0:T(2,128)(2,1)} %broadcast_in_dim.58), calls=%async_computation.3 | async-start | bytes 294912 | tf_op jit(solution)/shard_map/all_to_all | solution.py:19
  228.7 5.1 %all-to-all-done.3 = bf16[4,2,9216]{2,1,0:T(2,128)(2,1)S(1)} async-done(((bf16[4,2,9216]{2,1,0:T(2,128)(2,1)}), bf16[4,2,9216]{2,1,0:T(2,128)(2,1)S(1)}, u32[]{:S(2)}, u32[]{:S(2)}) %all-to-all-start.3) | async-done | bytes 147488 | tf_op jit(solution)/shard_map/all_to_all | solution.py:19
  235.7 9.8 %attention.1 = bf16[4,288,128]{2,1,0:T(8,128)(2,1)} custom-call(s32[1]{0:T(128)} %bitcast.1.core_ref, bf16[2,256,1152]{2,1,0:T(8,128)(2,1)} %bitcast.55, f32[2,1,1152]{2,1,0:T(1,128)} %get-tuple-element.56.shift_ref, f32[2,1,1152]{2,1,0:T(1,128)} %get-tuple-element.55.scale_ref, bf16[1152,1024]{1,0:T(8,128)(2,1)} %constant_dynamic-update-slice_fusion.mine_ref, ...), custom_call_target="tpu_custom_call" | custom-call | tf_op jit(solution)/shard_map/attention/pallas_call | solution.py:115
  245.6 3.5 %all-to-all-start.4 = ((bf16[4,288,128]{2,1,0:T(8,128)(2,1)}), bf16[4,288,128]{2,1,0:T(8,128)(2,1)S(1)}, u32[]{:S(2)}, u32[]{:S(2)}) async-start(bf16[4,288,128]{2,1,0:T(8,128)(2,1)} %attention.1), calls=%async_computation.4 | async-start | bytes 589824 | tf_op jit(solution)/shard_map/all_to_all | solution.py:390
  249.7 6.6 %all-to-all-done.4.mixed_ref = bf16[4,288,128]{2,1,0:T(8,128)(2,1)S(1)} async-done(((bf16[4,288,128]{2,1,0:T(8,128)(2,1)}), bf16[4,288,128]{2,1,0:T(8,128)(2,1)S(1)}, u32[]{:S(2)}, u32[]{:S(2)}) %all-to-all-start.4) | async-done | bytes 294944 | tf_op jit(solution)/shard_map/all_to_all | solution.py:390
  257.0 5.7 %project.1 = (f32[2,64,1152]{2,1,0:T(8,128)}, bf16[2,64,1152]{2,1,0:T(8,128)(2,1)}) custom-call(s32[1]{0:T(128)} %bitcast.base_ref, bf16[4,288,128]{2,1,0:T(8,128)(2,1)} %copy-done.3, bf16[1152,1024]{1,0:T(8,128)(2,1)} %constant_dynamic-update-slice_fusion.mine_ref, bf16[1152,1024]{1,0:T(8,128)(2,1)} %collective-permute-done.7.other_ref, ...), custom_call_target="tpu_custom_call" | custom-call | tf_op jit(solution)/shard_map/project/pallas_call | solution.py:155
  262.7 3.2 %collective-permute-start.8 = (bf16[128,1152]{1,0:T(8,128)(2,1)}, bf16[128,1152]{1,0:T(8,128)(2,1)S(1)}, u32[]{:S(2)}, u32[]{:S(2)}) collective-permute-start(bf16[128,1152]{1,0:T(8,128)(2,1)} %bitcast.51), channel_id=1, source_target_pairs={{0,1},{1,0},{2,3},{3,2},{4,5},{5,4},{6,7},{7,6},{8,9},{9,8},{10,11... | collective-permute-start | bytes 884744 | tf_op jit(solution)/shard_map/ppermute | solution.py:29
  265.9 5.6 %collective-permute-done.8.pair_ref = bf16[128,1152]{1,0:T(8,128)(2,1)S(1)} collective-permute-done((bf16[128,1152]{1,0:T(8,128)(2,1)}, bf16[128,1152]{1,0:T(8,128)(2,1)S(1)}, u32[]{:S(2)}, u32[]{:S(2)}) %collective-permute-start.8) | collective-permute-done | bytes 294944 | tf_op jit(solution)/shard_map/ppermute | solution.py:29
  272.2 6.2 %feed_first.1.before_ref = f32[1152,256]{1,0:T(8,128)} custom-call(bf16[128,1152]{1,0:T(8,128)(2,1)} %bitcast.52, bf16[128,1152]{1,0:T(8,128)(2,1)} %copy-done.2, bf16[1152,2304]{1,0:T(8,128)(2,1)} %all-gather.4.cloned.1.call-done.up_ref.down_ref, bf16[1152,2304]{1,0:T(8,128)(2,1)} %all-gather.4.cloned.1.call-done.up_ref.down_ref), custom_call_target="tpu_custom_call" | custom-call | tf_op jit(solution)/shard_map/feed_first/pallas_call | solution.py:222
  278.4 6.8 %feed_second.1 = (f32[128,1152]{1,0:T(8,128)}, bf16[128,1152]{1,0:T(8,128)(2,1)}) custom-call(bf16[128,1152]{1,0:T(8,128)(2,1)} %bitcast.53, bf16[128,1152]{1,0:T(8,128)(2,1)} %copy-done.2, bf16[1152,2304]{1,0:T(8,128)(2,1)} %collective-permute-done.9.up_ref.down_ref, bf16[1152,2304]{1,0:T(8,128)(2,1)} %collective-permute-done.9.up_ref.down_ref, ...), custom_call_target="tpu_custom_call" | custom-call | tf_op jit(solution)/shard_map/feed_second/pallas_call | solution.py:238
  285.3 3.2 %collective-permute-start.10 = (bf16[128,1152]{1,0:T(8,128)(2,1)}, bf16[128,1152]{1,0:T(8,128)(2,1)S(1)}, u32[]{:S(2)}, u32[]{:S(2)}) collective-permute-start(bf16[128,1152]{1,0:T(8,128)(2,1)} %get-tuple-element.19), channel_id=1, source_target_pairs={{0,1},{1,0},{2,3},{3,2},{4,5},{5,4},{6,7},{7,6},{8,9},{9,8},{10,11... | collective-permute-start | bytes 884744 | tf_op jit(solution)/shard_map/ppermute | solution.py:29
  290.1 4.0 %collective-permute-done.10.recv_ref = bf16[128,1152]{1,0:T(8,128)(2,1)S(1)} collective-permute-done((bf16[128,1152]{1,0:T(8,128)(2,1)}, bf16[128,1152]{1,0:T(8,128)(2,1)S(1)}, u32[]{:S(2)}, u32[]{:S(2)}) %collective-permute-start.10) | collective-permute-done | bytes 294944 | tf_op jit(solution)/shard_map/ppermute | solution.py:29
  294.8 2.7 finish.1
  (85 shorter events, 29.5 us)
Async XLA Ops:
  6.5 204.3 %copy-start = (bf16[288,2304]{1,0:T(8,128)(2,1)S(1)}, bf16[288,2304]{1,0:T(8,128)(2,1)}, u32[]{:S(2)}) copy-start(bf16[288,2304]{1,0:T(8,128)(2,1)} %param.22) | copy-start | bytes 3981316
  6.5 60.0 %all-gather.6.cloned.1.call-start = ((), (), s32[]{:S(2)}) async-start(), calls=%async_computation.6 | async-start | bytes 1484800 | tf_op jit(solution)/shard_map/all_gather | solution.py:350
  8.6 14.9 %collective-permute-start = (bf16[18,3024]{1,0:T(8,128)(2,1)S(1)}, bf16[18,3024]{1,0:T(8,128)(2,1)S(1)}, u32[]{:S(2)}, u32[]{:S(2)}) collective-permute-start(bf16[18,3024]{1,0:T(8,128)(2,1)S(1)} %concatenate.25), channel_id=1, source_target_pairs={{0,4},{4,0},{1,5},{5,1},{2,6},{6,2},{3,7},{7,3},{8,12},{12,8},{9,1... | collective-permute-start | bytes 326600 | tf_op jit(solution)/shard_map/ppermute | solution.py:29
  23.5 0.7 collective-permute-start.1
  25.0 129.2 %all-gather.4.cloned.1.call-start = ((), (), s32[]{:S(2)}) async-start(), calls=%async_computation.5 | async-start | bytes 5971968 | tf_op jit(solution)/shard_map/all_gather | solution.py:351
  72.6 17.4 %copy-start.9 = (bf16[2,288]{1,0:T(2,128)(2,1)}, bf16[2,288]{1,0:T(2,128)(2,1)S(1)}, u32[]{:S(2)}) copy-start(bf16[2,288]{1,0:T(2,128)(2,1)S(1)} %fusion.36) | copy-start | bytes 3460
  73.3 29.8 %all-to-all-start = ((bf16[64,2,288]{2,1,0:T(2,128)(2,1)}), bf16[64,2,288]{2,1,0:T(2,128)(2,1)S(1)}, u32[]{:S(2)}, u32[]{:S(2)}) async-start(bf16[64,2,288]{2,1,0:T(2,128)(2,1)} %broadcast_in_dim.56), calls=%async_computation | async-start | bytes 196608 | tf_op jit(solution)/shard_map/all_to_all | solution.py:19
  91.3 11.8 %collective-permute-start.2 = (bf16[36,288]{1,0:T(8,128)(2,1)S(1)}, bf16[36,288]{1,0:T(8,128)(2,1)S(1)}, u32[]{:S(2)}, u32[]{:S(2)}) collective-permute-start(bf16[36,288]{1,0:T(8,128)(2,1)S(1)} %pad_maximum_fusion.2), channel_id=1, source_target_pairs={{0,1},{1,0},{2,3},{3,2},{256,259},{257,258},{258,257},{259,256},{4... | collective-permute-start | bytes 62216 | tf_op jit(solution)/shard_map/ppermute | solution.py:337
  104.2 54.8 %all-to-all-start.1 = ((bf16[8,36,1024]{2,1,0:T(8,128)(2,1)}), bf16[8,36,1024]{2,1,0:T(8,128)(2,1)S(1)}, u32[]{:S(2)}, u32[]{:S(2)}) async-start(bf16[8,36,1024]{2,1,0:T(8,128)(2,1)} %broadcast_in_dim.57), calls=%async_computation.1 | async-start | bytes 1310720 | tf_op jit(solution)/shard_map/all_to_all | solution.py:19
  154.2 124.2 %collective-permute-start.9 = (bf16[1152,2304]{1,0:T(8,128)(2,1)}, bf16[1152,2304]{1,0:T(8,128)(2,1)}, u32[]{:S(2)}, u32[]{:S(2)}) collective-permute-start(bf16[1152,2304]{1,0:T(8,128)(2,1)} %all-gather.4.cloned.1.call-done.up_ref.down_ref), channel_id=1, source_target_pairs={{0,256},{256,0},{1,257},{257,1},{2,258},{258,2},{3,259},{259,3},{4... | collective-permute-start | bytes 15925256 | tf_op jit(solution)/shard_map/ppermute | solution.py:29
  159.0 6.9 %copy-start.7 = (s32[1152]{0:T(1024)S(1)}, s32[1152]{0:T(1024)}, u32[]{:S(2)}) copy-start(s32[1152]{0:T(1024)} %fusion.24) | copy-start | bytes 13828
  159.9 17.8 %collective-permute-start.3 = (bf16[288,1024]{1,0:T(8,128)(2,1)}, bf16[288,1024]{1,0:T(8,128)(2,1)S(1)}, u32[]{:S(2)}, u32[]{:S(2)}) collective-permute-start(bf16[288,1024]{1,0:T(8,128)(2,1)} %reshape.272), channel_id=1, source_target_pairs={{0,8},{8,16},{16,24},{24,0},{1,9},{9,17},{17,25},{25,1},{2,10},{10... | collective-permute-start | bytes 1769480 | tf_op jit(solution)/shard_map/ppermute | solution.py:24
  162.4 20.0 %collective-permute-start.4 = (bf16[288,1024]{1,0:T(8,128)(2,1)}, bf16[288,1024]{1,0:T(8,128)(2,1)S(1)}, u32[]{:S(2)}, u32[]{:S(2)}) collective-permute-start(bf16[288,1024]{1,0:T(8,128)(2,1)} %reshape.272), channel_id=1, source_target_pairs={{0,24},{8,0},{16,8},{24,16},{1,25},{9,1},{17,9},{25,17},{2,26},{10... | collective-permute-start | bytes 1769480 | tf_op jit(solution)/shard_map/ppermute | solution.py:24
  165.9 15.5 %copy-start.1 = (bf16[288,1024]{1,0:T(8,128)(2,1)S(1)}, bf16[288,1024]{1,0:T(8,128)(2,1)}, u32[]{:S(2)}) copy-start(bf16[288,1024]{1,0:T(8,128)(2,1)} %reshape.272) | copy-start | bytes 1769476
  177.8 10.4 %collective-permute-start.5 = (bf16[144,1024]{1,0:T(8,128)(2,1)S(1)}, bf16[144,1024]{1,0:T(8,128)(2,1)S(1)}, u32[]{:S(2)}, u32[]{:S(2)}) collective-permute-start(bf16[144,1024]{1,0:T(8,128)(2,1)S(1)} %slice.114), channel_id=1, source_target_pairs={{0,8},{8,16},{16,24},{24,0},{1,9},{9,17},{17,25},{25,1},{2,10},{10... | collective-permute-start | bytes 884744 | tf_op jit(solution)/shard_map/ppermute | solution.py:24
  182.3 14.3 %copy-start.5 = (bf16[288,108]{1,0:T(8,128)(2,1)S(1)}, bf16[288,108]{1,0:T(8,128)(2,1)}, u32[]{:S(2)}) copy-start(bf16[288,108]{1,0:T(8,128)(2,1)} %param.21) | copy-start | bytes 186628
  182.3 28.5 %copy-start.10 = (bf16[2,288]{1,0:T(2,128)(2,1)S(1)}, bf16[2,288]{1,0:T(2,128)(2,1)}, u32[]{:S(2)}) copy-start(bf16[2,288]{1,0:T(2,128)(2,1)} %copy-done.9) | copy-start | bytes 3460
  182.4 11.5 %collective-permute-start.6 = (bf16[144,1024]{1,0:T(8,128)(2,1)S(1)}, bf16[144,1024]{1,0:T(8,128)(2,1)S(1)}, u32[]{:S(2)}, u32[]{:S(2)}) collective-permute-start(bf16[144,1024]{1,0:T(8,128)(2,1)S(1)} %slice.115), channel_id=1, source_target_pairs={{0,24},{8,0},{16,8},{24,16},{1,25},{9,1},{17,9},{25,17},{2,26},{10... | collective-permute-start | bytes 884744 | tf_op jit(solution)/shard_map/ppermute | solution.py:24
  194.6 39.4 %copy-start.8 = (s32[1152]{0:T(1024)S(1)}, s32[1152]{0:T(1024)}, u32[]{:S(2)}) copy-start(s32[1152]{0:T(1024)} %fusion.24) | copy-start | bytes 13828
  194.6 41.1 %collective-permute-start.7 = (bf16[1152,1024]{1,0:T(8,128)(2,1)}, bf16[1152,1024]{1,0:T(8,128)(2,1)}, u32[]{:S(2)}, u32[]{:S(2)}) collective-permute-start(bf16[1152,1024]{1,0:T(8,128)(2,1)} %constant_dynamic-update-slice_fusion.mine_ref), channel_id=1, source_target_pairs={{0,256},{256,0},{1,257},{257,1},{2,258},{258,2},{3,259},{259,3},{4... | collective-permute-start | bytes 7077896 | tf_op jit(solution)/shard_map/ppermute | solution.py:29
  197.6 25.9 %all-to-all-start.2 = ((bf16[64,2,108]{2,1,0:T(2,128)(2,1)}), bf16[64,2,108]{2,1,0:T(2,128)(2,1)S(1)}, u32[]{:S(2)}, u32[]{:S(2)}) async-start(bf16[64,2,108]{2,1,0:T(2,128)(2,1)} %bitcast.12), calls=%async_computation.2 | async-start | bytes 65536 | tf_op jit(solution)/shard_map/all_to_all | solution.py:355
  224.4 9.3 %all-to-all-start.3 = ((bf16[4,2,9216]{2,1,0:T(2,128)(2,1)}), bf16[4,2,9216]{2,1,0:T(2,128)(2,1)S(1)}, u32[]{:S(2)}, u32[]{:S(2)}) async-start(bf16[4,2,9216]{2,1,0:T(2,128)(2,1)} %broadcast_in_dim.58), calls=%async_computation.3 | async-start | bytes 294912 | tf_op jit(solution)/shard_map/all_to_all | solution.py:19
  245.6 10.7 %all-to-all-start.4 = ((bf16[4,288,128]{2,1,0:T(8,128)(2,1)}), bf16[4,288,128]{2,1,0:T(8,128)(2,1)S(1)}, u32[]{:S(2)}, u32[]{:S(2)}) async-start(bf16[4,288,128]{2,1,0:T(8,128)(2,1)} %attention.1), calls=%async_computation.4 | async-start | bytes 589824 | tf_op jit(solution)/shard_map/all_to_all | solution.py:390
  256.2 0.7 copy-start.3
  262.7 8.8 %collective-permute-start.8 = (bf16[128,1152]{1,0:T(8,128)(2,1)}, bf16[128,1152]{1,0:T(8,128)(2,1)S(1)}, u32[]{:S(2)}, u32[]{:S(2)}) collective-permute-start(bf16[128,1152]{1,0:T(8,128)(2,1)} %bitcast.51), channel_id=1, source_target_pairs={{0,1},{1,0},{2,3},{3,2},{4,5},{5,4},{6,7},{7,6},{8,9},{9,8},{10,11... | collective-permute-start | bytes 884744 | tf_op jit(solution)/shard_map/ppermute | solution.py:29
  271.5 0.7 copy-start.2
  278.4 10.7 %copy-start.6 = (bf16[1152,16]{0,1:T(8,128)(2,1)S(1)}, bf16[1152,16]{0,1:T(8,128)(2,1)}, u32[]{:S(2)}) copy-start(bf16[1152,16]{0,1:T(8,128)(2,1)} %param.27) | copy-start | bytes 110596
  285.3 8.8 %collective-permute-start.10 = (bf16[128,1152]{1,0:T(8,128)(2,1)}, bf16[128,1152]{1,0:T(8,128)(2,1)S(1)}, u32[]{:S(2)}, u32[]{:S(2)}) collective-permute-start(bf16[128,1152]{1,0:T(8,128)(2,1)} %get-tuple-element.19), channel_id=1, source_target_pairs={{0,1},{1,0},{2,3},{3,2},{4,5},{5,4},{6,7},{7,6},{8,9},{9,8},{10,11... | collective-permute-start | bytes 884744 | tf_op jit(solution)/shard_map/ppermute | solution.py:29
  294.1 0.7 copy-start.4
Sparse Core Ops, SparseCore 0:
  25.1 41.4 all-gather.5
  69.0 85.2 all-gather.3

commit v8 on v7

--- a/solution.py
+++ b/solution.py
@@ -112,16 +112,18 @@
     images, tokens, width = x.shape
     vector = whole((images, 1, width))
     out_shape = (n_mp, quarter, images * tokens // n_mp)
+    lanes = whole((width, -(-3 * quarter // 2 // 128) * 128))
     return pl.pallas_call(
         attention_body,
         grid_spec=pltpu.PrefetchScalarGridSpec(
             num_scalar_prefetch=1,
             grid=(1,),
-            in_specs=[whole(x.shape), vector, vector, whole(mine.shape), whole(other.shape)],
+            in_specs=[whole(x.shape), vector, vector, lanes, lanes],
             out_specs=whole(out_shape),
         ),
         out_shape=jax.ShapeDtypeStruct(out_shape, BF16),
         name="attention",
+        compiler_params=pltpu.CompilerParams(vmem_limit_bytes=20 << 20),
     )(core, x, shift_a, scale_a, mine, other)
 
 
@@ -135,8 +137,8 @@
     for i in range(4):
         at = lead + i % 2 * quarter
         rows_ref[i // 2, at : at + quarter] = mixed_ref[base ^ i]
-    attn = dot(mine_ref[:, start - lead :], rows_ref[0])
-    attn = (attn + dot(other_ref[:, start - lead :], rows_ref[1])).astype(BF16)
+    attn = dot(mine_ref[...], rows_ref[0])
+    attn = (attn + dot(other_ref[...], rows_ref[1])).astype(BF16)
     attn = lax.dot_general(
         attn, change_ref[...], (((0,), (0,)), ((), ())), preferred_element_type=F32
     )
@@ -152,6 +154,9 @@
     vector = whole((2, 1, width))
     start = 3 * mixed.shape[1] // 2
     depth = mine.shape[1] - start // 128 * 128
+    lanes = pl.BlockSpec(
+        (pl.Element(width), pl.Element(depth)), lambda *_: (0, start // 128 * 128)
+    )
     return pl.pallas_call(
         project_body,
         grid_spec=pltpu.PrefetchScalarGridSpec(
@@ -159,8 +164,8 @@
             grid=(1,),
             in_specs=[
                 whole(mixed.shape),
-                whole(mine.shape),
-                whole(other.shape),
+                lanes,
+                lanes,
                 whole(change.shape),
                 whole(own.shape),
                 vector,
@@ -175,6 +180,7 @@
             jax.ShapeDtypeStruct(own.shape, BF16),
         ],
         name="project",
+        compiler_params=pltpu.CompilerParams(vmem_limit_bytes=20 << 20),
     )(base, mixed, mine, other, change, own, gate_a, shift_m, scale_m)
 
 
@@ -227,6 +233,7 @@
         out_shape=jax.ShapeDtypeStruct((width, 2 * count), F32),
         scratch_shapes=[pltpu.VMEM((2 * count, width), BF16)],
         name="feed_first",
+        compiler_params=pltpu.CompilerParams(vmem_limit_bytes=20 << 20),
     )(own, pair, weights, weights)
 
 
@@ -246,6 +253,7 @@
         ],
         scratch_shapes=[pltpu.VMEM((2 * count, width), BF16), pltpu.VMEM((width, 2 * count), F32)],
         name="feed_second",
+        compiler_params=pltpu.CompilerParams(vmem_limit_bytes=20 << 20),
     )(own, pair, weights, weights, before)
 
 
@@ -288,6 +296,7 @@
         ),
         out_shape=jax.ShapeDtypeStruct((1, share * out_local.shape[1]), F32),
         name="finish",
+        compiler_params=pltpu.CompilerParams(vmem_limit_bytes=20 << 20),
     )(guidance, keep, recv, first_sum, gate_m, shift_f, scale_f, out_local)
 
 
@@ -347,7 +356,8 @@
 
     wide = max(2 * width, -(-GATHER_FLOOR // (2 * n_x * feed.shape[0] * 128)) * 128)
     feed = jnp.pad(feed[:, : 2 * width], ((0, 0), (0, wide - 2 * width)))
-    feed = lax.all_gather(feed, "dp_1", axis=0, tiled=True)[:, : 2 * width]
+    feed = lax.all_gather(feed, "dp_1", axis=0)
+    feed = feed[:, :, : 2 * width].reshape(-1, 2 * width)
     feed = lax.all_gather(feed, "dp_0", axis=0, tiled=True)
     other_feed = swap(feed, "group", 1)
 

time: 306 us -> 297 us (0.971)
  Pallas kernels: 31.3 us -> 22.8 us
    unnamed x32 -> x29, local copies, waits for them, and re-layouts: 8.87 us -> 7.63 us
  transfers between devices with their start and end apart: 18 -> 18, of which waited for: 12 -> 12; matrix products, arithmetic and copies ran while one was open for 8% -> 7% of each run, Pallas kernels for 7% -> 6%
where the time goes in v8:
time: 297 us; the launch traced here: 295 us
  waiting for transfers between devices  152 us (51%)
  starting transfers between devices  76 us (26%)
  Pallas kernels  22.8 us (8%)
  local copies, waits for them, and re-layouts  18.1 us (6%)
  between operations  16.5 us (6%)
  other arithmetic  4.94 us (2%)
  matrix products  4.56 us (2%)
    all_gather x1, waiting for transfers between devices, on_device(): feed = lax.all_gather(feed, 'dp_0', axis=0, tiled=True)  46.5 us
    all_gather x1, waiting for transfers between devices, on_device(): feed = lax.all_gather(feed, 'dp_1', axis=0)  41.5 us
    all_to_all x3, starting transfers between devices, to_everyone(): lax.all_to_all(jnp.broadcast_to(x[None], (size, *x.shape)), axis, 0, 0, t...  23 us
    ppermute x5, starting transfers between devices, swap(): return lax.ppermute(x, axis, [(i, i ^ bit) for i in range(size)])  21.2 us
    ppermute x4, waiting for transfers between devices, shift(): return lax.ppermute(x, axis, [(i, (i + step) % size) for i in range(size)])  15.6 us
    all_to_all x3, waiting for transfers between devices, to_everyone(): lax.all_to_all(jnp.broadcast_to(x[None], (size, *x.shape)), axis, 0, 0, t...  14.8 us
    ppermute x5, waiting for transfers between devices, swap(): return lax.ppermute(x, axis, [(i, i ^ bit) for i in range(size)])  13.8 us
    all_to_all x1, starting transfers between devices, on_device(): lax.all_to_all(mod_part, DP, split_axis=0, concat_axis=1, tiled=True)  13.2 us
  transfers between devices with their start and end apart: 18, of which 12 were waited for; matrix products, arithmetic and copies ran while one was open for 7% of the time, Pallas kernels for 6%

profile of v8, /device:TPU:6, one launch (start us, length us, event | category | flops | bytes accessed | tf_op | source)
XLA Modules:
  0.0 294.7 jit_solution(15465054748921874725)
XLA Ops:
  8.6 10.9 %collective-permute-start = (bf16[18,3024]{1,0:T(8,128)(2,1)S(1)}, bf16[18,3024]{1,0:T(8,128)(2,1)S(1)}, u32[]{:S(2)}, u32[]{:S(2)}) collective-permute-start(bf16[18,3024]{1,0:T(8,128)(2,1)S(1)} %concatenate.25), channel_id=1, source_target_pairs={{0,4},{4,0},{1,5},{5,1},{2,6},{6,2},{3,7},{7,3},{8,12},{12,8},{9,1... | collective-permute-start | bytes 326600 | tf_op jit(solution)/shard_map/ppermute | solution.py:29
  19.5 3.9 %collective-permute-done = bf16[18,3024]{1,0:T(8,128)(2,1)S(1)} collective-permute-done((bf16[18,3024]{1,0:T(8,128)(2,1)S(1)}, bf16[18,3024]{1,0:T(8,128)(2,1)S(1)}, u32[]{:S(2)}, u32[]{:S(2)}) %collective-permute-start) | collective-permute-done | bytes 108896 | tf_op jit(solution)/shard_map/ppermute | solution.py:29
  25.0 41.5 %all-gather.7.cloned.1.call-done = bf16[4,36,3712]{2,1,0:T(8,128)(2,1)} async-done(((bf16[1,36,3712]{2,1,0:T(8,128)(2,1)}), bf16[4,36,3712]{2,1,0:T(8,128)(2,1)}) %all-gather.7.cloned.1.call-update) | async-done | bytes 1069072 | tf_op jit(solution)/shard_map/all_gather | solution.py:359
  73.1 16.0 %all-to-all-start = ((bf16[64,2,288]{2,1,0:T(2,128)(2,1)}), bf16[64,2,288]{2,1,0:T(2,128)(2,1)S(1)}, u32[]{:S(2)}, u32[]{:S(2)}) async-start(bf16[64,2,288]{2,1,0:T(2,128)(2,1)} %broadcast_in_dim.56), calls=%async_computation | async-start | bytes 196608 | tf_op jit(solution)/shard_map/all_to_all | solution.py:19
  91.2 2.7 collective-permute-start.2
  93.9 9.0 %all-to-all-done = bf16[64,2,288]{2,1,0:T(2,128)(2,1)S(1)} async-done(((bf16[64,2,288]{2,1,0:T(2,128)(2,1)}), bf16[64,2,288]{2,1,0:T(2,128)(2,1)S(1)}, u32[]{:S(2)}, u32[]{:S(2)}) %all-to-all-start) | async-done | bytes 73760 | tf_op jit(solution)/shard_map/all_to_all | solution.py:19
  104.1 3.5 %all-to-all-start.1 = ((bf16[8,36,1024]{2,1,0:T(8,128)(2,1)}), bf16[8,36,1024]{2,1,0:T(8,128)(2,1)S(1)}, u32[]{:S(2)}, u32[]{:S(2)}) async-start(bf16[8,36,1024]{2,1,0:T(8,128)(2,1)} %broadcast_in_dim.57), calls=%async_computation.1 | async-start | bytes 1310720 | tf_op jit(solution)/shard_map/all_to_all | solution.py:19
  107.6 46.5 %all-gather.5.cloned.1.call-done.up_ref.down_ref = bf16[1152,2304]{1,0:T(8,128)(2,1)} async-done(((bf16[144,2304]{1,0:T(8,128)(2,1)}), bf16[1152,2304]{1,0:T(8,128)(2,1)}) %all-gather.5.cloned.1.call-update) | async-done | bytes 5308432 | tf_op jit(solution)/shard_map/all_gather | solution.py:361
  154.1 1.9 collective-permute-start.9
  156.0 2.1 fusion.2.change_ref
  159.1 2.4 collective-permute-start.3
  161.5 3.4 %collective-permute-start.4 = (bf16[288,1024]{1,0:T(8,128)(2,1)}, bf16[288,1024]{1,0:T(8,128)(2,1)S(1)}, u32[]{:S(2)}, u32[]{:S(2)}) collective-permute-start(bf16[288,1024]{1,0:T(8,128)(2,1)} %reshape.275), channel_id=1, source_target_pairs={{0,24},{8,0},{16,8},{24,16},{1,25},{9,1},{17,9},{25,17},{2,26},{10... | collective-permute-start | bytes 1769480 | tf_op jit(solution)/shard_map/ppermute | solution.py:24
  165.1 3.0 %fusion.5 = bf16[512,1152]{1,0:T(8,128)(2,1)} fusion(bf16[512,1152]{1,0:T(8,128)(2,1)S(1)} %bitcast.57, s32[1152]{0:T(1024)S(1)} %fusion.24), kind=kOutput, calls=%fused_computation.7 | convolution fusion | flops 1360871424 | bytes 2363904 | tf_op jit(solution)/shard_map/dot_general | solution.py:63
  168.0 8.9 %collective-permute-done.3 = bf16[288,1024]{1,0:T(8,128)(2,1)S(1)} collective-permute-done((bf16[288,1024]{1,0:T(8,128)(2,1)}, bf16[288,1024]{1,0:T(8,128)(2,1)S(1)}, u32[]{:S(2)}, u32[]{:S(2)}) %collective-permute-start.3) | collective-permute-done | bytes 589856 | tf_op jit(solution)/shard_map/ppermute | solution.py:24
  176.9 3.7 %collective-permute-start.5 = (bf16[144,1024]{1,0:T(8,128)(2,1)S(1)}, bf16[144,1024]{1,0:T(8,128)(2,1)S(1)}, u32[]{:S(2)}, u32[]{:S(2)}) collective-permute-start(bf16[144,1024]{1,0:T(8,128)(2,1)S(1)} %slice.114), channel_id=1, source_target_pairs={{0,8},{8,16},{16,24},{24,0},{1,9},{9,17},{17,25},{25,1},{2,10},{10... | collective-permute-start | bytes 884744 | tf_op jit(solution)/shard_map/ppermute | solution.py:24
  181.5 2.2 collective-permute-start.6
  185.4 2.0 collective-permute-done.5
  188.1 4.8 %collective-permute-done.6 = bf16[144,1024]{1,0:T(8,128)(2,1)S(1)} collective-permute-done((bf16[144,1024]{1,0:T(8,128)(2,1)S(1)}, bf16[144,1024]{1,0:T(8,128)(2,1)S(1)}, u32[]{:S(2)}, u32[]{:S(2)}) %collective-permute-start.6) | collective-permute-done | bytes 294944 | tf_op jit(solution)/shard_map/ppermute | solution.py:24
  196.5 13.2 %all-to-all-start.2 = ((bf16[64,2,108]{2,1,0:T(2,128)(2,1)}), bf16[64,2,108]{2,1,0:T(2,128)(2,1)S(1)}, u32[]{:S(2)}, u32[]{:S(2)}) async-start(bf16[64,2,108]{2,1,0:T(2,128)(2,1)} %bitcast.12), calls=%async_computation.2 | async-start | bytes 65536 | tf_op jit(solution)/shard_map/all_to_all | solution.py:365
  210.0 12.4 %all-to-all-done.2 = bf16[64,2,108]{2,1,0:T(2,128)(2,1)S(1)} async-done(((bf16[64,2,108]{2,1,0:T(2,128)(2,1)}), bf16[64,2,108]{2,1,0:T(2,128)(2,1)S(1)}, u32[]{:S(2)}, u32[]{:S(2)}) %all-to-all-start.2) | async-done | bytes 27680 | tf_op jit(solution)/shard_map/all_to_all | solution.py:365
  223.4 3.5 %all-to-all-start.3 = ((bf16[4,2,9216]{2,1,0:T(2,128)(2,1)}), bf16[4,2,9216]{2,1,0:T(2,128)(2,1)S(1)}, u32[]{:S(2)}, u32[]{:S(2)}) async-start(bf16[4,2,9216]{2,1,0:T(2,128)(2,1)} %broadcast_in_dim.58), calls=%async_computation.3 | async-start | bytes 294912 | tf_op jit(solution)/shard_map/all_to_all | solution.py:19
  226.9 5.7 %all-to-all-done.3 = bf16[4,2,9216]{2,1,0:T(2,128)(2,1)S(1)} async-done(((bf16[4,2,9216]{2,1,0:T(2,128)(2,1)}), bf16[4,2,9216]{2,1,0:T(2,128)(2,1)S(1)}, u32[]{:S(2)}, u32[]{:S(2)}) %all-to-all-start.3) | async-done | bytes 147488 | tf_op jit(solution)/shard_map/all_to_all | solution.py:19
  235.3 8.8 %attention.1 = bf16[4,288,128]{2,1,0:T(8,128)(2,1)} custom-call(s32[1]{0:T(128)} %bitcast.1.core_ref, bf16[2,256,1152]{2,1,0:T(8,128)(2,1)S(1)} %bitcast.56, f32[2,1,1152]{2,1,0:T(1,128)S(1)} %get-tuple-element.56.shift_ref, f32[2,1,1152]{2,1,0:T(1,128)S(1)} %get-tuple-element.55.scale_ref, bf16[1152,1024]{1,0:T(8,128)(2,1)} %constant_dynamic-update-slice_fusion.mine_ref, ...), custom_call_target="tpu_custom_call" | custom-call | tf_op jit(solution)/shard_map/attention/pallas_call | solution.py:116
  244.1 3.5 %all-to-all-start.4 = ((bf16[4,288,128]{2,1,0:T(8,128)(2,1)}), bf16[4,288,128]{2,1,0:T(8,128)(2,1)S(1)}, u32[]{:S(2)}, u32[]{:S(2)}) async-start(bf16[4,288,128]{2,1,0:T(8,128)(2,1)} %attention.1), calls=%async_computation.4 | async-start | bytes 589824 | tf_op jit(solution)/shard_map/all_to_all | solution.py:400
  247.6 7.1 %all-to-all-done.4.mixed_ref = bf16[4,288,128]{2,1,0:T(8,128)(2,1)S(1)} async-done(((bf16[4,288,128]{2,1,0:T(8,128)(2,1)}), bf16[4,288,128]{2,1,0:T(8,128)(2,1)S(1)}, u32[]{:S(2)}, u32[]{:S(2)}) %all-to-all-start.4) | async-done | bytes 294944 | tf_op jit(solution)/shard_map/all_to_all | solution.py:400
  256.5 3.7 %project.1 = (f32[2,64,1152]{2,1,0:T(8,128)S(1)}, bf16[2,64,1152]{2,1,0:T(8,128)(2,1)S(1)}) custom-call(s32[1]{0:T(128)} %bitcast.base_ref, bf16[4,288,128]{2,1,0:T(8,128)(2,1)S(1)} %all-to-all-done.4.mixed_ref, bf16[1152,1024]{1,0:T(8,128)(2,1)} %constant_dynamic-update-slice_fusion.mine_ref, bf16[1152,1024]{1,0:T(8,128)(2,1)} %collective-permute-done.7.other_ref, ...), custom_call_target="tpu_custom_call" | custom-call | tf_op jit(solution)/shard_map/project/pallas_call | solution.py:160
  260.2 3.3 %collective-permute-start.8 = (bf16[128,1152]{1,0:T(8,128)(2,1)S(1)}, bf16[128,1152]{1,0:T(8,128)(2,1)S(1)}, u32[]{:S(2)}, u32[]{:S(2)}) collective-permute-start(bf16[128,1152]{1,0:T(8,128)(2,1)S(1)} %bitcast.53), channel_id=1, source_target_pairs={{0,1},{1,0},{2,3},{3,2},{4,5},{5,4},{6,7},{7,6},{8,9},{9,8},{10,11... | collective-permute-start | bytes 884744 | tf_op jit(solution)/shard_map/ppermute | solution.py:29
  263.5 5.4 %collective-permute-done.8.pair_ref = bf16[128,1152]{1,0:T(8,128)(2,1)S(1)} collective-permute-done((bf16[128,1152]{1,0:T(8,128)(2,1)S(1)}, bf16[128,1152]{1,0:T(8,128)(2,1)S(1)}, u32[]{:S(2)}, u32[]{:S(2)}) %collective-permute-start.8) | collective-permute-done | bytes 294944 | tf_op jit(solution)/shard_map/ppermute | solution.py:29
  268.8 3.7 %feed_first.1.before_ref = f32[1152,256]{1,0:T(8,128)S(1)} custom-call(bf16[128,1152]{1,0:T(8,128)(2,1)S(1)} %bitcast.54, bf16[128,1152]{1,0:T(8,128)(2,1)S(1)} %collective-permute-done.8.pair_ref, bf16[1152,2304]{1,0:T(8,128)(2,1)S(1)} %bitcast.52, bf16[1152,2304]{1,0:T(8,128)(2,1)S(1)} %bitcast.52), custom_call_target="tpu_custom_call" | custom-call | tf_op jit(solution)/shard_map/feed_first/pallas_call | solution.py:228
  272.6 5.4 %feed_second.1 = (f32[128,1152]{1,0:T(8,128)S(1)}, bf16[128,1152]{1,0:T(8,128)(2,1)S(1)}) custom-call(bf16[128,1152]{1,0:T(8,128)(2,1)S(1)} %bitcast.55, bf16[128,1152]{1,0:T(8,128)(2,1)S(1)} %collective-permute-done.8.pair_ref, bf16[1152,2304]{1,0:T(8,128)(2,1)} %collective-permute-done.9.up_ref.down_ref, ...), custom_call_target="tpu_custom_call" | custom-call | tf_op jit(solution)/shard_map/feed_second/pallas_call | solution.py:245
  278.0 3.2 %collective-permute-start.10 = (bf16[128,1152]{1,0:T(8,128)(2,1)S(1)}, bf16[128,1152]{1,0:T(8,128)(2,1)S(1)}, u32[]{:S(2)}, u32[]{:S(2)}) collective-permute-start(bf16[128,1152]{1,0:T(8,128)(2,1)S(1)} %get-tuple-element.19), channel_id=1, source_target_pairs={{0,1},{1,0},{2,3},{3,2},{4,5},{5,4},{6,7},{7,6},{8,9},{9,8},{10,11... | collective-permute-start | bytes 884744 | tf_op jit(solution)/shard_map/ppermute | solution.py:29
  282.1 4.5 %collective-permute-done.10.recv_ref = bf16[128,1152]{1,0:T(8,128)(2,1)S(1)} collective-permute-done((bf16[128,1152]{1,0:T(8,128)(2,1)S(1)}, bf16[128,1152]{1,0:T(8,128)(2,1)S(1)}, u32[]{:S(2)}, u32[]{:S(2)}) %collective-permute-start.10) | collective-permute-done | bytes 294944 | tf_op jit(solution)/shard_map/ppermute | solution.py:29
  (84 shorter events, 26.4 us)
Async XLA Ops:
  6.5 203.2 %copy-start = (bf16[288,2304]{1,0:T(8,128)(2,1)S(1)}, bf16[288,2304]{1,0:T(8,128)(2,1)}, u32[]{:S(2)}) copy-start(bf16[288,2304]{1,0:T(8,128)(2,1)} %param.22) | copy-start | bytes 3981316
  6.5 60.0 %all-gather.7.cloned.1.call-start = ((), (), s32[]{:S(2)}) async-start(), calls=%async_computation.6 | async-start | bytes 1484800 | tf_op jit(solution)/shard_map/all_gather | solution.py:359
  8.6 14.9 %collective-permute-start = (bf16[18,3024]{1,0:T(8,128)(2,1)S(1)}, bf16[18,3024]{1,0:T(8,128)(2,1)S(1)}, u32[]{:S(2)}, u32[]{:S(2)}) collective-permute-start(bf16[18,3024]{1,0:T(8,128)(2,1)S(1)} %concatenate.25), channel_id=1, source_target_pairs={{0,4},{4,0},{1,5},{5,1},{2,6},{6,2},{3,7},{7,3},{8,12},{12,8},{9,1... | collective-permute-start | bytes 326600 | tf_op jit(solution)/shard_map/ppermute | solution.py:29
  23.5 0.7 collective-permute-start.1
  25.0 129.1 %all-gather.5.cloned.1.call-start = ((), (), s32[]{:S(2)}) async-start(), calls=%async_computation.5 | async-start | bytes 5971968 | tf_op jit(solution)/shard_map/all_gather | solution.py:361
  73.1 29.8 %all-to-all-start = ((bf16[64,2,288]{2,1,0:T(2,128)(2,1)}), bf16[64,2,288]{2,1,0:T(2,128)(2,1)S(1)}, u32[]{:S(2)}, u32[]{:S(2)}) async-start(bf16[64,2,288]{2,1,0:T(2,128)(2,1)} %broadcast_in_dim.56), calls=%async_computation | async-start | bytes 196608 | tf_op jit(solution)/shard_map/all_to_all | solution.py:19
  91.2 11.8 %collective-permute-start.2 = (bf16[36,288]{1,0:T(8,128)(2,1)S(1)}, bf16[36,288]{1,0:T(8,128)(2,1)S(1)}, u32[]{:S(2)}, u32[]{:S(2)}) collective-permute-start(bf16[36,288]{1,0:T(8,128)(2,1)S(1)} %pad_maximum_fusion.2), channel_id=1, source_target_pairs={{0,1},{1,0},{2,3},{3,2},{256,259},{257,258},{258,257},{259,256},{4... | collective-permute-start | bytes 62216 | tf_op jit(solution)/shard_map/ppermute | solution.py:346
  104.1 54.1 %all-to-all-start.1 = ((bf16[8,36,1024]{2,1,0:T(8,128)(2,1)}), bf16[8,36,1024]{2,1,0:T(8,128)(2,1)S(1)}, u32[]{:S(2)}, u32[]{:S(2)}) async-start(bf16[8,36,1024]{2,1,0:T(8,128)(2,1)} %broadcast_in_dim.57), calls=%async_computation.1 | async-start | bytes 1310720 | tf_op jit(solution)/shard_map/all_to_all | solution.py:19
  154.1 118.5 %collective-permute-start.9 = (bf16[1152,2304]{1,0:T(8,128)(2,1)}, bf16[1152,2304]{1,0:T(8,128)(2,1)}, u32[]{:S(2)}, u32[]{:S(2)}) collective-permute-start(bf16[1152,2304]{1,0:T(8,128)(2,1)} %all-gather.5.cloned.1.call-done.up_ref.down_ref), channel_id=1, source_target_pairs={{0,256},{256,0},{1,257},{257,1},{2,258},{258,2},{3,259},{259,3},{4... | collective-permute-start | bytes 15925256 | tf_op jit(solution)/shard_map/ppermute | solution.py:29
  159.1 17.8 %collective-permute-start.3 = (bf16[288,1024]{1,0:T(8,128)(2,1)}, bf16[288,1024]{1,0:T(8,128)(2,1)S(1)}, u32[]{:S(2)}, u32[]{:S(2)}) collective-permute-start(bf16[288,1024]{1,0:T(8,128)(2,1)} %reshape.275), channel_id=1, source_target_pairs={{0,8},{8,16},{16,24},{24,0},{1,9},{9,17},{17,25},{25,1},{2,10},{10... | collective-permute-start | bytes 1769480 | tf_op jit(solution)/shard_map/ppermute | solution.py:24
  161.5 20.0 %collective-permute-start.4 = (bf16[288,1024]{1,0:T(8,128)(2,1)}, bf16[288,1024]{1,0:T(8,128)(2,1)S(1)}, u32[]{:S(2)}, u32[]{:S(2)}) collective-permute-start(bf16[288,1024]{1,0:T(8,128)(2,1)} %reshape.275), channel_id=1, source_target_pairs={{0,24},{8,0},{16,8},{24,16},{1,25},{9,1},{17,9},{25,17},{2,26},{10... | collective-permute-start | bytes 1769480 | tf_op jit(solution)/shard_map/ppermute | solution.py:24
  165.1 15.5 %copy-start.5 = (bf16[288,1024]{1,0:T(8,128)(2,1)S(1)}, bf16[288,1024]{1,0:T(8,128)(2,1)}, u32[]{:S(2)}) copy-start(bf16[288,1024]{1,0:T(8,128)(2,1)} %reshape.275) | copy-start | bytes 1769476
  176.9 10.4 %collective-permute-start.5 = (bf16[144,1024]{1,0:T(8,128)(2,1)S(1)}, bf16[144,1024]{1,0:T(8,128)(2,1)S(1)}, u32[]{:S(2)}, u32[]{:S(2)}) collective-permute-start(bf16[144,1024]{1,0:T(8,128)(2,1)S(1)} %slice.114), channel_id=1, source_target_pairs={{0,8},{8,16},{16,24},{24,0},{1,9},{9,17},{17,25},{25,1},{2,10},{10... | collective-permute-start | bytes 884744 | tf_op jit(solution)/shard_map/ppermute | solution.py:24
  181.5 14.1 %copy-start.6 = (bf16[288,108]{1,0:T(8,128)(2,1)S(1)}, bf16[288,108]{1,0:T(8,128)(2,1)}, u32[]{:S(2)}) copy-start(bf16[288,108]{1,0:T(8,128)(2,1)} %param.21) | copy-start | bytes 186628
  181.5 11.4 %collective-permute-start.6 = (bf16[144,1024]{1,0:T(8,128)(2,1)S(1)}, bf16[144,1024]{1,0:T(8,128)(2,1)S(1)}, u32[]{:S(2)}, u32[]{:S(2)}) collective-permute-start(bf16[144,1024]{1,0:T(8,128)(2,1)S(1)} %slice.115), channel_id=1, source_target_pairs={{0,24},{8,0},{16,8},{24,16},{1,25},{9,1},{17,9},{25,17},{2,26},{10... | collective-permute-start | bytes 884744 | tf_op jit(solution)/shard_map/ppermute | solution.py:24
  193.6 40.4 %collective-permute-start.7 = (bf16[1152,1024]{1,0:T(8,128)(2,1)}, bf16[1152,1024]{1,0:T(8,128)(2,1)}, u32[]{:S(2)}, u32[]{:S(2)}) collective-permute-start(bf16[1152,1024]{1,0:T(8,128)(2,1)} %constant_dynamic-update-slice_fusion.mine_ref), channel_id=1, source_target_pairs={{0,256},{256,0},{1,257},{257,1},{2,258},{258,2},{3,259},{259,3},{4... | collective-permute-start | bytes 7077896 | tf_op jit(solution)/shard_map/ppermute | solution.py:29
  196.5 25.9 %all-to-all-start.2 = ((bf16[64,2,108]{2,1,0:T(2,128)(2,1)}), bf16[64,2,108]{2,1,0:T(2,128)(2,1)S(1)}, u32[]{:S(2)}, u32[]{:S(2)}) async-start(bf16[64,2,108]{2,1,0:T(2,128)(2,1)} %bitcast.12), calls=%async_computation.2 | async-start | bytes 65536 | tf_op jit(solution)/shard_map/all_to_all | solution.py:365
  223.4 9.3 %all-to-all-start.3 = ((bf16[4,2,9216]{2,1,0:T(2,128)(2,1)}), bf16[4,2,9216]{2,1,0:T(2,128)(2,1)S(1)}, u32[]{:S(2)}, u32[]{:S(2)}) async-start(bf16[4,2,9216]{2,1,0:T(2,128)(2,1)} %broadcast_in_dim.58), calls=%async_computation.3 | async-start | bytes 294912 | tf_op jit(solution)/shard_map/all_to_all | solution.py:19
  234.0 1.3 copy-start.2
  235.3 33.5 %slice-start = ((s8[5308416]{0:T(1024)(128)(4,1)}), s8[1114112]{0:T(1024)(128)(4,1)S(1)}, s32[]{:S(2)}) async-start(s8[5308416]{0:T(1024)(128)(4,1)} %bitcast.51), calls=%async_computation.7 | async-start | bytes 2228224
  244.1 10.6 %all-to-all-start.4 = ((bf16[4,288,128]{2,1,0:T(8,128)(2,1)}), bf16[4,288,128]{2,1,0:T(8,128)(2,1)S(1)}, u32[]{:S(2)}, u32[]{:S(2)}) async-start(bf16[4,288,128]{2,1,0:T(8,128)(2,1)} %attention.1), calls=%async_computation.4 | async-start | bytes 589824 | tf_op jit(solution)/shard_map/all_to_all | solution.py:400
  254.7 1.8 copy-start.1
  256.5 12.3 %slice-start.1 = ((s8[5308416]{0:T(1024)(128)(4,1)}), s8[4194304]{0:T(1024)(128)(4,1)S(1)}, s32[]{:S(2)}) async-start(s8[5308416]{0:T(1024)(128)(4,1)} %bitcast.51), calls=%async_computation.8 | async-start | bytes 8388608
  260.2 12.4 %copy-start.3 = (f32[2,64,1152]{2,1,0:T(8,128)}, f32[2,64,1152]{2,1,0:T(8,128)S(1)}, u32[]{:S(2)}) copy-start(f32[2,64,1152]{2,1,0:T(8,128)S(1)} %get-tuple-element.20.first_ref) | copy-start | bytes 1769476
  260.2 8.6 %collective-permute-start.8 = (bf16[128,1152]{1,0:T(8,128)(2,1)S(1)}, bf16[128,1152]{1,0:T(8,128)(2,1)S(1)}, u32[]{:S(2)}, u32[]{:S(2)}) collective-permute-start(bf16[128,1152]{1,0:T(8,128)(2,1)S(1)} %bitcast.53), channel_id=1, source_target_pairs={{0,1},{1,0},{2,3},{3,2},{4,5},{5,4},{6,7},{7,6},{8,9},{9,8},{10,11... | collective-permute-start | bytes 884744 | tf_op jit(solution)/shard_map/ppermute | solution.py:29
  272.6 9.3 %copy-start.7 = (bf16[1152,16]{0,1:T(8,128)(2,1)S(1)}, bf16[1152,16]{0,1:T(8,128)(2,1)}, u32[]{:S(2)}) copy-start(bf16[1152,16]{0,1:T(8,128)(2,1)} %param.27) | copy-start | bytes 110596
  272.6 14.0 %copy-start.4 = (f32[2,64,1152]{2,1,0:T(8,128)S(1)}, f32[2,64,1152]{2,1,0:T(8,128)}, u32[]{:S(2)}) copy-start(f32[2,64,1152]{2,1,0:T(8,128)} %copy-done.3) | copy-start | bytes 1769476
  278.0 8.6 %collective-permute-start.10 = (bf16[128,1152]{1,0:T(8,128)(2,1)S(1)}, bf16[128,1152]{1,0:T(8,128)(2,1)S(1)}, u32[]{:S(2)}, u32[]{:S(2)}) collective-permute-start(bf16[128,1152]{1,0:T(8,128)(2,1)S(1)} %get-tuple-element.19), channel_id=1, source_target_pairs={{0,1},{1,0},{2,3},{3,2},{4,5},{5,4},{6,7},{7,6},{8,9},{9,8},{10,11... | collective-permute-start | bytes 884744 | tf_op jit(solution)/shard_map/ppermute | solution.py:29
Sparse Core Ops, SparseCore 0:
  25.1 41.4 all-gather.6
  68.8 85.2 all-gather.4

commit v9 on v8

--- a/solution.py
+++ b/solution.py
@@ -184,34 +184,31 @@
     )(base, mixed, mine, other, change, own, gate_a, shift_m, scale_m)
 
 
-def feed_part(rows_ref, own_ref, pair_ref, up_ref, down_ref, so_far):
+def feed_part(rows, up_ref, down_ref):
+    hidden = jax.nn.gelu(dot(rows, up_ref[...]), approximate=True).astype(BF16)
+    return dot_t(down_ref[...], hidden)
+
+
+def feed_first_body(rows_ref, up_ref, down_ref, sum_ref):
+    @pl.when(pl.program_id(0) == 0)
+    def _():
+        sum_ref[...] = jnp.zeros(sum_ref.shape, F32)
+
+    sum_ref[...] += feed_part(rows_ref[...], up_ref, down_ref)
+
+
+def feed_second_body(own_ref, pair_ref, up_ref, down_ref, before_ref, pair_before_ref,
+                     keep_ref, send_ref, rows_ref, sum_ref):
     count = own_ref.shape[0]
 
     @pl.when(pl.program_id(0) == 0)
     def _():
         rows_ref[:count] = own_ref[...]
         rows_ref[count:] = pair_ref[...]
-
-    hidden = jax.nn.gelu(dot(rows_ref[...], up_ref[...]), approximate=True).astype(BF16)
-    return so_far() + dot_t(down_ref[...], hidden)
-
-
-def feed_first_body(own_ref, pair_ref, up_ref, down_ref, sum_ref, rows_ref):
-    @pl.when(pl.program_id(0) == 0)
-    def _():
-        sum_ref[...] = jnp.zeros(sum_ref.shape, F32)
-
-    sum_ref[...] = feed_part(rows_ref, own_ref, pair_ref, up_ref, down_ref, lambda: sum_ref[...])
-
-
-def feed_second_body(own_ref, pair_ref, up_ref, down_ref, before_ref, keep_ref, send_ref, rows_ref, sum_ref):
-    count = own_ref.shape[0]
-
-    @pl.when(pl.program_id(0) == 0)
-    def _():
-        sum_ref[...] = before_ref[...]
-
-    sum_ref[...] = feed_part(rows_ref, own_ref, pair_ref, up_ref, down_ref, lambda: sum_ref[...])
+        sum_ref[:, :count] = before_ref[...]
+        sum_ref[:, count:] = pair_before_ref[...]
+
+    sum_ref[...] += feed_part(rows_ref[...], up_ref, down_ref)
 
     @pl.when(pl.program_id(0) == pl.num_programs(0) - 1)
     def _():
@@ -220,24 +217,23 @@
         send_ref[...] = total[count:].astype(BF16)
 
 
-def feed_first(own, pair, weights):
-    count, width = own.shape
+def feed_first(rows, weights):
+    count, width = rows.shape
     steps = 3
     up = pl.BlockSpec((width, width // steps), lambda i: (0, steps + i))
     down = pl.BlockSpec((width, width // steps), lambda i: (0, i))
     return pl.pallas_call(
         feed_first_body,
         grid=(steps,),
-        in_specs=[whole(own.shape), whole(own.shape), up, down],
-        out_specs=whole((width, 2 * count)),
-        out_shape=jax.ShapeDtypeStruct((width, 2 * count), F32),
-        scratch_shapes=[pltpu.VMEM((2 * count, width), BF16)],
+        in_specs=[whole(rows.shape), up, down],
+        out_specs=whole((width, count)),
+        out_shape=jax.ShapeDtypeStruct((width, count), F32),
         name="feed_first",
         compiler_params=pltpu.CompilerParams(vmem_limit_bytes=20 << 20),
-    )(own, pair, weights, weights)
-
-
-def feed_second(own, pair, weights, before):
+    )(rows, weights, weights)
+
+
+def feed_second(own, pair, weights, before, pair_before):
     count, width = own.shape
     steps = 3
     up = pl.BlockSpec((width, width // steps), lambda i: (0, steps + i))
@@ -245,7 +241,14 @@
     return pl.pallas_call(
         feed_second_body,
         grid=(steps,),
-        in_specs=[whole(own.shape), whole(own.shape), up, down, whole(before.shape)],
+        in_specs=[
+            whole(own.shape),
+            whole(own.shape),
+            up,
+            down,
+            whole(before.shape),
+            whole(before.shape),
+        ],
         out_specs=[whole(own.shape), whole(own.shape)],
         out_shape=[
             jax.ShapeDtypeStruct(own.shape, F32),
@@ -254,7 +257,7 @@
         scratch_shapes=[pltpu.VMEM((2 * count, width), BF16), pltpu.VMEM((width, 2 * count), F32)],
         name="feed_second",
         compiler_params=pltpu.CompilerParams(vmem_limit_bytes=20 << 20),
-    )(own, pair, weights, weights, before)
+    )(own, pair, weights, weights, before, pair_before)
 
 
 def finish_body(scale_by_ref, keep_ref, recv_ref, first_ref, gate_ref, shift_ref, scale_ref, out_w_ref, out_ref):
@@ -402,8 +405,9 @@
     first_sum, hidden_two = project(base, mixed, part_a, other_a, change, own, gate_a, shift_m, scale_m)
     hidden_two = hidden_two.reshape(2 * share, width)
     pair = swap(hidden_two, "mp", 1)
-    before = feed_first(hidden_two, pair, feed)
-    keep, send = feed_second(hidden_two, pair, other_feed, before)
+    before = feed_first(hidden_two, feed)
+    pair_before = feed_first(pair, feed)
+    keep, send = feed_second(hidden_two, pair, other_feed, before, pair_before)
     recv = swap(send, "mp", 1)
     return finish(guidance, keep, recv, first_sum, gate_m, shift_f, scale_f, out_weight)
 
@@ -429,4 +433,6 @@
         P("mp", DP),
         P(),
     )
-    return jax.shard_map(on_device, mesh=torus, in_specs=placed, out_specs=P(GROUP_DP, "mp"), check_vma=False)
+    return jax.shard_map(
+        on_device, mesh=torus, in_specs=placed, out_specs=P(GROUP_DP, "mp"), check_vma=False
+    )

time: 297 us -> 296 us (level)
  waiting for transfers between devices: 152 us -> 149 us
where the time goes in v9:
time: 296 us; the launch traced here: 294 us
  waiting for transfers between devices  149 us (50%)
  starting transfers between devices  76 us (26%)
  Pallas kernels  24.8 us (8%)
  local copies, waits for them, and re-layouts  18.1 us (6%)
  between operations  16.5 us (6%)
  other arithmetic  4.94 us (2%)
  matrix products  4.56 us (2%)
    all_gather x1, waiting for transfers between devices, on_device(): feed = lax.all_gather(feed, 'dp_0', axis=0, tiled=True)  46.5 us
    all_gather x1, waiting for transfers between devices, on_device(): feed = lax.all_gather(feed, 'dp_1', axis=0)  41.5 us
    all_to_all x3, starting transfers between devices, to_everyone(): lax.all_to_all(jnp.broadcast_to(x[None], (size, *x.shape)), axis, 0, 0, t...  23 us
    ppermute x5, starting transfers between devices, swap(): return lax.ppermute(x, axis, [(i, i ^ bit) for i in range(size)])  21.2 us
    ppermute x4, waiting for transfers between devices, shift(): return lax.ppermute(x, axis, [(i, (i + step) % size) for i in range(size)])  15.6 us
    all_to_all x3, waiting for transfers between devices, to_everyone(): lax.all_to_all(jnp.broadcast_to(x[None], (size, *x.shape)), axis, 0, 0, t...  14.8 us
    all_to_all x1, starting transfers between devices, on_device(): lax.all_to_all(mod_part, DP, split_axis=0, concat_axis=1, tiled=True)  13.2 us
    all_to_all x1, waiting for transfers between devices, on_device(): lax.all_to_all(mod_part, DP, split_axis=0, concat_axis=1, tiled=True)  12.4 us
  transfers between devices with their start and end apart: 18, of which 12 were waited for; matrix products, arithmetic and copies ran while one was open for 7% of the time, Pallas kernels for 6%

profile of v9, /device:TPU:6, one launch (start us, length us, event | category | flops | bytes accessed | tf_op | source)
XLA Modules:
  0.0 293.8 jit_solution(11298526479414034265)
XLA Ops:
  8.6 10.9 %collective-permute-start = (bf16[18,3024]{1,0:T(8,128)(2,1)S(1)}, bf16[18,3024]{1,0:T(8,128)(2,1)S(1)}, u32[]{:S(2)}, u32[]{:S(2)}) collective-permute-start(bf16[18,3024]{1,0:T(8,128)(2,1)S(1)} %concatenate.25), channel_id=1, source_target_pairs={{0,4},{4,0},{1,5},{5,1},{2,6},{6,2},{3,7},{7,3},{8,12},{12,8},{9,1... | collective-permute-start | bytes 326600 | tf_op jit(solution)/shard_map/ppermute | solution.py:29
  19.5 3.9 %collective-permute-done = bf16[18,3024]{1,0:T(8,128)(2,1)S(1)} collective-permute-done((bf16[18,3024]{1,0:T(8,128)(2,1)S(1)}, bf16[18,3024]{1,0:T(8,128)(2,1)S(1)}, u32[]{:S(2)}, u32[]{:S(2)}) %collective-permute-start) | collective-permute-done | bytes 108896 | tf_op jit(solution)/shard_map/ppermute | solution.py:29
  25.0 41.5 %all-gather.7.cloned.1.call-done = bf16[4,36,3712]{2,1,0:T(8,128)(2,1)} async-done(((bf16[1,36,3712]{2,1,0:T(8,128)(2,1)}), bf16[4,36,3712]{2,1,0:T(8,128)(2,1)}) %all-gather.7.cloned.1.call-update) | async-done | bytes 1069072 | tf_op jit(solution)/shard_map/all_gather | solution.py:362
  73.1 16.0 %all-to-all-start = ((bf16[64,2,288]{2,1,0:T(2,128)(2,1)}), bf16[64,2,288]{2,1,0:T(2,128)(2,1)S(1)}, u32[]{:S(2)}, u32[]{:S(2)}) async-start(bf16[64,2,288]{2,1,0:T(2,128)(2,1)} %broadcast_in_dim.56), calls=%async_computation | async-start | bytes 196608 | tf_op jit(solution)/shard_map/all_to_all | solution.py:19
  91.2 2.7 collective-permute-start.2
  93.9 9.0 %all-to-all-done = bf16[64,2,288]{2,1,0:T(2,128)(2,1)S(1)} async-done(((bf16[64,2,288]{2,1,0:T(2,128)(2,1)}), bf16[64,2,288]{2,1,0:T(2,128)(2,1)S(1)}, u32[]{:S(2)}, u32[]{:S(2)}) %all-to-all-start) | async-done | bytes 73760 | tf_op jit(solution)/shard_map/all_to_all | solution.py:19
  104.1 3.5 %all-to-all-start.1 = ((bf16[8,36,1024]{2,1,0:T(8,128)(2,1)}), bf16[8,36,1024]{2,1,0:T(8,128)(2,1)S(1)}, u32[]{:S(2)}, u32[]{:S(2)}) async-start(bf16[8,36,1024]{2,1,0:T(8,128)(2,1)} %broadcast_in_dim.57), calls=%async_computation.1 | async-start | bytes 1310720 | tf_op jit(solution)/shard_map/all_to_all | solution.py:19
  107.6 46.5 %all-gather.5.cloned.1.call-done.up_ref.down_ref = bf16[1152,2304]{1,0:T(8,128)(2,1)} async-done(((bf16[144,2304]{1,0:T(8,128)(2,1)}), bf16[1152,2304]{1,0:T(8,128)(2,1)}) %all-gather.5.cloned.1.call-update) | async-done | bytes 5308432 | tf_op jit(solution)/shard_map/all_gather | solution.py:364
  156.0 2.1 fusion.2.change_ref
  159.1 2.4 collective-permute-start.3
  161.5 3.4 %collective-permute-start.4 = (bf16[288,1024]{1,0:T(8,128)(2,1)}, bf16[288,1024]{1,0:T(8,128)(2,1)S(1)}, u32[]{:S(2)}, u32[]{:S(2)}) collective-permute-start(bf16[288,1024]{1,0:T(8,128)(2,1)} %reshape.275), channel_id=1, source_target_pairs={{0,24},{8,0},{16,8},{24,16},{1,25},{9,1},{17,9},{25,17},{2,26},{10... | collective-permute-start | bytes 1769480 | tf_op jit(solution)/shard_map/ppermute | solution.py:24
  165.1 3.0 %fusion.5 = bf16[512,1152]{1,0:T(8,128)(2,1)} fusion(bf16[512,1152]{1,0:T(8,128)(2,1)S(1)} %bitcast.57, s32[1152]{0:T(1024)S(1)} %fusion.24), kind=kOutput, calls=%fused_computation.7 | convolution fusion | flops 1360871424 | bytes 2363904 | tf_op jit(solution)/shard_map/dot_general | solution.py:63
  168.0 8.9 %collective-permute-done.3 = bf16[288,1024]{1,0:T(8,128)(2,1)S(1)} collective-permute-done((bf16[288,1024]{1,0:T(8,128)(2,1)}, bf16[288,1024]{1,0:T(8,128)(2,1)S(1)}, u32[]{:S(2)}, u32[]{:S(2)}) %collective-permute-start.3) | collective-permute-done | bytes 589856 | tf_op jit(solution)/shard_map/ppermute | solution.py:24
  176.9 3.7 %collective-permute-start.5 = (bf16[144,1024]{1,0:T(8,128)(2,1)S(1)}, bf16[144,1024]{1,0:T(8,128)(2,1)S(1)}, u32[]{:S(2)}, u32[]{:S(2)}) collective-permute-start(bf16[144,1024]{1,0:T(8,128)(2,1)S(1)} %slice.114), channel_id=1, source_target_pairs={{0,8},{8,16},{16,24},{24,0},{1,9},{9,17},{17,25},{25,1},{2,10},{10... | collective-permute-start | bytes 884744 | tf_op jit(solution)/shard_map/ppermute | solution.py:24
  181.5 2.2 collective-permute-start.6
  185.4 2.0 collective-permute-done.5
  188.1 4.8 %collective-permute-done.6 = bf16[144,1024]{1,0:T(8,128)(2,1)S(1)} collective-permute-done((bf16[144,1024]{1,0:T(8,128)(2,1)S(1)}, bf16[144,1024]{1,0:T(8,128)(2,1)S(1)}, u32[]{:S(2)}, u32[]{:S(2)}) %collective-permute-start.6) | collective-permute-done | bytes 294944 | tf_op jit(solution)/shard_map/ppermute | solution.py:24
  196.5 13.2 %all-to-all-start.2 = ((bf16[64,2,108]{2,1,0:T(2,128)(2,1)}), bf16[64,2,108]{2,1,0:T(2,128)(2,1)S(1)}, u32[]{:S(2)}, u32[]{:S(2)}) async-start(bf16[64,2,108]{2,1,0:T(2,128)(2,1)} %bitcast.12), calls=%async_computation.2 | async-start | bytes 65536 | tf_op jit(solution)/shard_map/all_to_all | solution.py:368
  210.0 12.4 %all-to-all-done.2 = bf16[64,2,108]{2,1,0:T(2,128)(2,1)S(1)} async-done(((bf16[64,2,108]{2,1,0:T(2,128)(2,1)}), bf16[64,2,108]{2,1,0:T(2,128)(2,1)S(1)}, u32[]{:S(2)}, u32[]{:S(2)}) %all-to-all-start.2) | async-done | bytes 27680 | tf_op jit(solution)/shard_map/all_to_all | solution.py:368
  223.4 3.5 %all-to-all-start.3 = ((bf16[4,2,9216]{2,1,0:T(2,128)(2,1)}), bf16[4,2,9216]{2,1,0:T(2,128)(2,1)S(1)}, u32[]{:S(2)}, u32[]{:S(2)}) async-start(bf16[4,2,9216]{2,1,0:T(2,128)(2,1)} %broadcast_in_dim.58), calls=%async_computation.3 | async-start | bytes 294912 | tf_op jit(solution)/shard_map/all_to_all | solution.py:19
  226.9 5.7 %all-to-all-done.3 = bf16[4,2,9216]{2,1,0:T(2,128)(2,1)S(1)} async-done(((bf16[4,2,9216]{2,1,0:T(2,128)(2,1)}), bf16[4,2,9216]{2,1,0:T(2,128)(2,1)S(1)}, u32[]{:S(2)}, u32[]{:S(2)}) %all-to-all-start.3) | async-done | bytes 147488 | tf_op jit(solution)/shard_map/all_to_all | solution.py:19
  235.3 8.8 %attention.1 = bf16[4,288,128]{2,1,0:T(8,128)(2,1)} custom-call(s32[1]{0:T(128)} %bitcast.1.core_ref, bf16[2,256,1152]{2,1,0:T(8,128)(2,1)S(1)} %bitcast.56, f32[2,1,1152]{2,1,0:T(1,128)S(1)} %get-tuple-element.56.shift_ref, f32[2,1,1152]{2,1,0:T(1,128)S(1)} %get-tuple-element.55.scale_ref, bf16[1152,1024]{1,0:T(8,128)(2,1)} %constant_dynamic-update-slice_fusion.mine_ref, ...), custom_call_target="tpu_custom_call" | custom-call | tf_op jit(solution)/shard_map/attention/pallas_call | solution.py:116
  244.1 3.5 %all-to-all-start.4 = ((bf16[4,288,128]{2,1,0:T(8,128)(2,1)}), bf16[4,288,128]{2,1,0:T(8,128)(2,1)S(1)}, u32[]{:S(2)}, u32[]{:S(2)}) async-start(bf16[4,288,128]{2,1,0:T(8,128)(2,1)} %attention.1), calls=%async_computation.4 | async-start | bytes 589824 | tf_op jit(solution)/shard_map/all_to_all | solution.py:403
  247.6 7.1 %all-to-all-done.4.mixed_ref = bf16[4,288,128]{2,1,0:T(8,128)(2,1)S(1)} async-done(((bf16[4,288,128]{2,1,0:T(8,128)(2,1)}), bf16[4,288,128]{2,1,0:T(8,128)(2,1)S(1)}, u32[]{:S(2)}, u32[]{:S(2)}) %all-to-all-start.4) | async-done | bytes 294944 | tf_op jit(solution)/shard_map/all_to_all | solution.py:403
  256.5 3.7 %project.1 = (f32[2,64,1152]{2,1,0:T(8,128)S(1)}, bf16[2,64,1152]{2,1,0:T(8,128)(2,1)S(1)}) custom-call(s32[1]{0:T(128)} %bitcast.base_ref, bf16[4,288,128]{2,1,0:T(8,128)(2,1)S(1)} %all-to-all-done.4.mixed_ref, bf16[1152,1024]{1,0:T(8,128)(2,1)} %constant_dynamic-update-slice_fusion.mine_ref, bf16[1152,1024]{1,0:T(8,128)(2,1)} %collective-permute-done.7.other_ref, ...), custom_call_target="tpu_custom_call" | custom-call | tf_op jit(solution)/shard_map/project/pallas_call | solution.py:160
  260.2 3.3 %collective-permute-start.8 = (bf16[128,1152]{1,0:T(8,128)(2,1)S(1)}, bf16[128,1152]{1,0:T(8,128)(2,1)S(1)}, u32[]{:S(2)}, u32[]{:S(2)}) collective-permute-start(bf16[128,1152]{1,0:T(8,128)(2,1)S(1)} %bitcast.53), channel_id=1, source_target_pairs={{0,1},{1,0},{2,3},{3,2},{4,5},{5,4},{6,7},{7,6},{8,9},{9,8},{10,11... | collective-permute-start | bytes 884744 | tf_op jit(solution)/shard_map/ppermute | solution.py:29
  263.5 2.8 feed_first.2.before_ref
  266.3 2.5 collective-permute-done.8.rows_ref.pair_ref
  268.8 2.8 feed_first.3.pair_before_ref
  271.7 5.4 %feed_second.1 = (f32[128,1152]{1,0:T(8,128)S(1)}, bf16[128,1152]{1,0:T(8,128)(2,1)S(1)}) custom-call(bf16[128,1152]{1,0:T(8,128)(2,1)S(1)} %bitcast.55, bf16[128,1152]{1,0:T(8,128)(2,1)S(1)} %collective-permute-done.8.rows_ref.pair_ref, bf16[1152,2304]{1,0:T(8,128)(2,1)} %collective-permute-done.9.up_ref.down_ref, ...), custom_call_target="tpu_custom_call" | custom-call | tf_op jit(solution)/shard_map/feed_second/pallas_call | solution.py:241
  277.1 3.3 %collective-permute-start.10 = (bf16[128,1152]{1,0:T(8,128)(2,1)S(1)}, bf16[128,1152]{1,0:T(8,128)(2,1)S(1)}, u32[]{:S(2)}, u32[]{:S(2)}) collective-permute-start(bf16[128,1152]{1,0:T(8,128)(2,1)S(1)} %get-tuple-element.19), channel_id=1, source_target_pairs={{0,1},{1,0},{2,3},{3,2},{4,5},{5,4},{6,7},{7,6},{8,9},{9,8},{10,11... | collective-permute-start | bytes 884744 | tf_op jit(solution)/shard_map/ppermute | solution.py:29
  281.2 4.5 %collective-permute-done.10.recv_ref = bf16[128,1152]{1,0:T(8,128)(2,1)S(1)} collective-permute-done((bf16[128,1152]{1,0:T(8,128)(2,1)S(1)}, bf16[128,1152]{1,0:T(8,128)(2,1)S(1)}, u32[]{:S(2)}, u32[]{:S(2)}) %collective-permute-start.10) | collective-permute-done | bytes 294944 | tf_op jit(solution)/shard_map/ppermute | solution.py:29
  (85 shorter events, 28.4 us)
Async XLA Ops:
  6.5 203.2 %copy-start = (bf16[288,2304]{1,0:T(8,128)(2,1)S(1)}, bf16[288,2304]{1,0:T(8,128)(2,1)}, u32[]{:S(2)}) copy-start(bf16[288,2304]{1,0:T(8,128)(2,1)} %param.22) | copy-start | bytes 3981316
  6.5 60.0 %all-gather.7.cloned.1.call-start = ((), (), s32[]{:S(2)}) async-start(), calls=%async_computation.6 | async-start | bytes 1484800 | tf_op jit(solution)/shard_map/all_gather | solution.py:362
  8.6 14.9 %collective-permute-start = (bf16[18,3024]{1,0:T(8,128)(2,1)S(1)}, bf16[18,3024]{1,0:T(8,128)(2,1)S(1)}, u32[]{:S(2)}, u32[]{:S(2)}) collective-permute-start(bf16[18,3024]{1,0:T(8,128)(2,1)S(1)} %concatenate.25), channel_id=1, source_target_pairs={{0,4},{4,0},{1,5},{5,1},{2,6},{6,2},{3,7},{7,3},{8,12},{12,8},{9,1... | collective-permute-start | bytes 326600 | tf_op jit(solution)/shard_map/ppermute | solution.py:29
  23.5 0.7 collective-permute-start.1
  25.0 129.1 %all-gather.5.cloned.1.call-start = ((), (), s32[]{:S(2)}) async-start(), calls=%async_computation.5 | async-start | bytes 5971968 | tf_op jit(solution)/shard_map/all_gather | solution.py:364
  73.1 29.8 %all-to-all-start = ((bf16[64,2,288]{2,1,0:T(2,128)(2,1)}), bf16[64,2,288]{2,1,0:T(2,128)(2,1)S(1)}, u32[]{:S(2)}, u32[]{:S(2)}) async-start(bf16[64,2,288]{2,1,0:T(2,128)(2,1)} %broadcast_in_dim.56), calls=%async_computation | async-start | bytes 196608 | tf_op jit(solution)/shard_map/all_to_all | solution.py:19
  91.2 11.8 %collective-permute-start.2 = (bf16[36,288]{1,0:T(8,128)(2,1)S(1)}, bf16[36,288]{1,0:T(8,128)(2,1)S(1)}, u32[]{:S(2)}, u32[]{:S(2)}) collective-permute-start(bf16[36,288]{1,0:T(8,128)(2,1)S(1)} %pad_maximum_fusion.2), channel_id=1, source_target_pairs={{0,1},{1,0},{2,3},{3,2},{256,259},{257,258},{258,257},{259,256},{4... | collective-permute-start | bytes 62216 | tf_op jit(solution)/shard_map/ppermute | solution.py:349
  104.1 54.1 %all-to-all-start.1 = ((bf16[8,36,1024]{2,1,0:T(8,128)(2,1)}), bf16[8,36,1024]{2,1,0:T(8,128)(2,1)S(1)}, u32[]{:S(2)}, u32[]{:S(2)}) async-start(bf16[8,36,1024]{2,1,0:T(8,128)(2,1)} %broadcast_in_dim.57), calls=%async_computation.1 | async-start | bytes 1310720 | tf_op jit(solution)/shard_map/all_to_all | solution.py:19
  154.1 117.6 %collective-permute-start.9 = (bf16[1152,2304]{1,0:T(8,128)(2,1)}, bf16[1152,2304]{1,0:T(8,128)(2,1)}, u32[]{:S(2)}, u32[]{:S(2)}) collective-permute-start(bf16[1152,2304]{1,0:T(8,128)(2,1)} %all-gather.5.cloned.1.call-done.up_ref.down_ref), channel_id=1, source_target_pairs={{0,256},{256,0},{1,257},{257,1},{2,258},{258,2},{3,259},{259,3},{4... | collective-permute-start | bytes 15925256 | tf_op jit(solution)/shard_map/ppermute | solution.py:29
  159.1 17.8 %collective-permute-start.3 = (bf16[288,1024]{1,0:T(8,128)(2,1)}, bf16[288,1024]{1,0:T(8,128)(2,1)S(1)}, u32[]{:S(2)}, u32[]{:S(2)}) collective-permute-start(bf16[288,1024]{1,0:T(8,128)(2,1)} %reshape.275), channel_id=1, source_target_pairs={{0,8},{8,16},{16,24},{24,0},{1,9},{9,17},{17,25},{25,1},{2,10},{10... | collective-permute-start | bytes 1769480 | tf_op jit(solution)/shard_map/ppermute | solution.py:24
  161.5 20.0 %collective-permute-start.4 = (bf16[288,1024]{1,0:T(8,128)(2,1)}, bf16[288,1024]{1,0:T(8,128)(2,1)S(1)}, u32[]{:S(2)}, u32[]{:S(2)}) collective-permute-start(bf16[288,1024]{1,0:T(8,128)(2,1)} %reshape.275), channel_id=1, source_target_pairs={{0,24},{8,0},{16,8},{24,16},{1,25},{9,1},{17,9},{25,17},{2,26},{10... | collective-permute-start | bytes 1769480 | tf_op jit(solution)/shard_map/ppermute | solution.py:24
  165.1 15.5 %copy-start.5 = (bf16[288,1024]{1,0:T(8,128)(2,1)S(1)}, bf16[288,1024]{1,0:T(8,128)(2,1)}, u32[]{:S(2)}) copy-start(bf16[288,1024]{1,0:T(8,128)(2,1)} %reshape.275) | copy-start | bytes 1769476
  176.9 10.4 %collective-permute-start.5 = (bf16[144,1024]{1,0:T(8,128)(2,1)S(1)}, bf16[144,1024]{1,0:T(8,128)(2,1)S(1)}, u32[]{:S(2)}, u32[]{:S(2)}) collective-permute-start(bf16[144,1024]{1,0:T(8,128)(2,1)S(1)} %slice.114), channel_id=1, source_target_pairs={{0,8},{8,16},{16,24},{24,0},{1,9},{9,17},{17,25},{25,1},{2,10},{10... | collective-permute-start | bytes 884744 | tf_op jit(solution)/shard_map/ppermute | solution.py:24
  181.5 14.1 %copy-start.6 = (bf16[288,108]{1,0:T(8,128)(2,1)S(1)}, bf16[288,108]{1,0:T(8,128)(2,1)}, u32[]{:S(2)}) copy-start(bf16[288,108]{1,0:T(8,128)(2,1)} %param.21) | copy-start | bytes 186628
  181.5 11.4 %collective-permute-start.6 = (bf16[144,1024]{1,0:T(8,128)(2,1)S(1)}, bf16[144,1024]{1,0:T(8,128)(2,1)S(1)}, u32[]{:S(2)}, u32[]{:S(2)}) collective-permute-start(bf16[144,1024]{1,0:T(8,128)(2,1)S(1)} %slice.115), channel_id=1, source_target_pairs={{0,24},{8,0},{16,8},{24,16},{1,25},{9,1},{17,9},{25,17},{2,26},{10... | collective-permute-start | bytes 884744 | tf_op jit(solution)/shard_map/ppermute | solution.py:24
  193.6 40.4 %collective-permute-start.7 = (bf16[1152,1024]{1,0:T(8,128)(2,1)}, bf16[1152,1024]{1,0:T(8,128)(2,1)}, u32[]{:S(2)}, u32[]{:S(2)}) collective-permute-start(bf16[1152,1024]{1,0:T(8,128)(2,1)} %constant_dynamic-update-slice_fusion.mine_ref), channel_id=1, source_target_pairs={{0,256},{256,0},{1,257},{257,1},{2,258},{258,2},{3,259},{259,3},{4... | collective-permute-start | bytes 7077896 | tf_op jit(solution)/shard_map/ppermute | solution.py:29
  196.5 25.9 %all-to-all-start.2 = ((bf16[64,2,108]{2,1,0:T(2,128)(2,1)}), bf16[64,2,108]{2,1,0:T(2,128)(2,1)S(1)}, u32[]{:S(2)}, u32[]{:S(2)}) async-start(bf16[64,2,108]{2,1,0:T(2,128)(2,1)} %bitcast.12), calls=%async_computation.2 | async-start | bytes 65536 | tf_op jit(solution)/shard_map/all_to_all | solution.py:368
  223.4 9.3 %all-to-all-start.3 = ((bf16[4,2,9216]{2,1,0:T(2,128)(2,1)}), bf16[4,2,9216]{2,1,0:T(2,128)(2,1)S(1)}, u32[]{:S(2)}, u32[]{:S(2)}) async-start(bf16[4,2,9216]{2,1,0:T(2,128)(2,1)} %broadcast_in_dim.58), calls=%async_computation.3 | async-start | bytes 294912 | tf_op jit(solution)/shard_map/all_to_all | solution.py:19
  234.0 1.3 copy-start.2
  235.3 28.2 %slice-start = ((s8[5308416]{0:T(1024)(128)(4,1)}), s8[1114112]{0:T(1024)(128)(4,1)S(1)}, s32[]{:S(2)}) async-start(s8[5308416]{0:T(1024)(128)(4,1)} %bitcast.51), calls=%async_computation.7 | async-start | bytes 2228224
  244.1 10.6 %all-to-all-start.4 = ((bf16[4,288,128]{2,1,0:T(8,128)(2,1)}), bf16[4,288,128]{2,1,0:T(8,128)(2,1)S(1)}, u32[]{:S(2)}, u32[]{:S(2)}) async-start(bf16[4,288,128]{2,1,0:T(8,128)(2,1)} %attention.1), calls=%async_computation.4 | async-start | bytes 589824 | tf_op jit(solution)/shard_map/all_to_all | solution.py:403
  254.7 1.8 copy-start.1
  256.5 7.0 %slice-start.1 = ((s8[5308416]{0:T(1024)(128)(4,1)}), s8[4194304]{0:T(1024)(128)(4,1)S(1)}, s32[]{:S(2)}) async-start(s8[5308416]{0:T(1024)(128)(4,1)} %bitcast.51), calls=%async_computation.8 | async-start | bytes 8388608
  260.2 6.1 %copy-start.3 = (f32[2,64,1152]{2,1,0:T(8,128)}, f32[2,64,1152]{2,1,0:T(8,128)S(1)}, u32[]{:S(2)}) copy-start(f32[2,64,1152]{2,1,0:T(8,128)S(1)} %get-tuple-element.20.first_ref) | copy-start | bytes 1769476
  260.2 8.6 %collective-permute-start.8 = (bf16[128,1152]{1,0:T(8,128)(2,1)S(1)}, bf16[128,1152]{1,0:T(8,128)(2,1)S(1)}, u32[]{:S(2)}, u32[]{:S(2)}) collective-permute-start(bf16[128,1152]{1,0:T(8,128)(2,1)S(1)} %bitcast.53), channel_id=1, source_target_pairs={{0,1},{1,0},{2,3},{3,2},{4,5},{5,4},{6,7},{7,6},{8,9},{9,8},{10,11... | collective-permute-start | bytes 884744 | tf_op jit(solution)/shard_map/ppermute | solution.py:29
  271.6 9.4 %copy-start.7 = (bf16[1152,16]{0,1:T(8,128)(2,1)S(1)}, bf16[1152,16]{0,1:T(8,128)(2,1)}, u32[]{:S(2)}) copy-start(bf16[1152,16]{0,1:T(8,128)(2,1)} %param.27) | copy-start | bytes 110596
  271.7 14.1 %copy-start.4 = (f32[2,64,1152]{2,1,0:T(8,128)S(1)}, f32[2,64,1152]{2,1,0:T(8,128)}, u32[]{:S(2)}) copy-start(f32[2,64,1152]{2,1,0:T(8,128)} %copy-done.3) | copy-start | bytes 1769476
  277.1 8.6 %collective-permute-start.10 = (bf16[128,1152]{1,0:T(8,128)(2,1)S(1)}, bf16[128,1152]{1,0:T(8,128)(2,1)S(1)}, u32[]{:S(2)}, u32[]{:S(2)}) collective-permute-start(bf16[128,1152]{1,0:T(8,128)(2,1)S(1)} %get-tuple-element.19), channel_id=1, source_target_pairs={{0,1},{1,0},{2,3},{3,2},{4,5},{5,4},{6,7},{7,6},{8,9},{9,8},{10,11... | collective-permute-start | bytes 884744 | tf_op jit(solution)/shard_map/ppermute | solution.py:29
Sparse Core Ops, SparseCore 0:
  25.1 41.4 all-gather.6
  68.8 85.2 all-gather.4

commit v10 on v9

--- a/solution.py
+++ b/solution.py
@@ -38,8 +38,10 @@
     half = block.shape[0] // 2
     left = shift(block, "dp_1", 1)
     right = shift(block, "dp_1", -1)
-    far_top = shift(left[:half], "dp_1", 1)
-    far_bottom = shift(right[half:], "dp_1", -1)
+    top, bottom = left[:half], right[half:]
+    left, right, top, bottom = lax.optimization_barrier((left, right, top, bottom))
+    far_top = shift(top, "dp_1", 1)
+    far_bottom = shift(bottom, "dp_1", -1)
     return jnp.concatenate([block, left, right, far_top, far_bottom], axis=0)
 
 

time: 296 us -> 297 us (level)
  transfers between devices with their start and end apart: 18 -> 18, of which waited for: 12 -> 13; matrix products, arithmetic and copies ran while one was open for 7% -> 7% of each run, Pallas kernels for 6% -> 6%
where the time goes in v10:
time: 297 us; the launch traced here: 296 us
  waiting for transfers between devices  150 us (51%)
  starting transfers between devices  76.1 us (26%)
  Pallas kernels  24.8 us (8%)
  local copies, waits for them, and re-layouts  18.1 us (6%)
  between operations  16.5 us (6%)
  other arithmetic  4.94 us (2%)
  matrix products  4.56 us (2%)
    all_gather x1, waiting for transfers between devices, on_device(): feed = lax.all_gather(feed, 'dp_0', axis=0, tiled=True)  46.5 us
    all_gather x1, waiting for transfers between devices, on_device(): feed = lax.all_gather(feed, 'dp_1', axis=0)  41.5 us
    all_to_all x3, starting transfers between devices, to_everyone(): lax.all_to_all(jnp.broadcast_to(x[None], (size, *x.shape)), axis, 0, 0, t...  23 us
    ppermute x5, starting transfers between devices, swap(): return lax.ppermute(x, axis, [(i, i ^ bit) for i in range(size)])  21.2 us
    ppermute x4, waiting for transfers between devices, shift(): return lax.ppermute(x, axis, [(i, (i + step) % size) for i in range(size)])  17.2 us
    all_to_all x3, waiting for transfers between devices, to_everyone(): lax.all_to_all(jnp.broadcast_to(x[None], (size, *x.shape)), axis, 0, 0, t...  14.8 us
    all_to_all x1, starting transfers between devices, on_device(): lax.all_to_all(mod_part, DP, split_axis=0, concat_axis=1, tiled=True)  13.2 us
    all_to_all x1, waiting for transfers between devices, on_device(): lax.all_to_all(mod_part, DP, split_axis=0, concat_axis=1, tiled=True)  12.4 us
  transfers between devices with their start and end apart: 18, of which 13 were waited for; matrix products, arithmetic and copies ran while one was open for 7% of the time, Pallas kernels for 6%

profile of v10, /device:TPU:6, one launch (start us, length us, event | category | flops | bytes accessed | tf_op | source)
XLA Modules:
  0.0 295.5 jit_solution(3086666811014701051)
XLA Ops:
  8.6 10.9 %collective-permute-start = (bf16[18,3024]{1,0:T(8,128)(2,1)S(1)}, bf16[18,3024]{1,0:T(8,128)(2,1)S(1)}, u32[]{:S(2)}, u32[]{:S(2)}) collective-permute-start(bf16[18,3024]{1,0:T(8,128)(2,1)S(1)} %concatenate.25), channel_id=1, source_target_pairs={{0,4},{4,0},{1,5},{5,1},{2,6},{6,2},{3,7},{7,3},{8,12},{12,8},{9,1... | collective-permute-start | bytes 326600 | tf_op jit(solution)/shard_map/ppermute | solution.py:29
  19.5 3.9 %collective-permute-done = bf16[18,3024]{1,0:T(8,128)(2,1)S(1)} collective-permute-done((bf16[18,3024]{1,0:T(8,128)(2,1)S(1)}, bf16[18,3024]{1,0:T(8,128)(2,1)S(1)}, u32[]{:S(2)}, u32[]{:S(2)}) %collective-permute-start) | collective-permute-done | bytes 108896 | tf_op jit(solution)/shard_map/ppermute | solution.py:29
  25.0 41.5 %all-gather.7.cloned.1.call-done = bf16[4,36,3712]{2,1,0:T(8,128)(2,1)} async-done(((bf16[1,36,3712]{2,1,0:T(8,128)(2,1)}), bf16[4,36,3712]{2,1,0:T(8,128)(2,1)}) %all-gather.7.cloned.1.call-update) | async-done | bytes 1069072 | tf_op jit(solution)/shard_map/all_gather | solution.py:364
  73.1 16.0 %all-to-all-start = ((bf16[64,2,288]{2,1,0:T(2,128)(2,1)}), bf16[64,2,288]{2,1,0:T(2,128)(2,1)S(1)}, u32[]{:S(2)}, u32[]{:S(2)}) async-start(bf16[64,2,288]{2,1,0:T(2,128)(2,1)} %broadcast_in_dim.56), calls=%async_computation | async-start | bytes 196608 | tf_op jit(solution)/shard_map/all_to_all | solution.py:19
  91.2 2.7 collective-permute-start.2
  93.9 9.0 %all-to-all-done = bf16[64,2,288]{2,1,0:T(2,128)(2,1)S(1)} async-done(((bf16[64,2,288]{2,1,0:T(2,128)(2,1)}), bf16[64,2,288]{2,1,0:T(2,128)(2,1)S(1)}, u32[]{:S(2)}, u32[]{:S(2)}) %all-to-all-start) | async-done | bytes 73760 | tf_op jit(solution)/shard_map/all_to_all | solution.py:19
  104.1 3.5 %all-to-all-start.1 = ((bf16[8,36,1024]{2,1,0:T(8,128)(2,1)}), bf16[8,36,1024]{2,1,0:T(8,128)(2,1)S(1)}, u32[]{:S(2)}, u32[]{:S(2)}) async-start(bf16[8,36,1024]{2,1,0:T(8,128)(2,1)} %broadcast_in_dim.57), calls=%async_computation.1 | async-start | bytes 1310720 | tf_op jit(solution)/shard_map/all_to_all | solution.py:19
  107.6 46.5 %all-gather.5.cloned.1.call-done.up_ref.down_ref = bf16[1152,2304]{1,0:T(8,128)(2,1)} async-done(((bf16[144,2304]{1,0:T(8,128)(2,1)}), bf16[1152,2304]{1,0:T(8,128)(2,1)}) %all-gather.5.cloned.1.call-update) | async-done | bytes 5308432 | tf_op jit(solution)/shard_map/all_gather | solution.py:366
  156.0 2.1 fusion.2.change_ref
  159.1 2.4 collective-permute-start.3
  161.5 3.4 %collective-permute-start.4 = (bf16[288,1024]{1,0:T(8,128)(2,1)}, bf16[288,1024]{1,0:T(8,128)(2,1)S(1)}, u32[]{:S(2)}, u32[]{:S(2)}) collective-permute-start(bf16[288,1024]{1,0:T(8,128)(2,1)} %reshape.275), channel_id=1, source_target_pairs={{0,24},{8,0},{16,8},{24,16},{1,25},{9,1},{17,9},{25,17},{2,26},{10... | collective-permute-start | bytes 1769480 | tf_op jit(solution)/shard_map/ppermute | solution.py:24
  165.1 3.0 fusion.5
  168.0 8.9 %collective-permute-done.3 = bf16[288,1024]{1,0:T(8,128)(2,1)S(1)} collective-permute-done((bf16[288,1024]{1,0:T(8,128)(2,1)}, bf16[288,1024]{1,0:T(8,128)(2,1)S(1)}, u32[]{:S(2)}, u32[]{:S(2)}) %collective-permute-start.3) | collective-permute-done | bytes 589856 | tf_op jit(solution)/shard_map/ppermute | solution.py:24
  176.9 3.4 %collective-permute-done.4 = bf16[288,1024]{1,0:T(8,128)(2,1)S(1)} collective-permute-done((bf16[288,1024]{1,0:T(8,128)(2,1)}, bf16[288,1024]{1,0:T(8,128)(2,1)S(1)}, u32[]{:S(2)}, u32[]{:S(2)}) %collective-permute-start.4) | collective-permute-done | bytes 589856 | tf_op jit(solution)/shard_map/ppermute | solution.py:24
  180.3 2.3 collective-permute-start.5
  183.5 3.7 %collective-permute-start.6 = (bf16[144,1024]{1,0:T(8,128)(2,1)S(1)}, bf16[144,1024]{1,0:T(8,128)(2,1)S(1)}, u32[]{:S(2)}, u32[]{:S(2)}) collective-permute-start(bf16[144,1024]{1,0:T(8,128)(2,1)S(1)} %slice.115), channel_id=1, source_target_pairs={{0,24},{8,0},{16,8},{24,16},{1,25},{9,1},{17,9},{25,17},{2,26},{10... | collective-permute-start | bytes 884744 | tf_op jit(solution)/shard_map/ppermute | solution.py:24
  191.4 3.3 %collective-permute-done.6 = bf16[144,1024]{1,0:T(8,128)(2,1)S(1)} collective-permute-done((bf16[144,1024]{1,0:T(8,128)(2,1)S(1)}, bf16[144,1024]{1,0:T(8,128)(2,1)S(1)}, u32[]{:S(2)}, u32[]{:S(2)}) %collective-permute-start.6) | collective-permute-done | bytes 294944 | tf_op jit(solution)/shard_map/ppermute | solution.py:24
  198.2 13.2 %all-to-all-start.2 = ((bf16[64,2,108]{2,1,0:T(2,128)(2,1)}), bf16[64,2,108]{2,1,0:T(2,128)(2,1)S(1)}, u32[]{:S(2)}, u32[]{:S(2)}) async-start(bf16[64,2,108]{2,1,0:T(2,128)(2,1)} %bitcast.12), calls=%async_computation.2 | async-start | bytes 65536 | tf_op jit(solution)/shard_map/all_to_all | solution.py:370
  211.8 12.4 %all-to-all-done.2 = bf16[64,2,108]{2,1,0:T(2,128)(2,1)S(1)} async-done(((bf16[64,2,108]{2,1,0:T(2,128)(2,1)}), bf16[64,2,108]{2,1,0:T(2,128)(2,1)S(1)}, u32[]{:S(2)}, u32[]{:S(2)}) %all-to-all-start.2) | async-done | bytes 27680 | tf_op jit(solution)/shard_map/all_to_all | solution.py:370
  225.1 3.5 %all-to-all-start.3 = ((bf16[4,2,9216]{2,1,0:T(2,128)(2,1)}), bf16[4,2,9216]{2,1,0:T(2,128)(2,1)S(1)}, u32[]{:S(2)}, u32[]{:S(2)}) async-start(bf16[4,2,9216]{2,1,0:T(2,128)(2,1)} %broadcast_in_dim.58), calls=%async_computation.3 | async-start | bytes 294912 | tf_op jit(solution)/shard_map/all_to_all | solution.py:19
  228.7 5.7 %all-to-all-done.3 = bf16[4,2,9216]{2,1,0:T(2,128)(2,1)S(1)} async-done(((bf16[4,2,9216]{2,1,0:T(2,128)(2,1)}), bf16[4,2,9216]{2,1,0:T(2,128)(2,1)S(1)}, u32[]{:S(2)}, u32[]{:S(2)}) %all-to-all-start.3) | async-done | bytes 147488 | tf_op jit(solution)/shard_map/all_to_all | solution.py:19
  237.1 8.8 %attention.1 = bf16[4,288,128]{2,1,0:T(8,128)(2,1)} custom-call(s32[1]{0:T(128)} %bitcast.1.core_ref, bf16[2,256,1152]{2,1,0:T(8,128)(2,1)S(1)} %bitcast.56, f32[2,1,1152]{2,1,0:T(1,128)S(1)} %get-tuple-element.64.shift_ref, f32[2,1,1152]{2,1,0:T(1,128)S(1)} %get-tuple-element.63.scale_ref, bf16[1152,1024]{1,0:T(8,128)(2,1)} %constant_dynamic-update-slice_fusion.mine_ref, ...), custom_call_target="tpu_custom_call" | custom-call | tf_op jit(solution)/shard_map/attention/pallas_call | solution.py:118
  245.9 3.5 %all-to-all-start.4 = ((bf16[4,288,128]{2,1,0:T(8,128)(2,1)}), bf16[4,288,128]{2,1,0:T(8,128)(2,1)S(1)}, u32[]{:S(2)}, u32[]{:S(2)}) async-start(bf16[4,288,128]{2,1,0:T(8,128)(2,1)} %attention.1), calls=%async_computation.4 | async-start | bytes 589824 | tf_op jit(solution)/shard_map/all_to_all | solution.py:405
  249.4 7.1 %all-to-all-done.4.mixed_ref = bf16[4,288,128]{2,1,0:T(8,128)(2,1)S(1)} async-done(((bf16[4,288,128]{2,1,0:T(8,128)(2,1)}), bf16[4,288,128]{2,1,0:T(8,128)(2,1)S(1)}, u32[]{:S(2)}, u32[]{:S(2)}) %all-to-all-start.4) | async-done | bytes 294944 | tf_op jit(solution)/shard_map/all_to_all | solution.py:405
  258.2 3.7 %project.1 = (f32[2,64,1152]{2,1,0:T(8,128)S(1)}, bf16[2,64,1152]{2,1,0:T(8,128)(2,1)S(1)}) custom-call(s32[1]{0:T(128)} %bitcast.base_ref, bf16[4,288,128]{2,1,0:T(8,128)(2,1)S(1)} %all-to-all-done.4.mixed_ref, bf16[1152,1024]{1,0:T(8,128)(2,1)} %constant_dynamic-update-slice_fusion.mine_ref, bf16[1152,1024]{1,0:T(8,128)(2,1)} %collective-permute-done.7.other_ref, ...), custom_call_target="tpu_custom_call" | custom-call | tf_op jit(solution)/shard_map/project/pallas_call | solution.py:162
  261.9 3.3 %collective-permute-start.8 = (bf16[128,1152]{1,0:T(8,128)(2,1)S(1)}, bf16[128,1152]{1,0:T(8,128)(2,1)S(1)}, u32[]{:S(2)}, u32[]{:S(2)}) collective-permute-start(bf16[128,1152]{1,0:T(8,128)(2,1)S(1)} %bitcast.53), channel_id=1, source_target_pairs={{0,1},{1,0},{2,3},{3,2},{4,5},{5,4},{6,7},{7,6},{8,9},{9,8},{10,11... | collective-permute-start | bytes 884744 | tf_op jit(solution)/shard_map/ppermute | solution.py:29
  265.2 2.8 feed_first.2.before_ref
  268.1 2.5 collective-permute-done.8.rows_ref.pair_ref
  270.6 2.8 feed_first.3.pair_before_ref
  273.4 5.4 %feed_second.1 = (f32[128,1152]{1,0:T(8,128)S(1)}, bf16[128,1152]{1,0:T(8,128)(2,1)S(1)}) custom-call(bf16[128,1152]{1,0:T(8,128)(2,1)S(1)} %bitcast.55, bf16[128,1152]{1,0:T(8,128)(2,1)S(1)} %collective-permute-done.8.rows_ref.pair_ref, bf16[1152,2304]{1,0:T(8,128)(2,1)} %collective-permute-done.9.up_ref.down_ref, ...), custom_call_target="tpu_custom_call" | custom-call | tf_op jit(solution)/shard_map/feed_second/pallas_call | solution.py:243
  278.8 3.3 %collective-permute-start.10 = (bf16[128,1152]{1,0:T(8,128)(2,1)S(1)}, bf16[128,1152]{1,0:T(8,128)(2,1)S(1)}, u32[]{:S(2)}, u32[]{:S(2)}) collective-permute-start(bf16[128,1152]{1,0:T(8,128)(2,1)S(1)} %get-tuple-element.27), channel_id=1, source_target_pairs={{0,1},{1,0},{2,3},{3,2},{4,5},{5,4},{6,7},{7,6},{8,9},{9,8},{10,11... | collective-permute-start | bytes 884744 | tf_op jit(solution)/shard_map/ppermute | solution.py:29
  283.0 4.5 %collective-permute-done.10.recv_ref = bf16[128,1152]{1,0:T(8,128)(2,1)S(1)} collective-permute-done((bf16[128,1152]{1,0:T(8,128)(2,1)S(1)}, bf16[128,1152]{1,0:T(8,128)(2,1)S(1)}, u32[]{:S(2)}, u32[]{:S(2)}) %collective-permute-start.10) | collective-permute-done | bytes 294944 | tf_op jit(solution)/shard_map/ppermute | solution.py:29
  (85 shorter events, 30.1 us)
Async XLA Ops:
  6.5 205.0 %copy-start = (bf16[288,2304]{1,0:T(8,128)(2,1)S(1)}, bf16[288,2304]{1,0:T(8,128)(2,1)}, u32[]{:S(2)}) copy-start(bf16[288,2304]{1,0:T(8,128)(2,1)} %param.22) | copy-start | bytes 3981316
  6.5 60.0 %all-gather.7.cloned.1.call-start = ((), (), s32[]{:S(2)}) async-start(), calls=%async_computation.6 | async-start | bytes 1484800 | tf_op jit(solution)/shard_map/all_gather | solution.py:364
  8.6 14.9 %collective-permute-start = (bf16[18,3024]{1,0:T(8,128)(2,1)S(1)}, bf16[18,3024]{1,0:T(8,128)(2,1)S(1)}, u32[]{:S(2)}, u32[]{:S(2)}) collective-permute-start(bf16[18,3024]{1,0:T(8,128)(2,1)S(1)} %concatenate.25), channel_id=1, source_target_pairs={{0,4},{4,0},{1,5},{5,1},{2,6},{6,2},{3,7},{7,3},{8,12},{12,8},{9,1... | collective-permute-start | bytes 326600 | tf_op jit(solution)/shard_map/ppermute | solution.py:29
  23.5 0.7 collective-permute-start.1
  25.0 129.1 %all-gather.5.cloned.1.call-start = ((), (), s32[]{:S(2)}) async-start(), calls=%async_computation.5 | async-start | bytes 5971968 | tf_op jit(solution)/shard_map/all_gather | solution.py:366
  73.1 29.8 %all-to-all-start = ((bf16[64,2,288]{2,1,0:T(2,128)(2,1)}), bf16[64,2,288]{2,1,0:T(2,128)(2,1)S(1)}, u32[]{:S(2)}, u32[]{:S(2)}) async-start(bf16[64,2,288]{2,1,0:T(2,128)(2,1)} %broadcast_in_dim.56), calls=%async_computation | async-start | bytes 196608 | tf_op jit(solution)/shard_map/all_to_all | solution.py:19
  91.2 11.8 %collective-permute-start.2 = (bf16[36,288]{1,0:T(8,128)(2,1)S(1)}, bf16[36,288]{1,0:T(8,128)(2,1)S(1)}, u32[]{:S(2)}, u32[]{:S(2)}) collective-permute-start(bf16[36,288]{1,0:T(8,128)(2,1)S(1)} %pad_maximum_fusion.2), channel_id=1, source_target_pairs={{0,1},{1,0},{2,3},{3,2},{256,259},{257,258},{258,257},{259,256},{4... | collective-permute-start | bytes 62216 | tf_op jit(solution)/shard_map/ppermute | solution.py:351
  104.1 54.1 %all-to-all-start.1 = ((bf16[8,36,1024]{2,1,0:T(8,128)(2,1)}), bf16[8,36,1024]{2,1,0:T(8,128)(2,1)S(1)}, u32[]{:S(2)}, u32[]{:S(2)}) async-start(bf16[8,36,1024]{2,1,0:T(8,128)(2,1)} %broadcast_in_dim.57), calls=%async_computation.1 | async-start | bytes 1310720 | tf_op jit(solution)/shard_map/all_to_all | solution.py:19
  154.1 119.3 %collective-permute-start.9 = (bf16[1152,2304]{1,0:T(8,128)(2,1)}, bf16[1152,2304]{1,0:T(8,128)(2,1)}, u32[]{:S(2)}, u32[]{:S(2)}) collective-permute-start(bf16[1152,2304]{1,0:T(8,128)(2,1)} %all-gather.5.cloned.1.call-done.up_ref.down_ref), channel_id=1, source_target_pairs={{0,256},{256,0},{1,257},{257,1},{2,258},{258,2},{3,259},{259,3},{4... | collective-permute-start | bytes 15925256 | tf_op jit(solution)/shard_map/ppermute | solution.py:29
  159.1 17.8 %collective-permute-start.3 = (bf16[288,1024]{1,0:T(8,128)(2,1)}, bf16[288,1024]{1,0:T(8,128)(2,1)S(1)}, u32[]{:S(2)}, u32[]{:S(2)}) collective-permute-start(bf16[288,1024]{1,0:T(8,128)(2,1)} %reshape.275), channel_id=1, source_target_pairs={{0,8},{8,16},{16,24},{24,0},{1,9},{9,17},{17,25},{25,1},{2,10},{10... | collective-permute-start | bytes 1769480 | tf_op jit(solution)/shard_map/ppermute | solution.py:24
  161.5 18.8 %collective-permute-start.4 = (bf16[288,1024]{1,0:T(8,128)(2,1)}, bf16[288,1024]{1,0:T(8,128)(2,1)S(1)}, u32[]{:S(2)}, u32[]{:S(2)}) collective-permute-start(bf16[288,1024]{1,0:T(8,128)(2,1)} %reshape.275), channel_id=1, source_target_pairs={{0,24},{8,0},{16,8},{24,16},{1,25},{9,1},{17,9},{25,17},{2,26},{10... | collective-permute-start | bytes 1769480 | tf_op jit(solution)/shard_map/ppermute | solution.py:24
  165.1 17.6 %copy-start.5 = (bf16[288,1024]{1,0:T(8,128)(2,1)S(1)}, bf16[288,1024]{1,0:T(8,128)(2,1)}, u32[]{:S(2)}) copy-start(bf16[288,1024]{1,0:T(8,128)(2,1)} %reshape.275) | copy-start | bytes 1769476
  180.3 17.0 %copy-start.6 = (bf16[288,108]{1,0:T(8,128)(2,1)S(1)}, bf16[288,108]{1,0:T(8,128)(2,1)}, u32[]{:S(2)}) copy-start(bf16[288,108]{1,0:T(8,128)(2,1)} %param.21) | copy-start | bytes 186628
  180.3 10.3 %collective-permute-start.5 = (bf16[144,1024]{1,0:T(8,128)(2,1)S(1)}, bf16[144,1024]{1,0:T(8,128)(2,1)S(1)}, u32[]{:S(2)}, u32[]{:S(2)}) collective-permute-start(bf16[144,1024]{1,0:T(8,128)(2,1)S(1)} %slice.114), channel_id=1, source_target_pairs={{0,8},{8,16},{16,24},{24,0},{1,9},{9,17},{17,25},{25,1},{2,10},{10... | collective-permute-start | bytes 884744 | tf_op jit(solution)/shard_map/ppermute | solution.py:24
  183.5 11.1 %collective-permute-start.6 = (bf16[144,1024]{1,0:T(8,128)(2,1)S(1)}, bf16[144,1024]{1,0:T(8,128)(2,1)S(1)}, u32[]{:S(2)}, u32[]{:S(2)}) collective-permute-start(bf16[144,1024]{1,0:T(8,128)(2,1)S(1)} %slice.115), channel_id=1, source_target_pairs={{0,24},{8,0},{16,8},{24,16},{1,25},{9,1},{17,9},{25,17},{2,26},{10... | collective-permute-start | bytes 884744 | tf_op jit(solution)/shard_map/ppermute | solution.py:24
  195.4 40.4 %collective-permute-start.7 = (bf16[1152,1024]{1,0:T(8,128)(2,1)}, bf16[1152,1024]{1,0:T(8,128)(2,1)}, u32[]{:S(2)}, u32[]{:S(2)}) collective-permute-start(bf16[1152,1024]{1,0:T(8,128)(2,1)} %constant_dynamic-update-slice_fusion.mine_ref), channel_id=1, source_target_pairs={{0,256},{256,0},{1,257},{257,1},{2,258},{258,2},{3,259},{259,3},{4... | collective-permute-start | bytes 7077896 | tf_op jit(solution)/shard_map/ppermute | solution.py:29
  198.2 25.9 %all-to-all-start.2 = ((bf16[64,2,108]{2,1,0:T(2,128)(2,1)}), bf16[64,2,108]{2,1,0:T(2,128)(2,1)S(1)}, u32[]{:S(2)}, u32[]{:S(2)}) async-start(bf16[64,2,108]{2,1,0:T(2,128)(2,1)} %bitcast.12), calls=%async_computation.2 | async-start | bytes 65536 | tf_op jit(solution)/shard_map/all_to_all | solution.py:370
  225.1 9.3 %all-to-all-start.3 = ((bf16[4,2,9216]{2,1,0:T(2,128)(2,1)}), bf16[4,2,9216]{2,1,0:T(2,128)(2,1)S(1)}, u32[]{:S(2)}, u32[]{:S(2)}) async-start(bf16[4,2,9216]{2,1,0:T(2,128)(2,1)} %broadcast_in_dim.58), calls=%async_computation.3 | async-start | bytes 294912 | tf_op jit(solution)/shard_map/all_to_all | solution.py:19
  235.8 1.3 copy-start.2
  237.1 28.2 %slice-start = ((s8[5308416]{0:T(1024)(128)(4,1)}), s8[1114112]{0:T(1024)(128)(4,1)S(1)}, s32[]{:S(2)}) async-start(s8[5308416]{0:T(1024)(128)(4,1)} %bitcast.51), calls=%async_computation.7 | async-start | bytes 2228224
  245.9 10.6 %all-to-all-start.4 = ((bf16[4,288,128]{2,1,0:T(8,128)(2,1)}), bf16[4,288,128]{2,1,0:T(8,128)(2,1)S(1)}, u32[]{:S(2)}, u32[]{:S(2)}) async-start(bf16[4,288,128]{2,1,0:T(8,128)(2,1)} %attention.1), calls=%async_computation.4 | async-start | bytes 589824 | tf_op jit(solution)/shard_map/all_to_all | solution.py:405
  256.5 1.8 copy-start.1
  258.2 7.0 %slice-start.1 = ((s8[5308416]{0:T(1024)(128)(4,1)}), s8[4194304]{0:T(1024)(128)(4,1)S(1)}, s32[]{:S(2)}) async-start(s8[5308416]{0:T(1024)(128)(4,1)} %bitcast.51), calls=%async_computation.8 | async-start | bytes 8388608
  261.9 6.1 %copy-start.3 = (f32[2,64,1152]{2,1,0:T(8,128)}, f32[2,64,1152]{2,1,0:T(8,128)S(1)}, u32[]{:S(2)}) copy-start(f32[2,64,1152]{2,1,0:T(8,128)S(1)} %get-tuple-element.28.first_ref) | copy-start | bytes 1769476
  261.9 8.6 %collective-permute-start.8 = (bf16[128,1152]{1,0:T(8,128)(2,1)S(1)}, bf16[128,1152]{1,0:T(8,128)(2,1)S(1)}, u32[]{:S(2)}, u32[]{:S(2)}) collective-permute-start(bf16[128,1152]{1,0:T(8,128)(2,1)S(1)} %bitcast.53), channel_id=1, source_target_pairs={{0,1},{1,0},{2,3},{3,2},{4,5},{5,4},{6,7},{7,6},{8,9},{9,8},{10,11... | collective-permute-start | bytes 884744 | tf_op jit(solution)/shard_map/ppermute | solution.py:29
  273.4 9.4 %copy-start.7 = (bf16[1152,16]{0,1:T(8,128)(2,1)S(1)}, bf16[1152,16]{0,1:T(8,128)(2,1)}, u32[]{:S(2)}) copy-start(bf16[1152,16]{0,1:T(8,128)(2,1)} %param.27) | copy-start | bytes 110596
  273.4 14.1 %copy-start.4 = (f32[2,64,1152]{2,1,0:T(8,128)S(1)}, f32[2,64,1152]{2,1,0:T(8,128)}, u32[]{:S(2)}) copy-start(f32[2,64,1152]{2,1,0:T(8,128)} %copy-done.3) | copy-start | bytes 1769476
  278.8 8.6 %collective-permute-start.10 = (bf16[128,1152]{1,0:T(8,128)(2,1)S(1)}, bf16[128,1152]{1,0:T(8,128)(2,1)S(1)}, u32[]{:S(2)}, u32[]{:S(2)}) collective-permute-start(bf16[128,1152]{1,0:T(8,128)(2,1)S(1)} %get-tuple-element.27), channel_id=1, source_target_pairs={{0,1},{1,0},{2,3},{3,2},{4,5},{5,4},{6,7},{7,6},{8,9},{9,8},{10,11... | collective-permute-start | bytes 884744 | tf_op jit(solution)/shard_map/ppermute | solution.py:29
Sparse Core Ops, SparseCore 0:
  25.1 41.4 all-gather.6
  68.8 85.2 all-gather.4
